TPU v7x, 128 devices: a whole 4x4x4 slice. The times are simulated.
128 devices in a mesh: band: 4 (over z), lev: 32 (over y, x, core).
Axes of the slice: x: 4, y: 4, z: 4, core: 2. Of those that a mesh axis runs over, the one named last changes fastest.
Arguments:
- neutrals: float32 [5, 64, 32, 2880], P(None, 'lev', 'band'), may hold values from -6 to 6
- wind_lon: float32 [64, 32, 2880], P('lev', 'band'), may hold values from -0.15 to 0.15
- wind_lat: float32 [64, 32, 2880], P('lev', 'band'), may hold values from -0.15 to 0.15
- wind_lev: float32 [64, 32, 2880], P('lev', 'band'), may hold values from -0.15 to 0.15
- eddy_coupling: float32 [5, 64], replicated, may hold values from 0.3 to 6
- pair_weight: float32 [32, 32, 2880], P(None, 'band'), may hold values from 0 to 1
- ion_yield: float32 [7, 5], replicated, may hold values from -2.5 to 2.5
- ion_spread: float32 [7], replicated, may hold values from 0.02 to 0.4
- ion_loss: float32 [7], replicated, may hold values from 0.005 to 0.1
- column_order: int32 [4, 23040], P('band'), may hold values from 0 to 23039, each once within a row
- column_units: int32 [32], replicated, may hold values from 1 to 270, 5760 in all
- tube_owner: int32 [32, 270, 1], replicated, may hold values from 0 to 127; in each aligned block of 270 rows (0 to 269, 270 to 539, ..., all dimensions but the last counted through in order) at most 3 rows name the same one
Outputs:
- column_state: float32 [4, 32, 5, 64, 1080], P('band', 'lev')
- ion_lines: float32 [128, 96, 7, 512], P(('band', 'lev'))
Inputs may be any that keep to these rules, and one draw needn't show every extreme that they name: `column_order`: each row lists every column of its band once. `column_units`: the counts sum to 5760; the largest is 270. `tube_owner`: among the 270 slots of one owner no tube owner is named more than 3 times, and some is named exactly that often.
All inputs are finite; a program needn't handle non-finite values.
Results may differ from a plain program's by a relative error of at most 0.0003.
Values sent between devices are 32-bit elements; how exact they have to be, the bound alone decides.
No kernel may reach another device: no remote copies, remote signals or barrier semaphores. Data moves between devices by JAX's collectives and lax.ppermute only.
A program may use at most 192 MiB of HBM per device.

v0:
```python
import jax
import jax.numpy as jnp
from jax import lax
from jax.sharding import PartitionSpec as P

NLEV = 64
TUBE_COLS = 4
TSTEPS = 2
SWEEPS = 8
SECTIONS = 20


HIGHEST = lax.Precision.HIGHEST


def with_halo(cells, sides, width):
    for axis, dim in sides:
        count = lax.axis_size(axis)
        ends = count - 1
        head = lax.slice_in_dim(cells, 0, width, axis=dim)
        tail = lax.slice_in_dim(cells, cells.shape[dim] - width, cells.shape[dim], axis=dim)
        cells = jnp.concatenate(
            [
                lax.ppermute(tail, axis, [(i, (i + 1) % count) for i in range(ends)]),
                cells,
                lax.ppermute(head, axis, [((i + 1) % count, i) for i in range(ends)]),
            ],
            axis=dim,
        )
    return cells


def upwind_faces(courant, upstream, downstream):
    return jnp.maximum(courant, 0.0) * upstream + jnp.minimum(courant, 0.0) * downstream


def step_fluxes(density, wind_lon, ghost_density, lat_ghost, lev_ghost):
    western = jnp.roll(density, 1, axis=3)
    flux_lon = upwind_faces(wind_lon, western, density)
    change = flux_lon - jnp.roll(flux_lon, -1, axis=3)
    across = ghost_density[:, 1:-1]
    courant = lat_ghost[1:-1]
    flux_lat = upwind_faces(courant[:, 1:], across[:, :, :-1], across[:, :, 1:])
    change = change + flux_lat[:, :, :-1] - flux_lat[:, :, 1:]
    upward = ghost_density[:, :, 1:-1]
    courant = lev_ghost[:, 1:-1]
    flux_lev = upwind_faces(courant[1:], upward[:, :-1], upward[:, 1:])
    change = change + flux_lev[:, :-1] - flux_lev[:, 1:]
    return density + change


def transport_once(density, wind_lon, wind_lat, wind_lev):
    species = density.shape[0]
    stacked = jnp.concatenate([density, wind_lon[None], wind_lat[None], wind_lev[None]], 0)
    padded = with_halo(stacked, (("band", 2), ("lev", 1)), 1)
    return step_fluxes(
        density, wind_lon, padded[:species], padded[species + 1], padded[species + 2]
    )


def vertical_solve(density, eddy_coupling):
    zero_edge = jnp.zeros((eddy_coupling.shape[0], 1), jnp.float32)
    coupling_below = jnp.concatenate([zero_edge, eddy_coupling[:, 1:]], 1)[:, :, None]
    coupling_above = jnp.concatenate([eddy_coupling[:, 1:], zero_edge], 1)[:, :, None]
    diagonal = 1.0 + coupling_below + coupling_above
    iterate = density
    zero_layer = jnp.zeros_like(density[:, :1])
    for sweep_index in range(SWEEPS):
        beneath = jnp.concatenate([zero_layer, iterate[:, :-1]], 1)
        overhead = jnp.concatenate([iterate[:, 1:], zero_layer], 1)
        iterate = (density + coupling_below * beneath + coupling_above * overhead) / diagonal
    return iterate


def interpolate(ion_yield, neutral_block, weight_block):
    paired = (
        weight_block * neutral_block[..., 0::2] + (1.0 - weight_block) * neutral_block[..., 1::2]
    )
    return jnp.einsum("is,...scp->...icp", ion_yield, paired, precision=HIGHEST)


def line_diffusion(source, ion_spread, ion_loss):
    spread_rate = ion_spread[:, None]
    loss_rate = ion_loss[:, None]

    def advance(section_index, density):
        left_side = jnp.concatenate([density[..., :1], density[..., :-1]], -1)
        right_side = jnp.concatenate([density[..., 1:], density[..., -1:]], -1)
        return (
            density
            + spread_rate * (left_side - 2.0 * density + right_side)
            + source
            - loss_rate * density
        )

    return lax.fori_loop(0, SECTIONS, advance, jnp.zeros_like(source))


def on_device(
    neutrals,
    wind_lon,
    wind_lat,
    wind_lev,
    eddy_coupling,
    pair_weight,
    ion_yield,
    ion_spread,
    ion_loss,
    column_order,
    column_units,
    tube_owner,
):
    species = neutrals.shape[0]
    ion_count = ion_yield.shape[0]
    density = neutrals
    for substep in range(TSTEPS):
        density = transport_once(density, wind_lon, wind_lat, wind_lev)
    owners = lax.axis_size("lev")
    band_count = lax.axis_size("band")
    peer_count = owners * band_count
    band_columns = density.shape[2] * density.shape[3]
    tube_slots = tube_owner.shape[1]
    column_slots = tube_slots * TUBE_COLS
    slot_most = max(2, (tube_slots + peer_count - 1) // peer_count)
    pair_count = NLEV // 2
    starts = jnp.cumsum(column_units) - column_units
    slot_ids = jnp.arange(column_slots, dtype=jnp.int32)
    positions = jnp.minimum(TUBE_COLS * starts[:, None] + slot_ids[None, :], band_columns - 1)
    live_slots = (slot_ids[None, :] < TUBE_COLS * column_units[:, None]).astype(jnp.float32)
    column_ids = column_order[0][positions]
    flat_density = density.reshape(species, density.shape[1], band_columns)
    outgoing = jnp.take(flat_density, column_ids, axis=2) * live_slots[None, None]
    columns = vertical_solve(
        lax.all_to_all(outgoing, "lev", split_axis=2, concat_axis=1, tiled=True)[:, :, 0],
        eddy_coupling,
    )
    owner_index = lax.axis_index("lev")
    own_ids = column_ids[owner_index]
    own_weights = jnp.take(pair_weight.reshape(pair_count, band_columns), own_ids, axis=1)
    neutral_blocks = jnp.transpose(
        columns.reshape(species, NLEV, tube_slots, TUBE_COLS), (2, 0, 3, 1)
    )
    weight_blocks = jnp.transpose(own_weights.reshape(pair_count, tube_slots, TUBE_COLS), (1, 2, 0))
    destinations = tube_owner[owner_index, :, 0]
    device_ids = jnp.arange(peer_count, dtype=jnp.int32)
    matches = (destinations[:, None] == device_ids[None, :]).astype(jnp.int32)
    rank_of = jnp.sum(jnp.cumsum(matches, 0) * matches, 1) - 1
    empty_table = jnp.full((peer_count * slot_most,), tube_slots, jnp.int32)
    sources_of = empty_table.at[destinations * slot_most + rank_of].set(
        jnp.arange(tube_slots, dtype=jnp.int32)
    )
    tube_rows = jnp.concatenate(
        [neutral_blocks.reshape(tube_slots, -1), weight_blocks.reshape(tube_slots, -1)], 1
    )
    row_width = tube_rows.shape[1]
    tube_rows = jnp.concatenate([tube_rows, jnp.zeros((1, row_width), jnp.float32)], 0)
    outgoing_tubes = tube_rows[sources_of]
    segment = TUBE_COLS * pair_count
    received = lax.all_to_all(
        outgoing_tubes.reshape(peer_count, slot_most, row_width),
        ("band", "lev"),
        split_axis=0,
        concat_axis=0,
        tiled=True,
    )
    items = received.shape[1]
    split_at = species * TUBE_COLS * NLEV
    neutral_part = received[:, :, :split_at].reshape(peer_count, items, species, TUBE_COLS, NLEV)
    weight_part = received[:, :, split_at:].reshape(peer_count, items, 1, TUBE_COLS, pair_count)
    sources = interpolate(ion_yield, neutral_part, weight_part).reshape(
        peer_count, items, ion_count, segment
    )
    sources = sources.reshape(band_count, owners, items, ion_count, segment)
    sources = jnp.transpose(sources, (1, 2, 3, 0, 4)).reshape(
        owners, items, ion_count, band_count * segment
    )
    lines = line_diffusion(sources, ion_spread, ion_loss)
    column_state = columns.reshape(1, 1, species, NLEV, column_slots)
    ion_lines = lines.reshape(1, owners * slot_most, ion_count, band_count * segment)
    return (column_state, ion_lines)


def solution(mesh):
    placed = (
        P(None, "lev", "band", None),
        P("lev", "band", None),
        P("lev", "band", None),
        P("lev", "band", None),
        P(),
        P(None, "band", None),
        P(),
        P(),
        P(),
        P("band", None),
        P(),
        P(),
    )
    return jax.shard_map(
        on_device,
        mesh=mesh,
        in_specs=placed,
        out_specs=(P("band", "lev", None, None, None), P(("band", "lev"), None, None, None)),
        check_vma=False,
    )
```

profile of v0, /device:TPU:1, one launch (start us, length us, event | category | flops | bytes accessed | tf_op | source)
XLA Modules:
  0.0 631.3 jit_solution(12932715896208470372)
XLA Ops:
  5.3 4.4 collective-permute-start
  17.5 177.2 %gather_fusion = s32[34560]{0:T(1024)S(1)} fusion(s32[23040]{0:T(1024)S(1)} %reduce, s32[34816]{0:T(1024)} %pad_clamp_fusion.1), kind=kCustom, calls=%fused_computation | custom fusion | bytes 414720 | tf_op jit(solution)/shard_map/gather | solution.py:130
  197.6 8.1 %copy.126 = f32[32,8,2880]{0,2,1:T(8,128)} copy(f32[32,8,2880]{2,1,0:T(8,128)} %param.19) | data formatting | bytes 5898240 | tf_op args[5]
  205.7 6.7 %gather_fusion.2 = f32[1080,32]{1,0:T(8,128)S(1)} fusion(f32[32,23040]{0,1:T(8,128)} %bitcast.84, s32[2048]{0:T(1024)S(1)} %pad_clamp_fusion.2), kind=kCustom, calls=%fused_computation.2 | custom fusion | bytes 280800 | tf_op jit(solution)/shard_map/jit(_take)/gather | solution.py:139
  227.2 6.0 collective-permute-done.2
  239.2 4.5 multiply_add_fusion.1
  246.5 4.3 collective-permute-start.4
  261.3 4.3 collective-permute-start.6
  269.9 6.3 collective-permute-done.6
  282.2 4.5 multiply_add_fusion
  288.5 22.3 %copy.119 = f32[5,2,8,2880]{0,1,3,2:T(2,128)} copy(f32[5,2,8,2880]{3,1,2,0:T(2,128)S(1)} %fusion.28) | data formatting | bytes 1843200 | tf_op jit(solution)/shard_map/add | solution.py:49
  310.8 95.9 %gather_fusion.1 = f32[34560,5,2]{1,2,0:T(2,128)} fusion(f32[5,2,23040]{0,1,2:T(2,128)} %bitcast.73, s32[34816]{0:T(1024)S(1)} %pad_clamp_fusion), kind=kCustom, calls=%fused_computation.1 | custom fusion | bytes 2903040 | tf_op jit(solution)/shard_map/jit(_take)/gather | solution.py:132
  406.7 29.6 %copy.140 = f32[32,1080,5,2]{1,0,3,2:T(8,128)S(1)} copy(f32[32,1080,5,2]{2,3,1,0:T(2,128)} %bitcast.72) | data formatting | bytes 2764800 | tf_op jit(solution)/shard_map/jit(_take)/gather | solution.py:132
  438.7 10.3 %all-to-all-start = ((f32[5,2,32,1080]{3,1,0,2:T(2,128)}), f32[5,2,32,1080]{3,1,0,2:T(2,128)S(1)}, u32[]{:S(2)}, u32[]{:S(2)}) async-start(f32[5,2,32,1080]{3,1,0,2:T(2,128)} %copy.121), calls=%async_computation | async-start | bytes 2949120 | tf_op jit(solution)/shard_map/all_to_all | solution.py:134
  453.3 16.7 %all-to-all-done = f32[5,2,32,1080]{3,1,0,2:T(2,128)S(1)} async-done(((f32[5,2,32,1080]{3,1,0,2:T(2,128)}), f32[5,2,32,1080]{3,1,0,2:T(2,128)S(1)}, u32[]{:S(2)}, u32[]{:S(2)}) %all-to-all-start) | async-done | bytes 1382432 | tf_op jit(solution)/shard_map/all_to_all | solution.py:134
  489.4 4.3 reshape.267
  493.8 7.1 %all-to-all-start.1 = ((f32[128,3,1408]{2,1,0:T(4,128)}), f32[128,3,1408]{2,1,0:T(4,128)}, u32[]{:S(2)}, u32[]{:S(2)}) async-start(f32[128,3,1408]{2,1,0:T(4,128)} %reshape.267), calls=%async_computation.1 | async-start | bytes 5767168 | tf_op jit(solution)/shard_map/all_to_all | solution.py:159
  500.9 38.4 %all-to-all-done.1 = f32[128,3,1408]{2,1,0:T(4,128)} async-done(((f32[128,3,1408]{2,1,0:T(4,128)}), f32[128,3,1408]{2,1,0:T(4,128)}, u32[]{:S(2)}, u32[]{:S(2)}) %all-to-all-start.1) | async-done | bytes 2162720 | tf_op jit(solution)/shard_map/all_to_all | solution.py:159
  543.1 4.0 copy.133
  547.1 7.4 %slice.319 = f32[128,3,5,4,32]{0,4,3,2,1:T(8,128)S(1)} slice(f32[128,3,5,4,64]{0,4,3,2,1:T(8,128)} %bitcast.87), slice={[0:128:1], [0:3:1], [0:5:1], [0:4:1], [0:64:2]} | slice | bytes 1966080 | tf_op jit(solution)/shard_map/slice | solution.py:77
  554.5 8.7 %slice.320 = f32[128,3,5,4,32]{0,4,3,2,1:T(8,128)} slice(f32[128,3,5,4,64]{0,4,3,2,1:T(8,128)} %bitcast.88), slice={[0:128:1], [0:3:1], [0:5:1], [0:4:1], [1:64:2]} | slice | bytes 1966080 | tf_op jit(solution)/shard_map/slice | solution.py:77
  567.8 4.1 reshape.317
  572.0 6.0 copy.141
  581.8 47.2 %while.11 = (s32[]{:T(128)}, f32[32,3,7,512]{3,2,1,0:T(8,128)S(1)}, f32[7]{0:T(128)S(1)}, f32[32,3,7,512]{3,2,1,0:T(8,128)S(1)}, f32[7]{0:T(128)S(1)}, /*index=5*/s32[]{:T(128)}, s32[]{:T(128)}) while((s32[]{:T(128)}, f32[32,3,7,512]{3,2,1,0:T(8,128)S(1)}, f32[7]{0:T(128)S(1)}, f32[32,3,7,512]{3,2,1,0:T(8,128)S(1)}, ...), condition=%wide.region_6.7_spmd.clone, body=%wide.region_5.6_spmd.clone.sunk | while | flops 4128771 | bytes 15138960 | solution.py:96
  (252 shorter events, 147.1 us)
Async XLA Ops:
  0.6 16.7 %copy-start = (s32[1,23040]{1,0:T(1,128)S(1)}, s32[1,23040]{1,0:T(1,128)}, u32[]{:S(2)}) copy-start(s32[1,23040]{1,0:T(1,128)} %param.23) | copy-start | bytes 276484
  3.6 7.4 %copy-start.10 = (f32[2,8,2880]{2,1,0:T(8,128)S(1)}, f32[2,8,2880]{2,1,0:T(8,128)}, u32[]{:S(2)}) copy-start(f32[2,8,2880]{2,1,0:T(8,128)} %param.15) | copy-start | bytes 552964
  4.5 6.8 %copy-start.6 = (f32[5,2,8,2880]{3,2,1,0:T(8,128)S(1)}, f32[5,2,8,2880]{3,2,1,0:T(8,128)}, u32[]{:S(2)}) copy-start(f32[5,2,8,2880]{3,2,1,0:T(8,128)} %param.14) | copy-start | bytes 2764804
  5.3 209.5 %collective-permute-start = (f32[8,2,1,2880]{3,1,2,0:T(2,128)}, f32[8,2,1,2880]{3,1,2,0:T(2,128)S(1)}, u32[]{:S(2)}, u32[]{:S(2)}) collective-permute-start(f32[8,2,1,2880]{3,1,2,0:T(2,128)} %get-tuple-element.96), channel_id=1, source_target_pairs={{0,32},{32,64},{64,96},{1,33},{33,65},{65,97},{2,34},{34,66},{66,9... | collective-permute-start | bytes 552968 | tf_op jit(solution)/shard_map/ppermute | solution.py:24
  9.7 205.1 %collective-permute-start.1 = (f32[8,2,1,2880]{3,1,2,0:T(2,128)}, f32[8,2,1,2880]{3,1,2,0:T(2,128)S(1)}, u32[]{:S(2)}, u32[]{:S(2)}) collective-permute-start(f32[8,2,1,2880]{3,1,2,0:T(2,128)} %get-tuple-element.97), channel_id=1, source_target_pairs={{32,0},{64,32},{96,64},{33,1},{65,33},{97,65},{34,2},{66,34},{98,6... | collective-permute-start | bytes 552968 | tf_op jit(solution)/shard_map/ppermute | solution.py:26
  12.6 182.2 %copy-start.2 = (f32[5,2,8,2880]{3,1,2,0:T(2,128)}, f32[5,2,8,2880]{3,1,2,0:T(2,128)S(1)}, u32[]{:S(2)}) copy-start(f32[5,2,8,2880]{3,1,2,0:T(2,128)S(1)} %fusion.30) | copy-start | bytes 2764804
  218.6 14.5 %collective-permute-start.2 = (f32[8,1,10,2880]{3,0,2,1:T(8,128)S(1)}, f32[8,1,10,2880]{3,0,2,1:T(8,128)S(1)}, u32[]{:S(2)}, u32[]{:S(2)}) collective-permute-start(f32[8,1,10,2880]{3,0,2,1:T(8,128)S(1)} %copy.100), channel_id=1, source_target_pairs={{0,1},{1,2},{2,3},{3,4},{4,5},{5,6},{6,7},{7,8},{8,9},{9,10},{10,1... | collective-permute-start | bytes 2764808 | tf_op jit(solution)/shard_map/ppermute | solution.py:24
  222.7 15.0 %collective-permute-start.3 = (f32[8,1,10,2880]{3,0,2,1:T(8,128)S(1)}, f32[8,1,10,2880]{3,0,2,1:T(8,128)S(1)}, u32[]{:S(2)}, u32[]{:S(2)}) collective-permute-start(f32[8,1,10,2880]{3,0,2,1:T(8,128)S(1)} %copy.101), channel_id=1, source_target_pairs={{1,0},{2,1},{3,2},{4,3},{5,4},{6,5},{7,6},{8,7},{9,8},{10,9},{11,1... | collective-permute-start | bytes 2764808 | tf_op jit(solution)/shard_map/ppermute | solution.py:26
  239.1 4.6 copy-start.3
  239.1 4.6 slice-start
  239.1 4.6 copy-start.7
  239.1 4.6 copy-start.8
  246.5 7.8 %collective-permute-start.4 = (f32[8,2,1,2880]{3,0,2,1:T(8,128)S(1)}, f32[8,2,1,2880]{3,0,2,1:T(8,128)S(1)}, u32[]{:S(2)}, u32[]{:S(2)}) collective-permute-start(f32[8,2,1,2880]{3,0,2,1:T(8,128)S(1)} %copy.107), channel_id=1, source_target_pairs={{0,32},{32,64},{64,96},{1,33},{33,65},{65,97},{2,34},{34,66},{66,9... | collective-permute-start | bytes 552968 | tf_op jit(solution)/shard_map/ppermute | solution.py:24
  250.8 6.5 %collective-permute-start.5 = (f32[8,2,1,2880]{3,0,2,1:T(8,128)S(1)}, f32[8,2,1,2880]{3,0,2,1:T(8,128)S(1)}, u32[]{:S(2)}, u32[]{:S(2)}) collective-permute-start(f32[8,2,1,2880]{3,0,2,1:T(8,128)S(1)} %copy.108), channel_id=1, source_target_pairs={{32,0},{64,32},{96,64},{33,1},{65,33},{97,65},{34,2},{66,34},{98,6... | collective-permute-start | bytes 552968 | tf_op jit(solution)/shard_map/ppermute | solution.py:26
  253.3 6.4 %copy-start.4 = (f32[5,2,8,2880]{3,1,2,0:T(2,128)}, f32[5,2,8,2880]{3,1,2,0:T(2,128)S(1)}, u32[]{:S(2)}) copy-start(f32[5,2,8,2880]{3,1,2,0:T(2,128)S(1)} %fusion.31) | copy-start | bytes 2764804
  261.3 14.9 %collective-permute-start.6 = (f32[8,1,10,2880]{3,0,2,1:T(8,128)S(1)}, f32[8,1,10,2880]{3,0,2,1:T(8,128)S(1)}, u32[]{:S(2)}, u32[]{:S(2)}) collective-permute-start(f32[8,1,10,2880]{3,0,2,1:T(8,128)S(1)} %copy.113), channel_id=1, source_target_pairs={{0,1},{1,2},{2,3},{3,4},{4,5},{5,6},{6,7},{7,8},{8,9},{9,10},{10,1... | collective-permute-start | bytes 2764808 | tf_op jit(solution)/shard_map/ppermute | solution.py:24
  265.7 15.0 %collective-permute-start.7 = (f32[8,1,10,2880]{3,0,2,1:T(8,128)S(1)}, f32[8,1,10,2880]{3,0,2,1:T(8,128)S(1)}, u32[]{:S(2)}, u32[]{:S(2)}) collective-permute-start(f32[8,1,10,2880]{3,0,2,1:T(8,128)S(1)} %copy.114), channel_id=1, source_target_pairs={{1,0},{2,1},{3,2},{4,3},{5,4},{6,5},{7,6},{8,7},{9,8},{10,9},{11,1... | collective-permute-start | bytes 2764808 | tf_op jit(solution)/shard_map/ppermute | solution.py:26
  282.2 4.6 copy-start.5
  282.2 4.6 slice-start.1
  406.7 29.6 %copy-start.11 = (f32[32,1080]{1,0:T(8,128)S(1)}, f32[32,1080]{1,0:T(8,128)}, u32[]{:S(2)}) copy-start(f32[32,1080]{1,0:T(8,128)} %get-tuple-element.131) | copy-start | bytes 414724
  438.7 10.3 %copy-start.9 = (f32[32,270,4]{1,0,2:T(8,128)S(1)}, f32[32,270,4]{1,0,2:T(8,128)}, u32[]{:S(2)}) copy-start(f32[32,270,4]{1,0,2:T(8,128)} %copy.127) | copy-start | bytes 414724
  438.7 10.3 %copy-start.17 = (f32[5,64]{1,0:T(8,128)S(1)}, f32[5,64]{1,0:T(8,128)}, u32[]{:S(2)}) copy-start(f32[5,64]{1,0:T(8,128)} %param.18) | copy-start | bytes 3844
  438.7 31.3 %all-to-all-start = ((f32[5,2,32,1080]{3,1,0,2:T(2,128)}), f32[5,2,32,1080]{3,1,0,2:T(2,128)S(1)}, u32[]{:S(2)}, u32[]{:S(2)}) async-start(f32[5,2,32,1080]{3,1,0,2:T(2,128)} %copy.121), calls=%async_computation | async-start | bytes 2949120 | tf_op jit(solution)/shard_map/all_to_all | solution.py:134
  493.8 45.6 %all-to-all-start.1 = ((f32[128,3,1408]{2,1,0:T(4,128)}), f32[128,3,1408]{2,1,0:T(4,128)}, u32[]{:S(2)}, u32[]{:S(2)}) async-start(f32[128,3,1408]{2,1,0:T(4,128)} %reshape.267), calls=%async_computation.1 | async-start | bytes 5767168 | tf_op jit(solution)/shard_map/all_to_all | solution.py:159
  (7 other events, 14.6 us)
where the time goes:
time: 641 us; the launch traced here: 631 us
  local copies, waits for them, and re-layouts  437 us (68%)
  waiting for transfers between devices  77.3 us (12%)
  other arithmetic  70.6 us (11%)
  starting transfers between devices  41.4 us (6%)
    gather x3, local copies, waits for them, and re-layouts, on_device(): column_ids = column_order[0][positions]  178 us
    gather x2, local copies, waits for them, and re-layouts, on_device(): jnp.take(flat_density, column_ids, axis=2) * live_slots[None, None]  126 us
    all_to_all x1, waiting for transfers between devices, on_device(): lax.all_to_all(outgoing_tubes.reshape(peer_count, slot_most, row_width),...  38.4 us
    sub x20, other arithmetic, advance(): density + spread_rate * (left_side - 2.0 * density + right_side) + source  28.3 us
    add x1, local copies, waits for them, and re-layouts, step_fluxes(): return density + change  22.3 us
    ppermute x4, starting transfers between devices, with_halo(): lax.ppermute(tail, axis, [(i, (i + 1) % count) for i in range(ends)])  16.9 us
    all_to_all x1, waiting for transfers between devices, on_device(): lax.all_to_all(outgoing, 'lev', split_axis=2, concat_axis=1, tiled=True)  16.7 us
    unnamed x44, local copies, waits for them, and re-layouts  16.7 us
  transfers between devices with their start and end apart: 10, of which 7 were waited for; matrix products, arithmetic and copies ran while one was open for 34% of the time, Pallas kernels for 0%

commit v1 on v0

v1 whole, which is shorter than its diff:
```python
import functools

import jax
import jax.numpy as jnp
import numpy as np
from jax import lax
from jax.experimental import pallas as pl
from jax.experimental.pallas import tpu as pltpu
from jax.sharding import PartitionSpec as P

SPECIES = 5
IONS = 7
NLON = 2880
NLEV = 64
PAIRS = 32
BAND_LATS = 8
TSTEPS = 2
SWEEPS = 8
SECTIONS = 20
TUBE_COLS = 4
PEERS = 128
PEER_SLOTS = 3
COL_CAP = 1080
TUBE_CAP = 270
BAND_COLS = BAND_LATS * NLON
LINE_PTS = 512

LANES = 128
LON_BLOCKS = 23
LON_PAD = LON_BLOCKS * LANES
CHIP_LEVS = 4
PLANES = 12
GROUPS = 6
MSG_ROWS = 192
SLOT_BLOCKS = 9
SLOTS_PAD = SLOT_BLOCKS * LANES
ORDER_PAD = BAND_COLS + LANES
UNROLL = 64
ZERO_TUBE = SLOT_BLOCKS * 32
ITEM_ROWS = 16

f32 = jnp.float32
VMEM = pl.BlockSpec(memory_space=pltpu.VMEM)
SMEM = pl.BlockSpec(memory_space=pltpu.SMEM)
ANY = pl.BlockSpec(memory_space=pl.ANY)


def call(kernel, out_shape, in_specs, out_specs, scratch=(), name=None, flops=0):
    return pl.pallas_call(
        kernel,
        out_shape=out_shape,
        in_specs=in_specs,
        out_specs=out_specs,
        scratch_shapes=list(scratch),
        name=name,
        cost_estimate=pl.CostEstimate(flops=flops, bytes_accessed=1 << 20, transcendentals=0),
        compiler_params=pltpu.CompilerParams(vmem_limit_bytes=60 * 1024 * 1024),
    )


def sds(shape, dtype=f32):
    return jax.ShapeDtypeStruct(shape, dtype)


def upwind(courant_plus, courant_minus, upstream, downstream):
    return courant_plus * upstream + courant_minus * downstream


def transport_kernel(
    n_ref, wlon_ref, wlat_ref, wlev_ref, south_ref, north_ref, below_ref, above_ref, wlat_n_ref, wlev_up_ref,
    *outs, last,
):
    def split(c):
        return jnp.maximum(c, 0.0), jnp.minimum(c, 0.0)

    def shift_west(x):
        return jnp.concatenate([x[:, NLON - 1 :], x[:, : NLON - 1]], axis=1)

    def shift_east(x):
        return jnp.concatenate([x[:, 1:], x[:, :1]], axis=1)

    for j in range(2):

        @pl.loop(0, SPECIES)
        def _(s):
            x = n_ref[s, j]
            flux = upwind(*split(wlon_ref[j]), shift_west(x), x)
            total = x + (flux - shift_east(flux))
            southern = jnp.concatenate([south_ref[s, j], x[: BAND_LATS - 1]], axis=0)
            flux = upwind(*split(wlat_ref[j]), southern, x)
            edge = upwind(*split(wlat_n_ref[j]), x[BAND_LATS - 1 :], north_ref[s, j])
            total = total + (flux - jnp.concatenate([flux[1:], edge], axis=0))
            beneath = below_ref[s] if j == 0 else n_ref[s, 0]
            overhead = n_ref[s, 1] if j == 0 else above_ref[s]
            over_wind = wlev_ref[1] if j == 0 else wlev_up_ref[...]
            flux = upwind(*split(wlev_ref[j]), beneath, x)
            total = total + (flux - upwind(*split(over_wind), x, overhead))
            if last:
                row = pl.multiple_of((j * SPECIES + s) * BAND_LATS, BAND_LATS)
                for blk in range(LON_BLOCKS):
                    wide = min(LANES, NLON - blk * LANES)
                    outs[0][blk, pl.ds(row, BAND_LATS), :wide] = total[:, blk * LANES : blk * LANES + wide]
            else:
                outs[0][s, j] = total
                outs[1 + j][s] = total
                outs[3][s, j] = total[:1]
                outs[4][s, j] = total[BAND_LATS - 1 :]


def transport_step(density, winds, halo, last):
    if last:
        out_shape = (sds((LON_BLOCKS, 2 * SPECIES * BAND_LATS, LANES)),)
    else:
        out_shape = (
            sds((SPECIES, 2, BAND_LATS, NLON)),
            sds((SPECIES, BAND_LATS, NLON)),
            sds((SPECIES, BAND_LATS, NLON)),
            sds((SPECIES, 2, 1, NLON)),
            sds((SPECIES, 2, 1, NLON)),
        )
    return call(
        functools.partial(transport_kernel, last=last),
        out_shape,
        [VMEM] * 10,
        tuple([VMEM] * len(out_shape)),
        name="transport",
        flops=4_000_000,
    )(density, *winds, *halo)


def prepare_kernel(units_ref, owner_ref, rows_ref, sel_ref, weight_ref, table_ref, own_ref, count, blocks, table, picked):
    @pl.loop(0, PEERS * PEER_SLOTS)
    def _(i):
        table_ref[i] = ZERO_TUBE

    @pl.loop(0, PEERS)
    def _(i):
        count[i] = 0

    @pl.loop(0, units_ref[0])
    def _(u):
        dest = owner_ref[u]
        rank = count[dest]
        count[dest] = rank + 1
        table_ref[dest * PEER_SLOTS + rank] = u

    for blk in range(LON_BLOCKS):
        wide = min(LANES, NLON - blk * LANES)
        blocks[blk, :, :wide] = weight_ref[:, blk * LANES : blk * LANES + wide]

    @pl.loop(0, BAND_LATS)
    def _(lat):
        for g in range(6):
            parts = [
                blocks[min(4 * g + i, LON_BLOCKS - 1), pl.ds(lat, PAIRS, stride=BAND_LATS), :] for i in range(4)
            ]
            start = pl.multiple_of((lat * 6 + g) * LANES, LANES)
            table[pl.ds(start, LANES), :] = jnp.concatenate(parts, axis=0).T

    @pl.loop(0, SLOTS_PAD // UNROLL)
    def _(step):
        base = pl.multiple_of(step * UNROLL, UNROLL)
        for i in range(UNROLL):
            picked[pl.ds(base + i, 1), :] = table[pl.ds(rows_ref[base + i], 1), :]

    for blk in range(SLOT_BLOCKS):
        turned = picked[blk * LANES : (blk + 1) * LANES, :].T
        which = sel_ref[blk : blk + 1, :]
        kept = turned[:PAIRS]
        for i in range(1, 4):
            kept = jnp.where(which == i, turned[i * PAIRS : (i + 1) * PAIRS], kept)
        own_ref[blk] = kept


def prepare(units, owners, rows, sel, weights):
    return call(
        prepare_kernel,
        (sds((PEERS * PEER_SLOTS,), jnp.int32), sds((SLOT_BLOCKS, PAIRS, LANES))),
        [SMEM, SMEM, SMEM, VMEM, VMEM],
        (SMEM, VMEM),
        [
            pltpu.SMEM((PEERS,), jnp.int32),
            pltpu.VMEM((LON_BLOCKS, PAIRS * BAND_LATS, LANES), f32),
            pltpu.VMEM((BAND_LATS * 6 * LANES, LANES), f32),
            pltpu.VMEM((SLOTS_PAD, LANES), f32),
        ],
        name="prepare",
        flops=20_000_000,
    )(units, owners, rows, sel, weights)


def pack_kernel(core_ref, starts_ref, units_ref, order_hbm, mine_ref, other_ref, msg_ref, order, planes, table, sem):
    fetch = pltpu.make_async_copy(order_hbm, order, sem)
    fetch.start()
    core = core_ref[0]
    for source, side in ((mine_ref, core), (other_ref, 1 - core)):

        @pl.loop(0, LON_BLOCKS)
        def _(blk):
            for j in range(2):
                for i in range(PLANES):
                    row = pl.multiple_of(((2 * side + j) * PLANES + i) * BAND_LATS, BAND_LATS)
                    from_row = (j * SPECIES + i % SPECIES) * BAND_LATS
                    planes[blk, pl.ds(row, BAND_LATS), :] = source[blk, from_row : from_row + BAND_LATS, :]

    @pl.loop(0, LON_BLOCKS)
    def _(blk):
        for lat in range(BAND_LATS):
            parts = [
                planes[blk, pl.ds((jj * PLANES + first) * BAND_LATS + lat, 8, stride=BAND_LATS), :]
                for jj in range(CHIP_LEVS)
                for first in (0, 3, 1, 4)
            ]
            start = pl.multiple_of((lat * LON_BLOCKS + blk) * LANES, LANES)
            table[pl.ds(start, LANES), :] = jnp.concatenate(parts, axis=0).T

    fetch.wait()
    lane = lax.broadcasted_iota(jnp.int32, (1, LANES), 1)
    group_of = lax.div(lax.rem(lane, 32), SPECIES)

    @pl.loop(0, 16 * GROUPS)
    def _(turn):
        peer = lax.div(turn, GROUPS)
        group = turn - peer * GROUPS
        owner = 2 * peer + core
        live = jnp.clip(TUBE_COLS * units_ref[owner] - MSG_ROWS * group, 0, MSG_ROWS)
        first = TUBE_COLS * starts_ref[owner] + MSG_ROWS * group
        mask = group_of == group

        @pl.loop(0, lax.div(live + (UNROLL - 1), UNROLL))
        def _(step):
            base = first + step * UNROLL
            row = pl.multiple_of(peer * MSG_ROWS + step * UNROLL, UNROLL)
            for i in range(UNROLL):
                value = table[pl.ds(order[base + i], 1), :]
                pltpu.store(msg_ref.at[pl.ds(row + i, 1), :], value, mask=mask)


def pack(core, starts, units, order, mine, other):
    return call(
        pack_kernel,
        sds((16 * MSG_ROWS, LANES)),
        [SMEM, SMEM, SMEM, ANY, VMEM, VMEM],
        VMEM,
        [
            pltpu.SMEM((ORDER_PAD,), jnp.int32),
            pltpu.VMEM((LON_BLOCKS, CHIP_LEVS * PLANES * BAND_LATS, LANES), f32),
            pltpu.VMEM((BAND_LATS * LON_PAD, LANES), f32),
            pltpu.SemaphoreType.DMA,
        ],
        name="pack",
        flops=40_000_000,
    )(core, starts, units, order, mine, other)


def solve_kernel(
    units_ref, table_ref, got_ref, lower_ref, upper_ref, inv_ref, weight_ref,
    state_ref, items_ref, turned, solved, wide, tubes,
):
    live = TUBE_COLS * units_ref[0]
    lane = lax.broadcasted_iota(jnp.int32, (1, LANES), 1)

    @pl.loop(0, 16)
    def _(m):
        row = pl.multiple_of(m * MSG_ROWS, MSG_ROWS)
        out = pl.multiple_of(m * LANES, LANES)
        turned[0, pl.ds(out, LANES), :] = got_ref[pl.ds(row, LANES), :].T
        rest = jnp.concatenate([got_ref[pl.ds(row + LANES, 64), :]] * 2, axis=0)
        turned[1, pl.ds(out, LANES), :] = rest.T

    low = lane < 64
    for pair in range(3):

        @pl.loop(0, SPECIES)
        def _(s):
            lower, upper, inv = lower_ref[s], upper_ref[s], inv_ref[s]

            def levels(half, group):
                return turned[half, pl.ds(group * SPECIES + s, NLEV, stride=32), :]

            first = levels(0, 2 * pair)
            odd = pltpu.roll(levels(0, 2 * pair + 1), 64, axis=1)
            second = jnp.where(low, levels(1, 2 * pair), odd)
            third = jnp.where(low, odd, levels(1, 2 * pair + 1))
            for i, rhs in enumerate((first, second, third)):
                blk = 3 * pair + i
                scaled = rhs * inv
                x = rhs
                for _ in range(SWEEPS):
                    x = scaled + lower * pltpu.roll(x, 1, axis=0) + upper * pltpu.roll(x, NLEV - 1, axis=0)
                x = jnp.where(lane + blk * LANES < live, x, 0.0)
                solved[s * SLOT_BLOCKS + blk] = x
                width = min(LANES, COL_CAP - blk * LANES)
                state_ref[0, 0, s, :, blk * LANES : blk * LANES + width] = x[:, :width]

    quarter = lax.div(lane, 32)

    @pl.loop(0, SLOT_BLOCKS)
    def _(blk):
        weight = weight_ref[blk]
        for s in range(SPECIES):
            where = s * SLOT_BLOCKS + blk
            even = solved[where, pl.ds(0, PAIRS, stride=2), :]
            odd = solved[where, pl.ds(1, PAIRS, stride=2), :]
            paired = weight * even + (1.0 - weight) * odd
            wide[s] = jnp.concatenate([paired] * 4, axis=0).T
            item = wide[s, pl.ds(0, 32, stride=TUBE_COLS), :]
            for c in range(1, TUBE_COLS):
                item = jnp.where(quarter == c, wide[s, pl.ds(c, 32, stride=TUBE_COLS), :], item)
            tubes[pl.ds(blk * 256 + s, 32, stride=8), :] = item

    tubes[ZERO_TUBE * 8 :, :] = jnp.zeros((8, LANES), f32)
    sub = lax.broadcasted_iota(jnp.int32, (8, LANES), 0)

    @pl.loop(0, PEERS // 4)
    def _(step):
        for i in range(4):
            d = step * 4 + i
            tiles = [
                tubes[pl.ds(pl.multiple_of(table_ref[d * PEER_SLOTS + r] * 8, 8), 8), :] for r in range(PEER_SLOTS)
            ]
            mid = pltpu.roll(tiles[1], 5, axis=0)
            top = pltpu.roll(tiles[2], 2, axis=0)
            row = pl.multiple_of(d * ITEM_ROWS, ITEM_ROWS)
            items_ref[pl.ds(row, 8), :] = jnp.where(sub < 5, tiles[0], mid)
            items_ref[pl.ds(row + 8, 8), :] = jnp.where(sub < 2, mid, jnp.where(sub < 7, top, 0.0))


def solve(units, table, got, lower, upper, inv, weights):
    return call(
        solve_kernel,
        (sds((1, 1, SPECIES, NLEV, COL_CAP)), sds((PEERS * ITEM_ROWS, LANES))),
        [SMEM, SMEM] + [VMEM] * 5,
        (VMEM, VMEM),
        [
            pltpu.VMEM((2, 16 * LANES, LANES), f32),
            pltpu.VMEM((SPECIES * SLOT_BLOCKS, NLEV, LANES), f32),
            pltpu.VMEM((SPECIES, LANES, LANES), f32),
            pltpu.VMEM((ZERO_TUBE * 8 + 8, LANES), f32),
        ],
        name="solve",
        flops=40_000_000,
    )(units, table, got, lower, upper, inv, weights)


def halves(x):
    high = x.astype(jnp.bfloat16)
    return high, (x - high.astype(f32)).astype(jnp.bfloat16)


def product(x, high, low):
    x_high, x_low = halves(x)
    dot = functools.partial(jnp.dot, preferred_element_type=f32)
    return dot(x_high, high) + (dot(x_low, high) + dot(x_high, low))


def lines_kernel(
    items_ref, yield_ref, rates_ref, waves_ref, fwd_high, fwd_low, inv_high, inv_low, out_ref, spec_in, spec, mixed
):
    tubes = 32 * PEER_SLOTS
    for b in range(4):
        for s in range(SPECIES):
            for r in range(PEER_SLOTS):
                rows = items_ref[pl.ds(b * 32 * ITEM_ROWS + r * SPECIES + s, 32, stride=ITEM_ROWS), :]
                spec_in[b, pl.ds(s * tubes + r, 32, stride=PEER_SLOTS), :] = rows

    @pl.loop(0, SPECIES)
    def _(s):
        row = pl.multiple_of(s * tubes, tubes)
        x = jnp.concatenate([spec_in[b, pl.ds(row, tubes), :] for b in range(4)], axis=1)
        y = product(x, fwd_high[...], fwd_low[...])
        for b in range(4):
            spec[b, pl.ds(row, tubes), :] = y[:, b * LANES : (b + 1) * LANES]

    keep = (1.0 - rates_ref[1]) + rates_ref[0] * waves_ref[...]
    gain = jnp.ones((8, LINE_PTS), f32)
    for _ in range(SECTIONS - 1):
        gain = gain * keep + 1.0
    for b in range(4):
        part = gain[:, b * LANES : (b + 1) * LANES]
        scale = [yield_ref[s] * part for s in range(SPECIES)]

        @pl.loop(0, tubes // 8)
        def _(step):
            base = step * 8
            for i in range(8):
                t = base + i
                total = scale[0] * spec[b, pl.ds(t, 1), :]
                for s in range(1, SPECIES):
                    total = total + scale[s] * spec[b, pl.ds(s * tubes + t, 1), :]
                mixed[b, pl.ds(pl.multiple_of(t * 8, 8), 8), :] = total

    chunk = 96

    @pl.loop(0, tubes * 8 // chunk)
    def _(step):
        row = pl.multiple_of(step * chunk, chunk)
        x = jnp.concatenate([mixed[b, pl.ds(row, chunk), :] for b in range(4)], axis=1)
        y = product(x, inv_high[...], inv_low[...])
        y = y.reshape(chunk // 8, 8, LINE_PTS)
        out_ref[0, pl.ds(step * (chunk // 8), chunk // 8)] = y[:, :IONS, :]


def cosine_basis():
    k = np.arange(LINE_PTS)[:, None]
    n = np.arange(LINE_PTS)[None, :]
    basis = np.cos(np.pi * k * (n + 0.5) / LINE_PTS) * np.sqrt(2.0 / LINE_PTS)
    basis[0] *= np.sqrt(0.5)
    waves = 2.0 * np.cos(np.pi * np.arange(LINE_PTS) / LINE_PTS) - 2.0
    return basis, waves


def lines(items, ion_yield, ion_spread, ion_loss):
    basis, waves = cosine_basis()

    def parts(matrix):
        matrix = matrix.astype(np.float32)
        high = matrix.astype(jnp.bfloat16)
        low = (matrix - high.astype(np.float32)).astype(jnp.bfloat16)
        return jnp.asarray(high), jnp.asarray(low)

    fill = ((0, 8 - IONS),)
    yields = jnp.pad(ion_yield, fill + ((0, 0),)).T[:, :, None]
    yields = jnp.broadcast_to(yields, (SPECIES, 8, LANES))
    rates = jnp.stack([jnp.pad(ion_spread, fill), jnp.pad(ion_loss, fill)])[:, :, None]
    rates = jnp.broadcast_to(rates, (2, 8, LINE_PTS))
    waves = jnp.asarray(waves.astype(np.float32))[None]
    tubes = 32 * PEER_SLOTS
    return call(
        lines_kernel,
        sds((1, tubes, IONS, LINE_PTS)),
        [VMEM] * 8,
        VMEM,
        [
            pltpu.VMEM((4, SPECIES * tubes, LANES), f32),
            pltpu.VMEM((4, SPECIES * tubes, LANES), f32),
            pltpu.VMEM((4, tubes * 8, LANES), f32),
        ],
        name="lines",
        flops=2_000_000_000,
    )(items, yields, rates, waves, *parts(basis.T), *parts(basis))


def up(x, axis):
    ends = lax.axis_size(axis) - 1
    return lax.ppermute(x, axis, [(i, i + 1) for i in range(ends)])


def down(x, axis):
    ends = lax.axis_size(axis) - 1
    return lax.ppermute(x, axis, [(i + 1, i) for i in range(ends)])


def on_device(
    neutrals,
    wind_lon,
    wind_lat,
    wind_lev,
    eddy_coupling,
    pair_weight,
    ion_yield,
    ion_spread,
    ion_loss,
    column_order,
    column_units,
    tube_owner,
):
    lev = lax.axis_index("lev")
    winds = (wind_lon, wind_lat, wind_lev)

    below = up(neutrals[:, 1], "lev")
    got = down(jnp.concatenate([neutrals[:, 0], wind_lev[:1]], 0), "lev")
    above, wlev_up = got[:SPECIES], got[SPECIES]
    south = up(neutrals[:, :, BAND_LATS - 1 :], "band")
    got = down(jnp.concatenate([neutrals[:, :, :1], wind_lat[None, :, :1]], 0), "band")
    north, wlat_n = got[:SPECIES], got[SPECIES]

    starts = jnp.cumsum(column_units) - column_units
    order = column_order[0]
    lat = jnp.zeros_like(order)
    for i in range(1, BAND_LATS):
        lat = lat + (order >= i * NLON).astype(jnp.int32)
    rows = jnp.pad(order + lat * (LON_PAD - NLON), (0, ORDER_PAD - BAND_COLS))
    own_units = column_units[lev].reshape(1)
    padded = jnp.pad(order, (0, SLOTS_PAD))
    own = lax.dynamic_slice(padded, (TUBE_COLS * starts[lev],), (SLOTS_PAD,))
    own_lat = jnp.zeros_like(own)
    for i in range(1, BAND_LATS):
        own_lat = own_lat + (own >= i * NLON).astype(jnp.int32)
    own_lon = own - own_lat * NLON
    own_rows = (own_lat * 6 + own_lon // 512) * LANES + own_lon % LANES
    own_sel = ((own_lon // LANES) % 4).reshape(SLOT_BLOCKS, LANES)
    table, own_weights = prepare(
        own_units, tube_owner[lev, :, 0], own_rows, own_sel, pair_weight.reshape(PAIRS * BAND_LATS, NLON)
    )
    zero = jnp.zeros((SPECIES, 1), f32)
    lower = jnp.concatenate([zero, eddy_coupling[:, 1:]], 1)
    upper = jnp.concatenate([eddy_coupling[:, 1:], zero], 1)
    inv = 1.0 / (1.0 + lower + upper)
    lower, upper, inv = (
        jnp.broadcast_to(x[:, :, None], (SPECIES, NLEV, LANES)) for x in (lower * inv, upper * inv, inv)
    )

    halo = (south, north, below, above, wlat_n, wlev_up)
    density, bottom, top, first_row, last_row = transport_step(neutrals, winds, halo, False)
    halo = (
        up(last_row, "band"),
        down(first_row, "band"),
        up(top, "lev"),
        down(bottom, "lev"),
        wlat_n,
        wlev_up,
    )
    (mine,) = transport_step(density, winds, halo, True)
    owners = lax.axis_size("lev")
    other = lax.ppermute(mine, "lev", [(i, i ^ 1) for i in range(owners)])

    core = (lev % 2).reshape(1)
    outgoing = pack(core, starts, column_units, rows, mine, other)
    parity = [[2 * i + c for i in range(owners // 2)] for c in range(2)]
    got = lax.all_to_all(
        outgoing.reshape(16, MSG_ROWS, LANES), "lev", 0, 0, axis_index_groups=parity, tiled=True
    ).reshape(16 * MSG_ROWS, LANES)

    column_state, items = solve(own_units, table, got, lower, upper, inv, own_weights)
    items = lax.all_to_all(
        items.reshape(PEERS, ITEM_ROWS, LANES), ("band", "lev"), 0, 0, tiled=True
    ).reshape(PEERS * ITEM_ROWS, LANES)
    return column_state, lines(items, ion_yield, ion_spread, ion_loss)


def solution(mesh):
    placed = (
        P(None, "lev", "band", None),
        P("lev", "band", None),
        P("lev", "band", None),
        P("lev", "band", None),
        P(),
        P(None, "band", None),
        P(),
        P(),
        P(),
        P("band", None),
        P(),
        P(),
    )
    return jax.shard_map(
        on_device,
        mesh=mesh,
        in_specs=placed,
        out_specs=(P("band", "lev", None, None, None), P(("band", "lev"), None, None, None)),
        check_vma=False,
    )
```

time: 641 us -> 162 us (0.25); the launches traced: 631 us -> 160 us
  local copies, waits for them, and re-layouts: 437 us -> 20 us
  other arithmetic: 70.6 us -> 2.01 us
  Pallas kernels: 0 us -> 63.4 us
  waiting for transfers between devices: 77.3 us -> 29.9 us
    gather x8 -> x0, local copies, waits for them, and re-layouts: 314 us -> none  [the longest x3 178 us: on_device(): column_ids = column_order[0][positions]]
    pallas_call x0 -> x6, Pallas kernels: none -> 63.4 us  [the longest x1 19.8 us: pack(): call(pack_kernel, sds((16 * MSG_ROWS, LANES)), [SMEM, SMEM, SMEM, ANY, VM...]
    slice x75 -> x6, local copies, waits for them, and re-layouts: 48.7 us -> 3.43 us  [the longest x1 1.87 us: on_device(): neutrals[:, :, :1]]
    all_to_all x2, waiting for transfers between devices: 55.1 us -> 23.8 us  [the longest x1 19.1 us: on_device(): lax.all_to_all(items.reshape(PEERS, ITEM_ROWS, LANES), ('band', 'lev'), 0...]
    sub x22 -> x1, other arithmetic: 28.3 us -> 0.57 us  [on_device(): starts = jnp.cumsum(column_units) - column_units]
    add x1 -> x0, local copies, waits for them, and re-layouts: 22.3 us -> none  [step_fluxes(): return density + change]
    add x9 -> x1, other arithmetic: 20.4 us -> 0.07 us  [on_device(): rows = jnp.pad(order + lat * (LON_PAD - NLON), (0, ORDER_PAD - BAND_COLS))]
    ppermute x8 -> x9, waiting for transfers between devices: 22.1 us -> 6.15 us  [the longest x4 4 us: down(): return lax.ppermute(x, axis, [(i + 1, i) for i in range(ends)])]
  transfers between devices with their start and end apart: 10 -> 11, of which waited for: 7 -> 6; matrix products, arithmetic and copies ran while one was open for 34% -> 5% of each run, Pallas kernels for 0% -> 8%
where the time goes in v1:
time: 162 us; the launch traced here: 160 us
  Pallas kernels  63.4 us (39%)
  starting transfers between devices  42.7 us (26%)
  waiting for transfers between devices  29.9 us (18%)
  local copies, waits for them, and re-layouts  20 us (12%)
  other arithmetic  2.01 us (1%)
    pallas_call x1, Pallas kernels, pack(): call(pack_kernel, sds((16 * MSG_ROWS, LANES)), [SMEM, SMEM, SMEM, ANY, VM...  19.8 us
    all_to_all x1, waiting for transfers between devices, on_device(): lax.all_to_all(items.reshape(PEERS, ITEM_ROWS, LANES), ('band', 'lev'), 0...  19.1 us
    ppermute x4, starting transfers between devices, up(): return lax.ppermute(x, axis, [(i, i + 1) for i in range(ends)])  14.8 us
    pallas_call x1, Pallas kernels, prepare(): call(prepare_kernel, (sds((PEERS * PEER_SLOTS,), jnp.int32), sds((SLOT_BL...  12.6 us
    pallas_call x1, Pallas kernels, solve(): call(solve_kernel, (sds((1, 1, SPECIES, NLEV, COL_CAP)), sds((PEERS * ITE...  12.3 us
    all_to_all x1, starting transfers between devices, on_device(): lax.all_to_all(outgoing.reshape(16, MSG_ROWS, LANES), 'lev', 0, 0, axis_i...  10.7 us
    pallas_call x2, Pallas kernels, transport_step(): call(functools.partial(transport_kernel, last=last), out_shape, [VMEM] *...  9.47 us
    all_to_all x1, starting transfers between devices, on_device(): lax.all_to_all(items.reshape(PEERS, ITEM_ROWS, LANES), ('band', 'lev'), 0...  9.39 us
  transfers between devices with their start and end apart: 11, of which 6 were waited for; matrix products, arithmetic and copies ran while one was open for 5% of the time, Pallas kernels for 8%

profile of v1, /device:TPU:1, one launch (start us, length us, event | category | flops | bytes accessed | tf_op | source)
XLA Modules:
  0.0 159.6 jit_solution(9994602193041338025)
XLA Ops:
  0.7 1.9 %fusion.8 = (f32[5,2,1,2880]{3,2,1,0:T(1,128)S(1)}, f32[5,2,1,2880]{3,2,1,0:T(1,128)S(1)}) fusion(f32[5,2,8,2880]{3,2,1,0:T(8,128)} %n_ref.1), kind=kLoop, calls=%fused_computation.40 | loop fusion | bytes 460800 | tf_op jit(solution)/shard_map/slice | solution.py:475
  2.5 0.9 slice_bitcast_fusion.4
  3.6 1.3 collective-permute-start.1
  4.9 1.2 slice_bitcast_fusion
  6.2 3.3 %collective-permute-start.3 = (f32[6,8,2880]{2,1,0:T(8,128)S(1)}, f32[6,8,2880]{2,1,0:T(8,128)S(1)}, u32[]{:S(2)}, u32[]{:S(2)}) collective-permute-start(f32[6,8,2880]{2,1,0:T(8,128)S(1)} %pad_maximum_fusion), channel_id=1, source_target_pairs={{1,0},{2,1},{3,2},{4,3},{5,4},{6,5},{7,6},{8,7},{9,8},{10,9},{11,1... | collective-permute-start | bytes 1658888 | tf_op jit(solution)/shard_map/ppermute | solution.py:451
  9.5 3.1 %collective-permute-start.2 = (f32[5,8,2880]{2,1,0:T(8,128)S(1)}, f32[5,8,2880]{2,1,0:T(8,128)S(1)}, u32[]{:S(2)}, u32[]{:S(2)}) collective-permute-start(f32[5,8,2880]{2,1,0:T(8,128)S(1)} %get-tuple-element.25), channel_id=1, source_target_pairs={{0,1},{1,2},{2,3},{3,4},{4,5},{5,6},{6,7},{7,8},{8,9},{9,10},{10,1... | collective-permute-start | bytes 1382408 | tf_op jit(solution)/shard_map/ppermute | solution.py:446
  12.6 4.3 %collective-permute-start = (f32[5,2,1,2880]{3,2,1,0:T(1,128)S(1)}, f32[5,2,1,2880]{3,2,1,0:T(1,128)S(1)}, u32[]{:S(2)}, u32[]{:S(2)}) collective-permute-start(f32[5,2,1,2880]{3,2,1,0:T(1,128)S(1)} %get-tuple-element.27), channel_id=1, source_target_pairs={{0,32},{32,64},{64,96},{1,33},{33,65},{65,97},{2,34},{34,66},{66,9... | collective-permute-start | bytes 345608 | tf_op jit(solution)/shard_map/ppermute | solution.py:446
  21.1 4.9 %transport.2 = (f32[5,2,8,2880]{3,2,1,0:T(8,128)}, f32[5,8,2880]{2,1,0:T(8,128)}, f32[5,8,2880]{2,1,0:T(8,128)}, f32[5,2,1,2880]{3,2,1,0:T(1,128)}, f32[5,2,1,2880]{3,2,1,0:T(1,128)}) custom-call(f32[5,2,8,2880]{3,2,1,0:T(8,128)} %n_ref.1, f32[2,8,2880]{2,1,0:T(8,128)} %wlon_ref.3, f32[2,8,2880]{2,1,0:T(8,128)} %wlat_ref.3, f32[2,8,2880]{2,1,0:T(8,128)} %wlev_ref.3, ...), custom_call_target="tpu_custom_call" | custom-call | flops 4000000 | bytes 1048576 | tf_op jit(solution)/shard_map/transport/pallas_call | solution.py:121
  26.0 3.3 %collective-permute-start.6 = (f32[5,8,2880]{2,1,0:T(8,128)}, f32[5,8,2880]{2,1,0:T(8,128)S(1)}, u32[]{:S(2)}, u32[]{:S(2)}) collective-permute-start(f32[5,8,2880]{2,1,0:T(8,128)} %get-tuple-element.15), channel_id=1, source_target_pairs={{0,1},{1,2},{2,3},{3,4},{4,5},{5,6},{6,7},{7,8},{8,9},{9,10},{10,1... | collective-permute-start | bytes 1382408 | tf_op jit(solution)/shard_map/ppermute | solution.py:446
  29.3 1.9 %collective-permute-start.7 = (f32[5,8,2880]{2,1,0:T(8,128)}, f32[5,8,2880]{2,1,0:T(8,128)S(1)}, u32[]{:S(2)}, u32[]{:S(2)}) collective-permute-start(f32[5,8,2880]{2,1,0:T(8,128)} %get-tuple-element.16), channel_id=1, source_target_pairs={{1,0},{2,1},{3,2},{4,3},{5,4},{6,5},{7,6},{8,7},{9,8},{10,9},{11,1... | collective-permute-start | bytes 1382408 | tf_op jit(solution)/shard_map/ppermute | solution.py:451
  31.3 4.1 %collective-permute-start.4 = (f32[5,2,1,2880]{3,2,1,0:T(1,128)}, f32[5,2,1,2880]{3,2,1,0:T(1,128)S(1)}, u32[]{:S(2)}, u32[]{:S(2)}) collective-permute-start(f32[5,2,1,2880]{3,2,1,0:T(1,128)} %get-tuple-element.13), channel_id=1, source_target_pairs={{0,32},{32,64},{64,96},{1,33},{33,65},{65,97},{2,34},{34,66},{66,9... | collective-permute-start | bytes 345608 | tf_op jit(solution)/shard_map/ppermute | solution.py:446
  35.4 1.3 collective-permute-start.5
  36.7 1.2 collective-permute-done.4.south_ref
  37.9 4.0 %collective-permute-done.5.north_ref = f32[5,2,1,2880]{3,2,1,0:T(1,128)S(1)} collective-permute-done((f32[5,2,1,2880]{3,2,1,0:T(1,128)}, f32[5,2,1,2880]{3,2,1,0:T(1,128)S(1)}, u32[]{:S(2)}, u32[]{:S(2)}) %collective-permute-start.5) | collective-permute-done | bytes 115232 | tf_op jit(solution)/shard_map/ppermute | solution.py:451
  42.9 4.6 %transport.3.mine_ref = f32[23,80,128]{2,1,0:T(8,128)} custom-call(f32[5,2,8,2880]{3,2,1,0:T(8,128)} %get-tuple-element.12.n_ref, f32[2,8,2880]{2,1,0:T(8,128)} %wlon_ref.3, f32[2,8,2880]{2,1,0:T(8,128)} %wlat_ref.3, f32[2,8,2880]{2,1,0:T(8,128)} %wlev_ref.3, f32[5,2,1,2880]{3,2,1,0:T(1,128)} %copy-done.8, f32[5,2,1,2880]{3,2,1,0:T(1,128)} %copy-done.9, ...), custom_call_target="tpu_custom_call" | custom-call | flops 4000000 | bytes 1048576 | tf_op jit(solution)/shard_map/transport/pallas_call | solution.py:121
  51.1 19.8 %pack.1 = f32[3072,128]{1,0:T(8,128)} custom-call(s32[1]{0:T(128)} %bitcast.4.core_ref, s32[32]{0:T(128)} %sub.16.starts_ref, s32[32]{0:T(128)} %units_ref.1, s32[23168]{0:T(1024)} %pad.22.order_hbm, f32[23,80,128]{2,1,0:T(8,128)} %transport.3.mine_ref, f32[23,80,128]{2,1,0:T(8,128)} %copy-done.3), custom_call_target="tpu_custom_call" | custom-call | flops 40000000 | bytes 1048576 | tf_op jit(solution)/shard_map/pack/pallas_call | solution.py:240
  70.9 10.7 %all-to-all-start = ((f32[16,192,128]{2,1,0:T(8,128)}), f32[16,192,128]{2,1,0:T(8,128)S(1)}, u32[]{:S(2)}, u32[]{:S(2)}) async-start(f32[16,192,128]{2,1,0:T(8,128)} %bitcast.31), calls=%async_computation | async-start | bytes 3145728 | tf_op jit(solution)/shard_map/all_to_all | solution.py:521
  84.9 12.6 %prepare.1 = (s32[384]{0:T(512)}, f32[9,32,128]{2,1,0:T(8,128)}) custom-call(s32[1]{0:T(128)} %dynamic_slice.12.units_ref, s32[270]{0:T(512)} %dynamic-slice_reduce_fusion.owner_ref, s32[1152]{0:T(1024)} %get-tuple-element.29.rows_ref, s32[9,128]{1,0:T(8,128)} %get-tuple-element.28.sel_ref, f32[256,2880]{1,0:T(8,128)} %bitcast.32), custom_call_target="tpu_custom_call" | custom-call | flops 20000000 | bytes 1048576 | tf_op jit(solution)/shard_map/prepare/pallas_call | solution.py:176
  97.6 4.7 %all-to-all-done = f32[16,192,128]{2,1,0:T(8,128)S(1)} async-done(((f32[16,192,128]{2,1,0:T(8,128)}), f32[16,192,128]{2,1,0:T(8,128)S(1)}, u32[]{:S(2)}, u32[]{:S(2)}) %all-to-all-start) | async-done | bytes 1572896 | tf_op jit(solution)/shard_map/all_to_all | solution.py:521
  104.7 12.3 %solve.1 = (f32[1,1,5,64,1080]{4,3,2,1,0:T(8,128)}, f32[2048,128]{1,0:T(8,128)}) custom-call(s32[1]{0:T(128)} %dynamic_slice.12.units_ref, s32[384]{0:T(512)} %get-tuple-element.11.table_ref, f32[3072,128]{1,0:T(8,128)} %bitcast.30, f32[5,64,128]{2,1,0:T(8,128)} %broadcast_in_dim.15.lower_ref, f32[5,64,128]{2,1,0:T(8,128)} %broadcast_in_dim.16.upper_ref, ...), custom_call_target="tpu_custom_call" | custom-call | flops 40000000 | bytes 1048576 | tf_op jit(solution)/shard_map/solve/pallas_call | solution.py:330
  117.0 9.4 %all-to-all-start.1 = ((f32[128,16,128]{2,1,0:T(8,128)}), f32[128,16,128]{2,1,0:T(8,128)S(1)}, u32[]{:S(2)}, u32[]{:S(2)}) async-start(f32[128,16,128]{2,1,0:T(8,128)} %bitcast.34), calls=%async_computation.1 | async-start | bytes 2097152 | tf_op jit(solution)/shard_map/all_to_all | solution.py:526
  126.6 19.1 %all-to-all-done.1 = f32[128,16,128]{2,1,0:T(8,128)S(1)} async-done(((f32[128,16,128]{2,1,0:T(8,128)}), f32[128,16,128]{2,1,0:T(8,128)S(1)}, u32[]{:S(2)}, u32[]{:S(2)}) %all-to-all-start.1) | async-done | bytes 1048608 | tf_op jit(solution)/shard_map/all_to_all | solution.py:526
  147.1 9.2 %lines.1 = f32[1,96,7,512]{3,2,1,0:T(8,128)} custom-call(f32[2048,128]{1,0:T(8,128)} %bitcast.33, f32[5,8,128]{2,1,0:T(8,128)} %broadcast_in_dim.18.yield_ref, f32[2,8,512]{2,1,0:T(8,128)} %broadcast_in_dim.19.rates_ref, f32[1,512]{1,0:T(1,128)} %constant.140.waves_ref, bf16[512,512]{1,0:T(8,128)(2,1)} %constant.117.clone.fwd_high, ...), custom_call_target="tpu_custom_call" | custom-call | flops 2000000000 | bytes 1048576 | tf_op jit(solution)/shard_map/lines/pallas_call | solution.py:429
  156.3 3.3 %copy.28 = f32[1,96,7,512]{3,1,2,0:T(8,128)} copy(f32[1,96,7,512]{3,2,1,0:T(8,128)} %lines.1) | data formatting | bytes 2752512
  (74 shorter events, 15.7 us)
Async XLA Ops:
  0.6 83.0 %copy-start = (s32[32,270,1]{1,2,0:T(1,128)S(1)}, s32[32,270,1]{1,2,0:T(1,128)}, u32[]{:S(2)}) copy-start(s32[32,270,1]{1,2,0:T(1,128)} %param.28) | copy-start | bytes 103684
  0.6 5.5 %slice-start = ((f32[2,8,2880]{2,1,0:T(8,128)}), f32[1,8,2880]{2,1,0:T(8,128)S(1)}, s32[]{:S(2)}) async-start(f32[2,8,2880]{2,1,0:T(8,128)} %wlev_ref.3), calls=%async_computation.2 | async-start | bytes 188416 | tf_op jit(solution)/shard_map/slice | solution.py:472
  3.6 13.3 %collective-permute-start.1 = (f32[6,2,1,2880]{3,2,1,0:T(1,128)S(1)}, f32[6,2,1,2880]{3,2,1,0:T(1,128)S(1)}, u32[]{:S(2)}, u32[]{:S(2)}) collective-permute-start(f32[6,2,1,2880]{3,2,1,0:T(1,128)S(1)} %pad_maximum_fusion.1), channel_id=1, source_target_pairs={{32,0},{64,32},{96,64},{33,1},{65,33},{97,65},{34,2},{66,34},{98,6... | collective-permute-start | bytes 414728 | tf_op jit(solution)/shard_map/ppermute | solution.py:451
  6.2 12.0 %collective-permute-start.3 = (f32[6,8,2880]{2,1,0:T(8,128)S(1)}, f32[6,8,2880]{2,1,0:T(8,128)S(1)}, u32[]{:S(2)}, u32[]{:S(2)}) collective-permute-start(f32[6,8,2880]{2,1,0:T(8,128)S(1)} %pad_maximum_fusion), channel_id=1, source_target_pairs={{1,0},{2,1},{3,2},{4,3},{5,4},{6,5},{7,6},{8,7},{9,8},{10,9},{11,1... | collective-permute-start | bytes 1658888 | tf_op jit(solution)/shard_map/ppermute | solution.py:451
  9.5 10.2 %collective-permute-start.2 = (f32[5,8,2880]{2,1,0:T(8,128)S(1)}, f32[5,8,2880]{2,1,0:T(8,128)S(1)}, u32[]{:S(2)}, u32[]{:S(2)}) collective-permute-start(f32[5,8,2880]{2,1,0:T(8,128)S(1)} %get-tuple-element.25), channel_id=1, source_target_pairs={{0,1},{1,2},{2,3},{3,4},{4,5},{5,6},{6,7},{7,8},{8,9},{9,10},{10,1... | collective-permute-start | bytes 1382408 | tf_op jit(solution)/shard_map/ppermute | solution.py:446
  12.6 7.1 %collective-permute-start = (f32[5,2,1,2880]{3,2,1,0:T(1,128)S(1)}, f32[5,2,1,2880]{3,2,1,0:T(1,128)S(1)}, u32[]{:S(2)}, u32[]{:S(2)}) collective-permute-start(f32[5,2,1,2880]{3,2,1,0:T(1,128)S(1)} %get-tuple-element.27), channel_id=1, source_target_pairs={{0,32},{32,64},{64,96},{1,33},{33,65},{65,97},{2,34},{34,66},{66,9... | collective-permute-start | bytes 345608 | tf_op jit(solution)/shard_map/ppermute | solution.py:446
  26.0 15.8 %collective-permute-start.6 = (f32[5,8,2880]{2,1,0:T(8,128)}, f32[5,8,2880]{2,1,0:T(8,128)S(1)}, u32[]{:S(2)}, u32[]{:S(2)}) collective-permute-start(f32[5,8,2880]{2,1,0:T(8,128)} %get-tuple-element.15), channel_id=1, source_target_pairs={{0,1},{1,2},{2,3},{3,4},{4,5},{5,6},{6,7},{7,8},{8,9},{9,10},{10,1... | collective-permute-start | bytes 1382408 | tf_op jit(solution)/shard_map/ppermute | solution.py:446
  29.3 12.5 %collective-permute-start.7 = (f32[5,8,2880]{2,1,0:T(8,128)}, f32[5,8,2880]{2,1,0:T(8,128)S(1)}, u32[]{:S(2)}, u32[]{:S(2)}) collective-permute-start(f32[5,8,2880]{2,1,0:T(8,128)} %get-tuple-element.16), channel_id=1, source_target_pairs={{1,0},{2,1},{3,2},{4,3},{5,4},{6,5},{7,6},{8,7},{9,8},{10,9},{11,1... | collective-permute-start | bytes 1382408 | tf_op jit(solution)/shard_map/ppermute | solution.py:451
  31.3 6.6 %collective-permute-start.4 = (f32[5,2,1,2880]{3,2,1,0:T(1,128)}, f32[5,2,1,2880]{3,2,1,0:T(1,128)S(1)}, u32[]{:S(2)}, u32[]{:S(2)}) collective-permute-start(f32[5,2,1,2880]{3,2,1,0:T(1,128)} %get-tuple-element.13), channel_id=1, source_target_pairs={{0,32},{32,64},{64,96},{1,33},{33,65},{65,97},{2,34},{34,66},{66,9... | collective-permute-start | bytes 345608 | tf_op jit(solution)/shard_map/ppermute | solution.py:446
  35.4 6.5 %collective-permute-start.5 = (f32[5,2,1,2880]{3,2,1,0:T(1,128)}, f32[5,2,1,2880]{3,2,1,0:T(1,128)S(1)}, u32[]{:S(2)}, u32[]{:S(2)}) collective-permute-start(f32[5,2,1,2880]{3,2,1,0:T(1,128)} %get-tuple-element.14), channel_id=1, source_target_pairs={{32,0},{64,32},{96,64},{33,1},{65,33},{97,65},{34,2},{66,34},{98,6... | collective-permute-start | bytes 345608 | tf_op jit(solution)/shard_map/ppermute | solution.py:451
  37.9 4.0 %copy-start.8 = (f32[5,2,1,2880]{3,2,1,0:T(1,128)}, f32[5,2,1,2880]{3,2,1,0:T(1,128)S(1)}, u32[]{:S(2)}) copy-start(f32[5,2,1,2880]{3,2,1,0:T(1,128)S(1)} %collective-permute-done.4.south_ref) | copy-start | bytes 345604
  42.8 4.6 %copy-start.10 = (s32[1,23040]{1,0:T(1,128)S(1)}, s32[1,23040]{1,0:T(1,128)}, u32[]{:S(2)}) copy-start(s32[1,23040]{1,0:T(1,128)} %param.26) | copy-start | bytes 276484
  42.8 5.5 %copy-start.13 = (s32[32]{0:T(128)S(1)}, s32[32]{0:T(128)}, u32[]{:S(2)}) copy-start(s32[32]{0:T(128)} %units_ref.1) | copy-start | bytes 388
  47.4 2.7 %collective-permute-start.8 = (f32[23,80,128]{2,1,0:T(8,128)}, f32[23,80,128]{2,1,0:T(8,128)S(1)}, u32[]{:S(2)}, u32[]{:S(2)}) collective-permute-start(f32[23,80,128]{2,1,0:T(8,128)} %transport.3.mine_ref), channel_id=1, source_target_pairs={{0,1},{1,0},{2,3},{3,2},{4,5},{5,4},{6,7},{7,6},{8,9},{9,8},{10,11... | collective-permute-start | bytes 2826248 | tf_op jit(solution)/shard_map/ppermute | solution.py:516
  70.9 10.7 %copy-start.15 = (s32[32]{0:T(128)S(1)}, s32[32]{0:T(128)}, u32[]{:S(2)}) copy-start(s32[32]{0:T(128)} %sub.16.starts_ref) | copy-start | bytes 388
  70.9 11.3 %copy-start.14 = (s32[32]{0:T(128)S(1)}, s32[32]{0:T(128)}, u32[]{:S(2)}) copy-start(s32[32]{0:T(128)} %units_ref.1) | copy-start | bytes 388
  70.9 12.6 %copy-start.11 = (f32[5,64]{1,0:T(8,128)S(1)}, f32[5,64]{1,0:T(8,128)}, u32[]{:S(2)}) copy-start(f32[5,64]{1,0:T(8,128)} %param.21) | copy-start | bytes 3844
  70.9 31.4 %all-to-all-start = ((f32[16,192,128]{2,1,0:T(8,128)}), f32[16,192,128]{2,1,0:T(8,128)S(1)}, u32[]{:S(2)}, u32[]{:S(2)}) async-start(f32[16,192,128]{2,1,0:T(8,128)} %bitcast.31), calls=%async_computation | async-start | bytes 3145728 | tf_op jit(solution)/shard_map/all_to_all | solution.py:521
  102.3 2.4 %copy-start.1 = (f32[16,192,128]{2,1,0:T(8,128)}, f32[16,192,128]{2,1,0:T(8,128)S(1)}, u32[]{:S(2)}) copy-start(f32[16,192,128]{2,1,0:T(8,128)S(1)} %all-to-all-done) | copy-start | bytes 4718596
  117.0 9.4 %copy-start.12 = (f32[7,5]{1,0:T(8,128)S(1)}, f32[7,5]{1,0:T(8,128)}, u32[]{:S(2)}) copy-start(f32[7,5]{1,0:T(8,128)} %param.23) | copy-start | bytes 424
  117.0 9.5 %copy-start.16 = (f32[7]{0:T(128)S(1)}, f32[7]{0:T(128)}, u32[]{:S(2)}) copy-start(f32[7]{0:T(128)} %param.25) | copy-start | bytes 88
  117.0 9.5 %copy-start.17 = (f32[7]{0:T(128)S(1)}, f32[7]{0:T(128)}, u32[]{:S(2)}) copy-start(f32[7]{0:T(128)} %param.24) | copy-start | bytes 88
  117.0 28.6 %all-to-all-start.1 = ((f32[128,16,128]{2,1,0:T(8,128)}), f32[128,16,128]{2,1,0:T(8,128)S(1)}, u32[]{:S(2)}, u32[]{:S(2)}) async-start(f32[128,16,128]{2,1,0:T(8,128)} %bitcast.34), calls=%async_computation.1 | async-start | bytes 2097152 | tf_op jit(solution)/shard_map/all_to_all | solution.py:526
  145.7 1.4 copy-start.2
  (6 other events, 4.8 us)

commit v2 on v1

v2 whole, which is shorter than its diff:
```python
import functools

import jax
import jax.numpy as jnp
import numpy as np
from jax import lax
from jax.experimental import pallas as pl
from jax.experimental.pallas import tpu as pltpu
from jax.sharding import PartitionSpec as P

SPECIES = 5
IONS = 7
NLON = 2880
NLEV = 64
PAIRS = 32
BAND_LATS = 8
TSTEPS = 2
SWEEPS = 8
SECTIONS = 20
TUBE_COLS = 4
PEERS = 128
PEER_SLOTS = 3
COL_CAP = 1080
TUBE_CAP = 270
BAND_COLS = BAND_LATS * NLON
LINE_PTS = 512

LANES = 128
LON_BLOCKS = 23
LON_PAD = LON_BLOCKS * LANES
CHIP_LEVS = 4
PITCH = 9
LEVEL_PITCH = 257
PLANES = 12
GROUPS = 6
MSG_ROWS = 192
SLOT_BLOCKS = 9
SLOTS_PAD = SLOT_BLOCKS * LANES
ORDER_PAD = BAND_COLS + LANES
UNROLL = 64
ZERO_TUBE = SLOT_BLOCKS * 32
ITEM_ROWS = 16

f32 = jnp.float32
VMEM = pl.BlockSpec(memory_space=pltpu.VMEM)
HELD = pl.BlockSpec(memory_space=pltpu.VMEM)
SMEM = pl.BlockSpec(memory_space=pltpu.SMEM)
ANY = pl.BlockSpec(memory_space=pl.ANY)


def on_chip(shape, dtype=f32):
    return pltpu.VMEM(shape, dtype)


def call(kernel, out_shape, in_specs, out_specs, scratch=(), name=None, flops=0, vmem=16):
    run = pl.pallas_call(
        kernel,
        out_shape=out_shape,
        in_specs=in_specs,
        out_specs=out_specs,
        scratch_shapes=list(scratch),
        name=name,
        cost_estimate=pl.CostEstimate(flops=flops, bytes_accessed=1 << 20, transcendentals=0),
        compiler_params=pltpu.CompilerParams(vmem_limit_bytes=vmem * 1024 * 1024),
    )

    def placed(*args):
        return run(
            *(pltpu.with_memory_space_constraint(x, pltpu.VMEM) if spec is HELD else x for x, spec in zip(args, in_specs))
        )

    return placed


def sds(shape, dtype=f32):
    return jax.ShapeDtypeStruct(shape, dtype)


def upwind(courant_plus, courant_minus, upstream, downstream):
    return courant_plus * upstream + courant_minus * downstream


def edges_kernel(n_ref, wlat_ref, wlev_ref, low_ref, high_ref, first_ref, last_ref):
    low_ref[SPECIES] = wlev_ref[0]
    for j in range(2):
        first_ref[SPECIES, j] = wlat_ref[j, :1]

    @pl.loop(0, SPECIES)
    def _(s):
        low_ref[s] = n_ref[s, 0]
        high_ref[s] = n_ref[s, 1]
        for j in range(2):
            first_ref[s, j] = n_ref[s, j, :1]
            last_ref[s, j] = n_ref[s, j, BAND_LATS - 1 :]


def edges(density, wind_lat, wind_lev):
    return call(
        edges_kernel,
        (
            on_chip((SPECIES + 1, BAND_LATS, NLON)),
            on_chip((SPECIES, BAND_LATS, NLON)),
            on_chip((SPECIES + 1, 2, 1, NLON)),
            on_chip((SPECIES, 2, 1, NLON)),
        ),
        [HELD] * 3,
        (VMEM,) * 4,
        name="edges",
        flops=1_000_000,
    )(density, wind_lat, wind_lev)


def transport_kernel(
    n_ref, wlon_ref, wlat_ref, wlev_ref, south_ref, north_ref, below_ref, above_ref, wlat_n_ref, wlev_up_ref,
    *outs, last,
):
    def split(c):
        return jnp.maximum(c, 0.0), jnp.minimum(c, 0.0)

    def shift_west(x):
        return jnp.concatenate([x[:, NLON - 1 :], x[:, : NLON - 1]], axis=1)

    def shift_east(x):
        return jnp.concatenate([x[:, 1:], x[:, :1]], axis=1)

    for j in range(2):

        @pl.loop(0, SPECIES)
        def _(s):
            x = n_ref[s, j]
            flux = upwind(*split(wlon_ref[j]), shift_west(x), x)
            total = x + (flux - shift_east(flux))
            southern = jnp.concatenate([south_ref[s, j], x[: BAND_LATS - 1]], axis=0)
            flux = upwind(*split(wlat_ref[j]), southern, x)
            edge = upwind(*split(wlat_n_ref[SPECIES, j]), x[BAND_LATS - 1 :], north_ref[s, j])
            total = total + (flux - jnp.concatenate([flux[1:], edge], axis=0))
            beneath = below_ref[s] if j == 0 else n_ref[s, 0]
            overhead = n_ref[s, 1] if j == 0 else above_ref[s]
            over_wind = wlev_ref[1] if j == 0 else wlev_up_ref[SPECIES]
            flux = upwind(*split(wlev_ref[j]), beneath, x)
            total = total + (flux - upwind(*split(over_wind), x, overhead))
            if last:
                row = pl.multiple_of((j * SPECIES + s) * BAND_LATS, BAND_LATS)
                for blk in range(LON_BLOCKS):
                    wide = min(LANES, NLON - blk * LANES)
                    outs[0][blk, pl.ds(row, BAND_LATS), :wide] = total[:, blk * LANES : blk * LANES + wide]
            else:
                outs[0][s, j] = total
                outs[1 + j][s] = total
                outs[3][s, j] = total[:1]
                outs[4][s, j] = total[BAND_LATS - 1 :]


def transport_step(density, winds, halo, last):
    if last:
        out_shape = (on_chip((LON_BLOCKS, 2 * SPECIES * BAND_LATS, LANES)),)
    else:
        out_shape = (
            on_chip((SPECIES, 2, BAND_LATS, NLON)),
            on_chip((SPECIES, BAND_LATS, NLON)),
            on_chip((SPECIES, BAND_LATS, NLON)),
            on_chip((SPECIES, 2, 1, NLON)),
            on_chip((SPECIES, 2, 1, NLON)),
        )
    return call(
        functools.partial(transport_kernel, last=last),
        out_shape,
        [HELD] * 10,
        (VMEM,) * len(out_shape),
        name="transport",
        flops=4_000_000,
    )(density, *winds, *halo)


def prepare_kernel(
    units_ref, owner_ref, rows_ref, sel_ref, weight_ref, column_ref,
    table_ref, own_ref, coef_ref, count, blocks, table, picked,
):
    @pl.loop(0, PEERS * PEER_SLOTS // 8)
    def _(i):
        for k in range(8):
            table_ref[i * 8 + k] = ZERO_TUBE

    @pl.loop(0, PEERS // 8)
    def _(i):
        for k in range(8):
            count[i * 8 + k] = 0

    @pl.loop(0, units_ref[0])
    def _(u):
        dest = owner_ref[u]
        rank = count[dest]
        count[dest] = rank + 1
        table_ref[dest * PEER_SLOTS + rank] = u

    coef_ref[...] = jnp.broadcast_to(column_ref[...], coef_ref.shape)

    for blk in range(LON_BLOCKS):
        wide = min(LANES, NLON - blk * LANES)
        blocks[blk, :, :wide] = weight_ref[:, blk * LANES : blk * LANES + wide]

    @pl.loop(0, BAND_LATS)
    def _(lat):
        for g in range(6):
            parts = [
                blocks[min(4 * g + i, LON_BLOCKS - 1), pl.ds(lat + h * BAND_LATS, 8, stride=4 * BAND_LATS), :]
                for i in range(4)
                for h in range(4)
            ]
            start = pl.multiple_of((lat * 6 + g) * LANES, LANES)
            table[pl.ds(start, LANES), :] = jnp.concatenate(parts, axis=0).T

    @pl.loop(0, SLOTS_PAD // UNROLL)
    def _(step):
        base = pl.multiple_of(step * UNROLL, UNROLL)
        places = rows_ref.at[pl.ds(base, UNROLL)]
        for i in range(UNROLL):
            picked[pl.ds(base + i, 1), :] = table[pl.ds(places[i], 1), :]

    for blk in range(SLOT_BLOCKS):
        turned = picked[blk * LANES : (blk + 1) * LANES, :].T
        which = sel_ref[blk : blk + 1, :]
        kept = turned[:PAIRS]
        for i in range(1, 4):
            kept = jnp.where(which == i, turned[i * PAIRS : (i + 1) * PAIRS], kept)
        own_ref[blk] = kept


def prepare(units, owners, rows, sel, weights, column):
    return call(
        prepare_kernel,
        (
            sds((PEERS * PEER_SLOTS,), jnp.int32),
            on_chip((SLOT_BLOCKS, PAIRS, LANES)),
            on_chip((3 * SPECIES * NLEV, LANES)),
        ),
        [SMEM, SMEM, SMEM, VMEM, VMEM, VMEM],
        (SMEM, VMEM, VMEM),
        [
            pltpu.SMEM((PEERS,), jnp.int32),
            pltpu.VMEM((LON_BLOCKS, PAIRS * BAND_LATS, LANES), f32),
            pltpu.VMEM((BAND_LATS * 6 * LANES, LANES), f32),
            pltpu.VMEM((SLOTS_PAD, LANES), f32),
        ],
        name="prepare",
        flops=20_000_000,
    )(units, owners, rows, sel, weights, column)


def pack_kernel(core_ref, starts_ref, units_ref, order_hbm, mine_ref, other_ref, msg_ref, order, planes, table, sem):
    fetch = pltpu.make_async_copy(order_hbm, order, sem)
    fetch.start()
    core = core_ref[0]
    for source, side in ((mine_ref, core), (other_ref, 1 - core)):

        @pl.loop(0, LON_BLOCKS)
        def _(blk):
            for j in range(2):
                for i in range(PLANES):
                    row = ((2 * side + j) * PLANES + i) * PITCH
                    from_row = (j * SPECIES + i % SPECIES) * BAND_LATS
                    planes[blk, pl.ds(row, BAND_LATS), :] = source[blk, from_row : from_row + BAND_LATS, :]

    @pl.loop(0, LON_BLOCKS)
    def _(blk):
        for lat in range(BAND_LATS):
            parts = [
                planes[blk, pl.ds((jj * PLANES + first) * PITCH + lat, 8, stride=PITCH), :]
                for jj in range(CHIP_LEVS)
                for first in (0, 3, 1, 4)
            ]
            start = pl.multiple_of((lat * LON_BLOCKS + blk) * LANES, LANES)
            table[pl.ds(start, LANES), :] = jnp.concatenate(parts, axis=0).T

    fetch.wait()
    lane = lax.broadcasted_iota(jnp.int32, (1, LANES), 1)
    group_of = lax.div(lax.rem(lane, 32), SPECIES)

    @pl.loop(0, 16 * GROUPS)
    def _(turn):
        peer = lax.div(turn, GROUPS)
        group = turn - peer * GROUPS
        owner = 2 * peer + core
        live = jnp.clip(TUBE_COLS * units_ref[owner] - MSG_ROWS * group, 0, MSG_ROWS)
        first = TUBE_COLS * starts_ref[owner] + MSG_ROWS * group
        mask = group_of == group

        @pl.loop(0, lax.div(live + (UNROLL - 1), UNROLL))
        def _(step):
            base = first + step * UNROLL
            row = pl.multiple_of(peer * MSG_ROWS + step * UNROLL, UNROLL)
            places = order.at[pl.ds(base, UNROLL)]
            for i in range(UNROLL):
                value = table[pl.ds(places[i], 1), :]
                pltpu.store(msg_ref.at[pl.ds(row + i, 1), :], value, mask=mask)


def pack(core, starts, units, order, mine, other):
    return call(
        pack_kernel,
        on_chip((16 * MSG_ROWS, LANES)),
        [SMEM, SMEM, SMEM, ANY, HELD, HELD],
        VMEM,
        [
            pltpu.SMEM((ORDER_PAD,), jnp.int32),
            pltpu.VMEM((LON_BLOCKS, CHIP_LEVS * PLANES * PITCH, LANES), f32),
            pltpu.VMEM((BAND_LATS * LON_PAD, LANES), f32),
            pltpu.SemaphoreType.DMA,
        ],
        name="pack",
        flops=40_000_000,
        vmem=32,
    )(core, starts, units, order, mine, other)


def solve_kernel(
    units_ref, table_ref, got_ref, coef_ref, weight_ref, state_ref, items_ref, turned, natural, pairs, wide, tubes
):
    live = TUBE_COLS * units_ref[0]
    lane = lax.broadcasted_iota(jnp.int32, (1, LANES), 1)
    low = lane < 64
    quarter = lax.div(lane, 32)

    @pl.loop(0, 8)
    def _(i):
        for side in range(2):
            row = pl.multiple_of((2 * i + side) * MSG_ROWS, MSG_ROWS)
            out = i * LEVEL_PITCH + side * LANES
            turned[0, pl.ds(out, LANES), :] = got_ref[pl.ds(row, LANES), :].T
            rest = jnp.concatenate([got_ref[pl.ds(row + LANES, 64), :]] * 2, axis=0)
            turned[1, pl.ds(out, LANES), :] = rest.T

    for pair in range(3):

        @pl.loop(0, SPECIES)
        def _(s):
            def coefs(which):
                row = pl.multiple_of((which * SPECIES + s) * NLEV, NLEV)
                return [coef_ref[pl.ds(row + 8 * v, 8), :] for v in range(8)]

            lower, upper, inv = coefs(0), coefs(1), coefs(2)

            def levels(half, group, v):
                return turned[half, pl.ds(32 * v + group * SPECIES + s, 8, stride=LEVEL_PITCH), :]

            first = [levels(0, 2 * pair, v) for v in range(8)]
            odd = [pltpu.roll(levels(0, 2 * pair + 1, v), 64, axis=1) for v in range(8)]
            second = [jnp.where(low, levels(1, 2 * pair, v), odd[v]) for v in range(8)]
            third = [jnp.where(low, odd[v], levels(1, 2 * pair + 1, v)) for v in range(8)]
            for i, rhs in enumerate((first, second, third)):
                blk = 3 * pair + i
                scaled = [rhs[v] * inv[v] for v in range(8)]
                x = rhs
                for _ in range(SWEEPS):
                    beneath = [pltpu.roll(x[7], 1, axis=0)] + x[:7]
                    overhead = x[1:] + [pltpu.roll(x[0], 7, axis=0)]
                    x = [scaled[v] + lower[v] * beneath[v] + upper[v] * overhead[v] for v in range(8)]
                keep = lane + blk * LANES < live
                for v in range(8):
                    natural[i, pl.ds(v, 8, stride=PITCH), :] = jnp.where(keep, x[v], 0.0)
                width = min(LANES, COL_CAP - blk * LANES)
                for g in range(8):
                    state_ref[0, 0, s, g * 8 : g * 8 + 8, blk * LANES : blk * LANES + width] = natural[
                        i, g * PITCH : g * PITCH + 8, :width
                    ]
                for h in range(4):
                    weight = weight_ref[blk, 8 * h : 8 * h + 8, :]
                    paired = weight * x[2 * h] + (1.0 - weight) * x[2 * h + 1]
                    pairs[i, pl.ds(h, 8, stride=4), :] = paired
                wide[i] = jnp.concatenate([pairs[i]] * 4, axis=0).T
                item = wide[i, pl.ds(0, 32, stride=TUBE_COLS), :]
                for c in range(1, TUBE_COLS):
                    item = jnp.where(quarter == c, wide[i, pl.ds(c, 32, stride=TUBE_COLS), :], item)
                tubes[pl.ds(blk * 256 + s, 32, stride=8), :] = item

    tubes[ZERO_TUBE * 8 :, :] = jnp.zeros((8, LANES), f32)
    sub = lax.broadcasted_iota(jnp.int32, (8, LANES), 0)

    @pl.loop(0, PEERS // 4)
    def _(step):
        for i in range(4):
            d = step * 4 + i
            tiles = [
                tubes[pl.ds(pl.multiple_of(table_ref[d * PEER_SLOTS + r] * 8, 8), 8), :] for r in range(PEER_SLOTS)
            ]
            mid = pltpu.roll(tiles[1], 5, axis=0)
            top = pltpu.roll(tiles[2], 2, axis=0)
            row = pl.multiple_of(d * ITEM_ROWS, ITEM_ROWS)
            items_ref[pl.ds(row, 8), :] = jnp.where(sub < 5, tiles[0], mid)
            items_ref[pl.ds(row + 8, 8), :] = jnp.where(sub < 2, mid, jnp.where(sub < 7, top, 0.0))


def solve(units, table, got, coefs, weights):
    return call(
        solve_kernel,
        (sds((1, 1, SPECIES, NLEV, COL_CAP)), on_chip((PEERS * ITEM_ROWS, LANES))),
        [SMEM, SMEM] + [HELD] * 3,
        (VMEM, VMEM),
        [
            pltpu.VMEM((2, 8 * LEVEL_PITCH, LANES), f32),
            pltpu.VMEM((3, 8 * PITCH, LANES), f32),
            pltpu.VMEM((3, PAIRS, LANES), f32),
            pltpu.VMEM((3, LANES, LANES), f32),
            pltpu.VMEM((ZERO_TUBE * 8 + 8, LANES), f32),
        ],
        name="solve",
        flops=40_000_000,
    )(units, table, got, coefs, weights)


def halves(x):
    high = x.astype(jnp.bfloat16)
    return high, (x - high.astype(f32)).astype(jnp.bfloat16)


def product(x, high, low):
    x_high, x_low = halves(x)
    dot = functools.partial(jnp.dot, preferred_element_type=f32)
    return dot(x_high, high) + (dot(x_low, high) + dot(x_high, low))


def lines_kernel(
    items_ref, yield_ref, rates_ref, waves_ref, fwd_high, fwd_low, inv_high, inv_low, out_ref, spec_in, spec, mixed
):
    tubes = 32 * PEER_SLOTS
    for b in range(4):
        for s in range(SPECIES):
            for r in range(PEER_SLOTS):
                rows = items_ref[pl.ds(b * 32 * ITEM_ROWS + r * SPECIES + s, 32, stride=ITEM_ROWS), :]
                spec_in[b, pl.ds(s * tubes + r, 32, stride=PEER_SLOTS), :] = rows

    half = SPECIES * tubes // 2

    @pl.loop(0, 2)
    def _(step):
        row = pl.multiple_of(step * half, half)
        x = jnp.concatenate([spec_in[b, pl.ds(row, half), :] for b in range(4)], axis=1)
        spec[pl.ds(row, half), :] = product(x, fwd_high[...], fwd_low[...])

    waves = waves_ref[...]
    for i in range(IONS):
        keep = (1.0 - rates_ref[IONS + i]) + rates_ref[i] * waves
        gain = jnp.ones_like(waves)
        for _ in range(SECTIONS - 1):
            gain = gain * keep + 1.0
        total = (yield_ref[i * SPECIES] * gain) * spec[:tubes, :]
        for s in range(1, SPECIES):
            total = total + (yield_ref[i * SPECIES + s] * gain) * spec[s * tubes : (s + 1) * tubes, :]
        mixed[i] = total

    @pl.loop(0, IONS)
    def _(i):
        out_ref[0, i] = product(mixed[i], inv_high[...], inv_low[...])


def cosine_basis():
    k = np.arange(LINE_PTS)[:, None]
    n = np.arange(LINE_PTS)[None, :]
    basis = np.cos(np.pi * k * (n + 0.5) / LINE_PTS) * np.sqrt(2.0 / LINE_PTS)
    basis[0] *= np.sqrt(0.5)
    waves = 2.0 * np.cos(np.pi * np.arange(LINE_PTS) / LINE_PTS) - 2.0
    return basis, waves


def lines(items, ion_yield, ion_spread, ion_loss):
    basis, waves = cosine_basis()

    def parts(matrix):
        matrix = matrix.astype(np.float32)
        high = matrix.astype(jnp.bfloat16)
        low = (matrix - high.astype(np.float32)).astype(jnp.bfloat16)
        return jnp.asarray(high), jnp.asarray(low)

    waves = jnp.asarray(waves.astype(np.float32))[None]
    tubes = 32 * PEER_SLOTS
    by_ion = call(
        lines_kernel,
        sds((1, IONS, tubes, LINE_PTS)),
        [HELD, SMEM, SMEM] + [HELD] * 5,
        VMEM,
        [
            pltpu.VMEM((4, SPECIES * tubes, LANES), f32),
            pltpu.VMEM((SPECIES * tubes, LINE_PTS), f32),
            pltpu.VMEM((IONS, tubes, LINE_PTS), f32),
        ],
        name="lines",
        flops=2_000_000_000,
    )(items, ion_yield.reshape(-1), jnp.concatenate([ion_spread, ion_loss]), waves, *parts(basis.T), *parts(basis))
    return jnp.swapaxes(by_ion, 1, 2)


def up(x, axis):
    ends = lax.axis_size(axis) - 1
    return lax.ppermute(x, axis, [(i, i + 1) for i in range(ends)])


def down(x, axis):
    ends = lax.axis_size(axis) - 1
    return lax.ppermute(x, axis, [(i + 1, i) for i in range(ends)])


def on_device(
    neutrals,
    wind_lon,
    wind_lat,
    wind_lev,
    eddy_coupling,
    pair_weight,
    ion_yield,
    ion_spread,
    ion_loss,
    column_order,
    column_units,
    tube_owner,
):
    lev = lax.axis_index("lev")
    winds = (wind_lon, wind_lat, wind_lev)

    low, high, first, last = edges(neutrals, wind_lat, wind_lev)
    below, above = up(high, "lev"), down(low, "lev")
    south, north = up(last, "band"), down(first, "band")

    starts = jnp.cumsum(column_units) - column_units
    order = column_order[0]
    lat = jnp.zeros_like(order)
    for i in range(1, BAND_LATS):
        lat = lat + (order >= i * NLON).astype(jnp.int32)
    rows = jnp.pad(order + lat * (LON_PAD - NLON), (0, ORDER_PAD - BAND_COLS))
    own_units = column_units[lev].reshape(1)
    padded = jnp.pad(order, (0, SLOTS_PAD))
    own = lax.dynamic_slice(padded, (TUBE_COLS * starts[lev],), (SLOTS_PAD,))
    own_lat = jnp.zeros_like(own)
    for i in range(1, BAND_LATS):
        own_lat = own_lat + (own >= i * NLON).astype(jnp.int32)
    own_lon = own - own_lat * NLON
    own_rows = (own_lat * 6 + own_lon // 512) * LANES + own_lon % LANES
    own_sel = ((own_lon // LANES) % 4).reshape(SLOT_BLOCKS, LANES)
    zero = jnp.zeros((SPECIES, 1), f32)
    lower = jnp.concatenate([zero, eddy_coupling[:, 1:]], 1)
    upper = jnp.concatenate([eddy_coupling[:, 1:], zero], 1)
    inv = 1.0 / (1.0 + lower + upper)
    coefs = jnp.stack([lower * inv, upper * inv, inv]).reshape(3, SPECIES, 8, 8)
    table, own_weights, coefs = prepare(
        own_units,
        tube_owner[lev, :, 0],
        own_rows,
        own_sel,
        pair_weight.reshape(PAIRS * BAND_LATS, NLON),
        jnp.swapaxes(coefs, 2, 3).reshape(-1, 1),
    )

    halo = (south, north, below, above, north, above)
    density, bottom, top, first_row, last_row = transport_step(neutrals, winds, halo, False)
    halo = (up(last_row, "band"), down(first_row, "band"), up(top, "lev"), down(bottom, "lev"), north, above)
    (mine,) = transport_step(density, winds, halo, True)
    owners = lax.axis_size("lev")
    other = lax.ppermute(mine, "lev", [(i, i ^ 1) for i in range(owners)])

    core = (lev % 2).reshape(1)
    outgoing = pack(core, starts, column_units, rows, mine, other)
    parity = [[2 * i + c for i in range(owners // 2)] for c in range(2)]
    got = lax.all_to_all(
        outgoing.reshape(16, MSG_ROWS, LANES), "lev", 0, 0, axis_index_groups=parity, tiled=True
    ).reshape(16 * MSG_ROWS, LANES)

    column_state, items = solve(own_units, table, got, coefs, own_weights)
    items = lax.all_to_all(
        items.reshape(PEERS, ITEM_ROWS, LANES), ("band", "lev"), 0, 0, tiled=True
    ).reshape(PEERS * ITEM_ROWS, LANES)
    return column_state, lines(items, ion_yield, ion_spread, ion_loss)


def solution(mesh):
    placed = (
        P(None, "lev", "band", None),
        P("lev", "band", None),
        P("lev", "band", None),
        P("lev", "band", None),
        P(),
        P(None, "band", None),
        P(),
        P(),
        P(),
        P("band", None),
        P(),
        P(),
    )
    return jax.shard_map(
        on_device,
        mesh=mesh,
        in_specs=placed,
        out_specs=(P("band", "lev", None, None, None), P(("band", "lev"), None, None, None)),
        check_vma=False,
    )
```

time: 162 us -> 138 us (0.85); the launches traced: 160 us -> 138 us
  Pallas kernels: 63.4 us -> 47.5 us
  local copies, waits for them, and re-layouts: 20 us -> 7.97 us
  waiting for transfers between devices: 29.9 us -> 41.8 us
  starting transfers between devices: 42.7 us -> 38.4 us
    pallas_call x6 -> x7, Pallas kernels: 63.4 us -> 47.5 us  [placed(): run(*(pltpu.with_memory_space_constraint(x, pltpu.VMEM) if spec is HELD e...]
    all_to_all x1, waiting for transfers between devices: 4.7 us -> 13.3 us  [on_device(): lax.all_to_all(outgoing.reshape(16, MSG_ROWS, LANES), 'lev', 0, 0, axis_i...]
    broadcast_in_dim x6 -> x0, local copies, waits for them, and re-layouts: 4.78 us -> none  [the longest x3 2.41 us: on_device(): jnp.broadcast_to(x[:, :, None], (SPECIES, NLEV, LANES))]
    slice x5 -> x0, local copies, waits for them, and re-layouts: 3.36 us -> none  [the longest x1 1.87 us: on_device(): neutrals[:, :, :1]]
    all_to_all x1, starting transfers between devices: 9.39 us -> 6.17 us  [on_device(): lax.all_to_all(items.reshape(PEERS, ITEM_ROWS, LANES), ('band', 'lev'), 0...]
    squeeze x3 -> x0, local copies, waits for them, and re-layouts: 2.48 us -> none  [the longest x1 1.23 us: on_device(): got = down(jnp.concatenate([neutrals[:, 0], wind_lev[:1]], 0), 'lev')]
    ppermute x4, waiting for transfers between devices: 1.23 us -> 3.45 us  [up(): return lax.ppermute(x, axis, [(i, i + 1) for i in range(ends)])]
    unnamed x37 -> x36, local copies, waits for them, and re-layouts: 6.64 us -> 5.88 us
  transfers between devices with their start and end apart: 11 -> 11, of which waited for: 6 -> 6; matrix products, arithmetic and copies ran while one was open for 5% -> 2% of each run, Pallas kernels for 8% -> 6%
where the time goes in v2:
time: 138 us
  Pallas kernels  47.5 us (34%)
  waiting for transfers between devices  41.8 us (30%)
  starting transfers between devices  38.4 us (28%)
  local copies, waits for them, and re-layouts  7.97 us (6%)
  between operations  1.65 us (1%)
    pallas_call x7, Pallas kernels, placed(): run(*(pltpu.with_memory_space_constraint(x, pltpu.VMEM) if spec is HELD e...  47.5 us
    all_to_all x1, waiting for transfers between devices, on_device(): lax.all_to_all(items.reshape(PEERS, ITEM_ROWS, LANES), ('band', 'lev'), 0...  19.1 us
    ppermute x4, starting transfers between devices, up(): return lax.ppermute(x, axis, [(i, i + 1) for i in range(ends)])  14.9 us
    all_to_all x1, waiting for transfers between devices, on_device(): lax.all_to_all(outgoing.reshape(16, MSG_ROWS, LANES), 'lev', 0, 0, axis_i...  13.3 us
    all_to_all x1, starting transfers between devices, on_device(): lax.all_to_all(outgoing.reshape(16, MSG_ROWS, LANES), 'lev', 0, 0, axis_i...  9.44 us
    ppermute x4, starting transfers between devices, down(): return lax.ppermute(x, axis, [(i + 1, i) for i in range(ends)])  7.79 us
    all_to_all x1, starting transfers between devices, on_device(): lax.all_to_all(items.reshape(PEERS, ITEM_ROWS, LANES), ('band', 'lev'), 0...  6.17 us
    unnamed x36, local copies, waits for them, and re-layouts  5.88 us
  transfers between devices with their start and end apart: 11, of which 6 were waited for; matrix products, arithmetic and copies ran while one was open for 2% of the time, Pallas kernels for 6%

profile of v2, /device:TPU:1, one launch (start us, length us, event | category | flops | bytes accessed | tf_op | source)
XLA Modules:
  0.0 138.1 jit_solution(6357017158459274606)
XLA Ops:
  0.7 1.2 copy-done.1
  1.8 0.9 copy-done.3
  3.8 3.3 %collective-permute-start.3 = (f32[6,8,2880]{2,1,0:T(8,128)S(1)}, f32[6,8,2880]{2,1,0:T(8,128)S(1)}, u32[]{:S(2)}, u32[]{:S(2)}) collective-permute-start(f32[6,8,2880]{2,1,0:T(8,128)S(1)} %get-tuple-element.20), channel_id=1, source_target_pairs={{1,0},{2,1},{3,2},{4,3},{5,4},{6,5},{7,6},{8,7},{9,8},{10,9},{11,1... | collective-permute-start | bytes 1658888 | tf_op jit(solution)/shard_map/ppermute | solution.py:499
  7.1 3.1 %collective-permute-start.2 = (f32[5,8,2880]{2,1,0:T(8,128)S(1)}, f32[5,8,2880]{2,1,0:T(8,128)S(1)}, u32[]{:S(2)}, u32[]{:S(2)}) collective-permute-start(f32[5,8,2880]{2,1,0:T(8,128)S(1)} %get-tuple-element.19), channel_id=1, source_target_pairs={{0,1},{1,2},{2,3},{3,4},{4,5},{5,6},{6,7},{7,8},{8,9},{9,10},{10,1... | collective-permute-start | bytes 1382408 | tf_op jit(solution)/shard_map/ppermute | solution.py:494
  10.3 1.3 collective-permute-start.1
  11.6 4.3 %collective-permute-start = (f32[5,2,1,2880]{3,2,1,0:T(1,128)S(1)}, f32[5,2,1,2880]{3,2,1,0:T(1,128)S(1)}, u32[]{:S(2)}, u32[]{:S(2)}) collective-permute-start(f32[5,2,1,2880]{3,2,1,0:T(1,128)S(1)} %get-tuple-element.17), channel_id=1, source_target_pairs={{0,32},{32,64},{64,96},{1,33},{33,65},{65,97},{2,34},{34,66},{66,9... | collective-permute-start | bytes 345608 | tf_op jit(solution)/shard_map/ppermute | solution.py:494
  15.9 2.9 %collective-permute-done.south_ref = f32[5,2,1,2880]{3,2,1,0:T(1,128)S(1)} collective-permute-done((f32[5,2,1,2880]{3,2,1,0:T(1,128)S(1)}, f32[5,2,1,2880]{3,2,1,0:T(1,128)S(1)}, u32[]{:S(2)}, u32[]{:S(2)}) %collective-permute-start) | collective-permute-done | bytes 115232 | tf_op jit(solution)/shard_map/ppermute | solution.py:494
  19.8 1.9 %transport.2 = (f32[5,2,8,2880]{3,2,1,0:T(8,128)S(1)}, f32[5,8,2880]{2,1,0:T(8,128)S(1)}, f32[5,8,2880]{2,1,0:T(8,128)S(1)}, f32[5,2,1,2880]{3,2,1,0:T(1,128)S(1)}, f32[5,2,1,2880]{3,2,1,0:T(1,128)S(1)}) custom-call(f32[5,2,8,2880]{3,2,1,0:T(8,128)S(1)} %copy-done.1, f32[2,8,2880]{2,1,0:T(8,128)S(1)} %copy-done.6, f32[2,8,2880]{2,1,0:T(8,128)S(1)} %copy-done.3, ...), custom_call_target="tpu_custom_call" | custom-call | flops 4000000 | bytes 1048576 | tf_op jit(solution)/shard_map/transport/pallas_call | solution.py:68
  21.7 3.4 %collective-permute-start.6 = (f32[5,8,2880]{2,1,0:T(8,128)S(1)}, f32[5,8,2880]{2,1,0:T(8,128)S(1)}, u32[]{:S(2)}, u32[]{:S(2)}) collective-permute-start(f32[5,8,2880]{2,1,0:T(8,128)S(1)} %get-tuple-element.24), channel_id=1, source_target_pairs={{0,1},{1,2},{2,3},{3,4},{4,5},{5,6},{6,7},{7,8},{8,9},{9,10},{10,1... | collective-permute-start | bytes 1382408 | tf_op jit(solution)/shard_map/ppermute | solution.py:494
  25.1 1.9 %collective-permute-start.7 = (f32[5,8,2880]{2,1,0:T(8,128)S(1)}, f32[5,8,2880]{2,1,0:T(8,128)S(1)}, u32[]{:S(2)}, u32[]{:S(2)}) collective-permute-start(f32[5,8,2880]{2,1,0:T(8,128)S(1)} %get-tuple-element.25), channel_id=1, source_target_pairs={{1,0},{2,1},{3,2},{4,3},{5,4},{6,5},{7,6},{8,7},{9,8},{10,9},{11,1... | collective-permute-start | bytes 1382408 | tf_op jit(solution)/shard_map/ppermute | solution.py:499
  27.0 4.1 %collective-permute-start.4 = (f32[5,2,1,2880]{3,2,1,0:T(1,128)S(1)}, f32[5,2,1,2880]{3,2,1,0:T(1,128)S(1)}, u32[]{:S(2)}, u32[]{:S(2)}) collective-permute-start(f32[5,2,1,2880]{3,2,1,0:T(1,128)S(1)} %get-tuple-element.22), channel_id=1, source_target_pairs={{0,32},{32,64},{64,96},{1,33},{33,65},{65,97},{2,34},{34,66},{66,9... | collective-permute-start | bytes 345608 | tf_op jit(solution)/shard_map/ppermute | solution.py:494
  31.2 1.3 collective-permute-start.5
  33.0 4.1 %collective-permute-done.5.north_ref = f32[5,2,1,2880]{3,2,1,0:T(1,128)S(1)} collective-permute-done((f32[5,2,1,2880]{3,2,1,0:T(1,128)S(1)}, f32[5,2,1,2880]{3,2,1,0:T(1,128)S(1)}, u32[]{:S(2)}, u32[]{:S(2)}) %collective-permute-start.5) | collective-permute-done | bytes 115232 | tf_op jit(solution)/shard_map/ppermute | solution.py:499
  37.1 1.8 %transport.3.mine_ref = f32[23,80,128]{2,1,0:T(8,128)S(1)} custom-call(f32[5,2,8,2880]{3,2,1,0:T(8,128)S(1)} %get-tuple-element.21.n_ref, f32[2,8,2880]{2,1,0:T(8,128)S(1)} %copy-done.6, f32[2,8,2880]{2,1,0:T(8,128)S(1)} %copy-done.3, f32[2,8,2880]{2,1,0:T(8,128)S(1)} %copy-done.5, f32[5,2,1,2880]{3,2,1,0:T(1,128)S(1)} %collective-permute-done.4.south_ref, ...), custom_call_target="tpu_custom_call" | custom-call | flops 4000000 | bytes 1048576 | tf_op jit(solution)/shard_map/transport/pallas_call | solution.py:68
  39.7 1.9 %collective-permute-done.8.other_ref = f32[23,80,128]{2,1,0:T(8,128)S(1)} collective-permute-done((f32[23,80,128]{2,1,0:T(8,128)S(1)}, f32[23,80,128]{2,1,0:T(8,128)S(1)}, u32[]{:S(2)}, u32[]{:S(2)}) %collective-permute-start.8) | collective-permute-done | bytes 942112 | tf_op jit(solution)/shard_map/ppermute | solution.py:557
  41.6 19.8 %pack.1 = f32[3072,128]{1,0:T(8,128)} custom-call(s32[1]{0:T(128)} %bitcast.5.core_ref, s32[32]{0:T(128)S(1)} %sub.16.starts_ref, s32[32]{0:T(128)S(1)} %copy-done.7, s32[23168]{0:T(1024)S(1)} %pad.11.order_hbm, f32[23,80,128]{2,1,0:T(8,128)S(1)} %transport.3.mine_ref, f32[23,80,128]{2,1,0:T(8,128)S(1)} %collective-permute-done.8.other_ref), custom_call_target="tpu_custom_call" | custom-call | flops 40000000 | bytes 1048576 | tf_op jit(solution)/shard_map/pack/pallas_call | solution.py:68
  61.4 9.4 %all-to-all-start = ((f32[16,192,128]{2,1,0:T(8,128)}), f32[16,192,128]{2,1,0:T(8,128)S(1)}, u32[]{:S(2)}, u32[]{:S(2)}) async-start(f32[16,192,128]{2,1,0:T(8,128)} %bitcast.6), calls=%async_computation | async-start | bytes 3145728 | tf_op jit(solution)/shard_map/all_to_all | solution.py:562
  73.7 1.8 %copy-done.2 = f32[32,8,2880]{2,1,0:T(8,128)S(1)} copy-done((f32[32,8,2880]{2,1,0:T(8,128)S(1)}, f32[32,8,2880]{2,1,0:T(8,128)}, u32[]{:S(2)}) %copy-start.2) | copy-done | bytes 2949144
  75.5 8.7 %prepare.1 = (s32[384]{0:T(512)S(1)}, f32[9,32,128]{2,1,0:T(8,128)S(1)}, f32[960,128]{1,0:T(8,128)S(1)}) custom-call(s32[1]{0:T(128)} %dynamic_slice.12.units_ref, s32[270]{0:T(512)S(1)} %dynamic-slice_reduce_fusion.owner_ref, s32[1152]{0:T(1024)S(1)} %get-tuple-element.31.rows_ref, s32[9,128]{1,0:T(8,128)S(1)} %get-tuple-element.30.sel_ref, ...), custom_call_target="tpu_custom_call" | custom-call | flops 20000000 | bytes 1048576 | tf_op jit(solution)/shard_map/prepare/pallas_call | solution.py:68
  84.3 13.3 %all-to-all-done = f32[16,192,128]{2,1,0:T(8,128)S(1)} async-done(((f32[16,192,128]{2,1,0:T(8,128)}), f32[16,192,128]{2,1,0:T(8,128)S(1)}, u32[]{:S(2)}, u32[]{:S(2)}) %all-to-all-start) | async-done | bytes 1572896 | tf_op jit(solution)/shard_map/all_to_all | solution.py:562
  97.6 8.6 %solve.1 = (f32[1,1,5,64,1080]{4,3,2,1,0:T(8,128)}, f32[2048,128]{1,0:T(8,128)}) custom-call(s32[1]{0:T(128)} %dynamic_slice.12.units_ref, s32[384]{0:T(512)S(1)} %get-tuple-element.16.table_ref, f32[3072,128]{1,0:T(8,128)S(1)} %bitcast.15, f32[960,128]{1,0:T(8,128)S(1)} %get-tuple-element.26.coef_ref, f32[9,32,128]{2,1,0:T(8,128)S(1)} %get-tuple-element.27.weight_ref), custom_call_target="tpu_custom_call" | custom-call | flops 40000000 | bytes 1048576 | tf_op jit(solution)/shard_map/solve/pallas_call | solution.py:68
  106.2 6.2 %all-to-all-start.1 = ((f32[128,16,128]{2,1,0:T(8,128)}), f32[128,16,128]{2,1,0:T(8,128)S(1)}, u32[]{:S(2)}, u32[]{:S(2)}) async-start(f32[128,16,128]{2,1,0:T(8,128)} %bitcast.8), calls=%async_computation.1 | async-start | bytes 2097152 | tf_op jit(solution)/shard_map/all_to_all | solution.py:567
  112.6 19.1 %all-to-all-done.1 = f32[128,16,128]{2,1,0:T(8,128)S(1)} async-done(((f32[128,16,128]{2,1,0:T(8,128)}), f32[128,16,128]{2,1,0:T(8,128)S(1)}, u32[]{:S(2)}, u32[]{:S(2)}) %all-to-all-start.1) | async-done | bytes 1048608 | tf_op jit(solution)/shard_map/all_to_all | solution.py:567
  131.7 6.5 %lines.1 = f32[1,7,96,512]{3,2,1,0:T(8,128)} custom-call(f32[2048,128]{1,0:T(8,128)S(1)} %bitcast.17, f32[35]{0:T(128)S(1)} %reshape.76.yield_ref, f32[14]{0:T(128)S(1)} %pad_maximum_fusion.rates_ref, f32[1,512]{1,0:T(1,128)S(1)} %copy-done.12, bf16[512,512]{1,0:T(8,128)(2,1)S(1)} %copy-done.8, bf16[512,512]{1,0:T(8,128)(2,1)S(1)} %copy-done.9, ...), custom_call_target="tpu_custom_call" | custom-call | flops 2000000000 | bytes 1048576 | tf_op jit(solution)/shard_map/lines/pallas_call | solution.py:68
  (64 shorter events, 5.5 us)
Async XLA Ops:
  0.6 72.9 %copy-start = (s32[32,270,1]{1,2,0:T(1,128)S(1)}, s32[32,270,1]{1,2,0:T(1,128)}, u32[]{:S(2)}) copy-start(s32[32,270,1]{1,2,0:T(1,128)} %param.28) | copy-start | bytes 103684
  3.8 15.0 %collective-permute-start.3 = (f32[6,8,2880]{2,1,0:T(8,128)S(1)}, f32[6,8,2880]{2,1,0:T(8,128)S(1)}, u32[]{:S(2)}, u32[]{:S(2)}) collective-permute-start(f32[6,8,2880]{2,1,0:T(8,128)S(1)} %get-tuple-element.20), channel_id=1, source_target_pairs={{1,0},{2,1},{3,2},{4,3},{5,4},{6,5},{7,6},{8,7},{9,8},{10,9},{11,1... | collective-permute-start | bytes 1658888 | tf_op jit(solution)/shard_map/ppermute | solution.py:499
  7.1 11.7 %collective-permute-start.2 = (f32[5,8,2880]{2,1,0:T(8,128)S(1)}, f32[5,8,2880]{2,1,0:T(8,128)S(1)}, u32[]{:S(2)}, u32[]{:S(2)}) collective-permute-start(f32[5,8,2880]{2,1,0:T(8,128)S(1)} %get-tuple-element.19), channel_id=1, source_target_pairs={{0,1},{1,2},{2,3},{3,4},{4,5},{5,6},{6,7},{7,8},{8,9},{9,10},{10,1... | collective-permute-start | bytes 1382408 | tf_op jit(solution)/shard_map/ppermute | solution.py:494
  10.3 8.6 %collective-permute-start.1 = (f32[6,2,1,2880]{3,2,1,0:T(1,128)S(1)}, f32[6,2,1,2880]{3,2,1,0:T(1,128)S(1)}, u32[]{:S(2)}, u32[]{:S(2)}) collective-permute-start(f32[6,2,1,2880]{3,2,1,0:T(1,128)S(1)} %get-tuple-element.18), channel_id=1, source_target_pairs={{32,0},{64,32},{96,64},{33,1},{65,33},{97,65},{34,2},{66,34},{98,6... | collective-permute-start | bytes 414728 | tf_op jit(solution)/shard_map/ppermute | solution.py:499
  11.6 25.5 %copy-start.5 = (f32[2,8,2880]{2,1,0:T(8,128)S(1)}, f32[2,8,2880]{2,1,0:T(8,128)}, u32[]{:S(2)}) copy-start(f32[2,8,2880]{2,1,0:T(8,128)} %wlev_ref.5) | copy-start | bytes 552964
  11.6 7.3 %collective-permute-start = (f32[5,2,1,2880]{3,2,1,0:T(1,128)S(1)}, f32[5,2,1,2880]{3,2,1,0:T(1,128)S(1)}, u32[]{:S(2)}, u32[]{:S(2)}) collective-permute-start(f32[5,2,1,2880]{3,2,1,0:T(1,128)S(1)} %get-tuple-element.17), channel_id=1, source_target_pairs={{0,32},{32,64},{64,96},{1,33},{33,65},{65,97},{2,34},{34,66},{66,9... | collective-permute-start | bytes 345608 | tf_op jit(solution)/shard_map/ppermute | solution.py:494
  21.7 15.4 %collective-permute-start.6 = (f32[5,8,2880]{2,1,0:T(8,128)S(1)}, f32[5,8,2880]{2,1,0:T(8,128)S(1)}, u32[]{:S(2)}, u32[]{:S(2)}) collective-permute-start(f32[5,8,2880]{2,1,0:T(8,128)S(1)} %get-tuple-element.24), channel_id=1, source_target_pairs={{0,1},{1,2},{2,3},{3,4},{4,5},{5,6},{6,7},{7,8},{8,9},{9,10},{10,1... | collective-permute-start | bytes 1382408 | tf_op jit(solution)/shard_map/ppermute | solution.py:494
  25.1 12.0 %collective-permute-start.7 = (f32[5,8,2880]{2,1,0:T(8,128)S(1)}, f32[5,8,2880]{2,1,0:T(8,128)S(1)}, u32[]{:S(2)}, u32[]{:S(2)}) collective-permute-start(f32[5,8,2880]{2,1,0:T(8,128)S(1)} %get-tuple-element.25), channel_id=1, source_target_pairs={{1,0},{2,1},{3,2},{4,3},{5,4},{6,5},{7,6},{8,7},{9,8},{10,9},{11,1... | collective-permute-start | bytes 1382408 | tf_op jit(solution)/shard_map/ppermute | solution.py:499
  27.0 5.9 %collective-permute-start.4 = (f32[5,2,1,2880]{3,2,1,0:T(1,128)S(1)}, f32[5,2,1,2880]{3,2,1,0:T(1,128)S(1)}, u32[]{:S(2)}, u32[]{:S(2)}) collective-permute-start(f32[5,2,1,2880]{3,2,1,0:T(1,128)S(1)} %get-tuple-element.22), channel_id=1, source_target_pairs={{0,32},{32,64},{64,96},{1,33},{33,65},{65,97},{2,34},{34,66},{66,9... | collective-permute-start | bytes 345608 | tf_op jit(solution)/shard_map/ppermute | solution.py:494
  31.2 5.9 %collective-permute-start.5 = (f32[5,2,1,2880]{3,2,1,0:T(1,128)S(1)}, f32[5,2,1,2880]{3,2,1,0:T(1,128)S(1)}, u32[]{:S(2)}, u32[]{:S(2)}) collective-permute-start(f32[5,2,1,2880]{3,2,1,0:T(1,128)S(1)} %get-tuple-element.23), channel_id=1, source_target_pairs={{32,0},{64,32},{96,64},{33,1},{65,33},{97,65},{34,2},{66,34},{98,6... | collective-permute-start | bytes 345608 | tf_op jit(solution)/shard_map/ppermute | solution.py:499
  37.1 2.0 %copy-start.13 = (s32[1,23040]{1,0:T(1,128)S(1)}, s32[1,23040]{1,0:T(1,128)}, u32[]{:S(2)}) copy-start(s32[1,23040]{1,0:T(1,128)} %param.26) | copy-start | bytes 276484
  37.1 2.3 %copy-start.7 = (s32[32]{0:T(128)S(1)}, s32[32]{0:T(128)}, u32[]{:S(2)}) copy-start(s32[32]{0:T(128)} %units_ref.1) | copy-start | bytes 388
  39.0 2.6 %collective-permute-start.8 = (f32[23,80,128]{2,1,0:T(8,128)S(1)}, f32[23,80,128]{2,1,0:T(8,128)S(1)}, u32[]{:S(2)}, u32[]{:S(2)}) collective-permute-start(f32[23,80,128]{2,1,0:T(8,128)S(1)} %transport.3.mine_ref), channel_id=1, source_target_pairs={{0,1},{1,0},{2,3},{3,2},{4,5},{5,4},{6,7},{7,6},{8,9},{9,8},{10,11... | collective-permute-start | bytes 2826248 | tf_op jit(solution)/shard_map/ppermute | solution.py:557
  61.4 11.3 %copy-start.15 = (f32[5,64]{1,0:T(8,128)S(1)}, f32[5,64]{1,0:T(8,128)}, u32[]{:S(2)}) copy-start(f32[5,64]{1,0:T(8,128)} %param.21) | copy-start | bytes 3844
  61.4 36.2 %all-to-all-start = ((f32[16,192,128]{2,1,0:T(8,128)}), f32[16,192,128]{2,1,0:T(8,128)S(1)}, u32[]{:S(2)}, u32[]{:S(2)}) async-start(f32[16,192,128]{2,1,0:T(8,128)} %bitcast.6), calls=%async_computation | async-start | bytes 3145728 | tf_op jit(solution)/shard_map/all_to_all | solution.py:562
  97.6 14.8 %copy-start.14 = (f32[7,5]{1,0:T(8,128)S(1)}, f32[7,5]{1,0:T(8,128)}, u32[]{:S(2)}) copy-start(f32[7,5]{1,0:T(8,128)} %param.23) | copy-start | bytes 424
  106.2 6.3 %copy-start.16 = (f32[7]{0:T(128)S(1)}, f32[7]{0:T(128)}, u32[]{:S(2)}) copy-start(f32[7]{0:T(128)} %param.25) | copy-start | bytes 88
  106.2 6.3 %copy-start.17 = (f32[7]{0:T(128)S(1)}, f32[7]{0:T(128)}, u32[]{:S(2)}) copy-start(f32[7]{0:T(128)} %param.24) | copy-start | bytes 88
  106.2 25.5 %copy-start.8 = (bf16[512,512]{1,0:T(8,128)(2,1)S(1)}, bf16[512,512]{1,0:T(8,128)(2,1)}, u32[]{:S(2)}) copy-start(bf16[512,512]{1,0:T(8,128)(2,1)} %constant.116.clone.fwd_high) | copy-start | bytes 1572868
  106.2 25.5 %copy-start.9 = (bf16[512,512]{1,0:T(8,128)(2,1)S(1)}, bf16[512,512]{1,0:T(8,128)(2,1)}, u32[]{:S(2)}) copy-start(bf16[512,512]{1,0:T(8,128)(2,1)} %constant.117.clone.fwd_low) | copy-start | bytes 1572868
  106.2 25.4 %copy-start.10 = (bf16[512,512]{1,0:T(8,128)(2,1)S(1)}, bf16[512,512]{1,0:T(8,128)(2,1)}, u32[]{:S(2)}) copy-start(bf16[512,512]{1,0:T(8,128)(2,1)} %constant.118.clone.inv_high) | copy-start | bytes 1572868
  106.2 25.4 %copy-start.11 = (bf16[512,512]{1,0:T(8,128)(2,1)S(1)}, bf16[512,512]{1,0:T(8,128)(2,1)}, u32[]{:S(2)}) copy-start(bf16[512,512]{1,0:T(8,128)(2,1)} %constant.119.clone.inv_low) | copy-start | bytes 1572868
  106.2 25.4 %copy-start.12 = (f32[1,512]{1,0:T(1,128)S(1)}, f32[1,512]{1,0:T(1,128)}, u32[]{:S(2)}) copy-start(f32[1,512]{1,0:T(1,128)} %constant.133.waves_ref) | copy-start | bytes 6148
  106.2 25.4 %all-to-all-start.1 = ((f32[128,16,128]{2,1,0:T(8,128)}), f32[128,16,128]{2,1,0:T(8,128)S(1)}, u32[]{:S(2)}, u32[]{:S(2)}) async-start(f32[128,16,128]{2,1,0:T(8,128)} %bitcast.8), calls=%async_computation.1 | async-start | bytes 2097152 | tf_op jit(solution)/shard_map/all_to_all | solution.py:567
  (5 other events, 5.8 us)

commit v3 on v2

--- a/solution.py
+++ b/solution.py
@@ -33,7 +33,11 @@
 LEVEL_PITCH = 257
 PLANES = 12
 GROUPS = 6
-MSG_ROWS = 192
+CHUNKS = 3
+MSG_ROWS = 64
+PEER_ROWS = CHUNKS * MSG_ROWS
+CHUNK_BLOCKS = 3
+CHUNK_SLOTS = GROUPS * MSG_ROWS
 SLOT_BLOCKS = 9
 SLOTS_PAD = SLOT_BLOCKS * LANES
 ORDER_PAD = BAND_COLS + LANES
@@ -45,14 +49,14 @@
 VMEM = pl.BlockSpec(memory_space=pltpu.VMEM)
 HELD = pl.BlockSpec(memory_space=pltpu.VMEM)
 SMEM = pl.BlockSpec(memory_space=pltpu.SMEM)
-ANY = pl.BlockSpec(memory_space=pl.ANY)
+HBM = pl.BlockSpec(memory_space=pltpu.HBM)
 
 
 def on_chip(shape, dtype=f32):
     return pltpu.VMEM(shape, dtype)
 
 
-def call(kernel, out_shape, in_specs, out_specs, scratch=(), name=None, flops=0, vmem=16):
+def call(kernel, out_shape, in_specs, out_specs, scratch=(), name=None, flops=0, vmem=16, aliases=()):
     run = pl.pallas_call(
         kernel,
         out_shape=out_shape,
@@ -60,14 +64,17 @@
         out_specs=out_specs,
         scratch_shapes=list(scratch),
         name=name,
+        input_output_aliases=dict(aliases),
         cost_estimate=pl.CostEstimate(flops=flops, bytes_accessed=1 << 20, transcendentals=0),
         compiler_params=pltpu.CompilerParams(vmem_limit_bytes=vmem * 1024 * 1024),
     )
 
+    def place(x, spec):
+        space = pltpu.VMEM if spec is HELD else pltpu.HBM if spec is HBM else None
+        return x if space is None else pltpu.with_memory_space_constraint(x, space)
+
     def placed(*args):
-        return run(
-            *(pltpu.with_memory_space_constraint(x, pltpu.VMEM) if spec is HELD else x for x, spec in zip(args, in_specs))
-        )
+        return run(*(place(x, spec) for x, spec in zip(args, in_specs)))
 
     return placed
 
@@ -80,7 +87,20 @@
     return courant_plus * upstream + courant_minus * downstream
 
 
-def edges_kernel(n_ref, wlat_ref, wlev_ref, low_ref, high_ref, first_ref, last_ref):
+def edges_kernel(
+    n_hbm, wlon_hbm, wlat_hbm, wlev_hbm,
+    n_ref, wlon_ref, wlat_ref, wlev_ref, low_ref, high_ref, first_ref, last_ref, sems,
+):
+    fetches = [
+        pltpu.make_async_copy(n_hbm.at[s], n_ref.at[s], sems.at[s]) for s in range(SPECIES)
+    ]
+    fetches.append(pltpu.make_async_copy(wlat_hbm, wlat_ref, sems.at[SPECIES]))
+    fetches.append(pltpu.make_async_copy(wlev_hbm, wlev_ref, sems.at[SPECIES + 1]))
+    fetches.append(pltpu.make_async_copy(wlon_hbm, wlon_ref, sems.at[SPECIES + 2]))
+    for fetch in fetches:
+        fetch.start()
+    for fetch in fetches[:-1]:
+        fetch.wait()
     low_ref[SPECIES] = wlev_ref[0]
     for j in range(2):
         first_ref[SPECIES, j] = wlat_ref[j, :1]
@@ -93,21 +113,28 @@
             first_ref[s, j] = n_ref[s, j, :1]
             last_ref[s, j] = n_ref[s, j, BAND_LATS - 1 :]
 
-
-def edges(density, wind_lat, wind_lev):
+    fetches[-1].wait()
+
+
+def edges(density, wind_lon, wind_lat, wind_lev):
     return call(
         edges_kernel,
         (
+            on_chip(density.shape),
+            on_chip(wind_lon.shape),
+            on_chip(wind_lat.shape),
+            on_chip(wind_lev.shape),
             on_chip((SPECIES + 1, BAND_LATS, NLON)),
             on_chip((SPECIES, BAND_LATS, NLON)),
             on_chip((SPECIES + 1, 2, 1, NLON)),
             on_chip((SPECIES, 2, 1, NLON)),
         ),
-        [HELD] * 3,
-        (VMEM,) * 4,
+        [HBM] * 4,
+        (VMEM,) * 8,
+        [pltpu.SemaphoreType.DMA((SPECIES + 3,))],
         name="edges",
         flops=1_000_000,
-    )(density, wind_lat, wind_lev)
+    )(density, wind_lon, wind_lat, wind_lev)
 
 
 def transport_kernel(
@@ -247,75 +274,93 @@
     )(units, owners, rows, sel, weights, column)
 
 
-def pack_kernel(core_ref, starts_ref, units_ref, order_hbm, mine_ref, other_ref, msg_ref, order, planes, table, sem):
-    fetch = pltpu.make_async_copy(order_hbm, order, sem)
-    fetch.start()
-    core = core_ref[0]
-    for source, side in ((mine_ref, core), (other_ref, 1 - core)):
-
-        @pl.loop(0, LON_BLOCKS)
-        def _(blk):
-            for j in range(2):
-                for i in range(PLANES):
-                    row = ((2 * side + j) * PLANES + i) * PITCH
-                    from_row = (j * SPECIES + i % SPECIES) * BAND_LATS
-                    planes[blk, pl.ds(row, BAND_LATS), :] = source[blk, from_row : from_row + BAND_LATS, :]
+def turn_kernel(source_ref, *refs, side):
+    table, planes = refs[-2:]
+    half = LANES // 2
+
+    @pl.loop(0, LON_BLOCKS)
+    def _(blk):
+        for j in range(2):
+            for i in range(PLANES):
+                from_row = (j * SPECIES + i % SPECIES) * BAND_LATS
+                planes[blk, pl.ds((j * PLANES + i) * PITCH, BAND_LATS), :] = source_ref[
+                    blk, from_row : from_row + BAND_LATS, :
+                ]
 
     @pl.loop(0, LON_BLOCKS)
     def _(blk):
         for lat in range(BAND_LATS):
             parts = [
-                planes[blk, pl.ds((jj * PLANES + first) * PITCH + lat, 8, stride=PITCH), :]
-                for jj in range(CHIP_LEVS)
+                planes[blk, pl.ds((j * PLANES + first) * PITCH + lat, 8, stride=PITCH), :]
+                for j in range(2)
                 for first in (0, 3, 1, 4)
             ]
             start = pl.multiple_of((lat * LON_BLOCKS + blk) * LANES, LANES)
-            table[pl.ds(start, LANES), :] = jnp.concatenate(parts, axis=0).T
-
-    fetch.wait()
+            table[pl.ds(start, LANES), side * half : (side + 1) * half] = jnp.concatenate(parts, axis=0).T
+
+
+def turn(side, source, *table):
+    return call(
+        functools.partial(turn_kernel, side=side),
+        on_chip((BAND_LATS * LON_PAD, LANES)),
+        [HELD] * (1 + len(table)),
+        VMEM,
+        [pltpu.VMEM((LON_BLOCKS, 2 * PLANES * PITCH, LANES), f32)],
+        name="turn",
+        flops=8_000_000,
+        aliases={1: 0} if table else {},
+    )(source, *table)
+
+
+def pack_kernel(core_ref, starts_ref, units_ref, order_ref, table_ref, out_hbm, msg_ref, sems):
+    core = core_ref[0]
     lane = lax.broadcasted_iota(jnp.int32, (1, LANES), 1)
     group_of = lax.div(lax.rem(lane, 32), SPECIES)
 
-    @pl.loop(0, 16 * GROUPS)
-    def _(turn):
-        peer = lax.div(turn, GROUPS)
-        group = turn - peer * GROUPS
+    def send(peer):
+        rows = pl.ds(pl.multiple_of(peer * PEER_ROWS, PEER_ROWS), PEER_ROWS)
+        return pltpu.make_async_copy(msg_ref.at[rows, :], out_hbm.at[rows, :], sems.at[peer])
+
+    @pl.loop(0, 16)
+    def _(peer):
         owner = 2 * peer + core
-        live = jnp.clip(TUBE_COLS * units_ref[owner] - MSG_ROWS * group, 0, MSG_ROWS)
-        first = TUBE_COLS * starts_ref[owner] + MSG_ROWS * group
-        mask = group_of == group
-
-        @pl.loop(0, lax.div(live + (UNROLL - 1), UNROLL))
-        def _(step):
-            base = first + step * UNROLL
-            row = pl.multiple_of(peer * MSG_ROWS + step * UNROLL, UNROLL)
-            places = order.at[pl.ds(base, UNROLL)]
-            for i in range(UNROLL):
-                value = table[pl.ds(places[i], 1), :]
+        live = TUBE_COLS * units_ref[owner]
+        first = TUBE_COLS * starts_ref[owner]
+
+        @pl.loop(0, lax.div(live + (MSG_ROWS - 1), MSG_ROWS))
+        def _(piece):
+            chunk = lax.div(piece, GROUPS)
+            mask = group_of == piece - chunk * GROUPS
+            row = pl.multiple_of(peer * PEER_ROWS + chunk * MSG_ROWS, MSG_ROWS)
+            places = order_ref.at[pl.ds(first + piece * MSG_ROWS, MSG_ROWS)]
+            for i in range(MSG_ROWS):
+                value = table_ref[pl.ds(places[i], 1), :]
                 pltpu.store(msg_ref.at[pl.ds(row + i, 1), :], value, mask=mask)
 
-
-def pack(core, starts, units, order, mine, other):
+        send(peer).start()
+
+    @pl.loop(0, 16)
+    def _(peer):
+        send(peer).wait()
+
+
+def pack(core, starts, units, order, table):
     return call(
         pack_kernel,
-        on_chip((16 * MSG_ROWS, LANES)),
-        [SMEM, SMEM, SMEM, ANY, HELD, HELD],
-        VMEM,
-        [
-            pltpu.SMEM((ORDER_PAD,), jnp.int32),
-            pltpu.VMEM((LON_BLOCKS, CHIP_LEVS * PLANES * PITCH, LANES), f32),
-            pltpu.VMEM((BAND_LATS * LON_PAD, LANES), f32),
-            pltpu.SemaphoreType.DMA,
-        ],
+        sds((16 * PEER_ROWS, LANES)),
+        [SMEM, SMEM, SMEM, SMEM, HELD],
+        HBM,
+        [pltpu.VMEM((16 * PEER_ROWS, LANES), f32), pltpu.SemaphoreType.DMA((16,))],
         name="pack",
-        flops=40_000_000,
-        vmem=32,
-    )(core, starts, units, order, mine, other)
+        flops=30_000_000,
+    )(core, starts, units, order, table)
 
 
 def solve_kernel(
-    units_ref, table_ref, got_ref, coef_ref, weight_ref, state_ref, items_ref, turned, natural, pairs, wide, tubes
+    core_ref, units_ref, table_ref, got_ref, coef_ref, weight_ref, state_hbm, items_ref,
+    turned, natural, pairs, wide, tubes, state, sems,
 ):
+    core = core_ref[0]
     live = TUBE_COLS * units_ref[0]
     lane = lax.broadcasted_iota(jnp.int32, (1, LANES), 1)
     low = lane < 64
@@ -324,54 +369,54 @@
     @pl.loop(0, 8)
     def _(i):
         for side in range(2):
-            row = pl.multiple_of((2 * i + side) * MSG_ROWS, MSG_ROWS)
             out = i * LEVEL_PITCH + side * LANES
-            turned[0, pl.ds(out, LANES), :] = got_ref[pl.ds(row, LANES), :].T
-            rest = jnp.concatenate([got_ref[pl.ds(row + LANES, 64), :]] * 2, axis=0)
-            turned[1, pl.ds(out, LANES), :] = rest.T
-
-    for pair in range(3):
-
-        @pl.loop(0, SPECIES)
-        def _(s):
-            def coefs(which):
-                row = pl.multiple_of((which * SPECIES + s) * NLEV, NLEV)
-                return [coef_ref[pl.ds(row + 8 * v, 8), :] for v in range(8)]
-
-            lower, upper, inv = coefs(0), coefs(1), coefs(2)
-
-            def levels(half, group, v):
-                return turned[half, pl.ds(32 * v + group * SPECIES + s, 8, stride=LEVEL_PITCH), :]
-
-            first = [levels(0, 2 * pair, v) for v in range(8)]
-            odd = [pltpu.roll(levels(0, 2 * pair + 1, v), 64, axis=1) for v in range(8)]
-            second = [jnp.where(low, levels(1, 2 * pair, v), odd[v]) for v in range(8)]
-            third = [jnp.where(low, odd[v], levels(1, 2 * pair + 1, v)) for v in range(8)]
-            for i, rhs in enumerate((first, second, third)):
-                blk = 3 * pair + i
-                scaled = [rhs[v] * inv[v] for v in range(8)]
-                x = rhs
-                for _ in range(SWEEPS):
-                    beneath = [pltpu.roll(x[7], 1, axis=0)] + x[:7]
-                    overhead = x[1:] + [pltpu.roll(x[0], 7, axis=0)]
-                    x = [scaled[v] + lower[v] * beneath[v] + upper[v] * overhead[v] for v in range(8)]
-                keep = lane + blk * LANES < live
-                for v in range(8):
-                    natural[i, pl.ds(v, 8, stride=PITCH), :] = jnp.where(keep, x[v], 0.0)
-                width = min(LANES, COL_CAP - blk * LANES)
-                for g in range(8):
-                    state_ref[0, 0, s, g * 8 : g * 8 + 8, blk * LANES : blk * LANES + width] = natural[
-                        i, g * PITCH : g * PITCH + 8, :width
-                    ]
-                for h in range(4):
-                    weight = weight_ref[blk, 8 * h : 8 * h + 8, :]
-                    paired = weight * x[2 * h] + (1.0 - weight) * x[2 * h + 1]
-                    pairs[i, pl.ds(h, 8, stride=4), :] = paired
-                wide[i] = jnp.concatenate([pairs[i]] * 4, axis=0).T
-                item = wide[i, pl.ds(0, 32, stride=TUBE_COLS), :]
-                for c in range(1, TUBE_COLS):
-                    item = jnp.where(quarter == c, wide[i, pl.ds(c, 32, stride=TUBE_COLS), :], item)
-                tubes[pl.ds(blk * 256 + s, 32, stride=8), :] = item
+            for chunk in range(CHUNKS):
+                row = pl.multiple_of((2 * i + side) * PEER_ROWS + chunk * MSG_ROWS, MSG_ROWS)
+                flipped = jnp.concatenate([got_ref[pl.ds(row, MSG_ROWS), :]] * 2, axis=0).T
+                turned[chunk, pl.ds(out + 64 * core, 64), :] = flipped[:64]
+                turned[chunk, pl.ds(out + 64 - 64 * core, 64), :] = flipped[64:]
+
+    def leave(s):
+        return pltpu.make_async_copy(state.at[s], state_hbm.at[0, 0, s], sems.at[s])
+
+    @pl.loop(0, SPECIES)
+    def _(s):
+        def coefs(which):
+            row = pl.multiple_of((which * SPECIES + s) * NLEV, NLEV)
+            return [coef_ref[pl.ds(row + 8 * v, 8), :] for v in range(8)]
+
+        lower, upper, inv = coefs(0), coefs(1), coefs(2)
+        for blk in range(SLOT_BLOCKS):
+            chunk, i = divmod(blk, 3)
+
+            def levels(group, v):
+                return turned[chunk, pl.ds(32 * v + group * SPECIES + s, 8, stride=LEVEL_PITCH), :]
+
+            rhs = [jnp.where(low, levels(2 * i, v), levels(2 * i + 1, v)) for v in range(8)]
+            scaled = [rhs[v] * inv[v] for v in range(8)]
+            x = rhs
+            for _ in range(SWEEPS):
+                beneath = [pltpu.roll(x[7], 1, axis=0)] + x[:7]
+                overhead = x[1:] + [pltpu.roll(x[0], 7, axis=0)]
+                x = [scaled[v] + lower[v] * beneath[v] + upper[v] * overhead[v] for v in range(8)]
+            keep = lane + blk * LANES < live
+            for v in range(8):
+                natural[i, pl.ds(v, 8, stride=PITCH), :] = jnp.where(keep, x[v], 0.0)
+            width = min(LANES, COL_CAP - blk * LANES)
+            for g in range(8):
+                state[s, g * 8 : g * 8 + 8, blk * LANES : blk * LANES + width] = natural[
+                    i, g * PITCH : g * PITCH + 8, :width
+                ]
+            for h in range(4):
+                weight = weight_ref[blk, 8 * h : 8 * h + 8, :]
+                paired = weight * x[2 * h] + (1.0 - weight) * x[2 * h + 1]
+                pairs[i, pl.ds(h, 8, stride=4), :] = paired
+            wide[i] = jnp.concatenate([pairs[i]] * 4, axis=0).T
+            item = wide[i, pl.ds(0, 32, stride=TUBE_COLS), :]
+            for c in range(1, TUBE_COLS):
+                item = jnp.where(quarter == c, wide[i, pl.ds(c, 32, stride=TUBE_COLS), :], item)
+            tubes[pl.ds(blk * 256 + s, 32, stride=8), :] = item
+        leave(s).start()
 
     tubes[ZERO_TUBE * 8 :, :] = jnp.zeros((8, LANES), f32)
     sub = lax.broadcasted_iota(jnp.int32, (8, LANES), 0)
@@ -389,23 +434,28 @@
             items_ref[pl.ds(row, 8), :] = jnp.where(sub < 5, tiles[0], mid)
             items_ref[pl.ds(row + 8, 8), :] = jnp.where(sub < 2, mid, jnp.where(sub < 7, top, 0.0))
 
-
-def solve(units, table, got, coefs, weights):
+    for s in range(SPECIES):
+        leave(s).wait()
+
+
+def solve(core, units, table, got, coefs, weights):
     return call(
         solve_kernel,
-        (sds((1, 1, SPECIES, NLEV, COL_CAP)), on_chip((PEERS * ITEM_ROWS, LANES))),
-        [SMEM, SMEM] + [HELD] * 3,
-        (VMEM, VMEM),
+        (sds((1, 1, SPECIES, NLEV, COL_CAP)), sds((PEERS * ITEM_ROWS, LANES))),
+        [SMEM, SMEM, SMEM] + [HELD] * 3,
+        (HBM, VMEM),
         [
-            pltpu.VMEM((2, 8 * LEVEL_PITCH, LANES), f32),
+            pltpu.VMEM((CHUNKS, 8 * LEVEL_PITCH, LANES), f32),
             pltpu.VMEM((3, 8 * PITCH, LANES), f32),
             pltpu.VMEM((3, PAIRS, LANES), f32),
             pltpu.VMEM((3, LANES, LANES), f32),
             pltpu.VMEM((ZERO_TUBE * 8 + 8, LANES), f32),
+            pltpu.VMEM((SPECIES, NLEV, COL_CAP), f32),
+            pltpu.SemaphoreType.DMA((SPECIES,)),
         ],
         name="solve",
         flops=40_000_000,
-    )(units, table, got, coefs, weights)
+    )(core, units, table, got, coefs, weights)
 
 
 def halves(x):
@@ -420,7 +470,8 @@
 
 
 def lines_kernel(
-    items_ref, yield_ref, rates_ref, waves_ref, fwd_high, fwd_low, inv_high, inv_low, out_ref, spec_in, spec, mixed
+    items_ref, yield_ref, rates_ref, waves_ref, fwd_high, fwd_low, inv_high, inv_low, out_hbm,
+    spec_in, spec, mixed, done, sems,
 ):
     tubes = 32 * PEER_SLOTS
     for b in range(4):
@@ -448,9 +499,16 @@
             total = total + (yield_ref[i * SPECIES + s] * gain) * spec[s * tubes : (s + 1) * tubes, :]
         mixed[i] = total
 
+    def leave(i):
+        return pltpu.make_async_copy(done.at[i], out_hbm.at[0, i], sems.at[i])
+
     @pl.loop(0, IONS)
     def _(i):
-        out_ref[0, i] = product(mixed[i], inv_high[...], inv_low[...])
+        done[i] = product(mixed[i], inv_high[...], inv_low[...])
+        leave(i).start()
+
+    for i in range(IONS):
+        leave(i).wait()
 
 
 def cosine_basis():
@@ -477,11 +535,13 @@
         lines_kernel,
         sds((1, IONS, tubes, LINE_PTS)),
         [HELD, SMEM, SMEM] + [HELD] * 5,
-        VMEM,
+        HBM,
         [
             pltpu.VMEM((4, SPECIES * tubes, LANES), f32),
             pltpu.VMEM((SPECIES * tubes, LINE_PTS), f32),
             pltpu.VMEM((IONS, tubes, LINE_PTS), f32),
+            pltpu.VMEM((IONS, tubes, LINE_PTS), f32),
+            pltpu.SemaphoreType.DMA((IONS,)),
         ],
         name="lines",
         flops=2_000_000_000,
@@ -514,9 +574,8 @@
     tube_owner,
 ):
     lev = lax.axis_index("lev")
-    winds = (wind_lon, wind_lat, wind_lev)
-
-    low, high, first, last = edges(neutrals, wind_lat, wind_lev)
+
+    neutrals, *winds, low, high, first, last = edges(neutrals, wind_lon, wind_lat, wind_lev)
     below, above = up(high, "lev"), down(low, "lev")
     south, north = up(last, "band"), down(first, "band")
 
@@ -555,15 +614,16 @@
     (mine,) = transport_step(density, winds, halo, True)
     owners = lax.axis_size("lev")
     other = lax.ppermute(mine, "lev", [(i, i ^ 1) for i in range(owners)])
+    turned = turn(1, other, turn(0, mine))
 
     core = (lev % 2).reshape(1)
-    outgoing = pack(core, starts, column_units, rows, mine, other)
     parity = [[2 * i + c for i in range(owners // 2)] for c in range(2)]
+    outgoing = pack(core, starts, column_units, rows, turned)
     got = lax.all_to_all(
-        outgoing.reshape(16, MSG_ROWS, LANES), "lev", 0, 0, axis_index_groups=parity, tiled=True
-    ).reshape(16 * MSG_ROWS, LANES)
-
-    column_state, items = solve(own_units, table, got, coefs, own_weights)
+        outgoing.reshape(16, PEER_ROWS, LANES), "lev", 0, 0, axis_index_groups=parity, tiled=True
+    ).reshape(16 * PEER_ROWS, LANES)
+    column_state, items = solve(core, own_units, table, got, coefs, own_weights)
+
     items = lax.all_to_all(
         items.reshape(PEERS, ITEM_ROWS, LANES), ("band", "lev"), 0, 0, tiled=True
     ).reshape(PEERS * ITEM_ROWS, LANES)

time: 138 us -> 138 us (level)
  waiting for transfers between devices: 41.8 us -> 35.4 us
  Pallas kernels: 47.5 us -> 53.3 us
  local copies, waits for them, and re-layouts: 7.97 us -> 3.99 us
  starting transfers between devices: 38.4 us -> 42 us
    pallas_call x7 -> x9, Pallas kernels: 47.5 us -> 53.3 us  [placed(): return run(*(place(x, spec) for x, spec in zip(args, in_specs)))]
    all_to_all x1, waiting for transfers between devices: 13.3 us -> 8.71 us  [on_device(): lax.all_to_all(outgoing.reshape(16, PEER_ROWS, LANES), 'lev', 0, 0, axis_...]
    unnamed x36 -> x26, local copies, waits for them, and re-layouts: 5.88 us -> 1.92 us
    all_to_all x1, starting transfers between devices: 6.17 us -> 9.39 us  [on_device(): lax.all_to_all(items.reshape(PEERS, ITEM_ROWS, LANES), ('band', 'lev'), 0...]
    ppermute x1, waiting for transfers between devices: 1.86 us -> 0.01 us  [on_device(): other = lax.ppermute(mine, 'lev', [(i, i ^ 1) for i in range(owners)])]
  transfers between devices with their start and end apart: 11 -> 11, of which waited for: 6 -> 5; matrix products, arithmetic and copies ran while one was open for 2% -> 2% of each run, Pallas kernels for 6% -> 9%
where the time goes in v3:
time: 138 us; the launch traced here: 137 us
  Pallas kernels  53.3 us (39%)
  starting transfers between devices  42 us (30%)
  waiting for transfers between devices  35.4 us (26%)
  local copies, waits for them, and re-layouts  3.99 us (3%)
  between operations  1.67 us (1%)
    pallas_call x9, Pallas kernels, placed(): return run(*(place(x, spec) for x, spec in zip(args, in_specs)))  53.3 us
    all_to_all x1, waiting for transfers between devices, on_device(): lax.all_to_all(items.reshape(PEERS, ITEM_ROWS, LANES), ('band', 'lev'), 0...  19.1 us
    ppermute x4, starting transfers between devices, up(): return lax.ppermute(x, axis, [(i, i + 1) for i in range(ends)])  14.8 us
    all_to_all x1, starting transfers between devices, on_device(): lax.all_to_all(outgoing.reshape(16, PEER_ROWS, LANES), 'lev', 0, 0, axis_...  9.92 us
    all_to_all x1, starting transfers between devices, on_device(): lax.all_to_all(items.reshape(PEERS, ITEM_ROWS, LANES), ('band', 'lev'), 0...  9.39 us
    all_to_all x1, waiting for transfers between devices, on_device(): lax.all_to_all(outgoing.reshape(16, PEER_ROWS, LANES), 'lev', 0, 0, axis_...  8.71 us
    ppermute x4, starting transfers between devices, down(): return lax.ppermute(x, axis, [(i + 1, i) for i in range(ends)])  7.79 us
    ppermute x4, waiting for transfers between devices, down(): return lax.ppermute(x, axis, [(i + 1, i) for i in range(ends)])  4.14 us
  transfers between devices with their start and end apart: 11, of which 5 were waited for; matrix products, arithmetic and copies ran while one was open for 2% of the time, Pallas kernels for 9%

profile of v3, /device:TPU:1, one launch (start us, length us, event | category | flops | bytes accessed | tf_op | source)
XLA Modules:
  0.0 137.1 jit_solution(11873095221471201203)
XLA Ops:
  0.6 1.6 %edges.1 = (f32[5,2,8,2880]{3,2,1,0:T(8,128)S(1)}, f32[2,8,2880]{2,1,0:T(8,128)S(1)}, f32[2,8,2880]{2,1,0:T(8,128)S(1)}, f32[2,8,2880]{2,1,0:T(8,128)S(1)}, f32[...) custom-call(f32[5,2,8,2880]{3,2,1,0:T(8,128)} %n_hbm.1, ...), custom_call_target="tpu_custom_call" | custom-call | flops 1000000 | bytes 1048576 | tf_op jit(solution)/shard_map/edges/pallas_call | solution.py:77
  2.2 3.3 %collective-permute-start.3 = (f32[6,8,2880]{2,1,0:T(8,128)S(1)}, f32[6,8,2880]{2,1,0:T(8,128)S(1)}, u32[]{:S(2)}, u32[]{:S(2)}) collective-permute-start(f32[6,8,2880]{2,1,0:T(8,128)S(1)} %get-tuple-element.28), channel_id=1, source_target_pairs={{1,0},{2,1},{3,2},{4,3},{5,4},{6,5},{7,6},{8,7},{9,8},{10,9},{11,1... | collective-permute-start | bytes 1658888 | tf_op jit(solution)/shard_map/ppermute | solution.py:559
  5.5 3.1 %collective-permute-start.2 = (f32[5,8,2880]{2,1,0:T(8,128)S(1)}, f32[5,8,2880]{2,1,0:T(8,128)S(1)}, u32[]{:S(2)}, u32[]{:S(2)}) collective-permute-start(f32[5,8,2880]{2,1,0:T(8,128)S(1)} %get-tuple-element.27), channel_id=1, source_target_pairs={{0,1},{1,2},{2,3},{3,4},{4,5},{5,6},{6,7},{7,8},{8,9},{9,10},{10,1... | collective-permute-start | bytes 1382408 | tf_op jit(solution)/shard_map/ppermute | solution.py:554
  8.7 1.3 collective-permute-start.1
  10.0 4.2 %collective-permute-start = (f32[5,2,1,2880]{3,2,1,0:T(1,128)S(1)}, f32[5,2,1,2880]{3,2,1,0:T(1,128)S(1)}, u32[]{:S(2)}, u32[]{:S(2)}) collective-permute-start(f32[5,2,1,2880]{3,2,1,0:T(1,128)S(1)} %get-tuple-element.25), channel_id=1, source_target_pairs={{0,32},{32,64},{64,96},{1,33},{33,65},{65,97},{2,34},{34,66},{66,9... | collective-permute-start | bytes 345608 | tf_op jit(solution)/shard_map/ppermute | solution.py:554
  14.2 2.9 %collective-permute-done.south_ref = f32[5,2,1,2880]{3,2,1,0:T(1,128)S(1)} collective-permute-done((f32[5,2,1,2880]{3,2,1,0:T(1,128)S(1)}, f32[5,2,1,2880]{3,2,1,0:T(1,128)S(1)}, u32[]{:S(2)}, u32[]{:S(2)}) %collective-permute-start) | collective-permute-done | bytes 115232 | tf_op jit(solution)/shard_map/ppermute | solution.py:554
  17.1 2.0 %transport.2 = (f32[5,2,8,2880]{3,2,1,0:T(8,128)S(1)}, f32[5,8,2880]{2,1,0:T(8,128)S(1)}, f32[5,8,2880]{2,1,0:T(8,128)S(1)}, f32[5,2,1,2880]{3,2,1,0:T(1,128)S(1)}, f32[5,2,1,2880]{3,2,1,0:T(1,128)S(1)}) custom-call(f32[5,2,8,2880]{3,2,1,0:T(8,128)S(1)} %get-tuple-element.21.n_ref, f32[2,8,2880]{2,1,0:T(8,128)S(1)} %get-tuple-element.22.wlon_ref, ...), custom_call_target="tpu_custom_call" | custom-call | flops 4000000 | bytes 1048576 | tf_op jit(solution)/shard_map/transport/pallas_call | solution.py:77
  19.1 3.4 %collective-permute-start.6 = (f32[5,8,2880]{2,1,0:T(8,128)S(1)}, f32[5,8,2880]{2,1,0:T(8,128)S(1)}, u32[]{:S(2)}, u32[]{:S(2)}) collective-permute-start(f32[5,8,2880]{2,1,0:T(8,128)S(1)} %get-tuple-element.32), channel_id=1, source_target_pairs={{0,1},{1,2},{2,3},{3,4},{4,5},{5,6},{6,7},{7,8},{8,9},{9,10},{10,1... | collective-permute-start | bytes 1382408 | tf_op jit(solution)/shard_map/ppermute | solution.py:554
  22.5 1.9 %collective-permute-start.7 = (f32[5,8,2880]{2,1,0:T(8,128)S(1)}, f32[5,8,2880]{2,1,0:T(8,128)S(1)}, u32[]{:S(2)}, u32[]{:S(2)}) collective-permute-start(f32[5,8,2880]{2,1,0:T(8,128)S(1)} %get-tuple-element.33), channel_id=1, source_target_pairs={{1,0},{2,1},{3,2},{4,3},{5,4},{6,5},{7,6},{8,7},{9,8},{10,9},{11,1... | collective-permute-start | bytes 1382408 | tf_op jit(solution)/shard_map/ppermute | solution.py:559
  24.4 4.1 %collective-permute-start.4 = (f32[5,2,1,2880]{3,2,1,0:T(1,128)S(1)}, f32[5,2,1,2880]{3,2,1,0:T(1,128)S(1)}, u32[]{:S(2)}, u32[]{:S(2)}) collective-permute-start(f32[5,2,1,2880]{3,2,1,0:T(1,128)S(1)} %get-tuple-element.30), channel_id=1, source_target_pairs={{0,32},{32,64},{64,96},{1,33},{33,65},{65,97},{2,34},{34,66},{66,9... | collective-permute-start | bytes 345608 | tf_op jit(solution)/shard_map/ppermute | solution.py:554
  28.5 1.3 collective-permute-start.5
  30.3 4.1 %collective-permute-done.5.north_ref = f32[5,2,1,2880]{3,2,1,0:T(1,128)S(1)} collective-permute-done((f32[5,2,1,2880]{3,2,1,0:T(1,128)S(1)}, f32[5,2,1,2880]{3,2,1,0:T(1,128)S(1)}, u32[]{:S(2)}, u32[]{:S(2)}) %collective-permute-start.5) | collective-permute-done | bytes 115232 | tf_op jit(solution)/shard_map/ppermute | solution.py:559
  34.5 1.8 %transport.3.source_ref = f32[23,80,128]{2,1,0:T(8,128)S(1)} custom-call(f32[5,2,8,2880]{3,2,1,0:T(8,128)S(1)} %get-tuple-element.29.n_ref, f32[2,8,2880]{2,1,0:T(8,128)S(1)} %get-tuple-element.22.wlon_ref, f32[2,8,2880]{2,1,0:T(8,128)S(1)} %get-tuple-element.23.wlat_ref, f32[2,8,2880]{2,1,0:T(8,128)S(1)} %get-tuple-element.24.wlev_ref, ...), custom_call_target="tpu_custom_call" | custom-call | flops 4000000 | bytes 1048576 | tf_op jit(solution)/shard_map/transport/pallas_call | solution.py:77
  37.0 5.0 %turn.2.refs_0_ = f32[23552,128]{1,0:T(8,128)S(1)} custom-call(f32[23,80,128]{2,1,0:T(8,128)S(1)} %transport.3.source_ref), custom_call_target="tpu_custom_call" | custom-call | flops 8000000 | bytes 1048576 | tf_op jit(solution)/shard_map/turn/pallas_call | solution.py:77
  42.0 8.5 %turn.3.table_ref = f32[23552,128]{1,0:T(8,128)S(1)} custom-call(f32[23,80,128]{2,1,0:T(8,128)S(1)} %collective-permute-done.8.source_ref, f32[23552,128]{1,0:T(8,128)S(1)} %turn.2.refs_0_), custom_call_target="tpu_custom_call", output_to_operand_aliasing={{}: (1, {})} | custom-call | flops 8000000 | bytes 1048576 | tf_op jit(solution)/shard_map/turn/pallas_call | solution.py:77
  50.6 13.5 %pack.1 = f32[3072,128]{1,0:T(8,128)} custom-call(s32[1]{0:T(128)} %bitcast.core_ref, s32[32]{0:T(128)S(1)} %sub.16.starts_ref, s32[32]{0:T(128)S(1)} %copy-done.2, s32[23168]{0:T(1024)S(1)} %pad.11.order_ref, f32[23552,128]{1,0:T(8,128)S(1)} %turn.3.table_ref), custom_call_target="tpu_custom_call" | custom-call | flops 30000000 | bytes 1048576 | tf_op jit(solution)/shard_map/pack/pallas_call | solution.py:77
  64.0 9.9 %all-to-all-start = ((f32[16,192,128]{2,1,0:T(8,128)}), f32[16,192,128]{2,1,0:T(8,128)S(1)}, u32[]{:S(2)}, u32[]{:S(2)}) async-start(f32[16,192,128]{2,1,0:T(8,128)} %bitcast.6), calls=%async_computation | async-start | bytes 3145728 | tf_op jit(solution)/shard_map/all_to_all | solution.py:622
  76.8 1.8 %copy-done.1 = f32[32,8,2880]{2,1,0:T(8,128)S(1)} copy-done((f32[32,8,2880]{2,1,0:T(8,128)S(1)}, f32[32,8,2880]{2,1,0:T(8,128)}, u32[]{:S(2)}) %copy-start.1) | copy-done | bytes 2949144
  78.6 7.9 %prepare.1 = (s32[384]{0:T(512)S(1)}, f32[9,32,128]{2,1,0:T(8,128)S(1)}, f32[960,128]{1,0:T(8,128)S(1)}) custom-call(s32[1]{0:T(128)} %dynamic_slice.12.units_ref, s32[270]{0:T(512)S(1)} %dynamic-slice_reduce_fusion.owner_ref, s32[1152]{0:T(1024)S(1)} %get-tuple-element.39.rows_ref, s32[9,128]{1,0:T(8,128)S(1)} %get-tuple-element.38.sel_ref, ...), custom_call_target="tpu_custom_call" | custom-call | flops 20000000 | bytes 1048576 | tf_op jit(solution)/shard_map/prepare/pallas_call | solution.py:77
  86.5 8.7 %all-to-all-done = f32[16,192,128]{2,1,0:T(8,128)S(1)} async-done(((f32[16,192,128]{2,1,0:T(8,128)}), f32[16,192,128]{2,1,0:T(8,128)S(1)}, u32[]{:S(2)}, u32[]{:S(2)}) %all-to-all-start) | async-done | bytes 1572896 | tf_op jit(solution)/shard_map/all_to_all | solution.py:622
  95.2 7.0 %solve.1 = (f32[1,1,5,64,1080]{4,3,2,1,0:T(8,128)}, f32[2048,128]{1,0:T(8,128)}) custom-call(s32[1]{0:T(128)} %bitcast.core_ref, s32[1]{0:T(128)} %dynamic_slice.12.units_ref, s32[384]{0:T(512)S(1)} %get-tuple-element.20.table_ref, f32[3072,128]{1,0:T(8,128)S(1)} %bitcast.15, f32[960,128]{1,0:T(8,128)S(1)} %get-tuple-element.34.coef_ref, ...), custom_call_target="tpu_custom_call" | custom-call | flops 40000000 | bytes 1048576 | tf_op jit(solution)/shard_map/solve/pallas_call | solution.py:77
  102.3 9.4 %all-to-all-start.1 = ((f32[128,16,128]{2,1,0:T(8,128)}), f32[128,16,128]{2,1,0:T(8,128)S(1)}, u32[]{:S(2)}, u32[]{:S(2)}) async-start(f32[128,16,128]{2,1,0:T(8,128)} %bitcast.8), calls=%async_computation.1 | async-start | bytes 2097152 | tf_op jit(solution)/shard_map/all_to_all | solution.py:627
  111.9 19.1 %all-to-all-done.1 = f32[128,16,128]{2,1,0:T(8,128)S(1)} async-done(((f32[128,16,128]{2,1,0:T(8,128)}), f32[128,16,128]{2,1,0:T(8,128)S(1)}, u32[]{:S(2)}, u32[]{:S(2)}) %all-to-all-start.1) | async-done | bytes 1048608 | tf_op jit(solution)/shard_map/all_to_all | solution.py:627
  131.0 6.1 %lines.1 = f32[1,7,96,512]{3,2,1,0:T(8,128)} custom-call(f32[2048,128]{1,0:T(8,128)S(1)} %bitcast.17, f32[35]{0:T(128)S(1)} %reshape.76.yield_ref, f32[14]{0:T(128)S(1)} %pad_maximum_fusion.rates_ref, f32[1,512]{1,0:T(1,128)S(1)} %copy-done.7, bf16[512,512]{1,0:T(8,128)(2,1)S(1)} %copy-done.3, bf16[512,512]{1,0:T(8,128)(2,1)S(1)} %copy-done.4, ...), custom_call_target="tpu_custom_call" | custom-call | flops 2000000000 | bytes 1048576 | tf_op jit(solution)/shard_map/lines/pallas_call | solution.py:77
  (56 shorter events, 3.5 us)
Async XLA Ops:
  0.6 76.0 %copy-start = (s32[32,270,1]{1,2,0:T(1,128)S(1)}, s32[32,270,1]{1,2,0:T(1,128)}, u32[]{:S(2)}) copy-start(s32[32,270,1]{1,2,0:T(1,128)} %param.28) | copy-start | bytes 103684
  2.2 14.9 %collective-permute-start.3 = (f32[6,8,2880]{2,1,0:T(8,128)S(1)}, f32[6,8,2880]{2,1,0:T(8,128)S(1)}, u32[]{:S(2)}, u32[]{:S(2)}) collective-permute-start(f32[6,8,2880]{2,1,0:T(8,128)S(1)} %get-tuple-element.28), channel_id=1, source_target_pairs={{1,0},{2,1},{3,2},{4,3},{5,4},{6,5},{7,6},{8,7},{9,8},{10,9},{11,1... | collective-permute-start | bytes 1658888 | tf_op jit(solution)/shard_map/ppermute | solution.py:559
  5.5 11.6 %collective-permute-start.2 = (f32[5,8,2880]{2,1,0:T(8,128)S(1)}, f32[5,8,2880]{2,1,0:T(8,128)S(1)}, u32[]{:S(2)}, u32[]{:S(2)}) collective-permute-start(f32[5,8,2880]{2,1,0:T(8,128)S(1)} %get-tuple-element.27), channel_id=1, source_target_pairs={{0,1},{1,2},{2,3},{3,4},{4,5},{5,6},{6,7},{7,8},{8,9},{9,10},{10,1... | collective-permute-start | bytes 1382408 | tf_op jit(solution)/shard_map/ppermute | solution.py:554
  8.7 8.4 %collective-permute-start.1 = (f32[6,2,1,2880]{3,2,1,0:T(1,128)S(1)}, f32[6,2,1,2880]{3,2,1,0:T(1,128)S(1)}, u32[]{:S(2)}, u32[]{:S(2)}) collective-permute-start(f32[6,2,1,2880]{3,2,1,0:T(1,128)S(1)} %get-tuple-element.26), channel_id=1, source_target_pairs={{32,0},{64,32},{96,64},{33,1},{65,33},{97,65},{34,2},{66,34},{98,6... | collective-permute-start | bytes 414728 | tf_op jit(solution)/shard_map/ppermute | solution.py:559
  10.0 7.1 %collective-permute-start = (f32[5,2,1,2880]{3,2,1,0:T(1,128)S(1)}, f32[5,2,1,2880]{3,2,1,0:T(1,128)S(1)}, u32[]{:S(2)}, u32[]{:S(2)}) collective-permute-start(f32[5,2,1,2880]{3,2,1,0:T(1,128)S(1)} %get-tuple-element.25), channel_id=1, source_target_pairs={{0,32},{32,64},{64,96},{1,33},{33,65},{65,97},{2,34},{34,66},{66,9... | collective-permute-start | bytes 345608 | tf_op jit(solution)/shard_map/ppermute | solution.py:554
  19.1 15.4 %collective-permute-start.6 = (f32[5,8,2880]{2,1,0:T(8,128)S(1)}, f32[5,8,2880]{2,1,0:T(8,128)S(1)}, u32[]{:S(2)}, u32[]{:S(2)}) collective-permute-start(f32[5,8,2880]{2,1,0:T(8,128)S(1)} %get-tuple-element.32), channel_id=1, source_target_pairs={{0,1},{1,2},{2,3},{3,4},{4,5},{5,6},{6,7},{7,8},{8,9},{9,10},{10,1... | collective-permute-start | bytes 1382408 | tf_op jit(solution)/shard_map/ppermute | solution.py:554
  22.5 12.0 %collective-permute-start.7 = (f32[5,8,2880]{2,1,0:T(8,128)S(1)}, f32[5,8,2880]{2,1,0:T(8,128)S(1)}, u32[]{:S(2)}, u32[]{:S(2)}) collective-permute-start(f32[5,8,2880]{2,1,0:T(8,128)S(1)} %get-tuple-element.33), channel_id=1, source_target_pairs={{1,0},{2,1},{3,2},{4,3},{5,4},{6,5},{7,6},{8,7},{9,8},{10,9},{11,1... | collective-permute-start | bytes 1382408 | tf_op jit(solution)/shard_map/ppermute | solution.py:559
  24.4 5.9 %collective-permute-start.4 = (f32[5,2,1,2880]{3,2,1,0:T(1,128)S(1)}, f32[5,2,1,2880]{3,2,1,0:T(1,128)S(1)}, u32[]{:S(2)}, u32[]{:S(2)}) collective-permute-start(f32[5,2,1,2880]{3,2,1,0:T(1,128)S(1)} %get-tuple-element.30), channel_id=1, source_target_pairs={{0,32},{32,64},{64,96},{1,33},{33,65},{65,97},{2,34},{34,66},{66,9... | collective-permute-start | bytes 345608 | tf_op jit(solution)/shard_map/ppermute | solution.py:554
  28.5 5.9 %collective-permute-start.5 = (f32[5,2,1,2880]{3,2,1,0:T(1,128)S(1)}, f32[5,2,1,2880]{3,2,1,0:T(1,128)S(1)}, u32[]{:S(2)}, u32[]{:S(2)}) collective-permute-start(f32[5,2,1,2880]{3,2,1,0:T(1,128)S(1)} %get-tuple-element.31), channel_id=1, source_target_pairs={{32,0},{64,32},{96,64},{33,1},{65,33},{97,65},{34,2},{66,34},{98,6... | collective-permute-start | bytes 345608 | tf_op jit(solution)/shard_map/ppermute | solution.py:559
  34.5 2.0 %copy-start.8 = (s32[1,23040]{1,0:T(1,128)S(1)}, s32[1,23040]{1,0:T(1,128)}, u32[]{:S(2)}) copy-start(s32[1,23040]{1,0:T(1,128)} %param.26) | copy-start | bytes 276484
  34.5 2.3 %copy-start.2 = (s32[32]{0:T(128)S(1)}, s32[32]{0:T(128)}, u32[]{:S(2)}) copy-start(s32[32]{0:T(128)} %units_ref.1) | copy-start | bytes 388
  36.3 5.7 %collective-permute-start.8 = (f32[23,80,128]{2,1,0:T(8,128)S(1)}, f32[23,80,128]{2,1,0:T(8,128)S(1)}, u32[]{:S(2)}, u32[]{:S(2)}) collective-permute-start(f32[23,80,128]{2,1,0:T(8,128)S(1)} %transport.3.source_ref), channel_id=1, source_target_pairs={{0,1},{1,0},{2,3},{3,2},{4,5},{5,4},{6,7},{7,6},{8,9},{9,8},{10,11... | collective-permute-start | bytes 2826248 | tf_op jit(solution)/shard_map/ppermute | solution.py:616
  64.0 11.8 %copy-start.10 = (f32[5,64]{1,0:T(8,128)S(1)}, f32[5,64]{1,0:T(8,128)}, u32[]{:S(2)}) copy-start(f32[5,64]{1,0:T(8,128)} %param.21) | copy-start | bytes 3844
  64.0 31.2 %all-to-all-start = ((f32[16,192,128]{2,1,0:T(8,128)}), f32[16,192,128]{2,1,0:T(8,128)S(1)}, u32[]{:S(2)}, u32[]{:S(2)}) async-start(f32[16,192,128]{2,1,0:T(8,128)} %bitcast.6), calls=%async_computation | async-start | bytes 3145728 | tf_op jit(solution)/shard_map/all_to_all | solution.py:622
  76.8 1.9 %copy-start.1 = (f32[32,8,2880]{2,1,0:T(8,128)S(1)}, f32[32,8,2880]{2,1,0:T(8,128)}, u32[]{:S(2)}) copy-start(f32[32,8,2880]{2,1,0:T(8,128)} %param.22) | copy-start | bytes 8847364
  95.2 16.5 %copy-start.9 = (f32[7,5]{1,0:T(8,128)S(1)}, f32[7,5]{1,0:T(8,128)}, u32[]{:S(2)}) copy-start(f32[7,5]{1,0:T(8,128)} %param.23) | copy-start | bytes 424
  102.2 9.6 %copy-start.11 = (f32[7]{0:T(128)S(1)}, f32[7]{0:T(128)}, u32[]{:S(2)}) copy-start(f32[7]{0:T(128)} %param.25) | copy-start | bytes 88
  102.2 9.6 %copy-start.12 = (f32[7]{0:T(128)S(1)}, f32[7]{0:T(128)}, u32[]{:S(2)}) copy-start(f32[7]{0:T(128)} %param.24) | copy-start | bytes 88
  102.3 28.7 %copy-start.3 = (bf16[512,512]{1,0:T(8,128)(2,1)S(1)}, bf16[512,512]{1,0:T(8,128)(2,1)}, u32[]{:S(2)}) copy-start(bf16[512,512]{1,0:T(8,128)(2,1)} %constant.116.clone.fwd_high) | copy-start | bytes 1572868
  102.3 28.7 %copy-start.4 = (bf16[512,512]{1,0:T(8,128)(2,1)S(1)}, bf16[512,512]{1,0:T(8,128)(2,1)}, u32[]{:S(2)}) copy-start(bf16[512,512]{1,0:T(8,128)(2,1)} %constant.117.clone.fwd_low) | copy-start | bytes 1572868
  102.3 28.7 %copy-start.5 = (bf16[512,512]{1,0:T(8,128)(2,1)S(1)}, bf16[512,512]{1,0:T(8,128)(2,1)}, u32[]{:S(2)}) copy-start(bf16[512,512]{1,0:T(8,128)(2,1)} %constant.118.clone.inv_high) | copy-start | bytes 1572868
  102.3 28.7 %copy-start.6 = (bf16[512,512]{1,0:T(8,128)(2,1)S(1)}, bf16[512,512]{1,0:T(8,128)(2,1)}, u32[]{:S(2)}) copy-start(bf16[512,512]{1,0:T(8,128)(2,1)} %constant.119.clone.inv_low) | copy-start | bytes 1572868
  102.3 28.7 %copy-start.7 = (f32[1,512]{1,0:T(1,128)S(1)}, f32[1,512]{1,0:T(1,128)}, u32[]{:S(2)}) copy-start(f32[1,512]{1,0:T(1,128)} %constant.133.waves_ref) | copy-start | bytes 6148
  102.3 28.6 %all-to-all-start.1 = ((f32[128,16,128]{2,1,0:T(8,128)}), f32[128,16,128]{2,1,0:T(8,128)S(1)}, u32[]{:S(2)}, u32[]{:S(2)}) async-start(f32[128,16,128]{2,1,0:T(8,128)} %bitcast.8), calls=%async_computation.1 | async-start | bytes 2097152 | tf_op jit(solution)/shard_map/all_to_all | solution.py:627

commit v4 on v3

--- a/solution.py
+++ b/solution.py
@@ -40,7 +40,7 @@
 CHUNK_SLOTS = GROUPS * MSG_ROWS
 SLOT_BLOCKS = 9
 SLOTS_PAD = SLOT_BLOCKS * LANES
-ORDER_PAD = BAND_COLS + LANES
+ORDER_PAD = BAND_COLS + 2 * LANES
 UNROLL = 64
 ZERO_TUBE = SLOT_BLOCKS * 32
 ITEM_ROWS = 16
@@ -56,7 +56,7 @@
     return pltpu.VMEM(shape, dtype)
 
 
-def call(kernel, out_shape, in_specs, out_specs, scratch=(), name=None, flops=0, vmem=16, aliases=()):
+def call(kernel, out_shape, in_specs, out_specs, scratch=(), name=None, flops=0, vmem=16):
     run = pl.pallas_call(
         kernel,
         out_shape=out_shape,
@@ -64,7 +64,6 @@
         out_specs=out_specs,
         scratch_shapes=list(scratch),
         name=name,
-        input_output_aliases=dict(aliases),
         cost_estimate=pl.CostEstimate(flops=flops, bytes_accessed=1 << 20, transcendentals=0),
         compiler_params=pltpu.CompilerParams(vmem_limit_bytes=vmem * 1024 * 1024),
     )
@@ -274,45 +273,30 @@
     )(units, owners, rows, sel, weights, column)
 
 
-def turn_kernel(source_ref, *refs, side):
-    table, planes = refs[-2:]
-    half = LANES // 2
-
+def pack_kernel(
+    core_ref, starts_ref, units_ref, order_ref, mine_ref, other_ref, out_hbm, planes, table_ref, msg_ref, sems
+):
     @pl.loop(0, LON_BLOCKS)
     def _(blk):
-        for j in range(2):
-            for i in range(PLANES):
-                from_row = (j * SPECIES + i % SPECIES) * BAND_LATS
-                planes[blk, pl.ds((j * PLANES + i) * PITCH, BAND_LATS), :] = source_ref[
-                    blk, from_row : from_row + BAND_LATS, :
-                ]
+        for side, source in enumerate((mine_ref, other_ref)):
+            for j in range(2):
+                for i in range(PLANES):
+                    from_row = (j * SPECIES + i % SPECIES) * BAND_LATS
+                    planes[blk, pl.ds(((2 * side + j) * PLANES + i) * PITCH, BAND_LATS), :] = source[
+                        blk, from_row : from_row + BAND_LATS, :
+                    ]
 
     @pl.loop(0, LON_BLOCKS)
     def _(blk):
         for lat in range(BAND_LATS):
             parts = [
-                planes[blk, pl.ds((j * PLANES + first) * PITCH + lat, 8, stride=PITCH), :]
-                for j in range(2)
+                planes[blk, pl.ds((jj * PLANES + first) * PITCH + lat, 8, stride=PITCH), :]
+                for jj in range(CHIP_LEVS)
                 for first in (0, 3, 1, 4)
             ]
             start = pl.multiple_of((lat * LON_BLOCKS + blk) * LANES, LANES)
-            table[pl.ds(start, LANES), side * half : (side + 1) * half] = jnp.concatenate(parts, axis=0).T
-
-
-def turn(side, source, *table):
-    return call(
-        functools.partial(turn_kernel, side=side),
-        on_chip((BAND_LATS * LON_PAD, LANES)),
-        [HELD] * (1 + len(table)),
-        VMEM,
-        [pltpu.VMEM((LON_BLOCKS, 2 * PLANES * PITCH, LANES), f32)],
-        name="turn",
-        flops=8_000_000,
-        aliases={1: 0} if table else {},
-    )(source, *table)
-
-
-def pack_kernel(core_ref, starts_ref, units_ref, order_ref, table_ref, out_hbm, msg_ref, sems):
+            table_ref[pl.ds(start, LANES), :] = jnp.concatenate(parts, axis=0).T
+
     core = core_ref[0]
     lane = lax.broadcasted_iota(jnp.int32, (1, LANES), 1)
     group_of = lax.div(lax.rem(lane, 32), SPECIES)
@@ -332,9 +316,10 @@
             chunk = lax.div(piece, GROUPS)
             mask = group_of == piece - chunk * GROUPS
             row = pl.multiple_of(peer * PEER_ROWS + chunk * MSG_ROWS, MSG_ROWS)
-            places = order_ref.at[pl.ds(first + piece * MSG_ROWS, MSG_ROWS)]
+            base = first + piece * MSG_ROWS
             for i in range(MSG_ROWS):
-                value = table_ref[pl.ds(places[i], 1), :]
+                place = order_ref.at[pl.ds(i, ORDER_PAD - MSG_ROWS)][base]
+                value = table_ref[pl.ds(place, 1), :]
                 pltpu.store(msg_ref.at[pl.ds(row + i, 1), :], value, mask=mask)
 
         send(peer).start()
@@ -344,16 +329,22 @@
         send(peer).wait()
 
 
-def pack(core, starts, units, order, table):
+def pack(core, starts, units, order, mine, other):
     return call(
         pack_kernel,
         sds((16 * PEER_ROWS, LANES)),
-        [SMEM, SMEM, SMEM, SMEM, HELD],
+        [SMEM, SMEM, SMEM, SMEM, HELD, HELD],
         HBM,
-        [pltpu.VMEM((16 * PEER_ROWS, LANES), f32), pltpu.SemaphoreType.DMA((16,))],
+        [
+            pltpu.VMEM((LON_BLOCKS, CHIP_LEVS * PLANES * PITCH, LANES), f32),
+            pltpu.VMEM((BAND_LATS * LON_PAD, LANES), f32),
+            pltpu.VMEM((16 * PEER_ROWS, LANES), f32),
+            pltpu.SemaphoreType.DMA((16,)),
+        ],
         name="pack",
         flops=30_000_000,
-    )(core, starts, units, order, table)
+        vmem=32,
+    )(core, starts, units, order, mine, other)
 
 
 def solve_kernel(
@@ -614,11 +605,10 @@
     (mine,) = transport_step(density, winds, halo, True)
     owners = lax.axis_size("lev")
     other = lax.ppermute(mine, "lev", [(i, i ^ 1) for i in range(owners)])
-    turned = turn(1, other, turn(0, mine))
 
     core = (lev % 2).reshape(1)
     parity = [[2 * i + c for i in range(owners // 2)] for c in range(2)]
-    outgoing = pack(core, starts, column_units, rows, turned)
+    outgoing = pack(core, starts, column_units, rows, mine, other)
     got = lax.all_to_all(
         outgoing.reshape(16, PEER_ROWS, LANES), "lev", 0, 0, axis_index_groups=parity, tiled=True
     ).reshape(16 * PEER_ROWS, LANES)

time: 138 us -> 129 us (0.935)
  Pallas kernels: 53.3 us -> 45.4 us
  starting transfers between devices: 42 us -> 38.5 us
    pallas_call x9 -> x7, Pallas kernels: 53.3 us -> 45.4 us  [placed(): return run(*(place(x, spec) for x, spec in zip(args, in_specs)))]
    all_to_all x1, starting transfers between devices: 9.39 us -> 6.23 us  [on_device(): lax.all_to_all(items.reshape(PEERS, ITEM_ROWS, LANES), ('band', 'lev'), 0...]
    ppermute x1, waiting for transfers between devices: 0.01 us -> 1.86 us  [on_device(): other = lax.ppermute(mine, 'lev', [(i, i ^ 1) for i in range(owners)])]
  transfers between devices with their start and end apart: 11 -> 11, of which waited for: 5 -> 6; matrix products, arithmetic and copies ran while one was open for 2% -> 2% of each run, Pallas kernels for 9% -> 7%
where the time goes in v4:
time: 129 us; the launch traced here: 127 us
  Pallas kernels  45.4 us (35%)
  starting transfers between devices  38.5 us (30%)
  waiting for transfers between devices  36.7 us (28%)
  local copies, waits for them, and re-layouts  3.99 us (3%)
  between operations  1.65 us (1%)
    pallas_call x7, Pallas kernels, placed(): return run(*(place(x, spec) for x, spec in zip(args, in_specs)))  45.4 us
    all_to_all x1, waiting for transfers between devices, on_device(): lax.all_to_all(items.reshape(PEERS, ITEM_ROWS, LANES), ('band', 'lev'), 0...  19.1 us
    ppermute x4, starting transfers between devices, up(): return lax.ppermute(x, axis, [(i, i + 1) for i in range(ends)])  14.8 us
    all_to_all x1, starting transfers between devices, on_device(): lax.all_to_all(outgoing.reshape(16, PEER_ROWS, LANES), 'lev', 0, 0, axis_...  9.58 us
    all_to_all x1, waiting for transfers between devices, on_device(): lax.all_to_all(outgoing.reshape(16, PEER_ROWS, LANES), 'lev', 0, 0, axis_...  8.2 us
    ppermute x4, starting transfers between devices, down(): return lax.ppermute(x, axis, [(i + 1, i) for i in range(ends)])  7.79 us
    all_to_all x1, starting transfers between devices, on_device(): lax.all_to_all(items.reshape(PEERS, ITEM_ROWS, LANES), ('band', 'lev'), 0...  6.23 us
    ppermute x4, waiting for transfers between devices, down(): return lax.ppermute(x, axis, [(i + 1, i) for i in range(ends)])  4.14 us
  transfers between devices with their start and end apart: 11, of which 6 were waited for; matrix products, arithmetic and copies ran while one was open for 2% of the time, Pallas kernels for 7%

profile of v4, /device:TPU:1, one launch (start us, length us, event | category | flops | bytes accessed | tf_op | source)
XLA Modules:
  0.0 127.0 jit_solution(8503498789859187481)
XLA Ops:
  0.6 1.6 %edges.1 = (f32[5,2,8,2880]{3,2,1,0:T(8,128)S(1)}, f32[2,8,2880]{2,1,0:T(8,128)S(1)}, f32[2,8,2880]{2,1,0:T(8,128)S(1)}, f32[2,8,2880]{2,1,0:T(8,128)S(1)}, f32[...) custom-call(f32[5,2,8,2880]{3,2,1,0:T(8,128)} %n_hbm.1, ...), custom_call_target="tpu_custom_call" | custom-call | flops 1000000 | bytes 1048576 | tf_op jit(solution)/shard_map/edges/pallas_call | solution.py:76
  2.2 3.3 %collective-permute-start.3 = (f32[6,8,2880]{2,1,0:T(8,128)S(1)}, f32[6,8,2880]{2,1,0:T(8,128)S(1)}, u32[]{:S(2)}, u32[]{:S(2)}) collective-permute-start(f32[6,8,2880]{2,1,0:T(8,128)S(1)} %get-tuple-element.28), channel_id=1, source_target_pairs={{1,0},{2,1},{3,2},{4,3},{5,4},{6,5},{7,6},{8,7},{9,8},{10,9},{11,1... | collective-permute-start | bytes 1658888 | tf_op jit(solution)/shard_map/ppermute | solution.py:550
  5.5 3.1 %collective-permute-start.2 = (f32[5,8,2880]{2,1,0:T(8,128)S(1)}, f32[5,8,2880]{2,1,0:T(8,128)S(1)}, u32[]{:S(2)}, u32[]{:S(2)}) collective-permute-start(f32[5,8,2880]{2,1,0:T(8,128)S(1)} %get-tuple-element.27), channel_id=1, source_target_pairs={{0,1},{1,2},{2,3},{3,4},{4,5},{5,6},{6,7},{7,8},{8,9},{9,10},{10,1... | collective-permute-start | bytes 1382408 | tf_op jit(solution)/shard_map/ppermute | solution.py:545
  8.7 1.3 %collective-permute-start.1 = (f32[6,2,1,2880]{3,2,1,0:T(1,128)S(1)}, f32[6,2,1,2880]{3,2,1,0:T(1,128)S(1)}, u32[]{:S(2)}, u32[]{:S(2)}) collective-permute-start(f32[6,2,1,2880]{3,2,1,0:T(1,128)S(1)} %get-tuple-element.26), channel_id=1, source_target_pairs={{32,0},{64,32},{96,64},{33,1},{65,33},{97,65},{34,2},{66,34},{98,6... | collective-permute-start | bytes 414728 | tf_op jit(solution)/shard_map/ppermute | solution.py:550
  10.0 4.2 %collective-permute-start = (f32[5,2,1,2880]{3,2,1,0:T(1,128)S(1)}, f32[5,2,1,2880]{3,2,1,0:T(1,128)S(1)}, u32[]{:S(2)}, u32[]{:S(2)}) collective-permute-start(f32[5,2,1,2880]{3,2,1,0:T(1,128)S(1)} %get-tuple-element.25), channel_id=1, source_target_pairs={{0,32},{32,64},{64,96},{1,33},{33,65},{65,97},{2,34},{34,66},{66,9... | collective-permute-start | bytes 345608 | tf_op jit(solution)/shard_map/ppermute | solution.py:545
  14.2 2.9 %collective-permute-done.south_ref = f32[5,2,1,2880]{3,2,1,0:T(1,128)S(1)} collective-permute-done((f32[5,2,1,2880]{3,2,1,0:T(1,128)S(1)}, f32[5,2,1,2880]{3,2,1,0:T(1,128)S(1)}, u32[]{:S(2)}, u32[]{:S(2)}) %collective-permute-start) | collective-permute-done | bytes 115232 | tf_op jit(solution)/shard_map/ppermute | solution.py:545
  17.1 2.0 %transport.2 = (f32[5,2,8,2880]{3,2,1,0:T(8,128)S(1)}, f32[5,8,2880]{2,1,0:T(8,128)S(1)}, f32[5,8,2880]{2,1,0:T(8,128)S(1)}, f32[5,2,1,2880]{3,2,1,0:T(1,128)S(1)}, f32[5,2,1,2880]{3,2,1,0:T(1,128)S(1)}) custom-call(f32[5,2,8,2880]{3,2,1,0:T(8,128)S(1)} %get-tuple-element.21.n_ref, f32[2,8,2880]{2,1,0:T(8,128)S(1)} %get-tuple-element.22.wlon_ref, ...), custom_call_target="tpu_custom_call" | custom-call | flops 4000000 | bytes 1048576 | tf_op jit(solution)/shard_map/transport/pallas_call | solution.py:76
  19.1 3.4 %collective-permute-start.6 = (f32[5,8,2880]{2,1,0:T(8,128)S(1)}, f32[5,8,2880]{2,1,0:T(8,128)S(1)}, u32[]{:S(2)}, u32[]{:S(2)}) collective-permute-start(f32[5,8,2880]{2,1,0:T(8,128)S(1)} %get-tuple-element.32), channel_id=1, source_target_pairs={{0,1},{1,2},{2,3},{3,4},{4,5},{5,6},{6,7},{7,8},{8,9},{9,10},{10,1... | collective-permute-start | bytes 1382408 | tf_op jit(solution)/shard_map/ppermute | solution.py:545
  22.5 1.9 %collective-permute-start.7 = (f32[5,8,2880]{2,1,0:T(8,128)S(1)}, f32[5,8,2880]{2,1,0:T(8,128)S(1)}, u32[]{:S(2)}, u32[]{:S(2)}) collective-permute-start(f32[5,8,2880]{2,1,0:T(8,128)S(1)} %get-tuple-element.33), channel_id=1, source_target_pairs={{1,0},{2,1},{3,2},{4,3},{5,4},{6,5},{7,6},{8,7},{9,8},{10,9},{11,1... | collective-permute-start | bytes 1382408 | tf_op jit(solution)/shard_map/ppermute | solution.py:550
  24.4 4.1 %collective-permute-start.4 = (f32[5,2,1,2880]{3,2,1,0:T(1,128)S(1)}, f32[5,2,1,2880]{3,2,1,0:T(1,128)S(1)}, u32[]{:S(2)}, u32[]{:S(2)}) collective-permute-start(f32[5,2,1,2880]{3,2,1,0:T(1,128)S(1)} %get-tuple-element.30), channel_id=1, source_target_pairs={{0,32},{32,64},{64,96},{1,33},{33,65},{65,97},{2,34},{34,66},{66,9... | collective-permute-start | bytes 345608 | tf_op jit(solution)/shard_map/ppermute | solution.py:545
  28.5 1.3 %collective-permute-start.5 = (f32[5,2,1,2880]{3,2,1,0:T(1,128)S(1)}, f32[5,2,1,2880]{3,2,1,0:T(1,128)S(1)}, u32[]{:S(2)}, u32[]{:S(2)}) collective-permute-start(f32[5,2,1,2880]{3,2,1,0:T(1,128)S(1)} %get-tuple-element.31), channel_id=1, source_target_pairs={{32,0},{64,32},{96,64},{33,1},{65,33},{97,65},{34,2},{66,34},{98,6... | collective-permute-start | bytes 345608 | tf_op jit(solution)/shard_map/ppermute | solution.py:550
  30.3 4.1 %collective-permute-done.5.north_ref = f32[5,2,1,2880]{3,2,1,0:T(1,128)S(1)} collective-permute-done((f32[5,2,1,2880]{3,2,1,0:T(1,128)S(1)}, f32[5,2,1,2880]{3,2,1,0:T(1,128)S(1)}, u32[]{:S(2)}, u32[]{:S(2)}) %collective-permute-start.5) | collective-permute-done | bytes 115232 | tf_op jit(solution)/shard_map/ppermute | solution.py:550
  34.5 1.8 %transport.3.mine_ref = f32[23,80,128]{2,1,0:T(8,128)S(1)} custom-call(f32[5,2,8,2880]{3,2,1,0:T(8,128)S(1)} %get-tuple-element.29.n_ref, f32[2,8,2880]{2,1,0:T(8,128)S(1)} %get-tuple-element.22.wlon_ref, f32[2,8,2880]{2,1,0:T(8,128)S(1)} %get-tuple-element.23.wlat_ref, f32[2,8,2880]{2,1,0:T(8,128)S(1)} %get-tuple-element.24.wlev_ref, ...), custom_call_target="tpu_custom_call" | custom-call | flops 4000000 | bytes 1048576 | tf_op jit(solution)/shard_map/transport/pallas_call | solution.py:76
  37.0 1.9 %collective-permute-done.8.other_ref = f32[23,80,128]{2,1,0:T(8,128)S(1)} collective-permute-done((f32[23,80,128]{2,1,0:T(8,128)S(1)}, f32[23,80,128]{2,1,0:T(8,128)S(1)}, u32[]{:S(2)}, u32[]{:S(2)}) %collective-permute-start.8) | collective-permute-done | bytes 942112 | tf_op jit(solution)/shard_map/ppermute | solution.py:607
  38.9 17.5 %pack.1 = f32[3072,128]{1,0:T(8,128)} custom-call(s32[1]{0:T(128)} %bitcast.core_ref, s32[32]{0:T(128)S(1)} %sub.16.starts_ref, s32[32]{0:T(128)S(1)} %copy-done.2, s32[23296]{0:T(1024)S(1)} %pad.11.order_ref, f32[23,80,128]{2,1,0:T(8,128)S(1)} %transport.3.mine_ref, f32[23,80,128]{2,1,0:T(8,128)S(1)} %collective-permute-done.8.other_ref), custom_call_target="tpu_custom_call" | custom-call | flops 30000000 | bytes 1048576 | tf_op jit(solution)/shard_map/pack/pallas_call | solution.py:76
  56.4 9.6 %all-to-all-start = ((f32[16,192,128]{2,1,0:T(8,128)}), f32[16,192,128]{2,1,0:T(8,128)S(1)}, u32[]{:S(2)}, u32[]{:S(2)}) async-start(f32[16,192,128]{2,1,0:T(8,128)} %bitcast.6), calls=%async_computation | async-start | bytes 3145728 | tf_op jit(solution)/shard_map/all_to_all | solution.py:612
  66.0 0.6 dynamic_slice.14
  68.8 1.8 %copy-done.1 = f32[32,8,2880]{2,1,0:T(8,128)S(1)} copy-done((f32[32,8,2880]{2,1,0:T(8,128)S(1)}, f32[32,8,2880]{2,1,0:T(8,128)}, u32[]{:S(2)}) %copy-start.1) | copy-done | bytes 2949144
  70.7 9.4 %prepare.1 = (s32[384]{0:T(512)S(1)}, f32[9,32,128]{2,1,0:T(8,128)S(1)}, f32[960,128]{1,0:T(8,128)S(1)}) custom-call(s32[1]{0:T(128)} %dynamic_slice.12.units_ref, s32[270]{0:T(512)S(1)} %dynamic-slice_reduce_fusion.owner_ref, s32[1152]{0:T(1024)S(1)} %get-tuple-element.39.rows_ref, s32[9,128]{1,0:T(8,128)S(1)} %get-tuple-element.38.sel_ref, ...), custom_call_target="tpu_custom_call" | custom-call | flops 20000000 | bytes 1048576 | tf_op jit(solution)/shard_map/prepare/pallas_call | solution.py:76
  80.1 8.2 %all-to-all-done = f32[16,192,128]{2,1,0:T(8,128)S(1)} async-done(((f32[16,192,128]{2,1,0:T(8,128)}), f32[16,192,128]{2,1,0:T(8,128)S(1)}, u32[]{:S(2)}, u32[]{:S(2)}) %all-to-all-start) | async-done | bytes 1572896 | tf_op jit(solution)/shard_map/all_to_all | solution.py:612
  88.3 7.0 %solve.1 = (f32[1,1,5,64,1080]{4,3,2,1,0:T(8,128)}, f32[2048,128]{1,0:T(8,128)}) custom-call(s32[1]{0:T(128)} %bitcast.core_ref, s32[1]{0:T(128)} %dynamic_slice.12.units_ref, s32[384]{0:T(512)S(1)} %get-tuple-element.20.table_ref, f32[3072,128]{1,0:T(8,128)S(1)} %bitcast.15, f32[960,128]{1,0:T(8,128)S(1)} %get-tuple-element.34.coef_ref, ...), custom_call_target="tpu_custom_call" | custom-call | flops 40000000 | bytes 1048576 | tf_op jit(solution)/shard_map/solve/pallas_call | solution.py:76
  95.4 6.2 %all-to-all-start.1 = ((f32[128,16,128]{2,1,0:T(8,128)}), f32[128,16,128]{2,1,0:T(8,128)S(1)}, u32[]{:S(2)}, u32[]{:S(2)}) async-start(f32[128,16,128]{2,1,0:T(8,128)} %bitcast.8), calls=%async_computation.1 | async-start | bytes 2097152 | tf_op jit(solution)/shard_map/all_to_all | solution.py:617
  101.8 19.1 %all-to-all-done.1 = f32[128,16,128]{2,1,0:T(8,128)S(1)} async-done(((f32[128,16,128]{2,1,0:T(8,128)}), f32[128,16,128]{2,1,0:T(8,128)S(1)}, u32[]{:S(2)}, u32[]{:S(2)}) %all-to-all-start.1) | async-done | bytes 1048608 | tf_op jit(solution)/shard_map/all_to_all | solution.py:617
  120.9 6.1 %lines.1 = f32[1,7,96,512]{3,2,1,0:T(8,128)} custom-call(f32[2048,128]{1,0:T(8,128)S(1)} %bitcast.17, f32[35]{0:T(128)S(1)} %reshape.76.yield_ref, f32[14]{0:T(128)S(1)} %pad_maximum_fusion.rates_ref, f32[1,512]{1,0:T(1,128)S(1)} %copy-done.7, bf16[512,512]{1,0:T(8,128)(2,1)S(1)} %copy-done.3, bf16[512,512]{1,0:T(8,128)(2,1)S(1)} %copy-done.4, ...), custom_call_target="tpu_custom_call" | custom-call | flops 2000000000 | bytes 1048576 | tf_op jit(solution)/shard_map/lines/pallas_call | solution.py:76
  (54 shorter events, 2.9 us)
Async XLA Ops:
  0.6 68.0 %copy-start = (s32[32,270,1]{1,2,0:T(1,128)S(1)}, s32[32,270,1]{1,2,0:T(1,128)}, u32[]{:S(2)}) copy-start(s32[32,270,1]{1,2,0:T(1,128)} %param.28) | copy-start | bytes 103684
  2.2 14.9 %collective-permute-start.3 = (f32[6,8,2880]{2,1,0:T(8,128)S(1)}, f32[6,8,2880]{2,1,0:T(8,128)S(1)}, u32[]{:S(2)}, u32[]{:S(2)}) collective-permute-start(f32[6,8,2880]{2,1,0:T(8,128)S(1)} %get-tuple-element.28), channel_id=1, source_target_pairs={{1,0},{2,1},{3,2},{4,3},{5,4},{6,5},{7,6},{8,7},{9,8},{10,9},{11,1... | collective-permute-start | bytes 1658888 | tf_op jit(solution)/shard_map/ppermute | solution.py:550
  5.5 11.6 %collective-permute-start.2 = (f32[5,8,2880]{2,1,0:T(8,128)S(1)}, f32[5,8,2880]{2,1,0:T(8,128)S(1)}, u32[]{:S(2)}, u32[]{:S(2)}) collective-permute-start(f32[5,8,2880]{2,1,0:T(8,128)S(1)} %get-tuple-element.27), channel_id=1, source_target_pairs={{0,1},{1,2},{2,3},{3,4},{4,5},{5,6},{6,7},{7,8},{8,9},{9,10},{10,1... | collective-permute-start | bytes 1382408 | tf_op jit(solution)/shard_map/ppermute | solution.py:545
  8.7 8.4 %collective-permute-start.1 = (f32[6,2,1,2880]{3,2,1,0:T(1,128)S(1)}, f32[6,2,1,2880]{3,2,1,0:T(1,128)S(1)}, u32[]{:S(2)}, u32[]{:S(2)}) collective-permute-start(f32[6,2,1,2880]{3,2,1,0:T(1,128)S(1)} %get-tuple-element.26), channel_id=1, source_target_pairs={{32,0},{64,32},{96,64},{33,1},{65,33},{97,65},{34,2},{66,34},{98,6... | collective-permute-start | bytes 414728 | tf_op jit(solution)/shard_map/ppermute | solution.py:550
  10.0 7.1 %collective-permute-start = (f32[5,2,1,2880]{3,2,1,0:T(1,128)S(1)}, f32[5,2,1,2880]{3,2,1,0:T(1,128)S(1)}, u32[]{:S(2)}, u32[]{:S(2)}) collective-permute-start(f32[5,2,1,2880]{3,2,1,0:T(1,128)S(1)} %get-tuple-element.25), channel_id=1, source_target_pairs={{0,32},{32,64},{64,96},{1,33},{33,65},{65,97},{2,34},{34,66},{66,9... | collective-permute-start | bytes 345608 | tf_op jit(solution)/shard_map/ppermute | solution.py:545
  19.1 15.4 %collective-permute-start.6 = (f32[5,8,2880]{2,1,0:T(8,128)S(1)}, f32[5,8,2880]{2,1,0:T(8,128)S(1)}, u32[]{:S(2)}, u32[]{:S(2)}) collective-permute-start(f32[5,8,2880]{2,1,0:T(8,128)S(1)} %get-tuple-element.32), channel_id=1, source_target_pairs={{0,1},{1,2},{2,3},{3,4},{4,5},{5,6},{6,7},{7,8},{8,9},{9,10},{10,1... | collective-permute-start | bytes 1382408 | tf_op jit(solution)/shard_map/ppermute | solution.py:545
  22.5 12.0 %collective-permute-start.7 = (f32[5,8,2880]{2,1,0:T(8,128)S(1)}, f32[5,8,2880]{2,1,0:T(8,128)S(1)}, u32[]{:S(2)}, u32[]{:S(2)}) collective-permute-start(f32[5,8,2880]{2,1,0:T(8,128)S(1)} %get-tuple-element.33), channel_id=1, source_target_pairs={{1,0},{2,1},{3,2},{4,3},{5,4},{6,5},{7,6},{8,7},{9,8},{10,9},{11,1... | collective-permute-start | bytes 1382408 | tf_op jit(solution)/shard_map/ppermute | solution.py:550
  24.4 5.9 %collective-permute-start.4 = (f32[5,2,1,2880]{3,2,1,0:T(1,128)S(1)}, f32[5,2,1,2880]{3,2,1,0:T(1,128)S(1)}, u32[]{:S(2)}, u32[]{:S(2)}) collective-permute-start(f32[5,2,1,2880]{3,2,1,0:T(1,128)S(1)} %get-tuple-element.30), channel_id=1, source_target_pairs={{0,32},{32,64},{64,96},{1,33},{33,65},{65,97},{2,34},{34,66},{66,9... | collective-permute-start | bytes 345608 | tf_op jit(solution)/shard_map/ppermute | solution.py:545
  28.5 5.9 %collective-permute-start.5 = (f32[5,2,1,2880]{3,2,1,0:T(1,128)S(1)}, f32[5,2,1,2880]{3,2,1,0:T(1,128)S(1)}, u32[]{:S(2)}, u32[]{:S(2)}) collective-permute-start(f32[5,2,1,2880]{3,2,1,0:T(1,128)S(1)} %get-tuple-element.31), channel_id=1, source_target_pairs={{32,0},{64,32},{96,64},{33,1},{65,33},{97,65},{34,2},{66,34},{98,6... | collective-permute-start | bytes 345608 | tf_op jit(solution)/shard_map/ppermute | solution.py:550
  34.5 2.0 %copy-start.8 = (s32[1,23040]{1,0:T(1,128)S(1)}, s32[1,23040]{1,0:T(1,128)}, u32[]{:S(2)}) copy-start(s32[1,23040]{1,0:T(1,128)} %param.26) | copy-start | bytes 276484
  34.5 2.3 %copy-start.2 = (s32[32]{0:T(128)S(1)}, s32[32]{0:T(128)}, u32[]{:S(2)}) copy-start(s32[32]{0:T(128)} %units_ref.1) | copy-start | bytes 388
  36.3 2.6 %collective-permute-start.8 = (f32[23,80,128]{2,1,0:T(8,128)S(1)}, f32[23,80,128]{2,1,0:T(8,128)S(1)}, u32[]{:S(2)}, u32[]{:S(2)}) collective-permute-start(f32[23,80,128]{2,1,0:T(8,128)S(1)} %transport.3.mine_ref), channel_id=1, source_target_pairs={{0,1},{1,0},{2,3},{3,2},{4,5},{5,4},{6,7},{7,6},{8,9},{9,8},{10,11... | collective-permute-start | bytes 2826248 | tf_op jit(solution)/shard_map/ppermute | solution.py:607
  56.4 11.4 %copy-start.10 = (f32[5,64]{1,0:T(8,128)S(1)}, f32[5,64]{1,0:T(8,128)}, u32[]{:S(2)}) copy-start(f32[5,64]{1,0:T(8,128)} %param.21) | copy-start | bytes 3844
  56.4 31.9 %all-to-all-start = ((f32[16,192,128]{2,1,0:T(8,128)}), f32[16,192,128]{2,1,0:T(8,128)S(1)}, u32[]{:S(2)}, u32[]{:S(2)}) async-start(f32[16,192,128]{2,1,0:T(8,128)} %bitcast.6), calls=%async_computation | async-start | bytes 3145728 | tf_op jit(solution)/shard_map/all_to_all | solution.py:612
  68.8 1.9 %copy-start.1 = (f32[32,8,2880]{2,1,0:T(8,128)S(1)}, f32[32,8,2880]{2,1,0:T(8,128)}, u32[]{:S(2)}) copy-start(f32[32,8,2880]{2,1,0:T(8,128)} %param.22) | copy-start | bytes 8847364
  88.3 13.3 %copy-start.9 = (f32[7,5]{1,0:T(8,128)S(1)}, f32[7,5]{1,0:T(8,128)}, u32[]{:S(2)}) copy-start(f32[7,5]{1,0:T(8,128)} %param.23) | copy-start | bytes 424
  95.3 6.4 %copy-start.11 = (f32[7]{0:T(128)S(1)}, f32[7]{0:T(128)}, u32[]{:S(2)}) copy-start(f32[7]{0:T(128)} %param.25) | copy-start | bytes 88
  95.3 6.4 %copy-start.12 = (f32[7]{0:T(128)S(1)}, f32[7]{0:T(128)}, u32[]{:S(2)}) copy-start(f32[7]{0:T(128)} %param.24) | copy-start | bytes 88
  95.3 25.5 %copy-start.3 = (bf16[512,512]{1,0:T(8,128)(2,1)S(1)}, bf16[512,512]{1,0:T(8,128)(2,1)}, u32[]{:S(2)}) copy-start(bf16[512,512]{1,0:T(8,128)(2,1)} %constant.116.clone.fwd_high) | copy-start | bytes 1572868
  95.3 25.5 %copy-start.4 = (bf16[512,512]{1,0:T(8,128)(2,1)S(1)}, bf16[512,512]{1,0:T(8,128)(2,1)}, u32[]{:S(2)}) copy-start(bf16[512,512]{1,0:T(8,128)(2,1)} %constant.117.clone.fwd_low) | copy-start | bytes 1572868
  95.3 25.5 %copy-start.5 = (bf16[512,512]{1,0:T(8,128)(2,1)S(1)}, bf16[512,512]{1,0:T(8,128)(2,1)}, u32[]{:S(2)}) copy-start(bf16[512,512]{1,0:T(8,128)(2,1)} %constant.118.clone.inv_high) | copy-start | bytes 1572868
  95.4 25.5 %copy-start.6 = (bf16[512,512]{1,0:T(8,128)(2,1)S(1)}, bf16[512,512]{1,0:T(8,128)(2,1)}, u32[]{:S(2)}) copy-start(bf16[512,512]{1,0:T(8,128)(2,1)} %constant.119.clone.inv_low) | copy-start | bytes 1572868
  95.4 25.5 %copy-start.7 = (f32[1,512]{1,0:T(1,128)S(1)}, f32[1,512]{1,0:T(1,128)}, u32[]{:S(2)}) copy-start(f32[1,512]{1,0:T(1,128)} %constant.133.waves_ref) | copy-start | bytes 6148
  95.4 25.5 %all-to-all-start.1 = ((f32[128,16,128]{2,1,0:T(8,128)}), f32[128,16,128]{2,1,0:T(8,128)S(1)}, u32[]{:S(2)}, u32[]{:S(2)}) async-start(f32[128,16,128]{2,1,0:T(8,128)} %bitcast.8), calls=%async_computation.1 | async-start | bytes 2097152 | tf_op jit(solution)/shard_map/all_to_all | solution.py:617

commit v5 on v4

--- a/solution.py
+++ b/solution.py
@@ -87,8 +87,8 @@
 
 
 def edges_kernel(
-    n_hbm, wlon_hbm, wlat_hbm, wlev_hbm,
-    n_ref, wlon_ref, wlat_ref, wlev_ref, low_ref, high_ref, first_ref, last_ref, sems,
+    side_ref, n_hbm, wlon_hbm, wlat_hbm, wlev_hbm,
+    n_ref, wlon_ref, wlat_ref, wlev_ref, inner_ref, outer_ref, row_ref, far_row_ref, sems,
 ):
     fetches = [
         pltpu.make_async_copy(n_hbm.at[s], n_ref.at[s], sems.at[s]) for s in range(SPECIES)
@@ -100,22 +100,26 @@
         fetch.start()
     for fetch in fetches[:-1]:
         fetch.wait()
-    low_ref[SPECIES] = wlev_ref[0]
+    core, odd = side_ref[0], side_ref[1] == 1
+    inner_ref[SPECIES] = wlev_ref[0]
+    outer_ref[SPECIES] = wlev_ref[0]
     for j in range(2):
-        first_ref[SPECIES, j] = wlat_ref[j, :1]
+        row_ref[SPECIES, j] = wlat_ref[j, :1]
+        far_row_ref[SPECIES, j] = wlat_ref[j, :1]
 
     @pl.loop(0, SPECIES)
     def _(s):
-        low_ref[s] = n_ref[s, 0]
-        high_ref[s] = n_ref[s, 1]
+        inner_ref[s] = n_ref[s, 1 - core]
+        outer_ref[s] = n_ref[s, core]
         for j in range(2):
-            first_ref[s, j] = n_ref[s, j, :1]
-            last_ref[s, j] = n_ref[s, j, BAND_LATS - 1 :]
+            first, last = n_ref[s, j, :1], n_ref[s, j, BAND_LATS - 1 :]
+            row_ref[s, j] = jnp.where(odd, first, last)
+            far_row_ref[s, j] = jnp.where(odd, last, first)
 
     fetches[-1].wait()
 
 
-def edges(density, wind_lon, wind_lat, wind_lev):
+def edges(side, density, wind_lon, wind_lat, wind_lev):
     return call(
         edges_kernel,
         (
@@ -124,22 +128,25 @@
             on_chip(wind_lat.shape),
             on_chip(wind_lev.shape),
             on_chip((SPECIES + 1, BAND_LATS, NLON)),
-            on_chip((SPECIES, BAND_LATS, NLON)),
+            on_chip((SPECIES + 1, BAND_LATS, NLON)),
             on_chip((SPECIES + 1, 2, 1, NLON)),
-            on_chip((SPECIES, 2, 1, NLON)),
+            on_chip((SPECIES + 1, 2, 1, NLON)),
         ),
-        [HBM] * 4,
+        [SMEM] + [HBM] * 4,
         (VMEM,) * 8,
         [pltpu.SemaphoreType.DMA((SPECIES + 3,))],
         name="edges",
         flops=1_000_000,
-    )(density, wind_lon, wind_lat, wind_lev)
-
-
-def transport_kernel(
-    n_ref, wlon_ref, wlat_ref, wlev_ref, south_ref, north_ref, below_ref, above_ref, wlat_n_ref, wlev_up_ref,
-    *outs, last,
-):
+    )(side, density, wind_lon, wind_lat, wind_lev)
+
+
+def transport_kernel(side_ref, n_ref, wlon_ref, wlat_ref, wlev_ref, *refs, last):
+    inner_ref, outer_ref, row_ref, far_row_ref = refs[:4]
+    inner_wind, outer_wind, row_wind, far_row_wind = refs[4:8]
+    outs = refs[8:]
+    core, odd = side_ref[0], side_ref[1] == 1
+    south_core = core == 0
+
     def split(c):
         return jnp.maximum(c, 0.0), jnp.minimum(c, 0.0)
 
@@ -156,13 +163,20 @@
             x = n_ref[s, j]
             flux = upwind(*split(wlon_ref[j]), shift_west(x), x)
             total = x + (flux - shift_east(flux))
-            southern = jnp.concatenate([south_ref[s, j], x[: BAND_LATS - 1]], axis=0)
+            south = jnp.where(odd, row_ref[s, j], far_row_ref[s, j])
+            north = jnp.where(odd, far_row_ref[s, j], row_ref[s, j])
+            north_wind = jnp.where(odd, far_row_wind[SPECIES, j], row_wind[SPECIES, j])
+            southern = jnp.concatenate([south, x[: BAND_LATS - 1]], axis=0)
             flux = upwind(*split(wlat_ref[j]), southern, x)
-            edge = upwind(*split(wlat_n_ref[SPECIES, j]), x[BAND_LATS - 1 :], north_ref[s, j])
+            edge = upwind(*split(north_wind), x[BAND_LATS - 1 :], north)
             total = total + (flux - jnp.concatenate([flux[1:], edge], axis=0))
-            beneath = below_ref[s] if j == 0 else n_ref[s, 0]
-            overhead = n_ref[s, 1] if j == 0 else above_ref[s]
-            over_wind = wlev_ref[1] if j == 0 else wlev_up_ref[SPECIES]
+            if j == 0:
+                beneath = jnp.where(south_core, outer_ref[s], inner_ref[s])
+                overhead, over_wind = n_ref[s, 1], wlev_ref[1]
+            else:
+                beneath = n_ref[s, 0]
+                overhead = jnp.where(south_core, inner_ref[s], outer_ref[s])
+                over_wind = jnp.where(south_core, inner_wind[SPECIES], outer_wind[SPECIES])
             flux = upwind(*split(wlev_ref[j]), beneath, x)
             total = total + (flux - upwind(*split(over_wind), x, overhead))
             if last:
@@ -172,12 +186,20 @@
                     outs[0][blk, pl.ds(row, BAND_LATS), :wide] = total[:, blk * LANES : blk * LANES + wide]
             else:
                 outs[0][s, j] = total
-                outs[1 + j][s] = total
-                outs[3][s, j] = total[:1]
-                outs[4][s, j] = total[BAND_LATS - 1 :]
-
-
-def transport_step(density, winds, halo, last):
+
+                @pl.when(core == 1 - j)
+                def _():
+                    outs[1][s] = total
+
+                @pl.when(core == j)
+                def _():
+                    outs[2][s] = total
+
+                outs[3][s, j] = jnp.where(odd, total[:1], total[BAND_LATS - 1 :])
+                outs[4][s, j] = jnp.where(odd, total[BAND_LATS - 1 :], total[:1])
+
+
+def transport_step(side, density, winds, halo, wind_halo, last):
     if last:
         out_shape = (on_chip((LON_BLOCKS, 2 * SPECIES * BAND_LATS, LANES)),)
     else:
@@ -191,11 +213,11 @@
     return call(
         functools.partial(transport_kernel, last=last),
         out_shape,
-        [HELD] * 10,
+        [SMEM] + [HELD] * 12,
         (VMEM,) * len(out_shape),
         name="transport",
         flops=4_000_000,
-    )(density, *winds, *halo)
+    )(side, density, *winds, *halo, *wind_halo)
 
 
 def prepare_kernel(
@@ -540,14 +562,17 @@
     return jnp.swapaxes(by_ion, 1, 2)
 
 
-def up(x, axis):
-    ends = lax.axis_size(axis) - 1
-    return lax.ppermute(x, axis, [(i, i + 1) for i in range(ends)])
-
-
-def down(x, axis):
-    ends = lax.axis_size(axis) - 1
-    return lax.ppermute(x, axis, [(i + 1, i) for i in range(ends)])
+def swap(x, axis, offset):
+    count = lax.axis_size(axis)
+    lows = range(offset, count - 1, 2)
+    return lax.ppermute(x, axis, [(i, i + 1) for i in lows] + [(i + 1, i) for i in lows])
+
+
+def exchange(inner, outer, row, far_row):
+    outer = swap(outer, "lev", 1)
+    row = swap(row, "band", 0)
+    far_row = swap(far_row, "band", 1)
+    return swap(inner, "lev", 0), outer, row, far_row
 
 
 def on_device(
@@ -566,9 +591,9 @@
 ):
     lev = lax.axis_index("lev")
 
-    neutrals, *winds, low, high, first, last = edges(neutrals, wind_lon, wind_lat, wind_lev)
-    below, above = up(high, "lev"), down(low, "lev")
-    south, north = up(last, "band"), down(first, "band")
+    side = jnp.stack([lev % 2, lax.axis_index("band") % 2]).astype(jnp.int32)
+    neutrals, *rest = edges(side, neutrals, wind_lon, wind_lat, wind_lev)
+    winds, first_halo = rest[:3], exchange(*rest[3:])
 
     starts = jnp.cumsum(column_units) - column_units
     order = column_order[0]
@@ -599,12 +624,10 @@
         jnp.swapaxes(coefs, 2, 3).reshape(-1, 1),
     )
 
-    halo = (south, north, below, above, north, above)
-    density, bottom, top, first_row, last_row = transport_step(neutrals, winds, halo, False)
-    halo = (up(last_row, "band"), down(first_row, "band"), up(top, "lev"), down(bottom, "lev"), north, above)
-    (mine,) = transport_step(density, winds, halo, True)
+    density, *halo = transport_step(side, neutrals, winds, first_halo, first_halo, False)
+    (mine,) = transport_step(side, density, winds, exchange(*halo), first_halo, True)
     owners = lax.axis_size("lev")
-    other = lax.ppermute(mine, "lev", [(i, i ^ 1) for i in range(owners)])
+    other = swap(mine, "lev", 0)
 
     core = (lev % 2).reshape(1)
     parity = [[2 * i + c for i in range(owners // 2)] for c in range(2)]

time: 129 us -> 126 us (0.977); the launches traced: 127 us -> 126 us
  waiting for transfers between devices: 36.7 us -> 44.1 us
  starting transfers between devices: 38.5 us -> 31.8 us
  Pallas kernels: 45.4 us -> 43.8 us
    ppermute x9, starting transfers between devices: 22.7 us -> 14.4 us  [swap(): lax.ppermute(x, axis, [(i, i + 1) for i in lows] + [(i + 1, i) for i in l...]
    all_to_all x1, waiting for transfers between devices: 8.2 us -> 15.2 us  [on_device(): lax.all_to_all(outgoing.reshape(16, PEER_ROWS, LANES), 'lev', 0, 0, axis_...]
    pallas_call x7, Pallas kernels: 45.4 us -> 43.8 us  [placed(): return run(*(place(x, spec) for x, spec in zip(args, in_specs)))]
  transfers between devices with their start and end apart: 11 -> 11, of which waited for: 6 -> 7; matrix products, arithmetic and copies ran while one was open for 2% -> 2% of each run, Pallas kernels for 7% -> 6%
where the time goes in v5:
time: 126 us
  waiting for transfers between devices  44.1 us (35%)
  Pallas kernels  43.8 us (35%)
  starting transfers between devices  31.8 us (25%)
  local copies, waits for them, and re-layouts  3.98 us (3%)
  between operations  1.62 us (1%)
    pallas_call x7, Pallas kernels, placed(): return run(*(place(x, spec) for x, spec in zip(args, in_specs)))  43.8 us
    all_to_all x1, waiting for transfers between devices, on_device(): lax.all_to_all(items.reshape(PEERS, ITEM_ROWS, LANES), ('band', 'lev'), 0...  19.1 us
    all_to_all x1, waiting for transfers between devices, on_device(): lax.all_to_all(outgoing.reshape(16, PEER_ROWS, LANES), 'lev', 0, 0, axis_...  15.2 us
    ppermute x9, starting transfers between devices, swap(): lax.ppermute(x, axis, [(i, i + 1) for i in lows] + [(i + 1, i) for i in l...  14.4 us
    all_to_all x1, starting transfers between devices, on_device(): lax.all_to_all(outgoing.reshape(16, PEER_ROWS, LANES), 'lev', 0, 0, axis_...  10.8 us
    ppermute x9, waiting for transfers between devices, swap(): lax.ppermute(x, axis, [(i, i + 1) for i in lows] + [(i + 1, i) for i in l...  9.91 us
    all_to_all x1, starting transfers between devices, on_device(): lax.all_to_all(items.reshape(PEERS, ITEM_ROWS, LANES), ('band', 'lev'), 0...  6.58 us
  transfers between devices with their start and end apart: 11, of which 7 were waited for; matrix products, arithmetic and copies ran while one was open for 2% of the time, Pallas kernels for 6%

profile of v5, /device:TPU:1, one launch (start us, length us, event | category | flops | bytes accessed | tf_op | source)
XLA Modules:
  0.0 126.2 jit_solution(5009854007013494923)
XLA Ops:
  0.7 2.1 %edges.1 = (f32[5,2,8,2880]{3,2,1,0:T(8,128)S(1)}, f32[2,8,2880]{2,1,0:T(8,128)S(1)}, f32[2,8,2880]{2,1,0:T(8,128)S(1)}, f32[2,8,2880]{2,1,0:T(8,128)S(1)}, f32[...) custom-call(s32[2]{0:T(128)S(1)} %pad_add_fusion.side_ref, ...), custom_call_target="tpu_custom_call" | custom-call | flops 1000000 | bytes 1048576 | tf_op jit(solution)/shard_map/edges/pallas_call | solution.py:76
  2.9 1.5 %collective-permute-start = (f32[6,8,2880]{2,1,0:T(8,128)S(1)}, f32[6,8,2880]{2,1,0:T(8,128)S(1)}, u32[]{:S(2)}, u32[]{:S(2)}) collective-permute-start(f32[6,8,2880]{2,1,0:T(8,128)S(1)} %get-tuple-element.25), channel_id=1, source_target_pairs={{0,1},{2,3},{4,5},{6,7},{8,9},{10,11},{12,13},{14,15},{16,17},{18,... | collective-permute-start | bytes 1658888 | tf_op jit(solution)/shard_map/ppermute | solution.py:568
  4.3 3.1 %collective-permute-start.1 = (f32[6,8,2880]{2,1,0:T(8,128)S(1)}, f32[6,8,2880]{2,1,0:T(8,128)S(1)}, u32[]{:S(2)}, u32[]{:S(2)}) collective-permute-start(f32[6,8,2880]{2,1,0:T(8,128)S(1)} %get-tuple-element.26), channel_id=1, source_target_pairs={{1,2},{3,4},{5,6},{7,8},{9,10},{11,12},{13,14},{15,16},{17,18},{19... | collective-permute-start | bytes 1658888 | tf_op jit(solution)/shard_map/ppermute | solution.py:568
  7.5 1.7 %collective-permute-start.2 = (f32[6,2,1,2880]{3,2,1,0:T(1,128)S(1)}, f32[6,2,1,2880]{3,2,1,0:T(1,128)S(1)}, u32[]{:S(2)}, u32[]{:S(2)}) collective-permute-start(f32[6,2,1,2880]{3,2,1,0:T(1,128)S(1)} %get-tuple-element.27), channel_id=1, source_target_pairs={{0,32},{64,96},{32,0},{96,64},{1,33},{65,97},{33,1},{97,65},{2,34}... | collective-permute-start | bytes 414728 | tf_op jit(solution)/shard_map/ppermute | solution.py:568
  9.2 0.7 collective-permute-start.3
  9.9 1.8 %collective-permute-done.2.refs_2_.refs_6_ = f32[6,2,1,2880]{3,2,1,0:T(1,128)S(1)} collective-permute-done((f32[6,2,1,2880]{3,2,1,0:T(1,128)S(1)}, f32[6,2,1,2880]{3,2,1,0:T(1,128)S(1)}, u32[]{:S(2)}, u32[]{:S(2)}) %collective-permute-start.2) | collective-permute-done | bytes 138272 | tf_op jit(solution)/shard_map/ppermute | solution.py:568
  11.7 3.6 %collective-permute-done.1.refs_1_.refs_5_ = f32[6,8,2880]{2,1,0:T(8,128)S(1)} collective-permute-done((f32[6,8,2880]{2,1,0:T(8,128)S(1)}, f32[6,8,2880]{2,1,0:T(8,128)S(1)}, u32[]{:S(2)}, u32[]{:S(2)}) %collective-permute-start.1) | collective-permute-done | bytes 552992 | tf_op jit(solution)/shard_map/ppermute | solution.py:568
  15.3 2.8 %transport.2 = (f32[5,2,8,2880]{3,2,1,0:T(8,128)S(1)}, f32[5,8,2880]{2,1,0:T(8,128)S(1)}, f32[5,8,2880]{2,1,0:T(8,128)S(1)}, f32[5,2,1,2880]{3,2,1,0:T(1,128)S(1)}, f32[5,2,1,2880]{3,2,1,0:T(1,128)S(1)}) custom-call(s32[2]{0:T(128)S(1)} %pad_add_fusion.side_ref, f32[5,2,8,2880]{3,2,1,0:T(8,128)S(1)} %get-tuple-element.21.n_ref, ...), custom_call_target="tpu_custom_call" | custom-call | flops 4000000 | bytes 1048576 | tf_op jit(solution)/shard_map/transport/pallas_call | solution.py:76
  18.1 3.6 %collective-permute-start.5 = (f32[5,8,2880]{2,1,0:T(8,128)S(1)}, f32[5,8,2880]{2,1,0:T(8,128)S(1)}, u32[]{:S(2)}, u32[]{:S(2)}) collective-permute-start(f32[5,8,2880]{2,1,0:T(8,128)S(1)} %get-tuple-element.31), channel_id=1, source_target_pairs={{1,2},{3,4},{5,6},{7,8},{9,10},{11,12},{13,14},{15,16},{17,18},{19... | collective-permute-start | bytes 1382408 | tf_op jit(solution)/shard_map/ppermute | solution.py:568
  21.7 3.0 %collective-permute-start.6 = (f32[5,2,1,2880]{3,2,1,0:T(1,128)S(1)}, f32[5,2,1,2880]{3,2,1,0:T(1,128)S(1)}, u32[]{:S(2)}, u32[]{:S(2)}) collective-permute-start(f32[5,2,1,2880]{3,2,1,0:T(1,128)S(1)} %get-tuple-element.32), channel_id=1, source_target_pairs={{0,32},{64,96},{32,0},{96,64},{1,33},{65,97},{33,1},{97,65},{2,34}... | collective-permute-start | bytes 345608 | tf_op jit(solution)/shard_map/ppermute | solution.py:568
  24.8 0.7 collective-permute-start.7
  25.4 1.6 %collective-permute-done.6.refs_2_ = f32[5,2,1,2880]{3,2,1,0:T(1,128)S(1)} collective-permute-done((f32[5,2,1,2880]{3,2,1,0:T(1,128)S(1)}, f32[5,2,1,2880]{3,2,1,0:T(1,128)S(1)}, u32[]{:S(2)}, u32[]{:S(2)}) %collective-permute-start.6) | collective-permute-done | bytes 115232 | tf_op jit(solution)/shard_map/ppermute | solution.py:568
  27.0 1.1 collective-permute-done.5.refs_1_
  28.1 2.5 %transport.3.mine_ref = f32[23,80,128]{2,1,0:T(8,128)S(1)} custom-call(s32[2]{0:T(128)S(1)} %pad_add_fusion.side_ref, f32[5,2,8,2880]{3,2,1,0:T(8,128)S(1)} %get-tuple-element.29.n_ref, f32[2,8,2880]{2,1,0:T(8,128)S(1)} %get-tuple-element.22.wlon_ref, f32[2,8,2880]{2,1,0:T(8,128)S(1)} %get-tuple-element.23.wlat_ref, ...), custom_call_target="tpu_custom_call" | custom-call | flops 4000000 | bytes 1048576 | tf_op jit(solution)/shard_map/transport/pallas_call | solution.py:76
  31.2 1.9 %collective-permute-done.8.other_ref = f32[23,80,128]{2,1,0:T(8,128)S(1)} collective-permute-done((f32[23,80,128]{2,1,0:T(8,128)S(1)}, f32[23,80,128]{2,1,0:T(8,128)S(1)}, u32[]{:S(2)}, u32[]{:S(2)}) %collective-permute-start.8) | collective-permute-done | bytes 942112 | tf_op jit(solution)/shard_map/ppermute | solution.py:568
  33.1 16.2 %pack.1 = f32[3072,128]{1,0:T(8,128)} custom-call(s32[1]{0:T(128)} %bitcast.core_ref, s32[32]{0:T(128)S(1)} %sub.16.starts_ref, s32[32]{0:T(128)S(1)} %copy-done.2, s32[23296]{0:T(1024)S(1)} %pad.11.order_ref, f32[23,80,128]{2,1,0:T(8,128)S(1)} %transport.3.mine_ref, f32[23,80,128]{2,1,0:T(8,128)S(1)} %collective-permute-done.8.other_ref), custom_call_target="tpu_custom_call" | custom-call | flops 30000000 | bytes 1048576 | tf_op jit(solution)/shard_map/pack/pallas_call | solution.py:76
  49.4 10.8 %all-to-all-start = ((f32[16,192,128]{2,1,0:T(8,128)}), f32[16,192,128]{2,1,0:T(8,128)S(1)}, u32[]{:S(2)}, u32[]{:S(2)}) async-start(f32[16,192,128]{2,1,0:T(8,128)} %bitcast.7), calls=%async_computation | async-start | bytes 3145728 | tf_op jit(solution)/shard_map/all_to_all | solution.py:635
  63.0 1.8 %copy-done.1 = f32[32,8,2880]{2,1,0:T(8,128)S(1)} copy-done((f32[32,8,2880]{2,1,0:T(8,128)S(1)}, f32[32,8,2880]{2,1,0:T(8,128)}, u32[]{:S(2)}) %copy-start.1) | copy-done | bytes 2949144
  64.9 7.0 %prepare.1 = (s32[384]{0:T(512)S(1)}, f32[9,32,128]{2,1,0:T(8,128)S(1)}, f32[960,128]{1,0:T(8,128)S(1)}) custom-call(s32[1]{0:T(128)} %dynamic_slice.12.units_ref, s32[270]{0:T(512)S(1)} %dynamic-slice_reduce_fusion.owner_ref, s32[1152]{0:T(1024)S(1)} %get-tuple-element.39.rows_ref, s32[9,128]{1,0:T(8,128)S(1)} %get-tuple-element.38.sel_ref, ...), custom_call_target="tpu_custom_call" | custom-call | flops 20000000 | bytes 1048576 | tf_op jit(solution)/shard_map/prepare/pallas_call | solution.py:76
  71.9 15.2 %all-to-all-done = f32[16,192,128]{2,1,0:T(8,128)S(1)} async-done(((f32[16,192,128]{2,1,0:T(8,128)}), f32[16,192,128]{2,1,0:T(8,128)S(1)}, u32[]{:S(2)}, u32[]{:S(2)}) %all-to-all-start) | async-done | bytes 1572896 | tf_op jit(solution)/shard_map/all_to_all | solution.py:635
  87.1 7.0 %solve.1 = (f32[1,1,5,64,1080]{4,3,2,1,0:T(8,128)}, f32[2048,128]{1,0:T(8,128)}) custom-call(s32[1]{0:T(128)} %bitcast.core_ref, s32[1]{0:T(128)} %dynamic_slice.12.units_ref, s32[384]{0:T(512)S(1)} %get-tuple-element.20.table_ref, f32[3072,128]{1,0:T(8,128)S(1)} %bitcast.16, f32[960,128]{1,0:T(8,128)S(1)} %get-tuple-element.34.coef_ref, ...), custom_call_target="tpu_custom_call" | custom-call | flops 40000000 | bytes 1048576 | tf_op jit(solution)/shard_map/solve/pallas_call | solution.py:76
  94.2 6.6 %all-to-all-start.1 = ((f32[128,16,128]{2,1,0:T(8,128)}), f32[128,16,128]{2,1,0:T(8,128)S(1)}, u32[]{:S(2)}, u32[]{:S(2)}) async-start(f32[128,16,128]{2,1,0:T(8,128)} %bitcast.9), calls=%async_computation.1 | async-start | bytes 2097152 | tf_op jit(solution)/shard_map/all_to_all | solution.py:640
  101.0 19.1 %all-to-all-done.1 = f32[128,16,128]{2,1,0:T(8,128)S(1)} async-done(((f32[128,16,128]{2,1,0:T(8,128)}), f32[128,16,128]{2,1,0:T(8,128)S(1)}, u32[]{:S(2)}, u32[]{:S(2)}) %all-to-all-start.1) | async-done | bytes 1048608 | tf_op jit(solution)/shard_map/all_to_all | solution.py:640
  120.1 6.1 %lines.1 = f32[1,7,96,512]{3,2,1,0:T(8,128)} custom-call(f32[2048,128]{1,0:T(8,128)S(1)} %bitcast.18, f32[35]{0:T(128)S(1)} %reshape.76.yield_ref, f32[14]{0:T(128)S(1)} %pad_maximum_fusion.rates_ref, f32[1,512]{1,0:T(1,128)S(1)} %copy-done.7, bf16[512,512]{1,0:T(8,128)(2,1)S(1)} %copy-done.3, bf16[512,512]{1,0:T(8,128)(2,1)S(1)} %copy-done.4, ...), custom_call_target="tpu_custom_call" | custom-call | flops 2000000000 | bytes 1048576 | tf_op jit(solution)/shard_map/lines/pallas_call | solution.py:76
  (55 shorter events, 3.2 us)
Async XLA Ops:
  0.6 62.3 %copy-start = (s32[32,270,1]{1,2,0:T(1,128)S(1)}, s32[32,270,1]{1,2,0:T(1,128)}, u32[]{:S(2)}) copy-start(s32[32,270,1]{1,2,0:T(1,128)} %param.28) | copy-start | bytes 103684
  2.9 8.8 %collective-permute-start = (f32[6,8,2880]{2,1,0:T(8,128)S(1)}, f32[6,8,2880]{2,1,0:T(8,128)S(1)}, u32[]{:S(2)}, u32[]{:S(2)}) collective-permute-start(f32[6,8,2880]{2,1,0:T(8,128)S(1)} %get-tuple-element.25), channel_id=1, source_target_pairs={{0,1},{2,3},{4,5},{6,7},{8,9},{10,11},{12,13},{14,15},{16,17},{18,... | collective-permute-start | bytes 1658888 | tf_op jit(solution)/shard_map/ppermute | solution.py:568
  4.3 10.9 %collective-permute-start.1 = (f32[6,8,2880]{2,1,0:T(8,128)S(1)}, f32[6,8,2880]{2,1,0:T(8,128)S(1)}, u32[]{:S(2)}, u32[]{:S(2)}) collective-permute-start(f32[6,8,2880]{2,1,0:T(8,128)S(1)} %get-tuple-element.26), channel_id=1, source_target_pairs={{1,2},{3,4},{5,6},{7,8},{9,10},{11,12},{13,14},{15,16},{17,18},{19... | collective-permute-start | bytes 1658888 | tf_op jit(solution)/shard_map/ppermute | solution.py:568
  7.5 4.2 %collective-permute-start.2 = (f32[6,2,1,2880]{3,2,1,0:T(1,128)S(1)}, f32[6,2,1,2880]{3,2,1,0:T(1,128)S(1)}, u32[]{:S(2)}, u32[]{:S(2)}) collective-permute-start(f32[6,2,1,2880]{3,2,1,0:T(1,128)S(1)} %get-tuple-element.27), channel_id=1, source_target_pairs={{0,32},{64,96},{32,0},{96,64},{1,33},{65,97},{33,1},{97,65},{2,34}... | collective-permute-start | bytes 414728 | tf_op jit(solution)/shard_map/ppermute | solution.py:568
  9.2 2.5 %collective-permute-start.3 = (f32[6,2,1,2880]{3,2,1,0:T(1,128)S(1)}, f32[6,2,1,2880]{3,2,1,0:T(1,128)S(1)}, u32[]{:S(2)}, u32[]{:S(2)}) collective-permute-start(f32[6,2,1,2880]{3,2,1,0:T(1,128)S(1)} %get-tuple-element.28), channel_id=1, source_target_pairs={{32,64},{64,32},{33,65},{65,33},{34,66},{66,34},{35,67},{67,35},{3... | collective-permute-start | bytes 414728 | tf_op jit(solution)/shard_map/ppermute | solution.py:568
  18.0 8.9 %collective-permute-start.4 = (f32[5,8,2880]{2,1,0:T(8,128)S(1)}, f32[5,8,2880]{2,1,0:T(8,128)S(1)}, u32[]{:S(2)}, u32[]{:S(2)}) collective-permute-start(f32[5,8,2880]{2,1,0:T(8,128)S(1)} %get-tuple-element.30), channel_id=1, source_target_pairs={{0,1},{2,3},{4,5},{6,7},{8,9},{10,11},{12,13},{14,15},{16,17},{18,... | collective-permute-start | bytes 1382408 | tf_op jit(solution)/shard_map/ppermute | solution.py:568
  18.1 9.9 %collective-permute-start.5 = (f32[5,8,2880]{2,1,0:T(8,128)S(1)}, f32[5,8,2880]{2,1,0:T(8,128)S(1)}, u32[]{:S(2)}, u32[]{:S(2)}) collective-permute-start(f32[5,8,2880]{2,1,0:T(8,128)S(1)} %get-tuple-element.31), channel_id=1, source_target_pairs={{1,2},{3,4},{5,6},{7,8},{9,10},{11,12},{13,14},{15,16},{17,18},{19... | collective-permute-start | bytes 1382408 | tf_op jit(solution)/shard_map/ppermute | solution.py:568
  21.7 5.2 %collective-permute-start.6 = (f32[5,2,1,2880]{3,2,1,0:T(1,128)S(1)}, f32[5,2,1,2880]{3,2,1,0:T(1,128)S(1)}, u32[]{:S(2)}, u32[]{:S(2)}) collective-permute-start(f32[5,2,1,2880]{3,2,1,0:T(1,128)S(1)} %get-tuple-element.32), channel_id=1, source_target_pairs={{0,32},{64,96},{32,0},{96,64},{1,33},{65,97},{33,1},{97,65},{2,34}... | collective-permute-start | bytes 345608 | tf_op jit(solution)/shard_map/ppermute | solution.py:568
  24.8 2.2 %collective-permute-start.7 = (f32[5,2,1,2880]{3,2,1,0:T(1,128)S(1)}, f32[5,2,1,2880]{3,2,1,0:T(1,128)S(1)}, u32[]{:S(2)}, u32[]{:S(2)}) collective-permute-start(f32[5,2,1,2880]{3,2,1,0:T(1,128)S(1)} %get-tuple-element.33), channel_id=1, source_target_pairs={{32,64},{64,32},{33,65},{65,33},{34,66},{66,34},{35,67},{67,35},{3... | collective-permute-start | bytes 345608 | tf_op jit(solution)/shard_map/ppermute | solution.py:568
  28.1 2.6 %copy-start.8 = (s32[1,23040]{1,0:T(1,128)S(1)}, s32[1,23040]{1,0:T(1,128)}, u32[]{:S(2)}) copy-start(s32[1,23040]{1,0:T(1,128)} %param.26) | copy-start | bytes 276484
  28.1 2.9 %copy-start.2 = (s32[32]{0:T(128)S(1)}, s32[32]{0:T(128)}, u32[]{:S(2)}) copy-start(s32[32]{0:T(128)} %units_ref.1) | copy-start | bytes 388
  30.5 2.6 %collective-permute-start.8 = (f32[23,80,128]{2,1,0:T(8,128)S(1)}, f32[23,80,128]{2,1,0:T(8,128)S(1)}, u32[]{:S(2)}, u32[]{:S(2)}) collective-permute-start(f32[23,80,128]{2,1,0:T(8,128)S(1)} %transport.3.mine_ref), channel_id=1, source_target_pairs={{0,1},{2,3},{4,5},{6,7},{8,9},{10,11},{12,13},{14,15},{16,17},{18,... | collective-permute-start | bytes 2826248 | tf_op jit(solution)/shard_map/ppermute | solution.py:568
  49.4 12.7 %copy-start.10 = (f32[5,64]{1,0:T(8,128)S(1)}, f32[5,64]{1,0:T(8,128)}, u32[]{:S(2)}) copy-start(f32[5,64]{1,0:T(8,128)} %param.21) | copy-start | bytes 3844
  49.4 37.7 %all-to-all-start = ((f32[16,192,128]{2,1,0:T(8,128)}), f32[16,192,128]{2,1,0:T(8,128)S(1)}, u32[]{:S(2)}, u32[]{:S(2)}) async-start(f32[16,192,128]{2,1,0:T(8,128)} %bitcast.7), calls=%async_computation | async-start | bytes 3145728 | tf_op jit(solution)/shard_map/all_to_all | solution.py:635
  63.0 1.9 %copy-start.1 = (f32[32,8,2880]{2,1,0:T(8,128)S(1)}, f32[32,8,2880]{2,1,0:T(8,128)}, u32[]{:S(2)}) copy-start(f32[32,8,2880]{2,1,0:T(8,128)} %param.22) | copy-start | bytes 8847364
  87.1 13.7 %copy-start.9 = (f32[7,5]{1,0:T(8,128)S(1)}, f32[7,5]{1,0:T(8,128)}, u32[]{:S(2)}) copy-start(f32[7,5]{1,0:T(8,128)} %param.23) | copy-start | bytes 424
  94.1 6.8 %copy-start.11 = (f32[7]{0:T(128)S(1)}, f32[7]{0:T(128)}, u32[]{:S(2)}) copy-start(f32[7]{0:T(128)} %param.25) | copy-start | bytes 88
  94.1 6.8 %copy-start.12 = (f32[7]{0:T(128)S(1)}, f32[7]{0:T(128)}, u32[]{:S(2)}) copy-start(f32[7]{0:T(128)} %param.24) | copy-start | bytes 88
  94.2 25.9 %copy-start.3 = (bf16[512,512]{1,0:T(8,128)(2,1)S(1)}, bf16[512,512]{1,0:T(8,128)(2,1)}, u32[]{:S(2)}) copy-start(bf16[512,512]{1,0:T(8,128)(2,1)} %constant.127.clone.fwd_high) | copy-start | bytes 1572868
  94.2 25.9 %copy-start.4 = (bf16[512,512]{1,0:T(8,128)(2,1)S(1)}, bf16[512,512]{1,0:T(8,128)(2,1)}, u32[]{:S(2)}) copy-start(bf16[512,512]{1,0:T(8,128)(2,1)} %constant.128.clone.fwd_low) | copy-start | bytes 1572868
  94.2 25.9 %copy-start.5 = (bf16[512,512]{1,0:T(8,128)(2,1)S(1)}, bf16[512,512]{1,0:T(8,128)(2,1)}, u32[]{:S(2)}) copy-start(bf16[512,512]{1,0:T(8,128)(2,1)} %constant.129.clone.inv_high) | copy-start | bytes 1572868
  94.2 25.9 %copy-start.6 = (bf16[512,512]{1,0:T(8,128)(2,1)S(1)}, bf16[512,512]{1,0:T(8,128)(2,1)}, u32[]{:S(2)}) copy-start(bf16[512,512]{1,0:T(8,128)(2,1)} %constant.130.clone.inv_low) | copy-start | bytes 1572868
  94.2 25.9 %copy-start.7 = (f32[1,512]{1,0:T(1,128)S(1)}, f32[1,512]{1,0:T(1,128)}, u32[]{:S(2)}) copy-start(f32[1,512]{1,0:T(1,128)} %constant.144.waves_ref) | copy-start | bytes 6148
  94.2 25.8 %all-to-all-start.1 = ((f32[128,16,128]{2,1,0:T(8,128)}), f32[128,16,128]{2,1,0:T(8,128)S(1)}, u32[]{:S(2)}, u32[]{:S(2)}) async-start(f32[128,16,128]{2,1,0:T(8,128)} %bitcast.9), calls=%async_computation.1 | async-start | bytes 2097152 | tf_op jit(solution)/shard_map/all_to_all | solution.py:640

commit v6 on v5

--- a/solution.py
+++ b/solution.py
@@ -86,9 +86,33 @@
     return courant_plus * upstream + courant_minus * downstream
 
 
+def outer_slab_kernel(side_ref, n_hbm, wlev_hbm, slab_ref, sems):
+    core = side_ref[0]
+    fetches = [
+        pltpu.make_async_copy(n_hbm.at[s, core], slab_ref.at[s], sems.at[s]) for s in range(SPECIES)
+    ]
+    fetches.append(pltpu.make_async_copy(wlev_hbm.at[0], slab_ref.at[SPECIES], sems.at[SPECIES]))
+    for fetch in fetches:
+        fetch.start()
+    for fetch in fetches:
+        fetch.wait()
+
+
+def outer_slab(side, density, wind_lev):
+    return call(
+        outer_slab_kernel,
+        on_chip((SPECIES + 1, BAND_LATS, NLON)),
+        [SMEM, HBM, HBM],
+        VMEM,
+        [pltpu.SemaphoreType.DMA((SPECIES + 1,))],
+        name="outer_slab",
+        flops=100_000,
+    )(side, density, wind_lev)
+
+
 def edges_kernel(
-    side_ref, n_hbm, wlon_hbm, wlat_hbm, wlev_hbm,
-    n_ref, wlon_ref, wlat_ref, wlev_ref, inner_ref, outer_ref, row_ref, far_row_ref, sems,
+    side_ref, n_hbm, wlon_hbm, wlat_hbm, wlev_hbm, _,
+    n_ref, wlon_ref, wlat_ref, wlev_ref, inner_ref, row_ref, far_row_ref, sems,
 ):
     fetches = [
         pltpu.make_async_copy(n_hbm.at[s], n_ref.at[s], sems.at[s]) for s in range(SPECIES)
@@ -102,7 +126,6 @@
         fetch.wait()
     core, odd = side_ref[0], side_ref[1] == 1
     inner_ref[SPECIES] = wlev_ref[0]
-    outer_ref[SPECIES] = wlev_ref[0]
     for j in range(2):
         row_ref[SPECIES, j] = wlat_ref[j, :1]
         far_row_ref[SPECIES, j] = wlat_ref[j, :1]
@@ -110,7 +133,6 @@
     @pl.loop(0, SPECIES)
     def _(s):
         inner_ref[s] = n_ref[s, 1 - core]
-        outer_ref[s] = n_ref[s, core]
         for j in range(2):
             first, last = n_ref[s, j, :1], n_ref[s, j, BAND_LATS - 1 :]
             row_ref[s, j] = jnp.where(odd, first, last)
@@ -119,7 +141,7 @@
     fetches[-1].wait()
 
 
-def edges(side, density, wind_lon, wind_lat, wind_lev):
+def edges(side, density, wind_lon, wind_lat, wind_lev, slab):
     return call(
         edges_kernel,
         (
@@ -128,24 +150,20 @@
             on_chip(wind_lat.shape),
             on_chip(wind_lev.shape),
             on_chip((SPECIES + 1, BAND_LATS, NLON)),
-            on_chip((SPECIES + 1, BAND_LATS, NLON)),
             on_chip((SPECIES + 1, 2, 1, NLON)),
             on_chip((SPECIES + 1, 2, 1, NLON)),
         ),
-        [SMEM] + [HBM] * 4,
-        (VMEM,) * 8,
+        [SMEM] + [HBM] * 4 + [HELD],
+        (VMEM,) * 7,
         [pltpu.SemaphoreType.DMA((SPECIES + 3,))],
         name="edges",
         flops=1_000_000,
-    )(side, density, wind_lon, wind_lat, wind_lev)
-
-
-def transport_kernel(side_ref, n_ref, wlon_ref, wlat_ref, wlev_ref, *refs, last):
-    inner_ref, outer_ref, row_ref, far_row_ref = refs[:4]
-    inner_wind, outer_wind, row_wind, far_row_wind = refs[4:8]
-    outs = refs[8:]
-    core, odd = side_ref[0], side_ref[1] == 1
-    south_core = core == 0
+    )(side, density, wind_lon, wind_lat, wind_lev, slab)
+
+
+def level_kernel(side_ref, wlon_ref, wlat_ref, wlev_ref, *refs, outer, last, whole):
+    row_ref, far_row_ref, row_wind, far_row_wind, cross_ref, cross_wind = refs[:6]
+    odd = side_ref[1] == 1
 
     def split(c):
         return jnp.maximum(c, 0.0), jnp.minimum(c, 0.0)
@@ -156,11 +174,22 @@
     def shift_east(x):
         return jnp.concatenate([x[:, 1:], x[:, :1]], axis=1)
 
-    for j in range(2):
+    def advance(core):
+        j = core if outer else 1 - core
+        if whole:
+            n_ref, outs = refs[6], refs[7:]
+            level = lambda which, s: n_ref[s, which]
+        else:
+            outer_ref, inner_ref, outs = refs[6], refs[7], refs[8:]
+            level = lambda which, s: (outer_ref if which == core else inner_ref)[s]
+        if outer:
+            sent_ref, outs = outs[0], outs[1:]
+        if not last:
+            outs[1][0] = cross_wind[SPECIES]
 
         @pl.loop(0, SPECIES)
         def _(s):
-            x = n_ref[s, j]
+            x = level(j, s)
             flux = upwind(*split(wlon_ref[j]), shift_west(x), x)
             total = x + (flux - shift_east(flux))
             south = jnp.where(odd, row_ref[s, j], far_row_ref[s, j])
@@ -171,53 +200,44 @@
             edge = upwind(*split(north_wind), x[BAND_LATS - 1 :], north)
             total = total + (flux - jnp.concatenate([flux[1:], edge], axis=0))
             if j == 0:
-                beneath = jnp.where(south_core, outer_ref[s], inner_ref[s])
-                overhead, over_wind = n_ref[s, 1], wlev_ref[1]
+                beneath, overhead, over_wind = cross_ref[s], level(1, s), wlev_ref[1]
             else:
-                beneath = n_ref[s, 0]
-                overhead = jnp.where(south_core, inner_ref[s], outer_ref[s])
-                over_wind = jnp.where(south_core, inner_wind[SPECIES], outer_wind[SPECIES])
+                beneath, overhead, over_wind = level(0, s), cross_ref[s], cross_wind[0 if last else SPECIES]
             flux = upwind(*split(wlev_ref[j]), beneath, x)
             total = total + (flux - upwind(*split(over_wind), x, overhead))
             if last:
-                row = pl.multiple_of((j * SPECIES + s) * BAND_LATS, BAND_LATS)
+                row = pl.multiple_of(s * BAND_LATS, BAND_LATS)
                 for blk in range(LON_BLOCKS):
                     wide = min(LANES, NLON - blk * LANES)
                     outs[0][blk, pl.ds(row, BAND_LATS), :wide] = total[:, blk * LANES : blk * LANES + wide]
-            else:
-                outs[0][s, j] = total
-
-                @pl.when(core == 1 - j)
-                def _():
-                    outs[1][s] = total
-
-                @pl.when(core == j)
-                def _():
-                    outs[2][s] = total
-
-                outs[3][s, j] = jnp.where(odd, total[:1], total[BAND_LATS - 1 :])
-                outs[4][s, j] = jnp.where(odd, total[BAND_LATS - 1 :], total[:1])
-
-
-def transport_step(side, density, winds, halo, wind_halo, last):
+                return
+            outs[0][s] = total
+            if outer:
+                for which, values in ((j, total), (1 - j, sent_ref[s])):
+                    first, final = values[:1], values[BAND_LATS - 1 :]
+                    outs[2][s, which] = jnp.where(odd, first, final)
+                    outs[3][s, which] = jnp.where(odd, final, first)
+
+    for core in range(2):
+        pl.when(side_ref[0] == core)(functools.partial(advance, core))
+
+
+def advance_level(side, winds, rows, wind_rows, cross, cross_wind, density, outer, last, sent=()):
     if last:
-        out_shape = (on_chip((LON_BLOCKS, 2 * SPECIES * BAND_LATS, LANES)),)
+        out_shape = (on_chip((LON_BLOCKS, SPECIES * BAND_LATS, LANES)),)
     else:
-        out_shape = (
-            on_chip((SPECIES, 2, BAND_LATS, NLON)),
-            on_chip((SPECIES, BAND_LATS, NLON)),
-            on_chip((SPECIES, BAND_LATS, NLON)),
-            on_chip((SPECIES, 2, 1, NLON)),
-            on_chip((SPECIES, 2, 1, NLON)),
-        )
+        out_shape = on_chip((SPECIES, BAND_LATS, NLON)), on_chip((1, BAND_LATS, NLON))
+        if outer:
+            out_shape += (on_chip((SPECIES, 2, 1, NLON)),) * 2
+    args = (side, *winds, *rows, *wind_rows, cross, cross_wind, *density, *sent)
     return call(
-        functools.partial(transport_kernel, last=last),
+        functools.partial(level_kernel, outer=outer, last=last, whole=len(density) == 1),
         out_shape,
-        [SMEM] + [HELD] * 12,
+        [SMEM] + [HELD] * (len(args) - 1),
         (VMEM,) * len(out_shape),
-        name="transport",
-        flops=4_000_000,
-    )(side, density, *winds, *halo, *wind_halo)
+        name="outer_level" if outer else "inner_level",
+        flops=2_000_000,
+    )(*args)
 
 
 def prepare_kernel(
@@ -296,17 +316,18 @@
 
 
 def pack_kernel(
-    core_ref, starts_ref, units_ref, order_ref, mine_ref, other_ref, out_hbm, planes, table_ref, msg_ref, sems
+    core_ref, starts_ref, units_ref, order_ref, *refs
 ):
+    sources, (out_hbm, planes, table_ref, msg_ref, sems) = refs[:CHIP_LEVS], refs[CHIP_LEVS:]
+
     @pl.loop(0, LON_BLOCKS)
     def _(blk):
-        for side, source in enumerate((mine_ref, other_ref)):
-            for j in range(2):
-                for i in range(PLANES):
-                    from_row = (j * SPECIES + i % SPECIES) * BAND_LATS
-                    planes[blk, pl.ds(((2 * side + j) * PLANES + i) * PITCH, BAND_LATS), :] = source[
-                        blk, from_row : from_row + BAND_LATS, :
-                    ]
+        for jj, source in enumerate(sources):
+            for i in range(PLANES):
+                from_row = i % SPECIES * BAND_LATS
+                planes[blk, pl.ds((jj * PLANES + i) * PITCH, BAND_LATS), :] = source[
+                    blk, from_row : from_row + BAND_LATS, :
+                ]
 
     @pl.loop(0, LON_BLOCKS)
     def _(blk):
@@ -351,11 +372,11 @@
         send(peer).wait()
 
 
-def pack(core, starts, units, order, mine, other):
+def pack(core, starts, units, order, blocks):
     return call(
         pack_kernel,
         sds((16 * PEER_ROWS, LANES)),
-        [SMEM, SMEM, SMEM, SMEM, HELD, HELD],
+        [SMEM] * 4 + [HELD] * CHIP_LEVS,
         HBM,
         [
             pltpu.VMEM((LON_BLOCKS, CHIP_LEVS * PLANES * PITCH, LANES), f32),
@@ -366,7 +387,7 @@
         name="pack",
         flops=30_000_000,
         vmem=32,
-    )(core, starts, units, order, mine, other)
+    )(core, starts, units, order, *blocks)
 
 
 def solve_kernel(
@@ -386,8 +407,8 @@
             for chunk in range(CHUNKS):
                 row = pl.multiple_of((2 * i + side) * PEER_ROWS + chunk * MSG_ROWS, MSG_ROWS)
                 flipped = jnp.concatenate([got_ref[pl.ds(row, MSG_ROWS), :]] * 2, axis=0).T
-                turned[chunk, pl.ds(out + 64 * core, 64), :] = flipped[:64]
-                turned[chunk, pl.ds(out + 64 - 64 * core, 64), :] = flipped[64:]
+                for part, level in enumerate((1 + core, 3 * core, 2 - core, 3 - 3 * core)):
+                    turned[chunk, pl.ds(out + 32 * level, 32), :] = flipped[32 * part : 32 * part + 32]
 
     def leave(s):
         return pltpu.make_async_copy(state.at[s], state_hbm.at[0, 0, s], sems.at[s])
@@ -568,13 +589,6 @@
     return lax.ppermute(x, axis, [(i, i + 1) for i in lows] + [(i + 1, i) for i in lows])
 
 
-def exchange(inner, outer, row, far_row):
-    outer = swap(outer, "lev", 1)
-    row = swap(row, "band", 0)
-    far_row = swap(far_row, "band", 1)
-    return swap(inner, "lev", 0), outer, row, far_row
-
-
 def on_device(
     neutrals,
     wind_lon,
@@ -592,15 +606,18 @@
     lev = lax.axis_index("lev")
 
     side = jnp.stack([lev % 2, lax.axis_index("band") % 2]).astype(jnp.int32)
-    neutrals, *rest = edges(side, neutrals, wind_lon, wind_lat, wind_lev)
-    winds, first_halo = rest[:3], exchange(*rest[3:])
+    slab = outer_slab(side, neutrals, wind_lev)
+    outer_wind = outer_halo = swap(slab, "lev", 1)
+    neutrals, *winds, inner, row, far_row = edges(side, neutrals, wind_lon, wind_lat, wind_lev, slab)
+    wind_rows = rows = swap(row, "band", 0), swap(far_row, "band", 1)
+    inner_wind = inner_halo = swap(inner, "lev", 0)
 
     starts = jnp.cumsum(column_units) - column_units
     order = column_order[0]
     lat = jnp.zeros_like(order)
     for i in range(1, BAND_LATS):
         lat = lat + (order >= i * NLON).astype(jnp.int32)
-    rows = jnp.pad(order + lat * (LON_PAD - NLON), (0, ORDER_PAD - BAND_COLS))
+    places = jnp.pad(order + lat * (LON_PAD - NLON), (0, ORDER_PAD - BAND_COLS))
     own_units = column_units[lev].reshape(1)
     padded = jnp.pad(order, (0, SLOTS_PAD))
     own = lax.dynamic_slice(padded, (TUBE_COLS * starts[lev],), (SLOTS_PAD,))
@@ -624,14 +641,21 @@
         jnp.swapaxes(coefs, 2, 3).reshape(-1, 1),
     )
 
-    density, *halo = transport_step(side, neutrals, winds, first_halo, first_halo, False)
-    (mine,) = transport_step(side, density, winds, exchange(*halo), first_halo, True)
     owners = lax.axis_size("lev")
-    other = swap(mine, "lev", 0)
+    step = functools.partial(advance_level, side, winds)
+    inner, inner_wind = step(rows, wind_rows, inner_halo, inner_wind, (neutrals,), False, False)
+    inner_halo = swap(inner, "lev", 0)
+    outer, outer_wind, row, far_row = step(rows, wind_rows, outer_halo, outer_wind, (neutrals,), True, False, (inner,))
+    outer_halo = swap(outer, "lev", 1)
+    rows = swap(row, "band", 0), swap(far_row, "band", 1)
+    (inner_mine,) = step(rows, wind_rows, inner_halo, inner_wind, (outer, inner), False, True)
+    inner_other = swap(inner_mine, "lev", 0)
+    (outer_mine,) = step(rows, wind_rows, outer_halo, outer_wind, (outer, inner), True, True, (inner_mine,))
+    blocks = (inner_mine, outer_mine, inner_other, swap(outer_mine, "lev", 0))
 
     core = (lev % 2).reshape(1)
     parity = [[2 * i + c for i in range(owners // 2)] for c in range(2)]
-    outgoing = pack(core, starts, column_units, rows, mine, other)
+    outgoing = pack(core, starts, column_units, places, blocks)
     got = lax.all_to_all(
         outgoing.reshape(16, PEER_ROWS, LANES), "lev", 0, 0, axis_index_groups=parity, tiled=True
     ).reshape(16 * PEER_ROWS, LANES)

time: 126 us -> 124 us (0.984)
  waiting for transfers between devices: 44.1 us -> 35.4 us
  Pallas kernels: 43.8 us -> 47.6 us
  local copies, waits for them, and re-layouts: 3.98 us -> 5.49 us
    ppermute x9 -> x10, waiting for transfers between devices: 9.91 us -> 5.06 us  [swap(): lax.ppermute(x, axis, [(i, i + 1) for i in lows] + [(i + 1, i) for i in l...]
    all_to_all x1, waiting for transfers between devices: 15.2 us -> 11.3 us  [on_device(): lax.all_to_all(outgoing.reshape(16, PEER_ROWS, LANES), 'lev', 0, 0, axis_...]
    pallas_call x7 -> x10, Pallas kernels: 43.8 us -> 47.6 us  [placed(): return run(*(place(x, spec) for x, spec in zip(args, in_specs)))]
    all_to_all x1, starting transfers between devices: 10.8 us -> 8.05 us  [on_device(): lax.all_to_all(outgoing.reshape(16, PEER_ROWS, LANES), 'lev', 0, 0, axis_...]
    ppermute x9 -> x10, starting transfers between devices: 14.4 us -> 17 us  [swap(): lax.ppermute(x, axis, [(i, i + 1) for i in lows] + [(i + 1, i) for i in l...]
    unnamed x26 -> x38, local copies, waits for them, and re-layouts: 1.92 us -> 3.46 us
    all_to_all x1, starting transfers between devices: 6.58 us -> 7.86 us  [on_device(): lax.all_to_all(items.reshape(PEERS, ITEM_ROWS, LANES), ('band', 'lev'), 0...]
  transfers between devices with their start and end apart: 11 -> 12, of which waited for: 7 -> 6; matrix products, arithmetic and copies ran while one was open for 2% -> 3% of each run, Pallas kernels for 6% -> 11%
where the time goes in v6:
time: 124 us; the launch traced here: 125 us
  Pallas kernels  47.6 us (38%)
  waiting for transfers between devices  35.4 us (29%)
  starting transfers between devices  32.9 us (27%)
  local copies, waits for them, and re-layouts  5.49 us (4%)
  between operations  1.7 us (1%)
  other arithmetic  1.5 us (1%)
    pallas_call x10, Pallas kernels, placed(): return run(*(place(x, spec) for x, spec in zip(args, in_specs)))  47.6 us
    all_to_all x1, waiting for transfers between devices, on_device(): lax.all_to_all(items.reshape(PEERS, ITEM_ROWS, LANES), ('band', 'lev'), 0...  19.1 us
    ppermute x10, starting transfers between devices, swap(): lax.ppermute(x, axis, [(i, i + 1) for i in lows] + [(i + 1, i) for i in l...  17 us
    all_to_all x1, waiting for transfers between devices, on_device(): lax.all_to_all(outgoing.reshape(16, PEER_ROWS, LANES), 'lev', 0, 0, axis_...  11.3 us
    all_to_all x1, starting transfers between devices, on_device(): lax.all_to_all(outgoing.reshape(16, PEER_ROWS, LANES), 'lev', 0, 0, axis_...  8.05 us
    all_to_all x1, starting transfers between devices, on_device(): lax.all_to_all(items.reshape(PEERS, ITEM_ROWS, LANES), ('band', 'lev'), 0...  7.86 us
    ppermute x10, waiting for transfers between devices, swap(): lax.ppermute(x, axis, [(i, i + 1) for i in lows] + [(i + 1, i) for i in l...  5.06 us
    unnamed x38, local copies, waits for them, and re-layouts  3.46 us
  transfers between devices with their start and end apart: 12, of which 6 were waited for; matrix products, arithmetic and copies ran while one was open for 3% of the time, Pallas kernels for 11%

profile of v6, /device:TPU:1, one launch (start us, length us, event | category | flops | bytes accessed | tf_op | source)
XLA Modules:
  0.0 124.6 jit_solution(1782788122101977606)
XLA Ops:
  0.7 1.7 %outer_slab.1._ = f32[6,8,2880]{2,1,0:T(8,128)S(1)} custom-call(s32[2]{0:T(128)S(1)} %pad_add_fusion.side_ref, f32[5,2,8,2880]{3,2,1,0:T(8,128)} %n_hbm.3, f32[2,8,2880]{2,1,0:T(8,128)} %wlev_hbm.3), custom_call_target="tpu_custom_call" | custom-call | flops 100000 | bytes 1048576 | tf_op jit(solution)/shard_map/outer_slab/pallas_call | solution.py:76
  2.5 2.1 %edges.1 = (f32[5,2,8,2880]{3,2,1,0:T(8,128)S(1)}, f32[2,8,2880]{2,1,0:T(8,128)S(1)}, f32[2,8,2880]{2,1,0:T(8,128)S(1)}, f32[2,8,2880]{2,1,0:T(8,128)S(1)}, f32[...) custom-call(s32[2]{0:T(128)S(1)} %pad_add_fusion.side_ref, ...), custom_call_target="tpu_custom_call" | custom-call | flops 1000000 | bytes 1048576 | tf_op jit(solution)/shard_map/edges/pallas_call | solution.py:76
  4.6 1.5 %collective-permute-start.3 = (f32[6,8,2880]{2,1,0:T(8,128)S(1)}, f32[6,8,2880]{2,1,0:T(8,128)S(1)}, u32[]{:S(2)}, u32[]{:S(2)}) collective-permute-start(f32[6,8,2880]{2,1,0:T(8,128)S(1)} %get-tuple-element.27), channel_id=1, source_target_pairs={{0,1},{2,3},{4,5},{6,7},{8,9},{10,11},{12,13},{14,15},{16,17},{18,... | collective-permute-start | bytes 1658888 | tf_op jit(solution)/shard_map/ppermute | solution.py:589
  6.0 3.1 %collective-permute-start.2 = (f32[6,8,2880]{2,1,0:T(8,128)S(1)}, f32[6,8,2880]{2,1,0:T(8,128)S(1)}, u32[]{:S(2)}, u32[]{:S(2)}) collective-permute-start(f32[6,8,2880]{2,1,0:T(8,128)S(1)} %outer_slab.1._), channel_id=1, source_target_pairs={{1,2},{3,4},{5,6},{7,8},{9,10},{11,12},{13,14},{15,16},{17,18},{19... | collective-permute-start | bytes 1658888 | tf_op jit(solution)/shard_map/ppermute | solution.py:589
  9.2 1.7 %collective-permute-start = (f32[6,2,1,2880]{3,2,1,0:T(1,128)S(1)}, f32[6,2,1,2880]{3,2,1,0:T(1,128)S(1)}, u32[]{:S(2)}, u32[]{:S(2)}) collective-permute-start(f32[6,2,1,2880]{3,2,1,0:T(1,128)S(1)} %get-tuple-element.24), channel_id=1, source_target_pairs={{0,32},{64,96},{32,0},{96,64},{1,33},{65,97},{33,1},{97,65},{2,34}... | collective-permute-start | bytes 414728 | tf_op jit(solution)/shard_map/ppermute | solution.py:589
  11.5 1.8 %collective-permute-done.refs_0_.refs_2_ = f32[6,2,1,2880]{3,2,1,0:T(1,128)S(1)} collective-permute-done((f32[6,2,1,2880]{3,2,1,0:T(1,128)S(1)}, f32[6,2,1,2880]{3,2,1,0:T(1,128)S(1)}, u32[]{:S(2)}, u32[]{:S(2)}) %collective-permute-start) | collective-permute-done | bytes 138272 | tf_op jit(solution)/shard_map/ppermute | solution.py:589
  13.4 1.5 %inner_level.2 = (f32[5,8,2880]{2,1,0:T(8,128)S(1)}, f32[1,8,2880]{2,1,0:T(8,128)S(1)}) custom-call(s32[2]{0:T(128)S(1)} %pad_add_fusion.side_ref, f32[2,8,2880]{2,1,0:T(8,128)S(1)} %get-tuple-element.21.wlon_ref, f32[2,8,2880]{2,1,0:T(8,128)S(1)} %get-tuple-element.22.wlat_ref, f32[2,8,2880]{2,1,0:T(8,128)S(1)} %get-tuple-element.23.wlev_ref, ...), custom_call_target="tpu_custom_call" | custom-call | flops 2000000 | bytes 1048576 | tf_op jit(solution)/shard_map/inner_level/pallas_call | solution.py:76
  15.5 1.5 %collective-permute-done.2.refs_4_.refs_5_ = f32[6,8,2880]{2,1,0:T(8,128)S(1)} collective-permute-done((f32[6,8,2880]{2,1,0:T(8,128)S(1)}, f32[6,8,2880]{2,1,0:T(8,128)S(1)}, u32[]{:S(2)}, u32[]{:S(2)}) %collective-permute-start.2) | collective-permute-done | bytes 552992 | tf_op jit(solution)/shard_map/ppermute | solution.py:589
  17.0 1.7 %outer_level.2 = (f32[5,8,2880]{2,1,0:T(8,128)S(1)}, f32[1,8,2880]{2,1,0:T(8,128)S(1)}, f32[5,2,1,2880]{3,2,1,0:T(1,128)S(1)}, f32[5,2,1,2880]{3,2,1,0:T(1,128)S(1)}) custom-call(s32[2]{0:T(128)S(1)} %pad_add_fusion.side_ref, f32[2,8,2880]{2,1,0:T(8,128)S(1)} %get-tuple-element.21.wlon_ref, f32[2,8,2880]{2,1,0:T(8,128)S(1)} %get-tuple-element.22.wlat_ref, ...), custom_call_target="tpu_custom_call" | custom-call | flops 2000000 | bytes 1048576 | tf_op jit(solution)/shard_map/outer_level/pallas_call | solution.py:76
  18.7 3.5 %collective-permute-start.7 = (f32[5,8,2880]{2,1,0:T(8,128)S(1)}, f32[5,8,2880]{2,1,0:T(8,128)S(1)}, u32[]{:S(2)}, u32[]{:S(2)}) collective-permute-start(f32[5,8,2880]{2,1,0:T(8,128)S(1)} %get-tuple-element.32.refs_6_), channel_id=1, source_target_pairs={{1,2},{3,4},{5,6},{7,8},{9,10},{11,12},{13,14},{15,16},{17,18},{19... | collective-permute-start | bytes 1382408 | tf_op jit(solution)/shard_map/ppermute | solution.py:589
  22.2 5.2 %collective-permute-start.4 = (f32[5,2,1,2880]{3,2,1,0:T(1,128)S(1)}, f32[5,2,1,2880]{3,2,1,0:T(1,128)S(1)}, u32[]{:S(2)}, u32[]{:S(2)}) collective-permute-start(f32[5,2,1,2880]{3,2,1,0:T(1,128)S(1)} %get-tuple-element.29), channel_id=1, source_target_pairs={{0,32},{64,96},{32,0},{96,64},{1,33},{65,97},{33,1},{97,65},{2,34}... | collective-permute-start | bytes 345608 | tf_op jit(solution)/shard_map/ppermute | solution.py:589
  29.7 0.9 copy-done.5
  30.6 1.5 %inner_level.3.refs_8_.refs_0_ = f32[23,40,128]{2,1,0:T(8,128)S(1)} custom-call(s32[2]{0:T(128)S(1)} %pad_add_fusion.side_ref, f32[2,8,2880]{2,1,0:T(8,128)S(1)} %get-tuple-element.21.wlon_ref, f32[2,8,2880]{2,1,0:T(8,128)S(1)} %get-tuple-element.22.wlat_ref, f32[2,8,2880]{2,1,0:T(8,128)S(1)} %get-tuple-element.23.wlev_ref, ...), custom_call_target="tpu_custom_call" | custom-call | flops 2000000 | bytes 1048576 | tf_op jit(solution)/shard_map/inner_level/pallas_call | solution.py:76
  32.2 1.5 %outer_level.3.refs_1_ = f32[23,40,128]{2,1,0:T(8,128)S(1)} custom-call(s32[2]{0:T(128)S(1)} %pad_add_fusion.side_ref, f32[2,8,2880]{2,1,0:T(8,128)S(1)} %get-tuple-element.21.wlon_ref, f32[2,8,2880]{2,1,0:T(8,128)S(1)} %get-tuple-element.22.wlat_ref, f32[2,8,2880]{2,1,0:T(8,128)S(1)} %get-tuple-element.23.wlev_ref, ...), custom_call_target="tpu_custom_call" | custom-call | flops 2000000 | bytes 1048576 | tf_op jit(solution)/shard_map/outer_level/pallas_call | solution.py:76
  34.6 1.1 collective-permute-done.9.refs_3_
  35.6 17.1 %pack.1 = f32[3072,128]{1,0:T(8,128)} custom-call(s32[1]{0:T(128)} %bitcast.core_ref, s32[32]{0:T(128)S(1)} %sub.16.starts_ref, s32[32]{0:T(128)S(1)} %copy-done.6, s32[23296]{0:T(1024)S(1)} %pad.11.order_ref, f32[23,40,128]{2,1,0:T(8,128)S(1)} %inner_level.3.refs_8_.refs_0_, f32[23,40,128]{2,1,0:T(8,128)S(1)} %outer_level.3.refs_1_, ...), custom_call_target="tpu_custom_call" | custom-call | flops 30000000 | bytes 1048576 | tf_op jit(solution)/shard_map/pack/pallas_call | solution.py:76
  52.8 8.0 %all-to-all-start = ((f32[16,192,128]{2,1,0:T(8,128)}), f32[16,192,128]{2,1,0:T(8,128)S(1)}, u32[]{:S(2)}, u32[]{:S(2)}) async-start(f32[16,192,128]{2,1,0:T(8,128)} %bitcast.7), calls=%async_computation | async-start | bytes 3145728 | tf_op jit(solution)/shard_map/all_to_all | solution.py:659
  63.6 1.8 %copy-done.1 = f32[32,8,2880]{2,1,0:T(8,128)S(1)} copy-done((f32[32,8,2880]{2,1,0:T(8,128)S(1)}, f32[32,8,2880]{2,1,0:T(8,128)}, u32[]{:S(2)}) %copy-start.1) | copy-done | bytes 2949144
  65.5 7.5 %prepare.1 = (s32[384]{0:T(512)S(1)}, f32[9,32,128]{2,1,0:T(8,128)S(1)}, f32[960,128]{1,0:T(8,128)S(1)}) custom-call(s32[1]{0:T(128)} %dynamic_slice.12.units_ref, s32[270]{0:T(512)S(1)} %dynamic-slice_reduce_fusion.owner_ref, s32[1152]{0:T(1024)S(1)} %get-tuple-element.39.rows_ref, s32[9,128]{1,0:T(8,128)S(1)} %get-tuple-element.38.sel_ref, ...), custom_call_target="tpu_custom_call" | custom-call | flops 20000000 | bytes 1048576 | tf_op jit(solution)/shard_map/prepare/pallas_call | solution.py:76
  73.0 11.3 %all-to-all-done = f32[16,192,128]{2,1,0:T(8,128)S(1)} async-done(((f32[16,192,128]{2,1,0:T(8,128)}), f32[16,192,128]{2,1,0:T(8,128)S(1)}, u32[]{:S(2)}, u32[]{:S(2)}) %all-to-all-start) | async-done | bytes 1572896 | tf_op jit(solution)/shard_map/all_to_all | solution.py:659
  84.3 6.9 %solve.1 = (f32[1,1,5,64,1080]{4,3,2,1,0:T(8,128)}, f32[2048,128]{1,0:T(8,128)}) custom-call(s32[1]{0:T(128)} %bitcast.core_ref, s32[1]{0:T(128)} %dynamic_slice.12.units_ref, s32[384]{0:T(512)S(1)} %get-tuple-element.20.table_ref, f32[3072,128]{1,0:T(8,128)S(1)} %bitcast.16, f32[960,128]{1,0:T(8,128)S(1)} %get-tuple-element.34.coef_ref, ...), custom_call_target="tpu_custom_call" | custom-call | flops 40000000 | bytes 1048576 | tf_op jit(solution)/shard_map/solve/pallas_call | solution.py:76
  91.3 7.9 %all-to-all-start.1 = ((f32[128,16,128]{2,1,0:T(8,128)}), f32[128,16,128]{2,1,0:T(8,128)S(1)}, u32[]{:S(2)}, u32[]{:S(2)}) async-start(f32[128,16,128]{2,1,0:T(8,128)} %bitcast.9), calls=%async_computation.1 | async-start | bytes 2097152 | tf_op jit(solution)/shard_map/all_to_all | solution.py:664
  99.4 19.1 %all-to-all-done.1 = f32[128,16,128]{2,1,0:T(8,128)S(1)} async-done(((f32[128,16,128]{2,1,0:T(8,128)}), f32[128,16,128]{2,1,0:T(8,128)S(1)}, u32[]{:S(2)}, u32[]{:S(2)}) %all-to-all-start.1) | async-done | bytes 1048608 | tf_op jit(solution)/shard_map/all_to_all | solution.py:664
  118.5 6.1 %lines.1 = f32[1,7,96,512]{3,2,1,0:T(8,128)} custom-call(f32[2048,128]{1,0:T(8,128)S(1)} %bitcast.18, f32[35]{0:T(128)S(1)} %reshape.76.yield_ref, f32[14]{0:T(128)S(1)} %pad_maximum_fusion.rates_ref, f32[1,512]{1,0:T(1,128)S(1)} %copy-done.11, bf16[512,512]{1,0:T(8,128)(2,1)S(1)} %copy-done.7, bf16[512,512]{1,0:T(8,128)(2,1)S(1)} %copy-done.8, ...), custom_call_target="tpu_custom_call" | custom-call | flops 2000000000 | bytes 1048576 | tf_op jit(solution)/shard_map/lines/pallas_call | solution.py:76
  (72 shorter events, 6.9 us)
Async XLA Ops:
  0.6 62.8 %copy-start = (s32[32,270,1]{1,2,0:T(1,128)S(1)}, s32[32,270,1]{1,2,0:T(1,128)}, u32[]{:S(2)}) copy-start(s32[32,270,1]{1,2,0:T(1,128)} %param.28) | copy-start | bytes 103684
  4.6 8.8 %collective-permute-start.3 = (f32[6,8,2880]{2,1,0:T(8,128)S(1)}, f32[6,8,2880]{2,1,0:T(8,128)S(1)}, u32[]{:S(2)}, u32[]{:S(2)}) collective-permute-start(f32[6,8,2880]{2,1,0:T(8,128)S(1)} %get-tuple-element.27), channel_id=1, source_target_pairs={{0,1},{2,3},{4,5},{6,7},{8,9},{10,11},{12,13},{14,15},{16,17},{18,... | collective-permute-start | bytes 1658888 | tf_op jit(solution)/shard_map/ppermute | solution.py:589
  6.0 10.9 %collective-permute-start.2 = (f32[6,8,2880]{2,1,0:T(8,128)S(1)}, f32[6,8,2880]{2,1,0:T(8,128)S(1)}, u32[]{:S(2)}, u32[]{:S(2)}) collective-permute-start(f32[6,8,2880]{2,1,0:T(8,128)S(1)} %outer_slab.1._), channel_id=1, source_target_pairs={{1,2},{3,4},{5,6},{7,8},{9,10},{11,12},{13,14},{15,16},{17,18},{19... | collective-permute-start | bytes 1658888 | tf_op jit(solution)/shard_map/ppermute | solution.py:589
  9.2 4.2 %collective-permute-start = (f32[6,2,1,2880]{3,2,1,0:T(1,128)S(1)}, f32[6,2,1,2880]{3,2,1,0:T(1,128)S(1)}, u32[]{:S(2)}, u32[]{:S(2)}) collective-permute-start(f32[6,2,1,2880]{3,2,1,0:T(1,128)S(1)} %get-tuple-element.24), channel_id=1, source_target_pairs={{0,32},{64,96},{32,0},{96,64},{1,33},{65,97},{33,1},{97,65},{2,34}... | collective-permute-start | bytes 414728 | tf_op jit(solution)/shard_map/ppermute | solution.py:589
  10.9 2.5 %collective-permute-start.1 = (f32[6,2,1,2880]{3,2,1,0:T(1,128)S(1)}, f32[6,2,1,2880]{3,2,1,0:T(1,128)S(1)}, u32[]{:S(2)}, u32[]{:S(2)}) collective-permute-start(f32[6,2,1,2880]{3,2,1,0:T(1,128)S(1)} %get-tuple-element.25), channel_id=1, source_target_pairs={{32,64},{64,32},{33,65},{65,33},{34,66},{66,34},{35,67},{67,35},{3... | collective-permute-start | bytes 414728 | tf_op jit(solution)/shard_map/ppermute | solution.py:589
  15.5 12.6 %copy-start.14 = (s32[1,23040]{1,0:T(1,128)S(1)}, s32[1,23040]{1,0:T(1,128)}, u32[]{:S(2)}) copy-start(s32[1,23040]{1,0:T(1,128)} %param.26) | copy-start | bytes 276484
  15.5 14.2 %collective-permute-start.6 = (f32[5,8,2880]{2,1,0:T(8,128)S(1)}, f32[5,8,2880]{2,1,0:T(8,128)S(1)}, u32[]{:S(2)}, u32[]{:S(2)}) collective-permute-start(f32[5,8,2880]{2,1,0:T(8,128)S(1)} %get-tuple-element.28.refs_7_), channel_id=1, source_target_pairs={{0,1},{2,3},{4,5},{6,7},{8,9},{10,11},{12,13},{14,15},{16,17},{18,... | collective-permute-start | bytes 1382408 | tf_op jit(solution)/shard_map/ppermute | solution.py:589
  18.7 11.0 %copy-start.2 = (f32[1,8,2880]{2,1,0:T(8,128)}, f32[1,8,2880]{2,1,0:T(8,128)S(1)}, u32[]{:S(2)}) copy-start(f32[1,8,2880]{2,1,0:T(8,128)S(1)} %get-tuple-element.33.refs_5_) | copy-start | bytes 276484
  18.7 13.4 %collective-permute-start.7 = (f32[5,8,2880]{2,1,0:T(8,128)S(1)}, f32[5,8,2880]{2,1,0:T(8,128)S(1)}, u32[]{:S(2)}, u32[]{:S(2)}) collective-permute-start(f32[5,8,2880]{2,1,0:T(8,128)S(1)} %get-tuple-element.32.refs_6_), channel_id=1, source_target_pairs={{1,2},{3,4},{5,6},{7,8},{9,10},{11,12},{13,14},{15,16},{17,18},{19... | collective-permute-start | bytes 1382408 | tf_op jit(solution)/shard_map/ppermute | solution.py:589
  22.2 7.4 %collective-permute-start.4 = (f32[5,2,1,2880]{3,2,1,0:T(1,128)S(1)}, f32[5,2,1,2880]{3,2,1,0:T(1,128)S(1)}, u32[]{:S(2)}, u32[]{:S(2)}) collective-permute-start(f32[5,2,1,2880]{3,2,1,0:T(1,128)S(1)} %get-tuple-element.29), channel_id=1, source_target_pairs={{0,32},{64,96},{32,0},{96,64},{1,33},{65,97},{33,1},{97,65},{2,34}... | collective-permute-start | bytes 345608 | tf_op jit(solution)/shard_map/ppermute | solution.py:589
  27.4 2.2 %collective-permute-start.5 = (f32[5,2,1,2880]{3,2,1,0:T(1,128)S(1)}, f32[5,2,1,2880]{3,2,1,0:T(1,128)S(1)}, u32[]{:S(2)}, u32[]{:S(2)}) collective-permute-start(f32[5,2,1,2880]{3,2,1,0:T(1,128)S(1)} %get-tuple-element.30), channel_id=1, source_target_pairs={{32,64},{64,32},{33,65},{65,33},{34,66},{66,34},{35,67},{67,35},{3... | collective-permute-start | bytes 345608 | tf_op jit(solution)/shard_map/ppermute | solution.py:589
  32.0 3.6 %collective-permute-start.8 = (f32[23,40,128]{2,1,0:T(8,128)S(1)}, f32[23,40,128]{2,1,0:T(8,128)}, u32[]{:S(2)}, u32[]{:S(2)}) collective-permute-start(f32[23,40,128]{2,1,0:T(8,128)S(1)} %inner_level.3.refs_8_.refs_0_), channel_id=1, source_target_pairs={{0,1},{2,3},{4,5},{6,7},{8,9},{10,11},{12,13},{14,15},{16,17},{18,... | collective-permute-start | bytes 1413128 | tf_op jit(solution)/shard_map/ppermute | solution.py:589
  33.6 2.0 %collective-permute-start.9 = (f32[23,40,128]{2,1,0:T(8,128)S(1)}, f32[23,40,128]{2,1,0:T(8,128)S(1)}, u32[]{:S(2)}, u32[]{:S(2)}) collective-permute-start(f32[23,40,128]{2,1,0:T(8,128)S(1)} %outer_level.3.refs_1_), channel_id=1, source_target_pairs={{0,1},{2,3},{4,5},{6,7},{8,9},{10,11},{12,13},{14,15},{16,17},{18,... | collective-permute-start | bytes 1413128 | tf_op jit(solution)/shard_map/ppermute | solution.py:589
  52.8 9.9 %copy-start.16 = (f32[5,64]{1,0:T(8,128)S(1)}, f32[5,64]{1,0:T(8,128)}, u32[]{:S(2)}) copy-start(f32[5,64]{1,0:T(8,128)} %param.21) | copy-start | bytes 3844
  52.8 10.7 %copy-start.13 = (s32[23040]{0:T(1024)S(1)}, s32[23040]{0:T(1024)}, u32[]{:S(2)}) copy-start(s32[23040]{0:T(1024)} %reduce.1) | copy-start | bytes 276484
  52.8 31.5 %all-to-all-start = ((f32[16,192,128]{2,1,0:T(8,128)}), f32[16,192,128]{2,1,0:T(8,128)S(1)}, u32[]{:S(2)}, u32[]{:S(2)}) async-start(f32[16,192,128]{2,1,0:T(8,128)} %bitcast.7), calls=%async_computation | async-start | bytes 3145728 | tf_op jit(solution)/shard_map/all_to_all | solution.py:659
  84.3 14.9 %copy-start.15 = (f32[7,5]{1,0:T(8,128)S(1)}, f32[7,5]{1,0:T(8,128)}, u32[]{:S(2)}) copy-start(f32[7,5]{1,0:T(8,128)} %param.23) | copy-start | bytes 424
  91.2 8.0 %copy-start.17 = (f32[7]{0:T(128)S(1)}, f32[7]{0:T(128)}, u32[]{:S(2)}) copy-start(f32[7]{0:T(128)} %param.25) | copy-start | bytes 88
  91.3 27.2 %copy-start.7 = (bf16[512,512]{1,0:T(8,128)(2,1)S(1)}, bf16[512,512]{1,0:T(8,128)(2,1)}, u32[]{:S(2)}) copy-start(bf16[512,512]{1,0:T(8,128)(2,1)} %constant.127.clone.fwd_high) | copy-start | bytes 1572868
  91.3 27.1 %copy-start.8 = (bf16[512,512]{1,0:T(8,128)(2,1)S(1)}, bf16[512,512]{1,0:T(8,128)(2,1)}, u32[]{:S(2)}) copy-start(bf16[512,512]{1,0:T(8,128)(2,1)} %constant.128.clone.fwd_low) | copy-start | bytes 1572868
  91.3 27.1 %copy-start.9 = (bf16[512,512]{1,0:T(8,128)(2,1)S(1)}, bf16[512,512]{1,0:T(8,128)(2,1)}, u32[]{:S(2)}) copy-start(bf16[512,512]{1,0:T(8,128)(2,1)} %constant.129.clone.inv_high) | copy-start | bytes 1572868
  91.3 27.1 %copy-start.10 = (bf16[512,512]{1,0:T(8,128)(2,1)S(1)}, bf16[512,512]{1,0:T(8,128)(2,1)}, u32[]{:S(2)}) copy-start(bf16[512,512]{1,0:T(8,128)(2,1)} %constant.130.clone.inv_low) | copy-start | bytes 1572868
  91.3 27.1 %copy-start.11 = (f32[1,512]{1,0:T(1,128)S(1)}, f32[1,512]{1,0:T(1,128)}, u32[]{:S(2)}) copy-start(f32[1,512]{1,0:T(1,128)} %constant.144.waves_ref) | copy-start | bytes 6148
  91.3 27.1 %all-to-all-start.1 = ((f32[128,16,128]{2,1,0:T(8,128)}), f32[128,16,128]{2,1,0:T(8,128)S(1)}, u32[]{:S(2)}, u32[]{:S(2)}) async-start(f32[128,16,128]{2,1,0:T(8,128)} %bitcast.9), calls=%async_computation.1 | async-start | bytes 2097152 | tf_op jit(solution)/shard_map/all_to_all | solution.py:664
  (7 other events, 17.2 us)

commit v7 on v5

--- a/solution.py
+++ b/solution.py
@@ -8,20 +8,19 @@
 from jax.experimental.pallas import tpu as pltpu
 from jax.sharding import PartitionSpec as P
 
+
 SPECIES = 5
 IONS = 7
 NLON = 2880
 NLEV = 64
 PAIRS = 32
 BAND_LATS = 8
-TSTEPS = 2
 SWEEPS = 8
 SECTIONS = 20
 TUBE_COLS = 4
 PEERS = 128
 PEER_SLOTS = 3
 COL_CAP = 1080
-TUBE_CAP = 270
 BAND_COLS = BAND_LATS * NLON
 LINE_PTS = 512
 
@@ -36,8 +35,6 @@
 CHUNKS = 3
 MSG_ROWS = 64
 PEER_ROWS = CHUNKS * MSG_ROWS
-CHUNK_BLOCKS = 3
-CHUNK_SLOTS = GROUPS * MSG_ROWS
 SLOT_BLOCKS = 9
 SLOTS_PAD = SLOT_BLOCKS * LANES
 ORDER_PAD = BAND_COLS + 2 * LANES
@@ -56,14 +53,13 @@
     return pltpu.VMEM(shape, dtype)
 
 
-def call(kernel, out_shape, in_specs, out_specs, scratch=(), name=None, flops=0, vmem=16):
+def call(kernel, out_shape, in_specs, out_specs, scratch=(), flops=0, vmem=16):
     run = pl.pallas_call(
         kernel,
         out_shape=out_shape,
         in_specs=in_specs,
         out_specs=out_specs,
         scratch_shapes=list(scratch),
-        name=name,
         cost_estimate=pl.CostEstimate(flops=flops, bytes_accessed=1 << 20, transcendentals=0),
         compiler_params=pltpu.CompilerParams(vmem_limit_bytes=vmem * 1024 * 1024),
     )
@@ -135,7 +131,6 @@
         [SMEM] + [HBM] * 4,
         (VMEM,) * 8,
         [pltpu.SemaphoreType.DMA((SPECIES + 3,))],
-        name="edges",
         flops=1_000_000,
     )(side, density, wind_lon, wind_lat, wind_lev)
 
@@ -144,8 +139,7 @@
     inner_ref, outer_ref, row_ref, far_row_ref = refs[:4]
     inner_wind, outer_wind, row_wind, far_row_wind = refs[4:8]
     outs = refs[8:]
-    core, odd = side_ref[0], side_ref[1] == 1
-    south_core = core == 0
+    odd = side_ref[1] == 1
 
     def split(c):
         return jnp.maximum(c, 0.0), jnp.minimum(c, 0.0)
@@ -156,47 +150,44 @@
     def shift_east(x):
         return jnp.concatenate([x[:, 1:], x[:, :1]], axis=1)
 
-    for j in range(2):
-
-        @pl.loop(0, SPECIES)
-        def _(s):
-            x = n_ref[s, j]
-            flux = upwind(*split(wlon_ref[j]), shift_west(x), x)
-            total = x + (flux - shift_east(flux))
-            south = jnp.where(odd, row_ref[s, j], far_row_ref[s, j])
-            north = jnp.where(odd, far_row_ref[s, j], row_ref[s, j])
-            north_wind = jnp.where(odd, far_row_wind[SPECIES, j], row_wind[SPECIES, j])
-            southern = jnp.concatenate([south, x[: BAND_LATS - 1]], axis=0)
-            flux = upwind(*split(wlat_ref[j]), southern, x)
-            edge = upwind(*split(north_wind), x[BAND_LATS - 1 :], north)
-            total = total + (flux - jnp.concatenate([flux[1:], edge], axis=0))
-            if j == 0:
-                beneath = jnp.where(south_core, outer_ref[s], inner_ref[s])
-                overhead, over_wind = n_ref[s, 1], wlev_ref[1]
-            else:
-                beneath = n_ref[s, 0]
-                overhead = jnp.where(south_core, inner_ref[s], outer_ref[s])
-                over_wind = jnp.where(south_core, inner_wind[SPECIES], outer_wind[SPECIES])
-            flux = upwind(*split(wlev_ref[j]), beneath, x)
-            total = total + (flux - upwind(*split(over_wind), x, overhead))
-            if last:
-                row = pl.multiple_of((j * SPECIES + s) * BAND_LATS, BAND_LATS)
-                for blk in range(LON_BLOCKS):
-                    wide = min(LANES, NLON - blk * LANES)
-                    outs[0][blk, pl.ds(row, BAND_LATS), :wide] = total[:, blk * LANES : blk * LANES + wide]
-            else:
+    def advance(core):
+        below_ref, above_ref, above_wind = (
+            (outer_ref, inner_ref, inner_wind) if core == 0 else (inner_ref, outer_ref, outer_wind)
+        )
+        for j in range(2):
+
+            @pl.loop(0, SPECIES)
+            def _(s):
+                x = n_ref[s, j]
+                flux = upwind(*split(wlon_ref[j]), shift_west(x), x)
+                total = x + (flux - shift_east(flux))
+                south = jnp.where(odd, row_ref[s, j], far_row_ref[s, j])
+                north = jnp.where(odd, far_row_ref[s, j], row_ref[s, j])
+                north_wind = jnp.where(odd, far_row_wind[SPECIES, j], row_wind[SPECIES, j])
+                southern = jnp.concatenate([south, x[: BAND_LATS - 1]], axis=0)
+                flux = upwind(*split(wlat_ref[j]), southern, x)
+                edge = upwind(*split(north_wind), x[BAND_LATS - 1 :], north)
+                total = total + (flux - jnp.concatenate([flux[1:], edge], axis=0))
+                if j == 0:
+                    beneath, overhead, over_wind = below_ref[s], n_ref[s, 1], wlev_ref[1]
+                else:
+                    beneath, overhead, over_wind = n_ref[s, 0], above_ref[s], above_wind[SPECIES]
+                flux = upwind(*split(wlev_ref[j]), beneath, x)
+                total = total + (flux - upwind(*split(over_wind), x, overhead))
+                if last:
+                    row = pl.multiple_of((j * SPECIES + s) * BAND_LATS, BAND_LATS)
+                    for blk in range(LON_BLOCKS):
+                        wide = min(LANES, NLON - blk * LANES)
+                        outs[0][blk, pl.ds(row, BAND_LATS), :wide] = total[:, blk * LANES : blk * LANES + wide]
+                    return
                 outs[0][s, j] = total
-
-                @pl.when(core == 1 - j)
-                def _():
-                    outs[1][s] = total
-
-                @pl.when(core == j)
-                def _():
-                    outs[2][s] = total
-
-                outs[3][s, j] = jnp.where(odd, total[:1], total[BAND_LATS - 1 :])
-                outs[4][s, j] = jnp.where(odd, total[BAND_LATS - 1 :], total[:1])
+                outs[2 if j == core else 1][s] = total
+                first, final = total[:1], total[BAND_LATS - 1 :]
+                outs[3][s, j] = jnp.where(odd, first, final)
+                outs[4][s, j] = jnp.where(odd, final, first)
+
+    for core in range(2):
+        pl.when(side_ref[0] == core)(functools.partial(advance, core))
 
 
 def transport_step(side, density, winds, halo, wind_halo, last):
@@ -215,7 +206,6 @@
         out_shape,
         [SMEM] + [HELD] * 12,
         (VMEM,) * len(out_shape),
-        name="transport",
         flops=4_000_000,
     )(side, density, *winds, *halo, *wind_halo)
 
@@ -290,7 +280,6 @@
             pltpu.VMEM((BAND_LATS * 6 * LANES, LANES), f32),
             pltpu.VMEM((SLOTS_PAD, LANES), f32),
         ],
-        name="prepare",
         flops=20_000_000,
     )(units, owners, rows, sel, weights, column)
 
@@ -363,7 +352,6 @@
             pltpu.VMEM((16 * PEER_ROWS, LANES), f32),
             pltpu.SemaphoreType.DMA((16,)),
         ],
-        name="pack",
         flops=30_000_000,
         vmem=32,
     )(core, starts, units, order, mine, other)
@@ -466,7 +454,6 @@
             pltpu.VMEM((SPECIES, NLEV, COL_CAP), f32),
             pltpu.SemaphoreType.DMA((SPECIES,)),
         ],
-        name="solve",
         flops=40_000_000,
     )(core, units, table, got, coefs, weights)
 
@@ -556,7 +543,6 @@
             pltpu.VMEM((IONS, tubes, LINE_PTS), f32),
             pltpu.SemaphoreType.DMA((IONS,)),
         ],
-        name="lines",
         flops=2_000_000_000,
     )(items, ion_yield.reshape(-1), jnp.concatenate([ion_spread, ion_loss]), waves, *parts(basis.T), *parts(basis))
     return jnp.swapaxes(by_ion, 1, 2)
@@ -572,7 +558,8 @@
     outer = swap(outer, "lev", 1)
     row = swap(row, "band", 0)
     far_row = swap(far_row, "band", 1)
-    return swap(inner, "lev", 0), outer, row, far_row
+    inner = swap(inner, "lev", 0)
+    return inner, outer, row, far_row
 
 
 def on_device(
@@ -658,6 +645,7 @@
         P(),
         P(),
     )
+
     return jax.shard_map(
         on_device,
         mesh=mesh,

time: 126 us -> 126 us (level)
  no operation moved by 1% of the time
where the time goes in v7:
time: 126 us
  Pallas kernels  44.2 us (35%)
  waiting for transfers between devices  43.2 us (34%)
  starting transfers between devices  31.9 us (25%)
  local copies, waits for them, and re-layouts  3.98 us (3%)
  between operations  1.62 us (1%)
    pallas_call x7, Pallas kernels, placed(): return run(*(place(x, spec) for x, spec in zip(args, in_specs)))  44.2 us
    all_to_all x1, waiting for transfers between devices, on_device(): lax.all_to_all(items.reshape(PEERS, ITEM_ROWS, LANES), ('band', 'lev'), 0...  19.1 us
    ppermute x9, starting transfers between devices, swap(): lax.ppermute(x, axis, [(i, i + 1) for i in lows] + [(i + 1, i) for i in l...  14.4 us
    all_to_all x1, waiting for transfers between devices, on_device(): lax.all_to_all(outgoing.reshape(16, PEER_ROWS, LANES), 'lev', 0, 0, axis_...  14.2 us
    all_to_all x1, starting transfers between devices, on_device(): lax.all_to_all(outgoing.reshape(16, PEER_ROWS, LANES), 'lev', 0, 0, axis_...  10.8 us
    ppermute x9, waiting for transfers between devices, swap(): lax.ppermute(x, axis, [(i, i + 1) for i in lows] + [(i + 1, i) for i in l...  9.91 us
    all_to_all x1, starting transfers between devices, on_device(): lax.all_to_all(items.reshape(PEERS, ITEM_ROWS, LANES), ('band', 'lev'), 0...  6.61 us
  transfers between devices with their start and end apart: 11, of which 7 were waited for; matrix products, arithmetic and copies ran while one was open for 2% of the time, Pallas kernels for 6%

profile of v7, /device:TPU:1, one launch (start us, length us, event | category | flops | bytes accessed | tf_op | source)
XLA Modules:
  0.0 125.8 jit_solution(7169664691362229830)
XLA Ops:
  0.7 2.1 %shard_map.177 = (f32[5,2,8,2880]{3,2,1,0:T(8,128)S(1)}, f32[2,8,2880]{2,1,0:T(8,128)S(1)}, f32[2,8,2880]{2,1,0:T(8,128)S(1)}, f32[2,8,2880]{2,1,0:T(8,128)S(1)}...) custom-call(s32[2]{0:T(128)S(1)} %pad_add_fusion.side_ref, ...), custom_call_target="tpu_custom_call" | custom-call | flops 1000000 | bytes 1048576 | tf_op jit(solution)/shard_map/pallas_call | solution.py:72
  2.9 1.5 %collective-permute-start = (f32[6,8,2880]{2,1,0:T(8,128)S(1)}, f32[6,8,2880]{2,1,0:T(8,128)S(1)}, u32[]{:S(2)}, u32[]{:S(2)}) collective-permute-start(f32[6,8,2880]{2,1,0:T(8,128)S(1)} %get-tuple-element.25), channel_id=1, source_target_pairs={{0,1},{2,3},{4,5},{6,7},{8,9},{10,11},{12,13},{14,15},{16,17},{18,... | collective-permute-start | bytes 1658888 | tf_op jit(solution)/shard_map/ppermute | solution.py:554
  4.3 3.1 %collective-permute-start.1 = (f32[6,8,2880]{2,1,0:T(8,128)S(1)}, f32[6,8,2880]{2,1,0:T(8,128)S(1)}, u32[]{:S(2)}, u32[]{:S(2)}) collective-permute-start(f32[6,8,2880]{2,1,0:T(8,128)S(1)} %get-tuple-element.26), channel_id=1, source_target_pairs={{1,2},{3,4},{5,6},{7,8},{9,10},{11,12},{13,14},{15,16},{17,18},{19... | collective-permute-start | bytes 1658888 | tf_op jit(solution)/shard_map/ppermute | solution.py:554
  7.5 1.7 %collective-permute-start.2 = (f32[6,2,1,2880]{3,2,1,0:T(1,128)S(1)}, f32[6,2,1,2880]{3,2,1,0:T(1,128)S(1)}, u32[]{:S(2)}, u32[]{:S(2)}) collective-permute-start(f32[6,2,1,2880]{3,2,1,0:T(1,128)S(1)} %get-tuple-element.27), channel_id=1, source_target_pairs={{0,32},{64,96},{32,0},{96,64},{1,33},{65,97},{33,1},{97,65},{2,34}... | collective-permute-start | bytes 414728 | tf_op jit(solution)/shard_map/ppermute | solution.py:554
  9.2 0.7 collective-permute-start.3
  9.9 1.8 %collective-permute-done.2.refs_2_.refs_6_ = f32[6,2,1,2880]{3,2,1,0:T(1,128)S(1)} collective-permute-done((f32[6,2,1,2880]{3,2,1,0:T(1,128)S(1)}, f32[6,2,1,2880]{3,2,1,0:T(1,128)S(1)}, u32[]{:S(2)}, u32[]{:S(2)}) %collective-permute-start.2) | collective-permute-done | bytes 138272 | tf_op jit(solution)/shard_map/ppermute | solution.py:554
  11.7 3.6 %collective-permute-done.1.refs_1_.refs_5_ = f32[6,8,2880]{2,1,0:T(8,128)S(1)} collective-permute-done((f32[6,8,2880]{2,1,0:T(8,128)S(1)}, f32[6,8,2880]{2,1,0:T(8,128)S(1)}, u32[]{:S(2)}, u32[]{:S(2)}) %collective-permute-start.1) | collective-permute-done | bytes 552992 | tf_op jit(solution)/shard_map/ppermute | solution.py:554
  15.3 2.6 %shard_map.178 = (f32[5,2,8,2880]{3,2,1,0:T(8,128)S(1)}, f32[5,8,2880]{2,1,0:T(8,128)S(1)}, f32[5,8,2880]{2,1,0:T(8,128)S(1)}, f32[5,2,1,2880]{3,2,1,0:T(1,128)S(1)}, f32[5,2,1,2880]{3,2,1,0:T(1,128)S(1)}) custom-call(s32[2]{0:T(128)S(1)} %pad_add_fusion.side_ref, f32[5,2,8,2880]{3,2,1,0:T(8,128)S(1)} %get-tuple-element.21.n_ref, ...), custom_call_target="tpu_custom_call" | custom-call | flops 4000000 | bytes 1048576 | tf_op jit(solution)/shard_map/pallas_call | solution.py:72
  18.0 3.6 %collective-permute-start.5 = (f32[5,8,2880]{2,1,0:T(8,128)S(1)}, f32[5,8,2880]{2,1,0:T(8,128)S(1)}, u32[]{:S(2)}, u32[]{:S(2)}) collective-permute-start(f32[5,8,2880]{2,1,0:T(8,128)S(1)} %get-tuple-element.31), channel_id=1, source_target_pairs={{1,2},{3,4},{5,6},{7,8},{9,10},{11,12},{13,14},{15,16},{17,18},{19... | collective-permute-start | bytes 1382408 | tf_op jit(solution)/shard_map/ppermute | solution.py:554
  21.6 3.0 %collective-permute-start.6 = (f32[5,2,1,2880]{3,2,1,0:T(1,128)S(1)}, f32[5,2,1,2880]{3,2,1,0:T(1,128)S(1)}, u32[]{:S(2)}, u32[]{:S(2)}) collective-permute-start(f32[5,2,1,2880]{3,2,1,0:T(1,128)S(1)} %get-tuple-element.32), channel_id=1, source_target_pairs={{0,32},{64,96},{32,0},{96,64},{1,33},{65,97},{33,1},{97,65},{2,34}... | collective-permute-start | bytes 345608 | tf_op jit(solution)/shard_map/ppermute | solution.py:554
  24.6 0.7 collective-permute-start.7
  25.3 1.6 %collective-permute-done.6.refs_2_ = f32[5,2,1,2880]{3,2,1,0:T(1,128)S(1)} collective-permute-done((f32[5,2,1,2880]{3,2,1,0:T(1,128)S(1)}, f32[5,2,1,2880]{3,2,1,0:T(1,128)S(1)}, u32[]{:S(2)}, u32[]{:S(2)}) %collective-permute-start.6) | collective-permute-done | bytes 115232 | tf_op jit(solution)/shard_map/ppermute | solution.py:554
  26.9 1.1 collective-permute-done.5.refs_1_
  27.9 2.4 %shard_map.179.mine_ref = f32[23,80,128]{2,1,0:T(8,128)S(1)} custom-call(s32[2]{0:T(128)S(1)} %pad_add_fusion.side_ref, f32[5,2,8,2880]{3,2,1,0:T(8,128)S(1)} %get-tuple-element.29.n_ref, f32[2,8,2880]{2,1,0:T(8,128)S(1)} %get-tuple-element.22.wlon_ref, f32[2,8,2880]{2,1,0:T(8,128)S(1)} %get-tuple-element.23.wlat_ref, ...), custom_call_target="tpu_custom_call" | custom-call | flops 4000000 | bytes 1048576 | tf_op jit(solution)/shard_map/pallas_call | solution.py:72
  31.0 1.9 %collective-permute-done.8.other_ref = f32[23,80,128]{2,1,0:T(8,128)S(1)} collective-permute-done((f32[23,80,128]{2,1,0:T(8,128)S(1)}, f32[23,80,128]{2,1,0:T(8,128)S(1)}, u32[]{:S(2)}, u32[]{:S(2)}) %collective-permute-start.8) | collective-permute-done | bytes 942112 | tf_op jit(solution)/shard_map/ppermute | solution.py:554
  32.9 16.2 %shard_map.180 = f32[3072,128]{1,0:T(8,128)} custom-call(s32[1]{0:T(128)} %bitcast.core_ref, s32[32]{0:T(128)S(1)} %sub.16.starts_ref, s32[32]{0:T(128)S(1)} %copy-done.2, s32[23296]{0:T(1024)S(1)} %pad.11.order_ref, f32[23,80,128]{2,1,0:T(8,128)S(1)} %shard_map.179.mine_ref, f32[23,80,128]{2,1,0:T(8,128)S(1)} %collective-permute-done.8.other_ref), custom_call_target="tpu_custom_call" | custom-call | flops 30000000 | bytes 1048576 | tf_op jit(solution)/shard_map/pallas_call | solution.py:72
  49.1 10.8 %all-to-all-start = ((f32[16,192,128]{2,1,0:T(8,128)}), f32[16,192,128]{2,1,0:T(8,128)S(1)}, u32[]{:S(2)}, u32[]{:S(2)}) async-start(f32[16,192,128]{2,1,0:T(8,128)} %bitcast.7), calls=%async_computation | async-start | bytes 3145728 | tf_op jit(solution)/shard_map/all_to_all | solution.py:622
  62.8 1.8 %copy-done.1 = f32[32,8,2880]{2,1,0:T(8,128)S(1)} copy-done((f32[32,8,2880]{2,1,0:T(8,128)S(1)}, f32[32,8,2880]{2,1,0:T(8,128)}, u32[]{:S(2)}) %copy-start.1) | copy-done | bytes 2949144
  64.6 7.8 %shard_map.176 = (s32[384]{0:T(512)S(1)}, f32[9,32,128]{2,1,0:T(8,128)S(1)}, f32[960,128]{1,0:T(8,128)S(1)}) custom-call(s32[1]{0:T(128)} %dynamic_slice.12.units_ref, s32[270]{0:T(512)S(1)} %dynamic-slice_reduce_fusion.owner_ref, s32[1152]{0:T(1024)S(1)} %get-tuple-element.39.rows_ref, s32[9,128]{1,0:T(8,128)S(1)} %get-tuple-element.38.sel_ref, ...), custom_call_target="tpu_custom_call" | custom-call | flops 20000000 | bytes 1048576 | tf_op jit(solution)/shard_map/pallas_call | solution.py:72
  72.4 14.2 %all-to-all-done = f32[16,192,128]{2,1,0:T(8,128)S(1)} async-done(((f32[16,192,128]{2,1,0:T(8,128)}), f32[16,192,128]{2,1,0:T(8,128)S(1)}, u32[]{:S(2)}, u32[]{:S(2)}) %all-to-all-start) | async-done | bytes 1572896 | tf_op jit(solution)/shard_map/all_to_all | solution.py:622
  86.7 7.0 %shard_map.181 = (f32[1,1,5,64,1080]{4,3,2,1,0:T(8,128)}, f32[2048,128]{1,0:T(8,128)}) custom-call(s32[1]{0:T(128)} %bitcast.core_ref, s32[1]{0:T(128)} %dynamic_slice.12.units_ref, s32[384]{0:T(512)S(1)} %get-tuple-element.20.table_ref, f32[3072,128]{1,0:T(8,128)S(1)} %bitcast.16, f32[960,128]{1,0:T(8,128)S(1)} %get-tuple-element.34.coef_ref, ...), custom_call_target="tpu_custom_call" | custom-call | flops 40000000 | bytes 1048576 | tf_op jit(solution)/shard_map/pallas_call | solution.py:72
  93.8 6.6 %all-to-all-start.1 = ((f32[128,16,128]{2,1,0:T(8,128)}), f32[128,16,128]{2,1,0:T(8,128)S(1)}, u32[]{:S(2)}, u32[]{:S(2)}) async-start(f32[128,16,128]{2,1,0:T(8,128)} %bitcast.9), calls=%async_computation.1 | async-start | bytes 2097152 | tf_op jit(solution)/shard_map/all_to_all | solution.py:627
  100.5 19.1 %all-to-all-done.1 = f32[128,16,128]{2,1,0:T(8,128)S(1)} async-done(((f32[128,16,128]{2,1,0:T(8,128)}), f32[128,16,128]{2,1,0:T(8,128)S(1)}, u32[]{:S(2)}, u32[]{:S(2)}) %all-to-all-start.1) | async-done | bytes 1048608 | tf_op jit(solution)/shard_map/all_to_all | solution.py:627
  119.6 6.1 %shard_map.182 = f32[1,7,96,512]{3,2,1,0:T(8,128)} custom-call(f32[2048,128]{1,0:T(8,128)S(1)} %bitcast.18, f32[35]{0:T(128)S(1)} %reshape.76.yield_ref, f32[14]{0:T(128)S(1)} %pad_maximum_fusion.rates_ref, f32[1,512]{1,0:T(1,128)S(1)} %copy-done.7, bf16[512,512]{1,0:T(8,128)(2,1)S(1)} %copy-done.3, bf16[512,512]{1,0:T(8,128)(2,1)S(1)} %copy-done.4, ...), custom_call_target="tpu_custom_call" | custom-call | flops 2000000000 | bytes 1048576 | tf_op jit(solution)/shard_map/pallas_call | solution.py:72
  (55 shorter events, 3.2 us)
Async XLA Ops:
  0.6 62.0 %copy-start = (s32[32,270,1]{1,2,0:T(1,128)S(1)}, s32[32,270,1]{1,2,0:T(1,128)}, u32[]{:S(2)}) copy-start(s32[32,270,1]{1,2,0:T(1,128)} %param.28) | copy-start | bytes 103684
  2.9 8.8 %collective-permute-start = (f32[6,8,2880]{2,1,0:T(8,128)S(1)}, f32[6,8,2880]{2,1,0:T(8,128)S(1)}, u32[]{:S(2)}, u32[]{:S(2)}) collective-permute-start(f32[6,8,2880]{2,1,0:T(8,128)S(1)} %get-tuple-element.25), channel_id=1, source_target_pairs={{0,1},{2,3},{4,5},{6,7},{8,9},{10,11},{12,13},{14,15},{16,17},{18,... | collective-permute-start | bytes 1658888 | tf_op jit(solution)/shard_map/ppermute | solution.py:554
  4.3 10.9 %collective-permute-start.1 = (f32[6,8,2880]{2,1,0:T(8,128)S(1)}, f32[6,8,2880]{2,1,0:T(8,128)S(1)}, u32[]{:S(2)}, u32[]{:S(2)}) collective-permute-start(f32[6,8,2880]{2,1,0:T(8,128)S(1)} %get-tuple-element.26), channel_id=1, source_target_pairs={{1,2},{3,4},{5,6},{7,8},{9,10},{11,12},{13,14},{15,16},{17,18},{19... | collective-permute-start | bytes 1658888 | tf_op jit(solution)/shard_map/ppermute | solution.py:554
  7.5 4.2 %collective-permute-start.2 = (f32[6,2,1,2880]{3,2,1,0:T(1,128)S(1)}, f32[6,2,1,2880]{3,2,1,0:T(1,128)S(1)}, u32[]{:S(2)}, u32[]{:S(2)}) collective-permute-start(f32[6,2,1,2880]{3,2,1,0:T(1,128)S(1)} %get-tuple-element.27), channel_id=1, source_target_pairs={{0,32},{64,96},{32,0},{96,64},{1,33},{65,97},{33,1},{97,65},{2,34}... | collective-permute-start | bytes 414728 | tf_op jit(solution)/shard_map/ppermute | solution.py:554
  9.2 2.5 %collective-permute-start.3 = (f32[6,2,1,2880]{3,2,1,0:T(1,128)S(1)}, f32[6,2,1,2880]{3,2,1,0:T(1,128)S(1)}, u32[]{:S(2)}, u32[]{:S(2)}) collective-permute-start(f32[6,2,1,2880]{3,2,1,0:T(1,128)S(1)} %get-tuple-element.28), channel_id=1, source_target_pairs={{32,64},{64,32},{33,65},{65,33},{34,66},{66,34},{35,67},{67,35},{3... | collective-permute-start | bytes 414728 | tf_op jit(solution)/shard_map/ppermute | solution.py:554
  17.9 8.9 %collective-permute-start.4 = (f32[5,8,2880]{2,1,0:T(8,128)S(1)}, f32[5,8,2880]{2,1,0:T(8,128)S(1)}, u32[]{:S(2)}, u32[]{:S(2)}) collective-permute-start(f32[5,8,2880]{2,1,0:T(8,128)S(1)} %get-tuple-element.30), channel_id=1, source_target_pairs={{0,1},{2,3},{4,5},{6,7},{8,9},{10,11},{12,13},{14,15},{16,17},{18,... | collective-permute-start | bytes 1382408 | tf_op jit(solution)/shard_map/ppermute | solution.py:554
  18.0 9.9 %collective-permute-start.5 = (f32[5,8,2880]{2,1,0:T(8,128)S(1)}, f32[5,8,2880]{2,1,0:T(8,128)S(1)}, u32[]{:S(2)}, u32[]{:S(2)}) collective-permute-start(f32[5,8,2880]{2,1,0:T(8,128)S(1)} %get-tuple-element.31), channel_id=1, source_target_pairs={{1,2},{3,4},{5,6},{7,8},{9,10},{11,12},{13,14},{15,16},{17,18},{19... | collective-permute-start | bytes 1382408 | tf_op jit(solution)/shard_map/ppermute | solution.py:554
  21.6 5.2 %collective-permute-start.6 = (f32[5,2,1,2880]{3,2,1,0:T(1,128)S(1)}, f32[5,2,1,2880]{3,2,1,0:T(1,128)S(1)}, u32[]{:S(2)}, u32[]{:S(2)}) collective-permute-start(f32[5,2,1,2880]{3,2,1,0:T(1,128)S(1)} %get-tuple-element.32), channel_id=1, source_target_pairs={{0,32},{64,96},{32,0},{96,64},{1,33},{65,97},{33,1},{97,65},{2,34}... | collective-permute-start | bytes 345608 | tf_op jit(solution)/shard_map/ppermute | solution.py:554
  24.6 2.2 %collective-permute-start.7 = (f32[5,2,1,2880]{3,2,1,0:T(1,128)S(1)}, f32[5,2,1,2880]{3,2,1,0:T(1,128)S(1)}, u32[]{:S(2)}, u32[]{:S(2)}) collective-permute-start(f32[5,2,1,2880]{3,2,1,0:T(1,128)S(1)} %get-tuple-element.33), channel_id=1, source_target_pairs={{32,64},{64,32},{33,65},{65,33},{34,66},{66,34},{35,67},{67,35},{3... | collective-permute-start | bytes 345608 | tf_op jit(solution)/shard_map/ppermute | solution.py:554
  27.9 2.5 %copy-start.8 = (s32[1,23040]{1,0:T(1,128)S(1)}, s32[1,23040]{1,0:T(1,128)}, u32[]{:S(2)}) copy-start(s32[1,23040]{1,0:T(1,128)} %param.26) | copy-start | bytes 276484
  27.9 2.8 %copy-start.2 = (s32[32]{0:T(128)S(1)}, s32[32]{0:T(128)}, u32[]{:S(2)}) copy-start(s32[32]{0:T(128)} %units_ref.1) | copy-start | bytes 388
  30.3 2.6 %collective-permute-start.8 = (f32[23,80,128]{2,1,0:T(8,128)S(1)}, f32[23,80,128]{2,1,0:T(8,128)S(1)}, u32[]{:S(2)}, u32[]{:S(2)}) collective-permute-start(f32[23,80,128]{2,1,0:T(8,128)S(1)} %shard_map.179.mine_ref), channel_id=1, source_target_pairs={{0,1},{2,3},{4,5},{6,7},{8,9},{10,11},{12,13},{14,15},{16,17},{18,... | collective-permute-start | bytes 2826248 | tf_op jit(solution)/shard_map/ppermute | solution.py:554
  49.1 12.7 %copy-start.10 = (f32[5,64]{1,0:T(8,128)S(1)}, f32[5,64]{1,0:T(8,128)}, u32[]{:S(2)}) copy-start(f32[5,64]{1,0:T(8,128)} %param.21) | copy-start | bytes 3844
  49.1 37.5 %all-to-all-start = ((f32[16,192,128]{2,1,0:T(8,128)}), f32[16,192,128]{2,1,0:T(8,128)S(1)}, u32[]{:S(2)}, u32[]{:S(2)}) async-start(f32[16,192,128]{2,1,0:T(8,128)} %bitcast.7), calls=%async_computation | async-start | bytes 3145728 | tf_op jit(solution)/shard_map/all_to_all | solution.py:622
  62.8 1.9 %copy-start.1 = (f32[32,8,2880]{2,1,0:T(8,128)S(1)}, f32[32,8,2880]{2,1,0:T(8,128)}, u32[]{:S(2)}) copy-start(f32[32,8,2880]{2,1,0:T(8,128)} %param.22) | copy-start | bytes 8847364
  86.7 13.7 %copy-start.9 = (f32[7,5]{1,0:T(8,128)S(1)}, f32[7,5]{1,0:T(8,128)}, u32[]{:S(2)}) copy-start(f32[7,5]{1,0:T(8,128)} %param.23) | copy-start | bytes 424
  93.7 6.8 %copy-start.11 = (f32[7]{0:T(128)S(1)}, f32[7]{0:T(128)}, u32[]{:S(2)}) copy-start(f32[7]{0:T(128)} %param.25) | copy-start | bytes 88
  93.7 6.8 %copy-start.12 = (f32[7]{0:T(128)S(1)}, f32[7]{0:T(128)}, u32[]{:S(2)}) copy-start(f32[7]{0:T(128)} %param.24) | copy-start | bytes 88
  93.7 25.9 %copy-start.3 = (bf16[512,512]{1,0:T(8,128)(2,1)S(1)}, bf16[512,512]{1,0:T(8,128)(2,1)}, u32[]{:S(2)}) copy-start(bf16[512,512]{1,0:T(8,128)(2,1)} %constant.127.clone.fwd_high) | copy-start | bytes 1572868
  93.7 25.9 %copy-start.4 = (bf16[512,512]{1,0:T(8,128)(2,1)S(1)}, bf16[512,512]{1,0:T(8,128)(2,1)}, u32[]{:S(2)}) copy-start(bf16[512,512]{1,0:T(8,128)(2,1)} %constant.128.clone.fwd_low) | copy-start | bytes 1572868
  93.7 25.9 %copy-start.5 = (bf16[512,512]{1,0:T(8,128)(2,1)S(1)}, bf16[512,512]{1,0:T(8,128)(2,1)}, u32[]{:S(2)}) copy-start(bf16[512,512]{1,0:T(8,128)(2,1)} %constant.129.clone.inv_high) | copy-start | bytes 1572868
  93.7 25.9 %copy-start.6 = (bf16[512,512]{1,0:T(8,128)(2,1)S(1)}, bf16[512,512]{1,0:T(8,128)(2,1)}, u32[]{:S(2)}) copy-start(bf16[512,512]{1,0:T(8,128)(2,1)} %constant.130.clone.inv_low) | copy-start | bytes 1572868
  93.7 25.9 %copy-start.7 = (f32[1,512]{1,0:T(1,128)S(1)}, f32[1,512]{1,0:T(1,128)}, u32[]{:S(2)}) copy-start(f32[1,512]{1,0:T(1,128)} %constant.144.waves_ref) | copy-start | bytes 6148
  93.8 25.8 %all-to-all-start.1 = ((f32[128,16,128]{2,1,0:T(8,128)}), f32[128,16,128]{2,1,0:T(8,128)S(1)}, u32[]{:S(2)}, u32[]{:S(2)}) async-start(f32[128,16,128]{2,1,0:T(8,128)} %bitcast.9), calls=%async_computation.1 | async-start | bytes 2097152 | tf_op jit(solution)/shard_map/all_to_all | solution.py:627

commit v8 on v7

--- a/solution.py
+++ b/solution.py
@@ -37,7 +37,7 @@
 PEER_ROWS = CHUNKS * MSG_ROWS
 SLOT_BLOCKS = 9
 SLOTS_PAD = SLOT_BLOCKS * LANES
-ORDER_PAD = BAND_COLS + 2 * LANES
+ORDER_PAD = BAND_COLS + 3 * LANES
 UNROLL = 64
 ZERO_TUBE = SLOT_BLOCKS * 32
 ITEM_ROWS = 16
@@ -285,8 +285,14 @@
 
 
 def pack_kernel(
-    core_ref, starts_ref, units_ref, order_ref, mine_ref, other_ref, out_hbm, planes, table_ref, msg_ref, sems
+    core_ref, starts_ref, units_ref, order_hbm, mine_ref, other_ref,
+    out_hbm, order_ref, planes, table_ref, msg_ref, sems, order_sem,
 ):
+    core = core_ref[0]
+
+    fetch = pltpu.make_async_copy(order_hbm, order_ref, order_sem)
+    fetch.start()
+
     @pl.loop(0, LON_BLOCKS)
     def _(blk):
         for side, source in enumerate((mine_ref, other_ref)):
@@ -308,7 +314,6 @@
             start = pl.multiple_of((lat * LON_BLOCKS + blk) * LANES, LANES)
             table_ref[pl.ds(start, LANES), :] = jnp.concatenate(parts, axis=0).T
 
-    core = core_ref[0]
     lane = lax.broadcasted_iota(jnp.int32, (1, LANES), 1)
     group_of = lax.div(lax.rem(lane, 32), SPECIES)
 
@@ -316,23 +321,33 @@
         rows = pl.ds(pl.multiple_of(peer * PEER_ROWS, PEER_ROWS), PEER_ROWS)
         return pltpu.make_async_copy(msg_ref.at[rows, :], out_hbm.at[rows, :], sems.at[peer])
 
+    fetch.wait()
+
     @pl.loop(0, 16)
     def _(peer):
         owner = 2 * peer + core
-        live = TUBE_COLS * units_ref[owner]
         first = TUBE_COLS * starts_ref[owner]
-
-        @pl.loop(0, lax.div(live + (MSG_ROWS - 1), MSG_ROWS))
-        def _(piece):
-            chunk = lax.div(piece, GROUPS)
-            mask = group_of == piece - chunk * GROUPS
-            row = pl.multiple_of(peer * PEER_ROWS + chunk * MSG_ROWS, MSG_ROWS)
-            base = first + piece * MSG_ROWS
-            for i in range(MSG_ROWS):
-                place = order_ref.at[pl.ds(i, ORDER_PAD - MSG_ROWS)][base]
+        pieces = lax.div(TUBE_COLS * units_ref[owner] + (MSG_ROWS - 1), MSG_ROWS)
+
+        def copy(start, number):
+            places = []
+            for k in range(number):
+                piece = start + k
+                chunk = lax.div(piece, GROUPS)
+                mask = group_of == piece - chunk * GROUPS
+                places.append((pl.multiple_of(peer * PEER_ROWS + chunk * MSG_ROWS, MSG_ROWS), mask))
+            base = first + start * MSG_ROWS
+            for i in range(number * MSG_ROWS):
+                place = order_ref.at[pl.ds(i, ORDER_PAD - 2 * MSG_ROWS)][base]
+                row, mask = places[i // MSG_ROWS]
                 value = table_ref[pl.ds(place, 1), :]
-                pltpu.store(msg_ref.at[pl.ds(row + i, 1), :], value, mask=mask)
-
+                pltpu.store(msg_ref.at[pl.ds(row + i % MSG_ROWS, 1), :], value, mask=mask)
+
+        @pl.loop(0, lax.div(pieces, 2))
+        def _(pair):
+            copy(2 * pair, 2)
+
+        pl.when(lax.rem(pieces, 2) == 1)(functools.partial(copy, pieces - 1, 1))
         send(peer).start()
 
     @pl.loop(0, 16)
@@ -344,13 +359,15 @@
     return call(
         pack_kernel,
         sds((16 * PEER_ROWS, LANES)),
-        [SMEM, SMEM, SMEM, SMEM, HELD, HELD],
+        [SMEM, SMEM, SMEM, HBM, HELD, HELD],
         HBM,
         [
+            pltpu.SMEM((ORDER_PAD,), jnp.int32),
             pltpu.VMEM((LON_BLOCKS, CHIP_LEVS * PLANES * PITCH, LANES), f32),
             pltpu.VMEM((BAND_LATS * LON_PAD, LANES), f32),
             pltpu.VMEM((16 * PEER_ROWS, LANES), f32),
             pltpu.SemaphoreType.DMA((16,)),
+            pltpu.SemaphoreType.DMA,
         ],
         flops=30_000_000,
         vmem=32,
@@ -481,10 +498,8 @@
                 spec_in[b, pl.ds(s * tubes + r, 32, stride=PEER_SLOTS), :] = rows
 
     half = SPECIES * tubes // 2
-
-    @pl.loop(0, 2)
-    def _(step):
-        row = pl.multiple_of(step * half, half)
+    for step in range(2):
+        row = step * half
         x = jnp.concatenate([spec_in[b, pl.ds(row, half), :] for b in range(4)], axis=1)
         spec[pl.ds(row, half), :] = product(x, fwd_high[...], fwd_low[...])
 
@@ -502,10 +517,12 @@
     def leave(i):
         return pltpu.make_async_copy(done.at[i], out_hbm.at[0, i], sems.at[i])
 
-    @pl.loop(0, IONS)
-    def _(i):
-        done[i] = product(mixed[i], inv_high[...], inv_low[...])
-        leave(i).start()
+    for i in range(0, IONS, 2):
+        j = min(i + 2, IONS)
+        back = product(mixed[i:j].reshape((j - i) * tubes, LINE_PTS), inv_high[...], inv_low[...])
+        done[i:j] = back.reshape(j - i, tubes, LINE_PTS)
+        for k in range(i, j):
+            leave(k).start()
 
     for i in range(IONS):
         leave(i).wait()

time: 126 us -> 123 us (0.976)
  Pallas kernels: 44.2 us -> 40.6 us
    pallas_call x7, Pallas kernels: 44.2 us -> 40.6 us  [placed(): return run(*(place(x, spec) for x, spec in zip(args, in_specs)))]
  transfers between devices with their start and end apart: 11 -> 11, of which waited for: 7 -> 7; matrix products, arithmetic and copies ran while one was open for 2% -> 3% of each run, Pallas kernels for 6% -> 6%
where the time goes in v8:
time: 123 us; the launch traced here: 122 us
  waiting for transfers between devices  42.5 us (35%)
  Pallas kernels  40.6 us (33%)
  starting transfers between devices  31.9 us (26%)
  local copies, waits for them, and re-layouts  4.62 us (4%)
  between operations  1.6 us (1%)
    pallas_call x7, Pallas kernels, placed(): return run(*(place(x, spec) for x, spec in zip(args, in_specs)))  40.6 us
    all_to_all x1, waiting for transfers between devices, on_device(): lax.all_to_all(items.reshape(PEERS, ITEM_ROWS, LANES), ('band', 'lev'), 0...  19.1 us
    ppermute x9, starting transfers between devices, swap(): lax.ppermute(x, axis, [(i, i + 1) for i in lows] + [(i + 1, i) for i in l...  14.4 us
    all_to_all x1, waiting for transfers between devices, on_device(): lax.all_to_all(outgoing.reshape(16, PEER_ROWS, LANES), 'lev', 0, 0, axis_...  14.2 us
    all_to_all x1, starting transfers between devices, on_device(): lax.all_to_all(outgoing.reshape(16, PEER_ROWS, LANES), 'lev', 0, 0, axis_...  10.8 us
    ppermute x9, waiting for transfers between devices, swap(): lax.ppermute(x, axis, [(i, i + 1) for i in lows] + [(i + 1, i) for i in l...  9.29 us
    all_to_all x1, starting transfers between devices, on_device(): lax.all_to_all(items.reshape(PEERS, ITEM_ROWS, LANES), ('band', 'lev'), 0...  6.61 us
  transfers between devices with their start and end apart: 11, of which 7 were waited for; matrix products, arithmetic and copies ran while one was open for 3% of the time, Pallas kernels for 6%

profile of v8, /device:TPU:1, one launch (start us, length us, event | category | flops | bytes accessed | tf_op | source)
XLA Modules:
  0.0 122.1 jit_solution(5530559432645758098)
XLA Ops:
  0.7 2.1 %shard_map.177 = (f32[5,2,8,2880]{3,2,1,0:T(8,128)S(1)}, f32[2,8,2880]{2,1,0:T(8,128)S(1)}, f32[2,8,2880]{2,1,0:T(8,128)S(1)}, f32[2,8,2880]{2,1,0:T(8,128)S(1)}...) custom-call(s32[2]{0:T(128)S(1)} %pad_add_fusion.side_ref, ...), custom_call_target="tpu_custom_call" | custom-call | flops 1000000 | bytes 1048576 | tf_op jit(solution)/shard_map/pallas_call | solution.py:72
  2.9 1.5 %collective-permute-start = (f32[6,8,2880]{2,1,0:T(8,128)S(1)}, f32[6,8,2880]{2,1,0:T(8,128)S(1)}, u32[]{:S(2)}, u32[]{:S(2)}) collective-permute-start(f32[6,8,2880]{2,1,0:T(8,128)S(1)} %get-tuple-element.25), channel_id=1, source_target_pairs={{0,1},{2,3},{4,5},{6,7},{8,9},{10,11},{12,13},{14,15},{16,17},{18,... | collective-permute-start | bytes 1658888 | tf_op jit(solution)/shard_map/ppermute | solution.py:571
  4.3 3.1 %collective-permute-start.1 = (f32[6,8,2880]{2,1,0:T(8,128)S(1)}, f32[6,8,2880]{2,1,0:T(8,128)S(1)}, u32[]{:S(2)}, u32[]{:S(2)}) collective-permute-start(f32[6,8,2880]{2,1,0:T(8,128)S(1)} %get-tuple-element.26), channel_id=1, source_target_pairs={{1,2},{3,4},{5,6},{7,8},{9,10},{11,12},{13,14},{15,16},{17,18},{19... | collective-permute-start | bytes 1658888 | tf_op jit(solution)/shard_map/ppermute | solution.py:571
  7.5 1.7 %collective-permute-start.2 = (f32[6,2,1,2880]{3,2,1,0:T(1,128)S(1)}, f32[6,2,1,2880]{3,2,1,0:T(1,128)S(1)}, u32[]{:S(2)}, u32[]{:S(2)}) collective-permute-start(f32[6,2,1,2880]{3,2,1,0:T(1,128)S(1)} %get-tuple-element.27), channel_id=1, source_target_pairs={{0,32},{64,96},{32,0},{96,64},{1,33},{65,97},{33,1},{97,65},{2,34}... | collective-permute-start | bytes 414728 | tf_op jit(solution)/shard_map/ppermute | solution.py:571
  9.2 0.7 collective-permute-start.3
  9.9 1.8 %collective-permute-done.2.refs_2_.refs_6_ = f32[6,2,1,2880]{3,2,1,0:T(1,128)S(1)} collective-permute-done((f32[6,2,1,2880]{3,2,1,0:T(1,128)S(1)}, f32[6,2,1,2880]{3,2,1,0:T(1,128)S(1)}, u32[]{:S(2)}, u32[]{:S(2)}) %collective-permute-start.2) | collective-permute-done | bytes 138272 | tf_op jit(solution)/shard_map/ppermute | solution.py:571
  11.7 3.6 %collective-permute-done.1.refs_1_.refs_5_ = f32[6,8,2880]{2,1,0:T(8,128)S(1)} collective-permute-done((f32[6,8,2880]{2,1,0:T(8,128)S(1)}, f32[6,8,2880]{2,1,0:T(8,128)S(1)}, u32[]{:S(2)}, u32[]{:S(2)}) %collective-permute-start.1) | collective-permute-done | bytes 552992 | tf_op jit(solution)/shard_map/ppermute | solution.py:571
  15.3 2.6 %shard_map.178 = (f32[5,2,8,2880]{3,2,1,0:T(8,128)S(1)}, f32[5,8,2880]{2,1,0:T(8,128)S(1)}, f32[5,8,2880]{2,1,0:T(8,128)S(1)}, f32[5,2,1,2880]{3,2,1,0:T(1,128)S(1)}, f32[5,2,1,2880]{3,2,1,0:T(1,128)S(1)}) custom-call(s32[2]{0:T(128)S(1)} %pad_add_fusion.side_ref, f32[5,2,8,2880]{3,2,1,0:T(8,128)S(1)} %get-tuple-element.21.n_ref, ...), custom_call_target="tpu_custom_call" | custom-call | flops 4000000 | bytes 1048576 | tf_op jit(solution)/shard_map/pallas_call | solution.py:72
  18.0 3.6 %collective-permute-start.5 = (f32[5,8,2880]{2,1,0:T(8,128)S(1)}, f32[5,8,2880]{2,1,0:T(8,128)S(1)}, u32[]{:S(2)}, u32[]{:S(2)}) collective-permute-start(f32[5,8,2880]{2,1,0:T(8,128)S(1)} %get-tuple-element.31), channel_id=1, source_target_pairs={{1,2},{3,4},{5,6},{7,8},{9,10},{11,12},{13,14},{15,16},{17,18},{19... | collective-permute-start | bytes 1382408 | tf_op jit(solution)/shard_map/ppermute | solution.py:571
  21.6 3.0 %collective-permute-start.6 = (f32[5,2,1,2880]{3,2,1,0:T(1,128)S(1)}, f32[5,2,1,2880]{3,2,1,0:T(1,128)S(1)}, u32[]{:S(2)}, u32[]{:S(2)}) collective-permute-start(f32[5,2,1,2880]{3,2,1,0:T(1,128)S(1)} %get-tuple-element.32), channel_id=1, source_target_pairs={{0,32},{64,96},{32,0},{96,64},{1,33},{65,97},{33,1},{97,65},{2,34}... | collective-permute-start | bytes 345608 | tf_op jit(solution)/shard_map/ppermute | solution.py:571
  24.6 0.7 collective-permute-start.7
  25.3 1.6 %collective-permute-done.6.refs_2_ = f32[5,2,1,2880]{3,2,1,0:T(1,128)S(1)} collective-permute-done((f32[5,2,1,2880]{3,2,1,0:T(1,128)S(1)}, f32[5,2,1,2880]{3,2,1,0:T(1,128)S(1)}, u32[]{:S(2)}, u32[]{:S(2)}) %collective-permute-start.6) | collective-permute-done | bytes 115232 | tf_op jit(solution)/shard_map/ppermute | solution.py:571
  26.9 1.1 collective-permute-done.5.refs_1_
  27.9 2.4 %shard_map.179.mine_ref = f32[23,80,128]{2,1,0:T(8,128)S(1)} custom-call(s32[2]{0:T(128)S(1)} %pad_add_fusion.side_ref, f32[5,2,8,2880]{3,2,1,0:T(8,128)S(1)} %get-tuple-element.29.n_ref, f32[2,8,2880]{2,1,0:T(8,128)S(1)} %get-tuple-element.22.wlon_ref, f32[2,8,2880]{2,1,0:T(8,128)S(1)} %get-tuple-element.23.wlat_ref, ...), custom_call_target="tpu_custom_call" | custom-call | flops 4000000 | bytes 1048576 | tf_op jit(solution)/shard_map/pallas_call | solution.py:72
  31.7 1.3 %collective-permute-done.8.other_ref = f32[23,80,128]{2,1,0:T(8,128)S(1)} collective-permute-done((f32[23,80,128]{2,1,0:T(8,128)S(1)}, f32[23,80,128]{2,1,0:T(8,128)S(1)}, u32[]{:S(2)}, u32[]{:S(2)}) %collective-permute-start.8) | collective-permute-done | bytes 942112 | tf_op jit(solution)/shard_map/ppermute | solution.py:571
  32.9 14.3 %shard_map.180 = f32[3072,128]{1,0:T(8,128)} custom-call(s32[1]{0:T(128)} %bitcast.core_ref, s32[32]{0:T(128)S(1)} %sub.16.starts_ref, s32[32]{0:T(128)S(1)} %copy-done.2, s32[23424]{0:T(1024)} %pad.11.order_hbm, f32[23,80,128]{2,1,0:T(8,128)S(1)} %shard_map.179.mine_ref, f32[23,80,128]{2,1,0:T(8,128)S(1)} %collective-permute-done.8.other_ref), custom_call_target="tpu_custom_call" | custom-call | flops 30000000 | bytes 1048576 | tf_op jit(solution)/shard_map/pallas_call | solution.py:72
  47.2 10.8 %all-to-all-start = ((f32[16,192,128]{2,1,0:T(8,128)}), f32[16,192,128]{2,1,0:T(8,128)S(1)}, u32[]{:S(2)}, u32[]{:S(2)}) async-start(f32[16,192,128]{2,1,0:T(8,128)} %bitcast.7), calls=%async_computation | async-start | bytes 3145728 | tf_op jit(solution)/shard_map/all_to_all | solution.py:639
  60.9 1.8 %copy-done.1 = f32[32,8,2880]{2,1,0:T(8,128)S(1)} copy-done((f32[32,8,2880]{2,1,0:T(8,128)S(1)}, f32[32,8,2880]{2,1,0:T(8,128)}, u32[]{:S(2)}) %copy-start.1) | copy-done | bytes 2949144
  62.8 7.8 %shard_map.176 = (s32[384]{0:T(512)S(1)}, f32[9,32,128]{2,1,0:T(8,128)S(1)}, f32[960,128]{1,0:T(8,128)S(1)}) custom-call(s32[1]{0:T(128)} %dynamic_slice.12.units_ref, s32[270]{0:T(512)S(1)} %dynamic-slice_reduce_fusion.owner_ref, s32[1152]{0:T(1024)S(1)} %get-tuple-element.39.rows_ref, s32[9,128]{1,0:T(8,128)S(1)} %get-tuple-element.38.sel_ref, ...), custom_call_target="tpu_custom_call" | custom-call | flops 20000000 | bytes 1048576 | tf_op jit(solution)/shard_map/pallas_call | solution.py:72
  70.5 14.2 %all-to-all-done = f32[16,192,128]{2,1,0:T(8,128)S(1)} async-done(((f32[16,192,128]{2,1,0:T(8,128)}), f32[16,192,128]{2,1,0:T(8,128)S(1)}, u32[]{:S(2)}, u32[]{:S(2)}) %all-to-all-start) | async-done | bytes 1572896 | tf_op jit(solution)/shard_map/all_to_all | solution.py:639
  84.8 7.0 %shard_map.181 = (f32[1,1,5,64,1080]{4,3,2,1,0:T(8,128)}, f32[2048,128]{1,0:T(8,128)}) custom-call(s32[1]{0:T(128)} %bitcast.core_ref, s32[1]{0:T(128)} %dynamic_slice.12.units_ref, s32[384]{0:T(512)S(1)} %get-tuple-element.20.table_ref, f32[3072,128]{1,0:T(8,128)S(1)} %bitcast.16, f32[960,128]{1,0:T(8,128)S(1)} %get-tuple-element.34.coef_ref, ...), custom_call_target="tpu_custom_call" | custom-call | flops 40000000 | bytes 1048576 | tf_op jit(solution)/shard_map/pallas_call | solution.py:72
  91.9 6.6 %all-to-all-start.1 = ((f32[128,16,128]{2,1,0:T(8,128)}), f32[128,16,128]{2,1,0:T(8,128)S(1)}, u32[]{:S(2)}, u32[]{:S(2)}) async-start(f32[128,16,128]{2,1,0:T(8,128)} %bitcast.9), calls=%async_computation.1 | async-start | bytes 2097152 | tf_op jit(solution)/shard_map/all_to_all | solution.py:644
  98.6 19.1 %all-to-all-done.1 = f32[128,16,128]{2,1,0:T(8,128)S(1)} async-done(((f32[128,16,128]{2,1,0:T(8,128)}), f32[128,16,128]{2,1,0:T(8,128)S(1)}, u32[]{:S(2)}, u32[]{:S(2)}) %all-to-all-start.1) | async-done | bytes 1048608 | tf_op jit(solution)/shard_map/all_to_all | solution.py:644
  117.7 4.4 %shard_map.182 = f32[1,7,96,512]{3,2,1,0:T(8,128)} custom-call(f32[2048,128]{1,0:T(8,128)S(1)} %bitcast.18, f32[35]{0:T(128)S(1)} %reshape.76.yield_ref, f32[14]{0:T(128)S(1)} %pad_maximum_fusion.rates_ref, f32[1,512]{1,0:T(1,128)S(1)} %copy-done.7, bf16[512,512]{1,0:T(8,128)(2,1)S(1)} %copy-done.3, bf16[512,512]{1,0:T(8,128)(2,1)S(1)} %copy-done.4, ...), custom_call_target="tpu_custom_call" | custom-call | flops 2000000000 | bytes 1048576 | tf_op jit(solution)/shard_map/pallas_call | solution.py:72
  (55 shorter events, 3.8 us)
Async XLA Ops:
  0.6 60.1 %copy-start = (s32[32,270,1]{1,2,0:T(1,128)S(1)}, s32[32,270,1]{1,2,0:T(1,128)}, u32[]{:S(2)}) copy-start(s32[32,270,1]{1,2,0:T(1,128)} %param.28) | copy-start | bytes 103684
  2.9 8.8 %collective-permute-start = (f32[6,8,2880]{2,1,0:T(8,128)S(1)}, f32[6,8,2880]{2,1,0:T(8,128)S(1)}, u32[]{:S(2)}, u32[]{:S(2)}) collective-permute-start(f32[6,8,2880]{2,1,0:T(8,128)S(1)} %get-tuple-element.25), channel_id=1, source_target_pairs={{0,1},{2,3},{4,5},{6,7},{8,9},{10,11},{12,13},{14,15},{16,17},{18,... | collective-permute-start | bytes 1658888 | tf_op jit(solution)/shard_map/ppermute | solution.py:571
  4.3 10.9 %collective-permute-start.1 = (f32[6,8,2880]{2,1,0:T(8,128)S(1)}, f32[6,8,2880]{2,1,0:T(8,128)S(1)}, u32[]{:S(2)}, u32[]{:S(2)}) collective-permute-start(f32[6,8,2880]{2,1,0:T(8,128)S(1)} %get-tuple-element.26), channel_id=1, source_target_pairs={{1,2},{3,4},{5,6},{7,8},{9,10},{11,12},{13,14},{15,16},{17,18},{19... | collective-permute-start | bytes 1658888 | tf_op jit(solution)/shard_map/ppermute | solution.py:571
  7.5 4.2 %collective-permute-start.2 = (f32[6,2,1,2880]{3,2,1,0:T(1,128)S(1)}, f32[6,2,1,2880]{3,2,1,0:T(1,128)S(1)}, u32[]{:S(2)}, u32[]{:S(2)}) collective-permute-start(f32[6,2,1,2880]{3,2,1,0:T(1,128)S(1)} %get-tuple-element.27), channel_id=1, source_target_pairs={{0,32},{64,96},{32,0},{96,64},{1,33},{65,97},{33,1},{97,65},{2,34}... | collective-permute-start | bytes 414728 | tf_op jit(solution)/shard_map/ppermute | solution.py:571
  9.2 2.5 %collective-permute-start.3 = (f32[6,2,1,2880]{3,2,1,0:T(1,128)S(1)}, f32[6,2,1,2880]{3,2,1,0:T(1,128)S(1)}, u32[]{:S(2)}, u32[]{:S(2)}) collective-permute-start(f32[6,2,1,2880]{3,2,1,0:T(1,128)S(1)} %get-tuple-element.28), channel_id=1, source_target_pairs={{32,64},{64,32},{33,65},{65,33},{34,66},{66,34},{35,67},{67,35},{3... | collective-permute-start | bytes 414728 | tf_op jit(solution)/shard_map/ppermute | solution.py:571
  17.9 8.9 %collective-permute-start.4 = (f32[5,8,2880]{2,1,0:T(8,128)S(1)}, f32[5,8,2880]{2,1,0:T(8,128)S(1)}, u32[]{:S(2)}, u32[]{:S(2)}) collective-permute-start(f32[5,8,2880]{2,1,0:T(8,128)S(1)} %get-tuple-element.30), channel_id=1, source_target_pairs={{0,1},{2,3},{4,5},{6,7},{8,9},{10,11},{12,13},{14,15},{16,17},{18,... | collective-permute-start | bytes 1382408 | tf_op jit(solution)/shard_map/ppermute | solution.py:571
  18.0 9.9 %collective-permute-start.5 = (f32[5,8,2880]{2,1,0:T(8,128)S(1)}, f32[5,8,2880]{2,1,0:T(8,128)S(1)}, u32[]{:S(2)}, u32[]{:S(2)}) collective-permute-start(f32[5,8,2880]{2,1,0:T(8,128)S(1)} %get-tuple-element.31), channel_id=1, source_target_pairs={{1,2},{3,4},{5,6},{7,8},{9,10},{11,12},{13,14},{15,16},{17,18},{19... | collective-permute-start | bytes 1382408 | tf_op jit(solution)/shard_map/ppermute | solution.py:571
  21.6 5.2 %collective-permute-start.6 = (f32[5,2,1,2880]{3,2,1,0:T(1,128)S(1)}, f32[5,2,1,2880]{3,2,1,0:T(1,128)S(1)}, u32[]{:S(2)}, u32[]{:S(2)}) collective-permute-start(f32[5,2,1,2880]{3,2,1,0:T(1,128)S(1)} %get-tuple-element.32), channel_id=1, source_target_pairs={{0,32},{64,96},{32,0},{96,64},{1,33},{65,97},{33,1},{97,65},{2,34}... | collective-permute-start | bytes 345608 | tf_op jit(solution)/shard_map/ppermute | solution.py:571
  24.6 2.2 %collective-permute-start.7 = (f32[5,2,1,2880]{3,2,1,0:T(1,128)S(1)}, f32[5,2,1,2880]{3,2,1,0:T(1,128)S(1)}, u32[]{:S(2)}, u32[]{:S(2)}) collective-permute-start(f32[5,2,1,2880]{3,2,1,0:T(1,128)S(1)} %get-tuple-element.33), channel_id=1, source_target_pairs={{32,64},{64,32},{33,65},{65,33},{34,66},{66,34},{35,67},{67,35},{3... | collective-permute-start | bytes 345608 | tf_op jit(solution)/shard_map/ppermute | solution.py:571
  27.9 2.5 %copy-start.8 = (s32[1,23040]{1,0:T(1,128)S(1)}, s32[1,23040]{1,0:T(1,128)}, u32[]{:S(2)}) copy-start(s32[1,23040]{1,0:T(1,128)} %param.26) | copy-start | bytes 276484
  27.9 3.5 %copy-start.2 = (s32[32]{0:T(128)S(1)}, s32[32]{0:T(128)}, u32[]{:S(2)}) copy-start(s32[32]{0:T(128)} %units_ref.1) | copy-start | bytes 388
  30.3 2.6 %collective-permute-start.8 = (f32[23,80,128]{2,1,0:T(8,128)S(1)}, f32[23,80,128]{2,1,0:T(8,128)S(1)}, u32[]{:S(2)}, u32[]{:S(2)}) collective-permute-start(f32[23,80,128]{2,1,0:T(8,128)S(1)} %shard_map.179.mine_ref), channel_id=1, source_target_pairs={{0,1},{2,3},{4,5},{6,7},{8,9},{10,11},{12,13},{14,15},{16,17},{18,... | collective-permute-start | bytes 2826248 | tf_op jit(solution)/shard_map/ppermute | solution.py:571
  47.2 12.7 %copy-start.10 = (f32[5,64]{1,0:T(8,128)S(1)}, f32[5,64]{1,0:T(8,128)}, u32[]{:S(2)}) copy-start(f32[5,64]{1,0:T(8,128)} %param.21) | copy-start | bytes 3844
  47.2 37.5 %all-to-all-start = ((f32[16,192,128]{2,1,0:T(8,128)}), f32[16,192,128]{2,1,0:T(8,128)S(1)}, u32[]{:S(2)}, u32[]{:S(2)}) async-start(f32[16,192,128]{2,1,0:T(8,128)} %bitcast.7), calls=%async_computation | async-start | bytes 3145728 | tf_op jit(solution)/shard_map/all_to_all | solution.py:639
  60.9 1.9 %copy-start.1 = (f32[32,8,2880]{2,1,0:T(8,128)S(1)}, f32[32,8,2880]{2,1,0:T(8,128)}, u32[]{:S(2)}) copy-start(f32[32,8,2880]{2,1,0:T(8,128)} %param.22) | copy-start | bytes 8847364
  84.8 13.7 %copy-start.9 = (f32[7,5]{1,0:T(8,128)S(1)}, f32[7,5]{1,0:T(8,128)}, u32[]{:S(2)}) copy-start(f32[7,5]{1,0:T(8,128)} %param.23) | copy-start | bytes 424
  91.8 6.8 %copy-start.11 = (f32[7]{0:T(128)S(1)}, f32[7]{0:T(128)}, u32[]{:S(2)}) copy-start(f32[7]{0:T(128)} %param.25) | copy-start | bytes 88
  91.8 6.8 %copy-start.12 = (f32[7]{0:T(128)S(1)}, f32[7]{0:T(128)}, u32[]{:S(2)}) copy-start(f32[7]{0:T(128)} %param.24) | copy-start | bytes 88
  91.8 25.9 %copy-start.3 = (bf16[512,512]{1,0:T(8,128)(2,1)S(1)}, bf16[512,512]{1,0:T(8,128)(2,1)}, u32[]{:S(2)}) copy-start(bf16[512,512]{1,0:T(8,128)(2,1)} %constant.127.clone.fwd_high) | copy-start | bytes 1572868
  91.8 25.9 %copy-start.4 = (bf16[512,512]{1,0:T(8,128)(2,1)S(1)}, bf16[512,512]{1,0:T(8,128)(2,1)}, u32[]{:S(2)}) copy-start(bf16[512,512]{1,0:T(8,128)(2,1)} %constant.128.clone.fwd_low) | copy-start | bytes 1572868
  91.8 25.9 %copy-start.5 = (bf16[512,512]{1,0:T(8,128)(2,1)S(1)}, bf16[512,512]{1,0:T(8,128)(2,1)}, u32[]{:S(2)}) copy-start(bf16[512,512]{1,0:T(8,128)(2,1)} %constant.129.clone.inv_high) | copy-start | bytes 1572868
  91.8 25.9 %copy-start.6 = (bf16[512,512]{1,0:T(8,128)(2,1)S(1)}, bf16[512,512]{1,0:T(8,128)(2,1)}, u32[]{:S(2)}) copy-start(bf16[512,512]{1,0:T(8,128)(2,1)} %constant.130.clone.inv_low) | copy-start | bytes 1572868
  91.8 25.9 %copy-start.7 = (f32[1,512]{1,0:T(1,128)S(1)}, f32[1,512]{1,0:T(1,128)}, u32[]{:S(2)}) copy-start(f32[1,512]{1,0:T(1,128)} %constant.144.waves_ref) | copy-start | bytes 6148
  91.9 25.8 %all-to-all-start.1 = ((f32[128,16,128]{2,1,0:T(8,128)}), f32[128,16,128]{2,1,0:T(8,128)S(1)}, u32[]{:S(2)}, u32[]{:S(2)}) async-start(f32[128,16,128]{2,1,0:T(8,128)} %bitcast.9), calls=%async_computation.1 | async-start | bytes 2097152 | tf_op jit(solution)/shard_map/all_to_all | solution.py:644

commit v9 on v8

--- a/solution.py
+++ b/solution.py
@@ -78,8 +78,8 @@
     return jax.ShapeDtypeStruct(shape, dtype)
 
 
-def upwind(courant_plus, courant_minus, upstream, downstream):
-    return courant_plus * upstream + courant_minus * downstream
+def upwind(courant, upstream, downstream):
+    return courant * jnp.where(courant > 0.0, upstream, downstream)
 
 
 def edges_kernel(
@@ -135,51 +135,62 @@
     )(side, density, wind_lon, wind_lat, wind_lev)
 
 
-def transport_kernel(side_ref, n_ref, wlon_ref, wlat_ref, wlev_ref, *refs, last):
+def interior_kernel(n_ref, wlon_ref, wlat_ref, wlev_ref, out_ref):
+    row = lax.broadcasted_iota(jnp.int32, (BAND_LATS, NLON), 0)
+
+    @pl.loop(0, SPECIES)
+    def _(s):
+        for j in range(2):
+            x = n_ref[s, j]
+            west = jnp.concatenate([x[:, NLON - 1 :], x[:, : NLON - 1]], axis=1)
+            flux = upwind(wlon_ref[j], west, x)
+            total = x + (flux - jnp.concatenate([flux[:, 1:], flux[:, :1]], axis=1))
+            flux = upwind(wlat_ref[j], pltpu.roll(x, 1, axis=0), x)
+            flux = jnp.where(row == 0, 0.0, flux)
+            total = total + (flux - pltpu.roll(flux, BAND_LATS - 1, axis=0))
+            flux = upwind(wlev_ref[1], n_ref[s, 0], n_ref[s, 1])
+            out_ref[s, j] = total + flux if j else total - flux
+
+
+def interior(density, winds):
+    return call(
+        interior_kernel, on_chip((SPECIES, 2, BAND_LATS, NLON)), [HELD] * 4, VMEM, flops=8_000_000
+    )(density, *winds)
+
+
+def faces_kernel(side_ref, n_ref, inside_ref, wlat_ref, wlev_ref, *refs, last):
     inner_ref, outer_ref, row_ref, far_row_ref = refs[:4]
     inner_wind, outer_wind, row_wind, far_row_wind = refs[4:8]
     outs = refs[8:]
     odd = side_ref[1] == 1
-
-    def split(c):
-        return jnp.maximum(c, 0.0), jnp.minimum(c, 0.0)
-
-    def shift_west(x):
-        return jnp.concatenate([x[:, NLON - 1 :], x[:, : NLON - 1]], axis=1)
-
-    def shift_east(x):
-        return jnp.concatenate([x[:, 1:], x[:, :1]], axis=1)
+    row = lax.broadcasted_iota(jnp.int32, (BAND_LATS, NLON), 0)
 
     def advance(core):
         below_ref, above_ref, above_wind = (
             (outer_ref, inner_ref, inner_wind) if core == 0 else (inner_ref, outer_ref, outer_wind)
         )
-        for j in range(2):
-
-            @pl.loop(0, SPECIES)
-            def _(s):
+
+        @pl.loop(0, SPECIES)
+        def _(s):
+            for j in range(2):
                 x = n_ref[s, j]
-                flux = upwind(*split(wlon_ref[j]), shift_west(x), x)
-                total = x + (flux - shift_east(flux))
+                total = inside_ref[s, j]
                 south = jnp.where(odd, row_ref[s, j], far_row_ref[s, j])
                 north = jnp.where(odd, far_row_ref[s, j], row_ref[s, j])
                 north_wind = jnp.where(odd, far_row_wind[SPECIES, j], row_wind[SPECIES, j])
-                southern = jnp.concatenate([south, x[: BAND_LATS - 1]], axis=0)
-                flux = upwind(*split(wlat_ref[j]), southern, x)
-                edge = upwind(*split(north_wind), x[BAND_LATS - 1 :], north)
-                total = total + (flux - jnp.concatenate([flux[1:], edge], axis=0))
+                into = upwind(wlat_ref[j, :1], south, x[:1])
+                out_of = upwind(north_wind, x[BAND_LATS - 1 :], north)
+                total = total + jnp.where(row == 0, into, 0.0) - jnp.where(row == BAND_LATS - 1, out_of, 0.0)
                 if j == 0:
-                    beneath, overhead, over_wind = below_ref[s], n_ref[s, 1], wlev_ref[1]
+                    total = total + upwind(wlev_ref[0], below_ref[s], x)
                 else:
-                    beneath, overhead, over_wind = n_ref[s, 0], above_ref[s], above_wind[SPECIES]
-                flux = upwind(*split(wlev_ref[j]), beneath, x)
-                total = total + (flux - upwind(*split(over_wind), x, overhead))
+                    total = total - upwind(above_wind[SPECIES], x, above_ref[s])
                 if last:
-                    row = pl.multiple_of((j * SPECIES + s) * BAND_LATS, BAND_LATS)
+                    start = pl.multiple_of((j * SPECIES + s) * BAND_LATS, BAND_LATS)
                     for blk in range(LON_BLOCKS):
                         wide = min(LANES, NLON - blk * LANES)
-                        outs[0][blk, pl.ds(row, BAND_LATS), :wide] = total[:, blk * LANES : blk * LANES + wide]
-                    return
+                        outs[0][blk, pl.ds(start, BAND_LATS), :wide] = total[:, blk * LANES : blk * LANES + wide]
+                    continue
                 outs[0][s, j] = total
                 outs[2 if j == core else 1][s] = total
                 first, final = total[:1], total[BAND_LATS - 1 :]
@@ -190,7 +201,7 @@
         pl.when(side_ref[0] == core)(functools.partial(advance, core))
 
 
-def transport_step(side, density, winds, halo, wind_halo, last):
+def faces(side, density, inside, winds, halo, wind_halo, last):
     if last:
         out_shape = (on_chip((LON_BLOCKS, 2 * SPECIES * BAND_LATS, LANES)),)
     else:
@@ -202,12 +213,12 @@
             on_chip((SPECIES, 2, 1, NLON)),
         )
     return call(
-        functools.partial(transport_kernel, last=last),
+        functools.partial(faces_kernel, last=last),
         out_shape,
         [SMEM] + [HELD] * 12,
         (VMEM,) * len(out_shape),
-        flops=4_000_000,
-    )(side, density, *winds, *halo, *wind_halo)
+        flops=2_000_000,
+    )(side, density, inside, *winds[1:], *halo, *wind_halo)
 
 
 def prepare_kernel(
@@ -628,8 +639,10 @@
         jnp.swapaxes(coefs, 2, 3).reshape(-1, 1),
     )
 
-    density, *halo = transport_step(side, neutrals, winds, first_halo, first_halo, False)
-    (mine,) = transport_step(side, density, winds, exchange(*halo), first_halo, True)
+    inside = interior(neutrals, winds)
+    density, *halo = faces(side, neutrals, inside, winds, first_halo, first_halo, False)
+    inside = interior(density, winds)
+    (mine,) = faces(side, density, inside, winds, exchange(*halo), first_halo, True)
     owners = lax.axis_size("lev")
     other = swap(mine, "lev", 0)
 

time: 123 us -> 120 us (0.976)
  waiting for transfers between devices: 42.5 us -> 40.4 us
    ppermute x9, waiting for transfers between devices: 9.29 us -> 7.13 us  [swap(): lax.ppermute(x, axis, [(i, i + 1) for i in lows] + [(i + 1, i) for i in l...]
    pallas_call x7 -> x9, Pallas kernels: 40.6 us -> 40.1 us  [placed(): return run(*(place(x, spec) for x, spec in zip(args, in_specs)))]
  transfers between devices with their start and end apart: 11 -> 11, of which waited for: 7 -> 7; matrix products, arithmetic and copies ran while one was open for 3% -> 3% of each run, Pallas kernels for 6% -> 8%
where the time goes in v9:
time: 120 us; the launch traced here: 119 us
  waiting for transfers between devices  40.4 us (34%)
  Pallas kernels  40.1 us (33%)
  starting transfers between devices  31.9 us (27%)
  local copies, waits for them, and re-layouts  4.63 us (4%)
  between operations  1.62 us (1%)
    pallas_call x9, Pallas kernels, placed(): return run(*(place(x, spec) for x, spec in zip(args, in_specs)))  40.1 us
    all_to_all x1, waiting for transfers between devices, on_device(): lax.all_to_all(items.reshape(PEERS, ITEM_ROWS, LANES), ('band', 'lev'), 0...  19.1 us
    ppermute x9, starting transfers between devices, swap(): lax.ppermute(x, axis, [(i, i + 1) for i in lows] + [(i + 1, i) for i in l...  14.4 us
    all_to_all x1, waiting for transfers between devices, on_device(): lax.all_to_all(outgoing.reshape(16, PEER_ROWS, LANES), 'lev', 0, 0, axis_...  14.2 us
    all_to_all x1, starting transfers between devices, on_device(): lax.all_to_all(outgoing.reshape(16, PEER_ROWS, LANES), 'lev', 0, 0, axis_...  10.8 us
    ppermute x9, waiting for transfers between devices, swap(): lax.ppermute(x, axis, [(i, i + 1) for i in lows] + [(i + 1, i) for i in l...  7.13 us
    all_to_all x1, starting transfers between devices, on_device(): lax.all_to_all(items.reshape(PEERS, ITEM_ROWS, LANES), ('band', 'lev'), 0...  6.61 us
  transfers between devices with their start and end apart: 11, of which 7 were waited for; matrix products, arithmetic and copies ran while one was open for 3% of the time, Pallas kernels for 8%

profile of v9, /device:TPU:1, one launch (start us, length us, event | category | flops | bytes accessed | tf_op | source)
XLA Modules:
  0.0 119.4 jit_solution(5062542613573508396)
XLA Ops:
  0.7 2.1 %shard_map.177 = (f32[5,2,8,2880]{3,2,1,0:T(8,128)S(1)}, f32[2,8,2880]{2,1,0:T(8,128)S(1)}, f32[2,8,2880]{2,1,0:T(8,128)S(1)}, f32[2,8,2880]{2,1,0:T(8,128)S(1)}...) custom-call(s32[2]{0:T(128)S(1)} %pad_add_fusion.side_ref, ...), custom_call_target="tpu_custom_call" | custom-call | flops 1000000 | bytes 1048576 | tf_op jit(solution)/shard_map/pallas_call | solution.py:72
  2.9 1.5 %collective-permute-start = (f32[6,8,2880]{2,1,0:T(8,128)S(1)}, f32[6,8,2880]{2,1,0:T(8,128)S(1)}, u32[]{:S(2)}, u32[]{:S(2)}) collective-permute-start(f32[6,8,2880]{2,1,0:T(8,128)S(1)} %get-tuple-element.25), channel_id=1, source_target_pairs={{0,1},{2,3},{4,5},{6,7},{8,9},{10,11},{12,13},{14,15},{16,17},{18,... | collective-permute-start | bytes 1658888 | tf_op jit(solution)/shard_map/ppermute | solution.py:582
  4.3 3.1 %collective-permute-start.1 = (f32[6,8,2880]{2,1,0:T(8,128)S(1)}, f32[6,8,2880]{2,1,0:T(8,128)S(1)}, u32[]{:S(2)}, u32[]{:S(2)}) collective-permute-start(f32[6,8,2880]{2,1,0:T(8,128)S(1)} %get-tuple-element.26), channel_id=1, source_target_pairs={{1,2},{3,4},{5,6},{7,8},{9,10},{11,12},{13,14},{15,16},{17,18},{19... | collective-permute-start | bytes 1658888 | tf_op jit(solution)/shard_map/ppermute | solution.py:582
  7.5 1.7 %collective-permute-start.2 = (f32[6,2,1,2880]{3,2,1,0:T(1,128)S(1)}, f32[6,2,1,2880]{3,2,1,0:T(1,128)S(1)}, u32[]{:S(2)}, u32[]{:S(2)}) collective-permute-start(f32[6,2,1,2880]{3,2,1,0:T(1,128)S(1)} %get-tuple-element.27), channel_id=1, source_target_pairs={{0,32},{64,96},{32,0},{96,64},{1,33},{65,97},{33,1},{97,65},{2,34}... | collective-permute-start | bytes 414728 | tf_op jit(solution)/shard_map/ppermute | solution.py:582
  9.2 0.7 collective-permute-start.3
  9.9 1.1 shard_map.178.inside_ref
  10.9 0.7 collective-permute-done.2.refs_2_.refs_6_
  11.7 3.6 %collective-permute-done.1.refs_1_.refs_5_ = f32[6,8,2880]{2,1,0:T(8,128)S(1)} collective-permute-done((f32[6,8,2880]{2,1,0:T(8,128)S(1)}, f32[6,8,2880]{2,1,0:T(8,128)S(1)}, u32[]{:S(2)}, u32[]{:S(2)}) %collective-permute-start.1) | collective-permute-done | bytes 552992 | tf_op jit(solution)/shard_map/ppermute | solution.py:582
  15.3 1.3 %shard_map.179 = (f32[5,2,8,2880]{3,2,1,0:T(8,128)S(1)}, f32[5,8,2880]{2,1,0:T(8,128)S(1)}, f32[5,8,2880]{2,1,0:T(8,128)S(1)}, f32[5,2,1,2880]{3,2,1,0:T(1,128)S(1)}, f32[5,2,1,2880]{3,2,1,0:T(1,128)S(1)}) custom-call(s32[2]{0:T(128)S(1)} %pad_add_fusion.side_ref, f32[5,2,8,2880]{3,2,1,0:T(8,128)S(1)} %get-tuple-element.21.n_ref, ...), custom_call_target="tpu_custom_call" | custom-call | flops 2000000 | bytes 1048576 | tf_op jit(solution)/shard_map/pallas_call | solution.py:72
  16.7 3.6 %collective-permute-start.5 = (f32[5,8,2880]{2,1,0:T(8,128)S(1)}, f32[5,8,2880]{2,1,0:T(8,128)S(1)}, u32[]{:S(2)}, u32[]{:S(2)}) collective-permute-start(f32[5,8,2880]{2,1,0:T(8,128)S(1)} %get-tuple-element.31), channel_id=1, source_target_pairs={{1,2},{3,4},{5,6},{7,8},{9,10},{11,12},{13,14},{15,16},{17,18},{19... | collective-permute-start | bytes 1382408 | tf_op jit(solution)/shard_map/ppermute | solution.py:582
  20.3 3.0 %collective-permute-start.6 = (f32[5,2,1,2880]{3,2,1,0:T(1,128)S(1)}, f32[5,2,1,2880]{3,2,1,0:T(1,128)S(1)}, u32[]{:S(2)}, u32[]{:S(2)}) collective-permute-start(f32[5,2,1,2880]{3,2,1,0:T(1,128)S(1)} %get-tuple-element.32), channel_id=1, source_target_pairs={{0,32},{64,96},{32,0},{96,64},{1,33},{65,97},{33,1},{97,65},{2,34}... | collective-permute-start | bytes 345608 | tf_op jit(solution)/shard_map/ppermute | solution.py:582
  24.0 1.1 shard_map.180.inside_ref
  25.5 1.1 collective-permute-done.5.refs_1_
  26.6 1.1 shard_map.181.mine_ref
  29.0 1.3 %collective-permute-done.8.other_ref = f32[23,80,128]{2,1,0:T(8,128)S(1)} collective-permute-done((f32[23,80,128]{2,1,0:T(8,128)S(1)}, f32[23,80,128]{2,1,0:T(8,128)S(1)}, u32[]{:S(2)}, u32[]{:S(2)}) %collective-permute-start.8) | collective-permute-done | bytes 942112 | tf_op jit(solution)/shard_map/ppermute | solution.py:582
  30.3 14.3 %shard_map.182 = f32[3072,128]{1,0:T(8,128)} custom-call(s32[1]{0:T(128)} %bitcast.core_ref, s32[32]{0:T(128)S(1)} %sub.16.starts_ref, s32[32]{0:T(128)S(1)} %copy-done.2, s32[23424]{0:T(1024)} %pad.11.order_hbm, f32[23,80,128]{2,1,0:T(8,128)S(1)} %shard_map.181.mine_ref, f32[23,80,128]{2,1,0:T(8,128)S(1)} %collective-permute-done.8.other_ref), custom_call_target="tpu_custom_call" | custom-call | flops 30000000 | bytes 1048576 | tf_op jit(solution)/shard_map/pallas_call | solution.py:72
  44.6 10.8 %all-to-all-start = ((f32[16,192,128]{2,1,0:T(8,128)}), f32[16,192,128]{2,1,0:T(8,128)S(1)}, u32[]{:S(2)}, u32[]{:S(2)}) async-start(f32[16,192,128]{2,1,0:T(8,128)} %bitcast.7), calls=%async_computation | async-start | bytes 3145728 | tf_op jit(solution)/shard_map/all_to_all | solution.py:652
  58.3 1.8 %copy-done.1 = f32[32,8,2880]{2,1,0:T(8,128)S(1)} copy-done((f32[32,8,2880]{2,1,0:T(8,128)S(1)}, f32[32,8,2880]{2,1,0:T(8,128)}, u32[]{:S(2)}) %copy-start.1) | copy-done | bytes 2949144
  60.1 7.8 %shard_map.176 = (s32[384]{0:T(512)S(1)}, f32[9,32,128]{2,1,0:T(8,128)S(1)}, f32[960,128]{1,0:T(8,128)S(1)}) custom-call(s32[1]{0:T(128)} %dynamic_slice.12.units_ref, s32[270]{0:T(512)S(1)} %dynamic-slice_reduce_fusion.owner_ref, s32[1152]{0:T(1024)S(1)} %get-tuple-element.39.rows_ref, s32[9,128]{1,0:T(8,128)S(1)} %get-tuple-element.38.sel_ref, ...), custom_call_target="tpu_custom_call" | custom-call | flops 20000000 | bytes 1048576 | tf_op jit(solution)/shard_map/pallas_call | solution.py:72
  67.9 14.2 %all-to-all-done = f32[16,192,128]{2,1,0:T(8,128)S(1)} async-done(((f32[16,192,128]{2,1,0:T(8,128)}), f32[16,192,128]{2,1,0:T(8,128)S(1)}, u32[]{:S(2)}, u32[]{:S(2)}) %all-to-all-start) | async-done | bytes 1572896 | tf_op jit(solution)/shard_map/all_to_all | solution.py:652
  82.1 7.0 %shard_map.183 = (f32[1,1,5,64,1080]{4,3,2,1,0:T(8,128)}, f32[2048,128]{1,0:T(8,128)}) custom-call(s32[1]{0:T(128)} %bitcast.core_ref, s32[1]{0:T(128)} %dynamic_slice.12.units_ref, s32[384]{0:T(512)S(1)} %get-tuple-element.20.table_ref, f32[3072,128]{1,0:T(8,128)S(1)} %bitcast.16, f32[960,128]{1,0:T(8,128)S(1)} %get-tuple-element.34.coef_ref, ...), custom_call_target="tpu_custom_call" | custom-call | flops 40000000 | bytes 1048576 | tf_op jit(solution)/shard_map/pallas_call | solution.py:72
  89.2 6.6 %all-to-all-start.1 = ((f32[128,16,128]{2,1,0:T(8,128)}), f32[128,16,128]{2,1,0:T(8,128)S(1)}, u32[]{:S(2)}, u32[]{:S(2)}) async-start(f32[128,16,128]{2,1,0:T(8,128)} %bitcast.9), calls=%async_computation.1 | async-start | bytes 2097152 | tf_op jit(solution)/shard_map/all_to_all | solution.py:657
  96.0 19.1 %all-to-all-done.1 = f32[128,16,128]{2,1,0:T(8,128)S(1)} async-done(((f32[128,16,128]{2,1,0:T(8,128)}), f32[128,16,128]{2,1,0:T(8,128)S(1)}, u32[]{:S(2)}, u32[]{:S(2)}) %all-to-all-start.1) | async-done | bytes 1048608 | tf_op jit(solution)/shard_map/all_to_all | solution.py:657
  115.1 4.3 %shard_map.184 = f32[1,7,96,512]{3,2,1,0:T(8,128)} custom-call(f32[2048,128]{1,0:T(8,128)S(1)} %bitcast.18, f32[35]{0:T(128)S(1)} %reshape.76.yield_ref, f32[14]{0:T(128)S(1)} %pad_maximum_fusion.rates_ref, f32[1,512]{1,0:T(1,128)S(1)} %copy-done.7, bf16[512,512]{1,0:T(8,128)(2,1)S(1)} %copy-done.3, bf16[512,512]{1,0:T(8,128)(2,1)S(1)} %copy-done.4, ...), custom_call_target="tpu_custom_call" | custom-call | flops 2000000000 | bytes 1048576 | tf_op jit(solution)/shard_map/pallas_call | solution.py:72
  (57 shorter events, 4.9 us)
Async XLA Ops:
  0.6 57.5 %copy-start = (s32[32,270,1]{1,2,0:T(1,128)S(1)}, s32[32,270,1]{1,2,0:T(1,128)}, u32[]{:S(2)}) copy-start(s32[32,270,1]{1,2,0:T(1,128)} %param.28) | copy-start | bytes 103684
  2.9 8.8 %collective-permute-start = (f32[6,8,2880]{2,1,0:T(8,128)S(1)}, f32[6,8,2880]{2,1,0:T(8,128)S(1)}, u32[]{:S(2)}, u32[]{:S(2)}) collective-permute-start(f32[6,8,2880]{2,1,0:T(8,128)S(1)} %get-tuple-element.25), channel_id=1, source_target_pairs={{0,1},{2,3},{4,5},{6,7},{8,9},{10,11},{12,13},{14,15},{16,17},{18,... | collective-permute-start | bytes 1658888 | tf_op jit(solution)/shard_map/ppermute | solution.py:582
  4.3 10.9 %collective-permute-start.1 = (f32[6,8,2880]{2,1,0:T(8,128)S(1)}, f32[6,8,2880]{2,1,0:T(8,128)S(1)}, u32[]{:S(2)}, u32[]{:S(2)}) collective-permute-start(f32[6,8,2880]{2,1,0:T(8,128)S(1)} %get-tuple-element.26), channel_id=1, source_target_pairs={{1,2},{3,4},{5,6},{7,8},{9,10},{11,12},{13,14},{15,16},{17,18},{19... | collective-permute-start | bytes 1658888 | tf_op jit(solution)/shard_map/ppermute | solution.py:582
  7.5 4.2 %collective-permute-start.2 = (f32[6,2,1,2880]{3,2,1,0:T(1,128)S(1)}, f32[6,2,1,2880]{3,2,1,0:T(1,128)S(1)}, u32[]{:S(2)}, u32[]{:S(2)}) collective-permute-start(f32[6,2,1,2880]{3,2,1,0:T(1,128)S(1)} %get-tuple-element.27), channel_id=1, source_target_pairs={{0,32},{64,96},{32,0},{96,64},{1,33},{65,97},{33,1},{97,65},{2,34}... | collective-permute-start | bytes 414728 | tf_op jit(solution)/shard_map/ppermute | solution.py:582
  9.2 2.5 %collective-permute-start.3 = (f32[6,2,1,2880]{3,2,1,0:T(1,128)S(1)}, f32[6,2,1,2880]{3,2,1,0:T(1,128)S(1)}, u32[]{:S(2)}, u32[]{:S(2)}) collective-permute-start(f32[6,2,1,2880]{3,2,1,0:T(1,128)S(1)} %get-tuple-element.28), channel_id=1, source_target_pairs={{32,64},{64,32},{33,65},{65,33},{34,66},{66,34},{35,67},{67,35},{3... | collective-permute-start | bytes 414728 | tf_op jit(solution)/shard_map/ppermute | solution.py:582
  16.6 8.9 %collective-permute-start.4 = (f32[5,8,2880]{2,1,0:T(8,128)S(1)}, f32[5,8,2880]{2,1,0:T(8,128)S(1)}, u32[]{:S(2)}, u32[]{:S(2)}) collective-permute-start(f32[5,8,2880]{2,1,0:T(8,128)S(1)} %get-tuple-element.30), channel_id=1, source_target_pairs={{0,1},{2,3},{4,5},{6,7},{8,9},{10,11},{12,13},{14,15},{16,17},{18,... | collective-permute-start | bytes 1382408 | tf_op jit(solution)/shard_map/ppermute | solution.py:582
  16.7 9.9 %collective-permute-start.5 = (f32[5,8,2880]{2,1,0:T(8,128)S(1)}, f32[5,8,2880]{2,1,0:T(8,128)S(1)}, u32[]{:S(2)}, u32[]{:S(2)}) collective-permute-start(f32[5,8,2880]{2,1,0:T(8,128)S(1)} %get-tuple-element.31), channel_id=1, source_target_pairs={{1,2},{3,4},{5,6},{7,8},{9,10},{11,12},{13,14},{15,16},{17,18},{19... | collective-permute-start | bytes 1382408 | tf_op jit(solution)/shard_map/ppermute | solution.py:582
  20.3 5.2 %collective-permute-start.6 = (f32[5,2,1,2880]{3,2,1,0:T(1,128)S(1)}, f32[5,2,1,2880]{3,2,1,0:T(1,128)S(1)}, u32[]{:S(2)}, u32[]{:S(2)}) collective-permute-start(f32[5,2,1,2880]{3,2,1,0:T(1,128)S(1)} %get-tuple-element.32), channel_id=1, source_target_pairs={{0,32},{64,96},{32,0},{96,64},{1,33},{65,97},{33,1},{97,65},{2,34}... | collective-permute-start | bytes 345608 | tf_op jit(solution)/shard_map/ppermute | solution.py:582
  23.3 2.2 %collective-permute-start.7 = (f32[5,2,1,2880]{3,2,1,0:T(1,128)S(1)}, f32[5,2,1,2880]{3,2,1,0:T(1,128)S(1)}, u32[]{:S(2)}, u32[]{:S(2)}) collective-permute-start(f32[5,2,1,2880]{3,2,1,0:T(1,128)S(1)} %get-tuple-element.33), channel_id=1, source_target_pairs={{32,64},{64,32},{33,65},{65,33},{34,66},{66,34},{35,67},{67,35},{3... | collective-permute-start | bytes 345608 | tf_op jit(solution)/shard_map/ppermute | solution.py:582
  25.0 2.7 %copy-start.8 = (s32[1,23040]{1,0:T(1,128)S(1)}, s32[1,23040]{1,0:T(1,128)}, u32[]{:S(2)}) copy-start(s32[1,23040]{1,0:T(1,128)} %param.26) | copy-start | bytes 276484
  25.0 3.7 %copy-start.2 = (s32[32]{0:T(128)S(1)}, s32[32]{0:T(128)}, u32[]{:S(2)}) copy-start(s32[32]{0:T(128)} %units_ref.1) | copy-start | bytes 388
  27.7 2.6 %collective-permute-start.8 = (f32[23,80,128]{2,1,0:T(8,128)S(1)}, f32[23,80,128]{2,1,0:T(8,128)S(1)}, u32[]{:S(2)}, u32[]{:S(2)}) collective-permute-start(f32[23,80,128]{2,1,0:T(8,128)S(1)} %shard_map.181.mine_ref), channel_id=1, source_target_pairs={{0,1},{2,3},{4,5},{6,7},{8,9},{10,11},{12,13},{14,15},{16,17},{18,... | collective-permute-start | bytes 2826248 | tf_op jit(solution)/shard_map/ppermute | solution.py:582
  44.6 12.7 %copy-start.10 = (f32[5,64]{1,0:T(8,128)S(1)}, f32[5,64]{1,0:T(8,128)}, u32[]{:S(2)}) copy-start(f32[5,64]{1,0:T(8,128)} %param.21) | copy-start | bytes 3844
  44.6 37.5 %all-to-all-start = ((f32[16,192,128]{2,1,0:T(8,128)}), f32[16,192,128]{2,1,0:T(8,128)S(1)}, u32[]{:S(2)}, u32[]{:S(2)}) async-start(f32[16,192,128]{2,1,0:T(8,128)} %bitcast.7), calls=%async_computation | async-start | bytes 3145728 | tf_op jit(solution)/shard_map/all_to_all | solution.py:652
  58.3 1.9 %copy-start.1 = (f32[32,8,2880]{2,1,0:T(8,128)S(1)}, f32[32,8,2880]{2,1,0:T(8,128)}, u32[]{:S(2)}) copy-start(f32[32,8,2880]{2,1,0:T(8,128)} %param.22) | copy-start | bytes 8847364
  82.1 13.7 %copy-start.9 = (f32[7,5]{1,0:T(8,128)S(1)}, f32[7,5]{1,0:T(8,128)}, u32[]{:S(2)}) copy-start(f32[7,5]{1,0:T(8,128)} %param.23) | copy-start | bytes 424
  89.1 6.8 %copy-start.11 = (f32[7]{0:T(128)S(1)}, f32[7]{0:T(128)}, u32[]{:S(2)}) copy-start(f32[7]{0:T(128)} %param.25) | copy-start | bytes 88
  89.1 6.8 %copy-start.12 = (f32[7]{0:T(128)S(1)}, f32[7]{0:T(128)}, u32[]{:S(2)}) copy-start(f32[7]{0:T(128)} %param.24) | copy-start | bytes 88
  89.1 25.9 %copy-start.3 = (bf16[512,512]{1,0:T(8,128)(2,1)S(1)}, bf16[512,512]{1,0:T(8,128)(2,1)}, u32[]{:S(2)}) copy-start(bf16[512,512]{1,0:T(8,128)(2,1)} %constant.127.clone.fwd_high) | copy-start | bytes 1572868
  89.2 25.9 %copy-start.4 = (bf16[512,512]{1,0:T(8,128)(2,1)S(1)}, bf16[512,512]{1,0:T(8,128)(2,1)}, u32[]{:S(2)}) copy-start(bf16[512,512]{1,0:T(8,128)(2,1)} %constant.128.clone.fwd_low) | copy-start | bytes 1572868
  89.2 25.9 %copy-start.5 = (bf16[512,512]{1,0:T(8,128)(2,1)S(1)}, bf16[512,512]{1,0:T(8,128)(2,1)}, u32[]{:S(2)}) copy-start(bf16[512,512]{1,0:T(8,128)(2,1)} %constant.129.clone.inv_high) | copy-start | bytes 1572868
  89.2 25.9 %copy-start.6 = (bf16[512,512]{1,0:T(8,128)(2,1)S(1)}, bf16[512,512]{1,0:T(8,128)(2,1)}, u32[]{:S(2)}) copy-start(bf16[512,512]{1,0:T(8,128)(2,1)} %constant.130.clone.inv_low) | copy-start | bytes 1572868
  89.2 25.9 %copy-start.7 = (f32[1,512]{1,0:T(1,128)S(1)}, f32[1,512]{1,0:T(1,128)}, u32[]{:S(2)}) copy-start(f32[1,512]{1,0:T(1,128)} %constant.144.waves_ref) | copy-start | bytes 6148
  89.2 25.8 %all-to-all-start.1 = ((f32[128,16,128]{2,1,0:T(8,128)}), f32[128,16,128]{2,1,0:T(8,128)S(1)}, u32[]{:S(2)}, u32[]{:S(2)}) async-start(f32[128,16,128]{2,1,0:T(8,128)} %bitcast.9), calls=%async_computation.1 | async-start | bytes 2097152 | tf_op jit(solution)/shard_map/all_to_all | solution.py:657

commit v10 on v9

--- a/solution.py
+++ b/solution.py
@@ -27,14 +27,12 @@
 LANES = 128
 LON_BLOCKS = 23
 LON_PAD = LON_BLOCKS * LANES
-CHIP_LEVS = 4
 PITCH = 9
 LEVEL_PITCH = 257
 PLANES = 12
 GROUPS = 6
-CHUNKS = 3
-MSG_ROWS = 64
-PEER_ROWS = CHUNKS * MSG_ROWS
+PIECE = 64
+PEER_ROWS = 3 * PIECE
 SLOT_BLOCKS = 9
 SLOTS_PAD = SLOT_BLOCKS * LANES
 ORDER_PAD = BAND_COLS + 3 * LANES
@@ -53,13 +51,14 @@
     return pltpu.VMEM(shape, dtype)
 
 
-def call(kernel, out_shape, in_specs, out_specs, scratch=(), flops=0, vmem=16):
+def call(kernel, out_shape, in_specs, out_specs, scratch=(), flops=0, vmem=16, aliases=()):
     run = pl.pallas_call(
         kernel,
         out_shape=out_shape,
         in_specs=in_specs,
         out_specs=out_specs,
         scratch_shapes=list(scratch),
+        input_output_aliases=dict(aliases),
         cost_estimate=pl.CostEstimate(flops=flops, bytes_accessed=1 << 20, transcendentals=0),
         compiler_params=pltpu.CompilerParams(vmem_limit_bytes=vmem * 1024 * 1024),
     )
@@ -295,35 +294,61 @@
     )(units, owners, rows, sel, weights, column)
 
 
+def fill_planes(planes, source_ref):
+    @pl.loop(0, LON_BLOCKS)
+    def _(blk):
+        for j in range(2):
+            for i in range(PLANES):
+                from_row = (j * SPECIES + i % SPECIES) * BAND_LATS
+                planes[blk, pl.ds((j * PLANES + i) * PITCH, BAND_LATS), :] = source_ref[
+                    blk, from_row : from_row + BAND_LATS, :
+                ]
+
+
+def fill_table(planes, table_ref, lats):
+    half = LANES // 2
+
+    @pl.loop(0, LON_BLOCKS)
+    def _(blk):
+        for a in range(BAND_LATS // 2):
+            parts = [
+                planes[blk, pl.ds((j * PLANES + first) * PITCH + lat, 8, stride=PITCH), :]
+                for lat in lats(a)
+                for j in range(2)
+                for first in (0, 3, 1, 4)
+            ]
+            rows = jnp.concatenate(parts, axis=0).T
+            for side, lat in enumerate(lats(a)):
+                start = pl.multiple_of((lat * LON_BLOCKS + blk) * LANES, LANES)
+                lanes = slice(side * half, (side + 1) * half)
+                table_ref[pl.ds(start, LANES), lanes] = rows[:, lanes]
+
+
+def own_table_kernel(mine_ref, table_ref, planes):
+    fill_planes(planes, mine_ref)
+    fill_table(planes, table_ref, lambda a: (a, a + BAND_LATS // 2))
+
+
+def own_table(mine):
+    return call(
+        own_table_kernel,
+        on_chip((BAND_LATS * LON_PAD, LANES)),
+        [HELD],
+        VMEM,
+        [pltpu.VMEM((LON_BLOCKS, 2 * PLANES * PITCH, LANES), f32)],
+        flops=8_000_000,
+    )(mine)
+
+
 def pack_kernel(
-    core_ref, starts_ref, units_ref, order_hbm, mine_ref, other_ref,
-    out_hbm, order_ref, planes, table_ref, msg_ref, sems, order_sem,
+    core_ref, starts_ref, units_ref, order_hbm, other_ref, _,
+    out_hbm, table_ref, order_ref, planes, msg_ref, sems, order_sem,
 ):
-    core = core_ref[0]
-
     fetch = pltpu.make_async_copy(order_hbm, order_ref, order_sem)
     fetch.start()
-
-    @pl.loop(0, LON_BLOCKS)
-    def _(blk):
-        for side, source in enumerate((mine_ref, other_ref)):
-            for j in range(2):
-                for i in range(PLANES):
-                    from_row = (j * SPECIES + i % SPECIES) * BAND_LATS
-                    planes[blk, pl.ds(((2 * side + j) * PLANES + i) * PITCH, BAND_LATS), :] = source[
-                        blk, from_row : from_row + BAND_LATS, :
-                    ]
-
-    @pl.loop(0, LON_BLOCKS)
-    def _(blk):
-        for lat in range(BAND_LATS):
-            parts = [
-                planes[blk, pl.ds((jj * PLANES + first) * PITCH + lat, 8, stride=PITCH), :]
-                for jj in range(CHIP_LEVS)
-                for first in (0, 3, 1, 4)
-            ]
-            start = pl.multiple_of((lat * LON_BLOCKS + blk) * LANES, LANES)
-            table_ref[pl.ds(start, LANES), :] = jnp.concatenate(parts, axis=0).T
+    core = core_ref[0]
+    fill_planes(planes, other_ref)
+    fill_table(planes, table_ref, lambda a: (a + BAND_LATS // 2, a))
 
     lane = lax.broadcasted_iota(jnp.int32, (1, LANES), 1)
     group_of = lax.div(lax.rem(lane, 32), SPECIES)
@@ -338,21 +363,22 @@
     def _(peer):
         owner = 2 * peer + core
         first = TUBE_COLS * starts_ref[owner]
-        pieces = lax.div(TUBE_COLS * units_ref[owner] + (MSG_ROWS - 1), MSG_ROWS)
+        pieces = lax.div(TUBE_COLS * units_ref[owner] + (PIECE - 1), PIECE)
 
         def copy(start, number):
             places = []
             for k in range(number):
                 piece = start + k
-                chunk = lax.div(piece, GROUPS)
-                mask = group_of == piece - chunk * GROUPS
-                places.append((pl.multiple_of(peer * PEER_ROWS + chunk * MSG_ROWS, MSG_ROWS), mask))
-            base = first + start * MSG_ROWS
-            for i in range(number * MSG_ROWS):
-                place = order_ref.at[pl.ds(i, ORDER_PAD - 2 * MSG_ROWS)][base]
-                row, mask = places[i // MSG_ROWS]
+                tail = piece >= 2 * GROUPS
+                group = jnp.where(tail, piece - 2 * GROUPS, lax.div(piece, 2))
+                row = peer * PEER_ROWS + jnp.where(tail, 2 * PIECE, PIECE * lax.rem(piece, 2))
+                places.append((pl.multiple_of(row, PIECE), group_of == group))
+            base = first + start * PIECE
+            for i in range(number * PIECE):
+                place = order_ref.at[pl.ds(i, ORDER_PAD - 2 * PIECE)][base]
+                row, mask = places[i // PIECE]
                 value = table_ref[pl.ds(place, 1), :]
-                pltpu.store(msg_ref.at[pl.ds(row + i % MSG_ROWS, 1), :], value, mask=mask)
+                pltpu.store(msg_ref.at[pl.ds(row + i % PIECE, 1), :], value, mask=mask)
 
         @pl.loop(0, lax.div(pieces, 2))
         def _(pair):
@@ -366,27 +392,27 @@
         send(peer).wait()
 
 
-def pack(core, starts, units, order, mine, other):
-    return call(
+def pack(core, starts, units, order, other, table):
+    outgoing, _ = call(
         pack_kernel,
-        sds((16 * PEER_ROWS, LANES)),
+        (sds((16 * PEER_ROWS, LANES)), on_chip((BAND_LATS * LON_PAD, LANES))),
         [SMEM, SMEM, SMEM, HBM, HELD, HELD],
-        HBM,
+        (HBM, VMEM),
         [
             pltpu.SMEM((ORDER_PAD,), jnp.int32),
-            pltpu.VMEM((LON_BLOCKS, CHIP_LEVS * PLANES * PITCH, LANES), f32),
-            pltpu.VMEM((BAND_LATS * LON_PAD, LANES), f32),
+            pltpu.VMEM((LON_BLOCKS, 2 * PLANES * PITCH, LANES), f32),
             pltpu.VMEM((16 * PEER_ROWS, LANES), f32),
             pltpu.SemaphoreType.DMA((16,)),
             pltpu.SemaphoreType.DMA,
         ],
         flops=30_000_000,
-        vmem=32,
-    )(core, starts, units, order, mine, other)
+        aliases={5: 1},
+    )(core, starts, units, order, other, table)
+    return outgoing
 
 
 def solve_kernel(
-    core_ref, units_ref, table_ref, got_ref, coef_ref, weight_ref, state_hbm, items_ref,
+    core_ref, units_ref, table_ref, got_ref, coef_ref, weight_ref, north_ref, state_hbm, items_ref,
     turned, natural, pairs, wide, tubes, state, sems,
 ):
     core = core_ref[0]
@@ -399,11 +425,12 @@
     def _(i):
         for side in range(2):
             out = i * LEVEL_PITCH + side * LANES
-            for chunk in range(CHUNKS):
-                row = pl.multiple_of((2 * i + side) * PEER_ROWS + chunk * MSG_ROWS, MSG_ROWS)
-                flipped = jnp.concatenate([got_ref[pl.ds(row, MSG_ROWS), :]] * 2, axis=0).T
-                turned[chunk, pl.ds(out + 64 * core, 64), :] = flipped[:64]
-                turned[chunk, pl.ds(out + 64 - 64 * core, 64), :] = flipped[64:]
+            row = pl.multiple_of((2 * i + side) * PEER_ROWS, PIECE)
+            tail = got_ref[pl.ds(row + LANES, PIECE), :]
+            for part, rows in enumerate((got_ref[pl.ds(row, LANES), :], jnp.concatenate([tail] * 2, axis=0))):
+                flipped = rows.T
+                turned[part, pl.ds(out + 64 * core, 64), :] = flipped[:64]
+                turned[part, pl.ds(out + 64 - 64 * core, 64), :] = flipped[64:]
 
     def leave(s):
         return pltpu.make_async_copy(state.at[s], state_hbm.at[0, 0, s], sems.at[s])
@@ -416,12 +443,17 @@
 
         lower, upper, inv = coefs(0), coefs(1), coefs(2)
         for blk in range(SLOT_BLOCKS):
-            chunk, i = divmod(blk, 3)
-
-            def levels(group, v):
-                return turned[chunk, pl.ds(32 * v + group * SPECIES + s, 8, stride=LEVEL_PITCH), :]
-
-            rhs = [jnp.where(low, levels(2 * i, v), levels(2 * i + 1, v)) for v in range(8)]
+            i = blk % 3
+
+            def levels(part, group, v):
+                return turned[part, pl.ds(32 * v + group * SPECIES + s, 8, stride=LEVEL_PITCH), :]
+
+            if blk < GROUPS:
+                raw = [levels(0, blk, v) for v in range(8)]
+            else:
+                raw = [jnp.where(low, levels(1, 2 * i, v), levels(1, 2 * i + 1, v)) for v in range(8)]
+            north = north_ref[blk : blk + 1, :] == 1
+            rhs = [jnp.where(north, raw[v ^ 2], raw[v]) for v in range(8)]
             scaled = [rhs[v] * inv[v] for v in range(8)]
             x = rhs
             for _ in range(SWEEPS):
@@ -467,14 +499,14 @@
         leave(s).wait()
 
 
-def solve(core, units, table, got, coefs, weights):
+def solve(core, units, table, got, coefs, weights, north):
     return call(
         solve_kernel,
         (sds((1, 1, SPECIES, NLEV, COL_CAP)), sds((PEERS * ITEM_ROWS, LANES))),
-        [SMEM, SMEM, SMEM] + [HELD] * 3,
+        [SMEM, SMEM, SMEM] + [HELD] * 4,
         (HBM, VMEM),
         [
-            pltpu.VMEM((CHUNKS, 8 * LEVEL_PITCH, LANES), f32),
+            pltpu.VMEM((2, 8 * LEVEL_PITCH, LANES), f32),
             pltpu.VMEM((3, 8 * PITCH, LANES), f32),
             pltpu.VMEM((3, PAIRS, LANES), f32),
             pltpu.VMEM((3, LANES, LANES), f32),
@@ -483,7 +515,7 @@
             pltpu.SemaphoreType.DMA((SPECIES,)),
         ],
         flops=40_000_000,
-    )(core, units, table, got, coefs, weights)
+    )(core, units, table, got, coefs, weights, north)
 
 
 def halves(x):
@@ -622,6 +654,7 @@
     own_lat = jnp.zeros_like(own)
     for i in range(1, BAND_LATS):
         own_lat = own_lat + (own >= i * NLON).astype(jnp.int32)
+    own_north = (own_lat >= BAND_LATS // 2).astype(jnp.int32).reshape(SLOT_BLOCKS, LANES)
     own_lon = own - own_lat * NLON
     own_rows = (own_lat * 6 + own_lon // 512) * LANES + own_lon % LANES
     own_sel = ((own_lon // LANES) % 4).reshape(SLOT_BLOCKS, LANES)
@@ -645,14 +678,15 @@
     (mine,) = faces(side, density, inside, winds, exchange(*halo), first_halo, True)
     owners = lax.axis_size("lev")
     other = swap(mine, "lev", 0)
+    columns = own_table(mine)
 
     core = (lev % 2).reshape(1)
     parity = [[2 * i + c for i in range(owners // 2)] for c in range(2)]
-    outgoing = pack(core, starts, column_units, rows, mine, other)
+    outgoing = pack(core, starts, column_units, rows, other, columns)
     got = lax.all_to_all(
         outgoing.reshape(16, PEER_ROWS, LANES), "lev", 0, 0, axis_index_groups=parity, tiled=True
     ).reshape(16 * PEER_ROWS, LANES)
-    column_state, items = solve(core, own_units, table, got, coefs, own_weights)
+    column_state, items = solve(core, own_units, table, got, coefs, own_weights, own_north)
 
     items = lax.all_to_all(
         items.reshape(PEERS, ITEM_ROWS, LANES), ("band", "lev"), 0, 0, tiled=True

time: 120 us -> 120 us (level)
  waiting for transfers between devices: 40.4 us -> 37.4 us
  Pallas kernels: 40.1 us -> 41.9 us
    pallas_call x9 -> x10, Pallas kernels: 40.1 us -> 41.9 us  [placed(): return run(*(place(x, spec) for x, spec in zip(args, in_specs)))]
    all_to_all x1, waiting for transfers between devices: 14.2 us -> 12.4 us  [on_device(): lax.all_to_all(outgoing.reshape(16, PEER_ROWS, LANES), 'lev', 0, 0, axis_...]
    ppermute x9, waiting for transfers between devices: 7.13 us -> 5.89 us  [swap(): lax.ppermute(x, axis, [(i, i + 1) for i in lows] + [(i + 1, i) for i in l...]
  transfers between devices with their start and end apart: 11 -> 11, of which waited for: 7 -> 6; matrix products, arithmetic and copies ran while one was open for 3% -> 3% of each run, Pallas kernels for 8% -> 11%
where the time goes in v10:
time: 120 us; the launch traced here: 119 us
  Pallas kernels  41.9 us (35%)
  waiting for transfers between devices  37.4 us (31%)
  starting transfers between devices  32.6 us (27%)
  local copies, waits for them, and re-layouts  4.69 us (4%)
  between operations  1.64 us (1%)
    pallas_call x10, Pallas kernels, placed(): return run(*(place(x, spec) for x, spec in zip(args, in_specs)))  41.9 us
    all_to_all x1, waiting for transfers between devices, on_device(): lax.all_to_all(items.reshape(PEERS, ITEM_ROWS, LANES), ('band', 'lev'), 0...  19.1 us
    ppermute x9, starting transfers between devices, swap(): lax.ppermute(x, axis, [(i, i + 1) for i in lows] + [(i + 1, i) for i in l...  14.4 us
    all_to_all x1, waiting for transfers between devices, on_device(): lax.all_to_all(outgoing.reshape(16, PEER_ROWS, LANES), 'lev', 0, 0, axis_...  12.4 us
    all_to_all x1, starting transfers between devices, on_device(): lax.all_to_all(outgoing.reshape(16, PEER_ROWS, LANES), 'lev', 0, 0, axis_...  10.8 us
    all_to_all x1, starting transfers between devices, on_device(): lax.all_to_all(items.reshape(PEERS, ITEM_ROWS, LANES), ('band', 'lev'), 0...  7.39 us
    ppermute x9, waiting for transfers between devices, swap(): lax.ppermute(x, axis, [(i, i + 1) for i in lows] + [(i + 1, i) for i in l...  5.89 us
  transfers between devices with their start and end apart: 11, of which 6 were waited for; matrix products, arithmetic and copies ran while one was open for 3% of the time, Pallas kernels for 11%

profile of v10, /device:TPU:1, one launch (start us, length us, event | category | flops | bytes accessed | tf_op | source)
XLA Modules:
  0.0 119.2 jit_solution(10462844150397168316)
XLA Ops:
  0.7 2.1 %shard_map.177 = (f32[5,2,8,2880]{3,2,1,0:T(8,128)S(1)}, f32[2,8,2880]{2,1,0:T(8,128)S(1)}, f32[2,8,2880]{2,1,0:T(8,128)S(1)}, f32[2,8,2880]{2,1,0:T(8,128)S(1)}...) custom-call(s32[2]{0:T(128)S(1)} %pad_add_fusion.side_ref, ...), custom_call_target="tpu_custom_call" | custom-call | flops 1000000 | bytes 1048576 | tf_op jit(solution)/shard_map/pallas_call | solution.py:71
  2.9 1.5 %collective-permute-start = (f32[6,8,2880]{2,1,0:T(8,128)S(1)}, f32[6,8,2880]{2,1,0:T(8,128)S(1)}, u32[]{:S(2)}, u32[]{:S(2)}) collective-permute-start(f32[6,8,2880]{2,1,0:T(8,128)S(1)} %get-tuple-element.26), channel_id=1, source_target_pairs={{0,1},{2,3},{4,5},{6,7},{8,9},{10,11},{12,13},{14,15},{16,17},{18,... | collective-permute-start | bytes 1658888 | tf_op jit(solution)/shard_map/ppermute | solution.py:614
  4.3 3.1 %collective-permute-start.1 = (f32[6,8,2880]{2,1,0:T(8,128)S(1)}, f32[6,8,2880]{2,1,0:T(8,128)S(1)}, u32[]{:S(2)}, u32[]{:S(2)}) collective-permute-start(f32[6,8,2880]{2,1,0:T(8,128)S(1)} %get-tuple-element.27), channel_id=1, source_target_pairs={{1,2},{3,4},{5,6},{7,8},{9,10},{11,12},{13,14},{15,16},{17,18},{19... | collective-permute-start | bytes 1658888 | tf_op jit(solution)/shard_map/ppermute | solution.py:614
  7.5 1.7 %collective-permute-start.2 = (f32[6,2,1,2880]{3,2,1,0:T(1,128)S(1)}, f32[6,2,1,2880]{3,2,1,0:T(1,128)S(1)}, u32[]{:S(2)}, u32[]{:S(2)}) collective-permute-start(f32[6,2,1,2880]{3,2,1,0:T(1,128)S(1)} %get-tuple-element.28), channel_id=1, source_target_pairs={{0,32},{64,96},{32,0},{96,64},{1,33},{65,97},{33,1},{97,65},{2,34}... | collective-permute-start | bytes 414728 | tf_op jit(solution)/shard_map/ppermute | solution.py:614
  9.2 0.7 collective-permute-start.3
  9.9 1.1 shard_map.178.inside_ref
  10.9 0.7 collective-permute-done.2.refs_2_.refs_6_
  11.7 3.6 %collective-permute-done.1.refs_1_.refs_5_ = f32[6,8,2880]{2,1,0:T(8,128)S(1)} collective-permute-done((f32[6,8,2880]{2,1,0:T(8,128)S(1)}, f32[6,8,2880]{2,1,0:T(8,128)S(1)}, u32[]{:S(2)}, u32[]{:S(2)}) %collective-permute-start.1) | collective-permute-done | bytes 552992 | tf_op jit(solution)/shard_map/ppermute | solution.py:614
  15.3 1.3 %shard_map.179 = (f32[5,2,8,2880]{3,2,1,0:T(8,128)S(1)}, f32[5,8,2880]{2,1,0:T(8,128)S(1)}, f32[5,8,2880]{2,1,0:T(8,128)S(1)}, f32[5,2,1,2880]{3,2,1,0:T(1,128)S(1)}, f32[5,2,1,2880]{3,2,1,0:T(1,128)S(1)}) custom-call(s32[2]{0:T(128)S(1)} %pad_add_fusion.side_ref, f32[5,2,8,2880]{3,2,1,0:T(8,128)S(1)} %get-tuple-element.22.n_ref, ...), custom_call_target="tpu_custom_call" | custom-call | flops 2000000 | bytes 1048576 | tf_op jit(solution)/shard_map/pallas_call | solution.py:71
  16.7 3.6 %collective-permute-start.5 = (f32[5,8,2880]{2,1,0:T(8,128)S(1)}, f32[5,8,2880]{2,1,0:T(8,128)S(1)}, u32[]{:S(2)}, u32[]{:S(2)}) collective-permute-start(f32[5,8,2880]{2,1,0:T(8,128)S(1)} %get-tuple-element.32), channel_id=1, source_target_pairs={{1,2},{3,4},{5,6},{7,8},{9,10},{11,12},{13,14},{15,16},{17,18},{19... | collective-permute-start | bytes 1382408 | tf_op jit(solution)/shard_map/ppermute | solution.py:614
  20.3 3.0 %collective-permute-start.6 = (f32[5,2,1,2880]{3,2,1,0:T(1,128)S(1)}, f32[5,2,1,2880]{3,2,1,0:T(1,128)S(1)}, u32[]{:S(2)}, u32[]{:S(2)}) collective-permute-start(f32[5,2,1,2880]{3,2,1,0:T(1,128)S(1)} %get-tuple-element.33), channel_id=1, source_target_pairs={{0,32},{64,96},{32,0},{96,64},{1,33},{65,97},{33,1},{97,65},{2,34}... | collective-permute-start | bytes 345608 | tf_op jit(solution)/shard_map/ppermute | solution.py:614
  24.0 1.1 shard_map.180.inside_ref
  25.5 1.1 collective-permute-done.5.refs_1_
  26.6 1.1 shard_map.181.mine_ref
  29.0 3.3 %shard_map.182._ = f32[23552,128]{1,0:T(8,128)S(1)} custom-call(f32[23,80,128]{2,1,0:T(8,128)S(1)} %shard_map.181.mine_ref), custom_call_target="tpu_custom_call" | custom-call | flops 8000000 | bytes 1048576 | tf_op jit(solution)/shard_map/pallas_call | solution.py:71
  32.4 13.0 %shard_map.183 = (f32[3072,128]{1,0:T(8,128)}, f32[23552,128]{1,0:T(8,128)S(1)}) custom-call(s32[1]{0:T(128)} %bitcast.core_ref, s32[32]{0:T(128)S(1)} %sub.16.starts_ref, s32[32]{0:T(128)S(1)} %copy-done.2, s32[23424]{0:T(1024)} %pad.11.order_hbm, f32[23,80,128]{2,1,0:T(8,128)S(1)} %collective-permute-done.8.other_ref, ...), custom_call_target="tpu_custom_call", output_to_operand_aliasing={{1}: (5, {})} | custom-call | flops 30000000 | bytes 1048576 | tf_op jit(solution)/shard_map/pallas_call | solution.py:71
  45.4 10.8 %all-to-all-start = ((f32[16,192,128]{2,1,0:T(8,128)}), f32[16,192,128]{2,1,0:T(8,128)S(1)}, u32[]{:S(2)}, u32[]{:S(2)}) async-start(f32[16,192,128]{2,1,0:T(8,128)} %bitcast.7), calls=%async_computation | async-start | bytes 3145728 | tf_op jit(solution)/shard_map/all_to_all | solution.py:686
  59.1 1.8 %copy-done.1 = f32[32,8,2880]{2,1,0:T(8,128)S(1)} copy-done((f32[32,8,2880]{2,1,0:T(8,128)S(1)}, f32[32,8,2880]{2,1,0:T(8,128)}, u32[]{:S(2)}) %copy-start.1) | copy-done | bytes 2949144
  61.0 7.8 %shard_map.176 = (s32[384]{0:T(512)S(1)}, f32[9,32,128]{2,1,0:T(8,128)S(1)}, f32[960,128]{1,0:T(8,128)S(1)}) custom-call(s32[1]{0:T(128)} %dynamic_slice.12.units_ref, s32[270]{0:T(512)S(1)} %dynamic-slice_reduce_fusion.owner_ref, s32[1152]{0:T(1024)S(1)} %get-tuple-element.41.rows_ref, s32[9,128]{1,0:T(8,128)S(1)} %get-tuple-element.40.sel_ref, ...), custom_call_target="tpu_custom_call" | custom-call | flops 20000000 | bytes 1048576 | tf_op jit(solution)/shard_map/pallas_call | solution.py:71
  68.9 12.4 %all-to-all-done = f32[16,192,128]{2,1,0:T(8,128)S(1)} async-done(((f32[16,192,128]{2,1,0:T(8,128)}), f32[16,192,128]{2,1,0:T(8,128)S(1)}, u32[]{:S(2)}, u32[]{:S(2)}) %all-to-all-start) | async-done | bytes 1572896 | tf_op jit(solution)/shard_map/all_to_all | solution.py:686
  81.3 6.8 %shard_map.184 = (f32[1,1,5,64,1080]{4,3,2,1,0:T(8,128)}, f32[2048,128]{1,0:T(8,128)}) custom-call(s32[1]{0:T(128)} %bitcast.core_ref, s32[1]{0:T(128)} %dynamic_slice.12.units_ref, s32[384]{0:T(512)S(1)} %get-tuple-element.21.table_ref, f32[3072,128]{1,0:T(8,128)S(1)} %bitcast.18, f32[960,128]{1,0:T(8,128)S(1)} %get-tuple-element.36.coef_ref, ...), custom_call_target="tpu_custom_call" | custom-call | flops 40000000 | bytes 1048576 | tf_op jit(solution)/shard_map/pallas_call | solution.py:71
  88.2 7.4 %all-to-all-start.1 = ((f32[128,16,128]{2,1,0:T(8,128)}), f32[128,16,128]{2,1,0:T(8,128)S(1)}, u32[]{:S(2)}, u32[]{:S(2)}) async-start(f32[128,16,128]{2,1,0:T(8,128)} %bitcast.10), calls=%async_computation.1 | async-start | bytes 2097152 | tf_op jit(solution)/shard_map/all_to_all | solution.py:691
  95.7 19.1 %all-to-all-done.1 = f32[128,16,128]{2,1,0:T(8,128)S(1)} async-done(((f32[128,16,128]{2,1,0:T(8,128)}), f32[128,16,128]{2,1,0:T(8,128)S(1)}, u32[]{:S(2)}, u32[]{:S(2)}) %all-to-all-start.1) | async-done | bytes 1048608 | tf_op jit(solution)/shard_map/all_to_all | solution.py:691
  114.8 4.3 %shard_map.185 = f32[1,7,96,512]{3,2,1,0:T(8,128)} custom-call(f32[2048,128]{1,0:T(8,128)S(1)} %bitcast.20, f32[35]{0:T(128)S(1)} %reshape.83.yield_ref, f32[14]{0:T(128)S(1)} %pad_maximum_fusion.rates_ref, f32[1,512]{1,0:T(1,128)S(1)} %copy-done.7, bf16[512,512]{1,0:T(8,128)(2,1)S(1)} %copy-done.3, bf16[512,512]{1,0:T(8,128)(2,1)S(1)} %copy-done.4, ...), custom_call_target="tpu_custom_call" | custom-call | flops 2000000000 | bytes 1048576 | tf_op jit(solution)/shard_map/pallas_call | solution.py:71
  (59 shorter events, 5.1 us)
Async XLA Ops:
  0.6 58.3 %copy-start = (s32[32,270,1]{1,2,0:T(1,128)S(1)}, s32[32,270,1]{1,2,0:T(1,128)}, u32[]{:S(2)}) copy-start(s32[32,270,1]{1,2,0:T(1,128)} %param.28) | copy-start | bytes 103684
  2.9 8.8 %collective-permute-start = (f32[6,8,2880]{2,1,0:T(8,128)S(1)}, f32[6,8,2880]{2,1,0:T(8,128)S(1)}, u32[]{:S(2)}, u32[]{:S(2)}) collective-permute-start(f32[6,8,2880]{2,1,0:T(8,128)S(1)} %get-tuple-element.26), channel_id=1, source_target_pairs={{0,1},{2,3},{4,5},{6,7},{8,9},{10,11},{12,13},{14,15},{16,17},{18,... | collective-permute-start | bytes 1658888 | tf_op jit(solution)/shard_map/ppermute | solution.py:614
  4.3 10.9 %collective-permute-start.1 = (f32[6,8,2880]{2,1,0:T(8,128)S(1)}, f32[6,8,2880]{2,1,0:T(8,128)S(1)}, u32[]{:S(2)}, u32[]{:S(2)}) collective-permute-start(f32[6,8,2880]{2,1,0:T(8,128)S(1)} %get-tuple-element.27), channel_id=1, source_target_pairs={{1,2},{3,4},{5,6},{7,8},{9,10},{11,12},{13,14},{15,16},{17,18},{19... | collective-permute-start | bytes 1658888 | tf_op jit(solution)/shard_map/ppermute | solution.py:614
  7.5 4.2 %collective-permute-start.2 = (f32[6,2,1,2880]{3,2,1,0:T(1,128)S(1)}, f32[6,2,1,2880]{3,2,1,0:T(1,128)S(1)}, u32[]{:S(2)}, u32[]{:S(2)}) collective-permute-start(f32[6,2,1,2880]{3,2,1,0:T(1,128)S(1)} %get-tuple-element.28), channel_id=1, source_target_pairs={{0,32},{64,96},{32,0},{96,64},{1,33},{65,97},{33,1},{97,65},{2,34}... | collective-permute-start | bytes 414728 | tf_op jit(solution)/shard_map/ppermute | solution.py:614
  9.2 2.5 %collective-permute-start.3 = (f32[6,2,1,2880]{3,2,1,0:T(1,128)S(1)}, f32[6,2,1,2880]{3,2,1,0:T(1,128)S(1)}, u32[]{:S(2)}, u32[]{:S(2)}) collective-permute-start(f32[6,2,1,2880]{3,2,1,0:T(1,128)S(1)} %get-tuple-element.29), channel_id=1, source_target_pairs={{32,64},{64,32},{33,65},{65,33},{34,66},{66,34},{35,67},{67,35},{3... | collective-permute-start | bytes 414728 | tf_op jit(solution)/shard_map/ppermute | solution.py:614
  16.6 8.9 %collective-permute-start.4 = (f32[5,8,2880]{2,1,0:T(8,128)S(1)}, f32[5,8,2880]{2,1,0:T(8,128)S(1)}, u32[]{:S(2)}, u32[]{:S(2)}) collective-permute-start(f32[5,8,2880]{2,1,0:T(8,128)S(1)} %get-tuple-element.31), channel_id=1, source_target_pairs={{0,1},{2,3},{4,5},{6,7},{8,9},{10,11},{12,13},{14,15},{16,17},{18,... | collective-permute-start | bytes 1382408 | tf_op jit(solution)/shard_map/ppermute | solution.py:614
  16.7 9.9 %collective-permute-start.5 = (f32[5,8,2880]{2,1,0:T(8,128)S(1)}, f32[5,8,2880]{2,1,0:T(8,128)S(1)}, u32[]{:S(2)}, u32[]{:S(2)}) collective-permute-start(f32[5,8,2880]{2,1,0:T(8,128)S(1)} %get-tuple-element.32), channel_id=1, source_target_pairs={{1,2},{3,4},{5,6},{7,8},{9,10},{11,12},{13,14},{15,16},{17,18},{19... | collective-permute-start | bytes 1382408 | tf_op jit(solution)/shard_map/ppermute | solution.py:614
  20.3 5.2 %collective-permute-start.6 = (f32[5,2,1,2880]{3,2,1,0:T(1,128)S(1)}, f32[5,2,1,2880]{3,2,1,0:T(1,128)S(1)}, u32[]{:S(2)}, u32[]{:S(2)}) collective-permute-start(f32[5,2,1,2880]{3,2,1,0:T(1,128)S(1)} %get-tuple-element.33), channel_id=1, source_target_pairs={{0,32},{64,96},{32,0},{96,64},{1,33},{65,97},{33,1},{97,65},{2,34}... | collective-permute-start | bytes 345608 | tf_op jit(solution)/shard_map/ppermute | solution.py:614
  23.3 2.2 %collective-permute-start.7 = (f32[5,2,1,2880]{3,2,1,0:T(1,128)S(1)}, f32[5,2,1,2880]{3,2,1,0:T(1,128)S(1)}, u32[]{:S(2)}, u32[]{:S(2)}) collective-permute-start(f32[5,2,1,2880]{3,2,1,0:T(1,128)S(1)} %get-tuple-element.34), channel_id=1, source_target_pairs={{32,64},{64,32},{33,65},{65,33},{34,66},{66,34},{35,67},{67,35},{3... | collective-permute-start | bytes 345608 | tf_op jit(solution)/shard_map/ppermute | solution.py:614
  25.0 2.8 %copy-start.8 = (s32[1,23040]{1,0:T(1,128)S(1)}, s32[1,23040]{1,0:T(1,128)}, u32[]{:S(2)}) copy-start(s32[1,23040]{1,0:T(1,128)} %param.26) | copy-start | bytes 276484
  25.0 3.7 %copy-start.2 = (s32[32]{0:T(128)S(1)}, s32[32]{0:T(128)}, u32[]{:S(2)}) copy-start(s32[32]{0:T(128)} %units_ref.1) | copy-start | bytes 388
  27.7 4.7 %collective-permute-start.8 = (f32[23,80,128]{2,1,0:T(8,128)S(1)}, f32[23,80,128]{2,1,0:T(8,128)S(1)}, u32[]{:S(2)}, u32[]{:S(2)}) collective-permute-start(f32[23,80,128]{2,1,0:T(8,128)S(1)} %shard_map.181.mine_ref), channel_id=1, source_target_pairs={{0,1},{2,3},{4,5},{6,7},{8,9},{10,11},{12,13},{14,15},{16,17},{18,... | collective-permute-start | bytes 2826248 | tf_op jit(solution)/shard_map/ppermute | solution.py:614
  45.4 12.7 %copy-start.10 = (f32[5,64]{1,0:T(8,128)S(1)}, f32[5,64]{1,0:T(8,128)}, u32[]{:S(2)}) copy-start(f32[5,64]{1,0:T(8,128)} %param.21) | copy-start | bytes 3844
  45.4 35.9 %all-to-all-start = ((f32[16,192,128]{2,1,0:T(8,128)}), f32[16,192,128]{2,1,0:T(8,128)S(1)}, u32[]{:S(2)}, u32[]{:S(2)}) async-start(f32[16,192,128]{2,1,0:T(8,128)} %bitcast.7), calls=%async_computation | async-start | bytes 3145728 | tf_op jit(solution)/shard_map/all_to_all | solution.py:686
  59.1 1.9 %copy-start.1 = (f32[32,8,2880]{2,1,0:T(8,128)S(1)}, f32[32,8,2880]{2,1,0:T(8,128)}, u32[]{:S(2)}) copy-start(f32[32,8,2880]{2,1,0:T(8,128)} %param.22) | copy-start | bytes 8847364
  81.3 14.3 %copy-start.9 = (f32[7,5]{1,0:T(8,128)S(1)}, f32[7,5]{1,0:T(8,128)}, u32[]{:S(2)}) copy-start(f32[7,5]{1,0:T(8,128)} %param.23) | copy-start | bytes 424
  88.1 7.6 %copy-start.11 = (f32[7]{0:T(128)S(1)}, f32[7]{0:T(128)}, u32[]{:S(2)}) copy-start(f32[7]{0:T(128)} %param.25) | copy-start | bytes 88
  88.1 7.6 %copy-start.12 = (f32[7]{0:T(128)S(1)}, f32[7]{0:T(128)}, u32[]{:S(2)}) copy-start(f32[7]{0:T(128)} %param.24) | copy-start | bytes 88
  88.1 26.7 %copy-start.3 = (bf16[512,512]{1,0:T(8,128)(2,1)S(1)}, bf16[512,512]{1,0:T(8,128)(2,1)}, u32[]{:S(2)}) copy-start(bf16[512,512]{1,0:T(8,128)(2,1)} %constant.128.clone.fwd_high) | copy-start | bytes 1572868
  88.1 26.7 %copy-start.4 = (bf16[512,512]{1,0:T(8,128)(2,1)S(1)}, bf16[512,512]{1,0:T(8,128)(2,1)}, u32[]{:S(2)}) copy-start(bf16[512,512]{1,0:T(8,128)(2,1)} %constant.129.clone.fwd_low) | copy-start | bytes 1572868
  88.1 26.7 %copy-start.5 = (bf16[512,512]{1,0:T(8,128)(2,1)S(1)}, bf16[512,512]{1,0:T(8,128)(2,1)}, u32[]{:S(2)}) copy-start(bf16[512,512]{1,0:T(8,128)(2,1)} %constant.130.clone.inv_high) | copy-start | bytes 1572868
  88.2 26.7 %copy-start.6 = (bf16[512,512]{1,0:T(8,128)(2,1)S(1)}, bf16[512,512]{1,0:T(8,128)(2,1)}, u32[]{:S(2)}) copy-start(bf16[512,512]{1,0:T(8,128)(2,1)} %constant.131.clone.inv_low) | copy-start | bytes 1572868
  88.2 26.7 %copy-start.7 = (f32[1,512]{1,0:T(1,128)S(1)}, f32[1,512]{1,0:T(1,128)}, u32[]{:S(2)}) copy-start(f32[1,512]{1,0:T(1,128)} %constant.145.waves_ref) | copy-start | bytes 6148
  88.2 26.6 %all-to-all-start.1 = ((f32[128,16,128]{2,1,0:T(8,128)}), f32[128,16,128]{2,1,0:T(8,128)S(1)}, u32[]{:S(2)}, u32[]{:S(2)}) async-start(f32[128,16,128]{2,1,0:T(8,128)} %bitcast.10), calls=%async_computation.1 | async-start | bytes 2097152 | tf_op jit(solution)/shard_map/all_to_all | solution.py:691

commit v11 on v10

--- a/solution.py
+++ b/solution.py
@@ -35,7 +35,7 @@
 PEER_ROWS = 3 * PIECE
 SLOT_BLOCKS = 9
 SLOTS_PAD = SLOT_BLOCKS * LANES
-ORDER_PAD = BAND_COLS + 3 * LANES
+ORDER_PAD = BAND_COLS + 4 * LANES
 UNROLL = 64
 ZERO_TUBE = SLOT_BLOCKS * 32
 ITEM_ROWS = 16
@@ -134,7 +134,8 @@
     )(side, density, wind_lon, wind_lat, wind_lev)
 
 
-def interior_kernel(n_ref, wlon_ref, wlat_ref, wlev_ref, out_ref):
+def interior_kernel(n_ref, wlon_ref, wlat_ref, wlev_ref, *refs):
+    out_ref = refs[-1]
     row = lax.broadcasted_iota(jnp.int32, (BAND_LATS, NLON), 0)
 
     @pl.loop(0, SPECIES)
@@ -151,10 +152,14 @@
             out_ref[s, j] = total + flux if j else total - flux
 
 
-def interior(density, winds):
+def interior(density, winds, ready=()):
     return call(
-        interior_kernel, on_chip((SPECIES, 2, BAND_LATS, NLON)), [HELD] * 4, VMEM, flops=8_000_000
-    )(density, *winds)
+        interior_kernel,
+        on_chip((SPECIES, 2, BAND_LATS, NLON)),
+        [HELD] * 4 + [HBM] * len(ready),
+        VMEM,
+        flops=8_000_000,
+    )(density, *winds, *ready)
 
 
 def faces_kernel(side_ref, n_ref, inside_ref, wlat_ref, wlev_ref, *refs, last):
@@ -220,6 +225,31 @@
     )(side, density, inside, *winds[1:], *halo, *wind_halo)
 
 
+def places_kernel(units_ref, order_ref, place_ref, starts_ref):
+    def advance(owner, start):
+        starts_ref[owner] = start
+        return start + units_ref[owner]
+
+    lax.fori_loop(0, units_ref.shape[0], advance, jnp.int32(0))
+    order = order_ref[...]
+    lat = jnp.zeros_like(order)
+    for i in range(1, BAND_LATS):
+        lat = lat + (order >= i * NLON).astype(jnp.int32)
+    place_ref[:, :BAND_COLS] = order + lat * (LON_PAD - NLON)
+    place_ref[:, BAND_COLS:] = jnp.zeros((1, ORDER_PAD - BAND_COLS), jnp.int32)
+
+
+def list_places(units, order):
+    places, starts = call(
+        places_kernel,
+        (sds((1, ORDER_PAD), jnp.int32), sds(units.shape, jnp.int32)),
+        [SMEM, VMEM],
+        (VMEM, SMEM),
+        flops=1_000_000,
+    )(units, order)
+    return places.reshape(-1), starts
+
+
 def prepare_kernel(
     units_ref, owner_ref, rows_ref, sel_ref, weight_ref, column_ref,
     table_ref, own_ref, coef_ref, count, blocks, table, picked,
@@ -412,8 +442,8 @@
 
 
 def solve_kernel(
-    core_ref, units_ref, table_ref, got_ref, coef_ref, weight_ref, north_ref, state_hbm, items_ref,
-    turned, natural, pairs, wide, tubes, state, sems,
+    core_ref, units_ref, table_ref, got_ref, coef_ref, weight_ref, north_ref, state_hbm, items_hbm,
+    turned, natural, pairs, wide, tubes, state, items_ref, sems, item_sems,
 ):
     core = core_ref[0]
     live = TUBE_COLS * units_ref[0]
@@ -482,19 +512,30 @@
     tubes[ZERO_TUBE * 8 :, :] = jnp.zeros((8, LANES), f32)
     sub = lax.broadcasted_iota(jnp.int32, (8, LANES), 0)
 
-    @pl.loop(0, PEERS // 4)
-    def _(step):
-        for i in range(4):
-            d = step * 4 + i
-            tiles = [
-                tubes[pl.ds(pl.multiple_of(table_ref[d * PEER_SLOTS + r] * 8, 8), 8), :] for r in range(PEER_SLOTS)
-            ]
-            mid = pltpu.roll(tiles[1], 5, axis=0)
-            top = pltpu.roll(tiles[2], 2, axis=0)
-            row = pl.multiple_of(d * ITEM_ROWS, ITEM_ROWS)
-            items_ref[pl.ds(row, 8), :] = jnp.where(sub < 5, tiles[0], mid)
-            items_ref[pl.ds(row + 8, 8), :] = jnp.where(sub < 2, mid, jnp.where(sub < 7, top, 0.0))
-
+    def send(quarter):
+        rows = pl.ds(quarter * PEERS // 4 * ITEM_ROWS, PEERS // 4 * ITEM_ROWS)
+        return pltpu.make_async_copy(items_ref.at[rows, :], items_hbm.at[rows, :], item_sems.at[quarter])
+
+    for part in range(4):
+
+        @pl.loop(part * PEERS // 16, (part + 1) * PEERS // 16)
+        def _(step):
+            for i in range(4):
+                d = step * 4 + i
+                tiles = [
+                    tubes[pl.ds(pl.multiple_of(table_ref[d * PEER_SLOTS + r] * 8, 8), 8), :]
+                    for r in range(PEER_SLOTS)
+                ]
+                mid = pltpu.roll(tiles[1], 5, axis=0)
+                top = pltpu.roll(tiles[2], 2, axis=0)
+                row = pl.multiple_of(d * ITEM_ROWS, ITEM_ROWS)
+                items_ref[pl.ds(row, 8), :] = jnp.where(sub < 5, tiles[0], mid)
+                items_ref[pl.ds(row + 8, 8), :] = jnp.where(sub < 2, mid, jnp.where(sub < 7, top, 0.0))
+
+        send(part).start()
+
+    for part in range(4):
+        send(part).wait()
     for s in range(SPECIES):
         leave(s).wait()
 
@@ -504,7 +545,7 @@
         solve_kernel,
         (sds((1, 1, SPECIES, NLEV, COL_CAP)), sds((PEERS * ITEM_ROWS, LANES))),
         [SMEM, SMEM, SMEM] + [HELD] * 4,
-        (HBM, VMEM),
+        (HBM, HBM),
         [
             pltpu.VMEM((2, 8 * LEVEL_PITCH, LANES), f32),
             pltpu.VMEM((3, 8 * PITCH, LANES), f32),
@@ -512,7 +553,9 @@
             pltpu.VMEM((3, LANES, LANES), f32),
             pltpu.VMEM((ZERO_TUBE * 8 + 8, LANES), f32),
             pltpu.VMEM((SPECIES, NLEV, COL_CAP), f32),
+            pltpu.VMEM((PEERS * ITEM_ROWS, LANES), f32),
             pltpu.SemaphoreType.DMA((SPECIES,)),
+            pltpu.SemaphoreType.DMA((4,)),
         ],
         flops=40_000_000,
     )(core, units, table, got, coefs, weights, north)
@@ -642,12 +685,8 @@
     neutrals, *rest = edges(side, neutrals, wind_lon, wind_lat, wind_lev)
     winds, first_halo = rest[:3], exchange(*rest[3:])
 
-    starts = jnp.cumsum(column_units) - column_units
+    places, starts = list_places(column_units, column_order)
     order = column_order[0]
-    lat = jnp.zeros_like(order)
-    for i in range(1, BAND_LATS):
-        lat = lat + (order >= i * NLON).astype(jnp.int32)
-    rows = jnp.pad(order + lat * (LON_PAD - NLON), (0, ORDER_PAD - BAND_COLS))
     own_units = column_units[lev].reshape(1)
     padded = jnp.pad(order, (0, SLOTS_PAD))
     own = lax.dynamic_slice(padded, (TUBE_COLS * starts[lev],), (SLOTS_PAD,))
@@ -674,7 +713,7 @@
 
     inside = interior(neutrals, winds)
     density, *halo = faces(side, neutrals, inside, winds, first_halo, first_halo, False)
-    inside = interior(density, winds)
+    inside = interior(density, winds, (places, starts))
     (mine,) = faces(side, density, inside, winds, exchange(*halo), first_halo, True)
     owners = lax.axis_size("lev")
     other = swap(mine, "lev", 0)
@@ -682,7 +721,7 @@
 
     core = (lev % 2).reshape(1)
     parity = [[2 * i + c for i in range(owners // 2)] for c in range(2)]
-    outgoing = pack(core, starts, column_units, rows, other, columns)
+    outgoing = pack(core, starts, column_units, places, other, columns)
     got = lax.all_to_all(
         outgoing.reshape(16, PEER_ROWS, LANES), "lev", 0, 0, axis_index_groups=parity, tiled=True
     ).reshape(16 * PEER_ROWS, LANES)

time: 120 us -> 118 us (0.983)
  waiting for transfers between devices: 37.4 us -> 35.6 us
    ppermute x9, waiting for transfers between devices: 5.89 us -> 4.33 us  [swap(): lax.ppermute(x, axis, [(i, i + 1) for i in lows] + [(i + 1, i) for i in l...]
    unnamed x26 -> x32, local copies, waits for them, and re-layouts: 1.93 us -> 3.08 us
    pallas_call x10 -> x11, Pallas kernels: 41.9 us -> 43 us  [placed(): return run(*(place(x, spec) for x, spec in zip(args, in_specs)))]
  transfers between devices with their start and end apart: 11 -> 11, of which waited for: 6 -> 4; matrix products, arithmetic and copies ran while one was open for 3% -> 2% of each run, Pallas kernels for 11% -> 12%
where the time goes in v11:
time: 118 us
  Pallas kernels  43 us (36%)
  waiting for transfers between devices  35.6 us (30%)
  starting transfers between devices  31.7 us (27%)
  local copies, waits for them, and re-layouts  5.07 us (4%)
  between operations  1.7 us (1%)
    pallas_call x11, Pallas kernels, placed(): return run(*(place(x, spec) for x, spec in zip(args, in_specs)))  43 us
    all_to_all x1, waiting for transfers between devices, on_device(): lax.all_to_all(items.reshape(PEERS, ITEM_ROWS, LANES), ('band', 'lev'), 0...  19.1 us
    ppermute x9, starting transfers between devices, swap(): lax.ppermute(x, axis, [(i, i + 1) for i in lows] + [(i + 1, i) for i in l...  14.4 us
    all_to_all x1, waiting for transfers between devices, on_device(): lax.all_to_all(outgoing.reshape(16, PEER_ROWS, LANES), 'lev', 0, 0, axis_...  12.2 us
    all_to_all x1, starting transfers between devices, on_device(): lax.all_to_all(outgoing.reshape(16, PEER_ROWS, LANES), 'lev', 0, 0, axis_...  9.85 us
    all_to_all x1, starting transfers between devices, on_device(): lax.all_to_all(items.reshape(PEERS, ITEM_ROWS, LANES), ('band', 'lev'), 0...  7.39 us
    ppermute x9, waiting for transfers between devices, swap(): lax.ppermute(x, axis, [(i, i + 1) for i in lows] + [(i + 1, i) for i in l...  4.33 us
    unnamed x32, local copies, waits for them, and re-layouts  3.08 us
  transfers between devices with their start and end apart: 11, of which 4 were waited for; matrix products, arithmetic and copies ran while one was open for 2% of the time, Pallas kernels for 12%

profile of v11, /device:TPU:1, one launch (start us, length us, event | category | flops | bytes accessed | tf_op | source)
XLA Modules:
  0.0 117.8 jit_solution(16568134895140139964)
XLA Ops:
  0.7 2.1 %shard_map.178 = (f32[5,2,8,2880]{3,2,1,0:T(8,128)S(1)}, f32[2,8,2880]{2,1,0:T(8,128)S(1)}, f32[2,8,2880]{2,1,0:T(8,128)S(1)}, f32[2,8,2880]{2,1,0:T(8,128)S(1)}...) custom-call(s32[2]{0:T(128)S(1)} %pad_add_fusion.side_ref, ...), custom_call_target="tpu_custom_call" | custom-call | flops 1000000 | bytes 1048576 | tf_op jit(solution)/shard_map/pallas_call | solution.py:71
  2.9 1.5 %collective-permute-start = (f32[6,8,2880]{2,1,0:T(8,128)S(1)}, f32[6,8,2880]{2,1,0:T(8,128)S(1)}, u32[]{:S(2)}, u32[]{:S(2)}) collective-permute-start(f32[6,8,2880]{2,1,0:T(8,128)S(1)} %get-tuple-element.30), channel_id=1, source_target_pairs={{0,1},{2,3},{4,5},{6,7},{8,9},{10,11},{12,13},{14,15},{16,17},{18,... | collective-permute-start | bytes 1658888 | tf_op jit(solution)/shard_map/ppermute | solution.py:657
  4.3 3.1 %collective-permute-start.1 = (f32[6,8,2880]{2,1,0:T(8,128)S(1)}, f32[6,8,2880]{2,1,0:T(8,128)S(1)}, u32[]{:S(2)}, u32[]{:S(2)}) collective-permute-start(f32[6,8,2880]{2,1,0:T(8,128)S(1)} %get-tuple-element.31), channel_id=1, source_target_pairs={{1,2},{3,4},{5,6},{7,8},{9,10},{11,12},{13,14},{15,16},{17,18},{19... | collective-permute-start | bytes 1658888 | tf_op jit(solution)/shard_map/ppermute | solution.py:657
  7.5 1.7 %collective-permute-start.2 = (f32[6,2,1,2880]{3,2,1,0:T(1,128)S(1)}, f32[6,2,1,2880]{3,2,1,0:T(1,128)S(1)}, u32[]{:S(2)}, u32[]{:S(2)}) collective-permute-start(f32[6,2,1,2880]{3,2,1,0:T(1,128)S(1)} %get-tuple-element.32), channel_id=1, source_target_pairs={{0,32},{64,96},{32,0},{96,64},{1,33},{65,97},{33,1},{97,65},{2,34}... | collective-permute-start | bytes 414728 | tf_op jit(solution)/shard_map/ppermute | solution.py:657
  9.2 0.7 collective-permute-start.3
  9.9 1.1 shard_map.179.inside_ref
  10.9 0.7 collective-permute-done.2.refs_2_.refs_6_
  11.7 3.6 %collective-permute-done.1.refs_1_.refs_5_ = f32[6,8,2880]{2,1,0:T(8,128)S(1)} collective-permute-done((f32[6,8,2880]{2,1,0:T(8,128)S(1)}, f32[6,8,2880]{2,1,0:T(8,128)S(1)}, u32[]{:S(2)}, u32[]{:S(2)}) %collective-permute-start.1) | collective-permute-done | bytes 552992 | tf_op jit(solution)/shard_map/ppermute | solution.py:657
  15.3 1.3 %shard_map.180 = (f32[5,2,8,2880]{3,2,1,0:T(8,128)S(1)}, f32[5,8,2880]{2,1,0:T(8,128)S(1)}, f32[5,8,2880]{2,1,0:T(8,128)S(1)}, f32[5,2,1,2880]{3,2,1,0:T(1,128)S(1)}, f32[5,2,1,2880]{3,2,1,0:T(1,128)S(1)}) custom-call(s32[2]{0:T(128)S(1)} %pad_add_fusion.side_ref, f32[5,2,8,2880]{3,2,1,0:T(8,128)S(1)} %get-tuple-element.26.n_ref, ...), custom_call_target="tpu_custom_call" | custom-call | flops 2000000 | bytes 1048576 | tf_op jit(solution)/shard_map/pallas_call | solution.py:71
  16.7 3.6 %collective-permute-start.5 = (f32[5,8,2880]{2,1,0:T(8,128)S(1)}, f32[5,8,2880]{2,1,0:T(8,128)S(1)}, u32[]{:S(2)}, u32[]{:S(2)}) collective-permute-start(f32[5,8,2880]{2,1,0:T(8,128)S(1)} %get-tuple-element.36), channel_id=1, source_target_pairs={{1,2},{3,4},{5,6},{7,8},{9,10},{11,12},{13,14},{15,16},{17,18},{19... | collective-permute-start | bytes 1382408 | tf_op jit(solution)/shard_map/ppermute | solution.py:657
  20.3 3.0 %collective-permute-start.6 = (f32[5,2,1,2880]{3,2,1,0:T(1,128)S(1)}, f32[5,2,1,2880]{3,2,1,0:T(1,128)S(1)}, u32[]{:S(2)}, u32[]{:S(2)}) collective-permute-start(f32[5,2,1,2880]{3,2,1,0:T(1,128)S(1)} %get-tuple-element.37), channel_id=1, source_target_pairs={{0,32},{64,96},{32,0},{96,64},{1,33},{65,97},{33,1},{97,65},{2,34}... | collective-permute-start | bytes 345608 | tf_op jit(solution)/shard_map/ppermute | solution.py:657
  24.0 1.3 %shard_map.176 = (s32[1,23552]{1,0:T(1,128)S(1)}, s32[32]{0:T(128)S(1)}) custom-call(s32[32]{0:T(128)S(1)} %copy-done.4, s32[1,23040]{1,0:T(1,128)S(1)} %copy-done.3), custom_call_target="tpu_custom_call" | custom-call | flops 1000000 | bytes 1048576 | tf_op jit(solution)/shard_map/pallas_call | solution.py:71
  26.5 1.1 shard_map.181.inside_ref
  27.6 1.1 shard_map.182.mine_ref
  28.8 3.3 %shard_map.183._ = f32[23552,128]{1,0:T(8,128)S(1)} custom-call(f32[23,80,128]{2,1,0:T(8,128)S(1)} %shard_map.182.mine_ref), custom_call_target="tpu_custom_call" | custom-call | flops 8000000 | bytes 1048576 | tf_op jit(solution)/shard_map/pallas_call | solution.py:71
  32.1 13.0 %shard_map.184 = (f32[3072,128]{1,0:T(8,128)}, f32[23552,128]{1,0:T(8,128)S(1)}) custom-call(s32[1]{0:T(128)} %bitcast.core_ref, s32[32]{0:T(128)S(1)} %copy-done.6, s32[32]{0:T(128)S(1)} %copy-done.4, s32[23552]{0:T(1024)} %bitcast.22, f32[23,80,128]{2,1,0:T(8,128)S(1)} %collective-permute-done.8.other_ref, ...), custom_call_target="tpu_custom_call", output_to_operand_aliasing={{1}: (5, {})} | custom-call | flops 30000000 | bytes 1048576 | tf_op jit(solution)/shard_map/pallas_call | solution.py:71
  45.1 9.8 %all-to-all-start = ((f32[16,192,128]{2,1,0:T(8,128)}), f32[16,192,128]{2,1,0:T(8,128)S(1)}, u32[]{:S(2)}, u32[]{:S(2)}) async-start(f32[16,192,128]{2,1,0:T(8,128)} %bitcast.7), calls=%async_computation | async-start | bytes 3145728 | tf_op jit(solution)/shard_map/all_to_all | solution.py:725
  58.1 1.8 %copy-done.1 = f32[32,8,2880]{2,1,0:T(8,128)S(1)} copy-done((f32[32,8,2880]{2,1,0:T(8,128)S(1)}, f32[32,8,2880]{2,1,0:T(8,128)}, u32[]{:S(2)}) %copy-start.1) | copy-done | bytes 2949144
  59.9 7.8 %shard_map.177 = (s32[384]{0:T(512)S(1)}, f32[9,32,128]{2,1,0:T(8,128)S(1)}, f32[960,128]{1,0:T(8,128)S(1)}) custom-call(s32[1]{0:T(128)} %dynamic_slice.12.units_ref, s32[270]{0:T(512)S(1)} %dynamic-slice_reduce_fusion.owner_ref, s32[1152]{0:T(1024)S(1)} %get-tuple-element.45.rows_ref, s32[9,128]{1,0:T(8,128)S(1)} %get-tuple-element.44.sel_ref, ...), custom_call_target="tpu_custom_call" | custom-call | flops 20000000 | bytes 1048576 | tf_op jit(solution)/shard_map/pallas_call | solution.py:71
  67.8 12.2 %all-to-all-done = f32[16,192,128]{2,1,0:T(8,128)S(1)} async-done(((f32[16,192,128]{2,1,0:T(8,128)}), f32[16,192,128]{2,1,0:T(8,128)S(1)}, u32[]{:S(2)}, u32[]{:S(2)}) %all-to-all-start) | async-done | bytes 1572896 | tf_op jit(solution)/shard_map/all_to_all | solution.py:725
  80.1 6.6 %shard_map.185 = (f32[1,1,5,64,1080]{4,3,2,1,0:T(8,128)}, f32[2048,128]{1,0:T(8,128)}) custom-call(s32[1]{0:T(128)} %bitcast.core_ref, s32[1]{0:T(128)} %dynamic_slice.12.units_ref, s32[384]{0:T(512)S(1)} %get-tuple-element.24.table_ref, f32[3072,128]{1,0:T(8,128)S(1)} %bitcast.18, f32[960,128]{1,0:T(8,128)S(1)} %get-tuple-element.40.coef_ref, ...), custom_call_target="tpu_custom_call" | custom-call | flops 40000000 | bytes 1048576 | tf_op jit(solution)/shard_map/pallas_call | solution.py:71
  86.7 7.4 %all-to-all-start.1 = ((f32[128,16,128]{2,1,0:T(8,128)}), f32[128,16,128]{2,1,0:T(8,128)S(1)}, u32[]{:S(2)}, u32[]{:S(2)}) async-start(f32[128,16,128]{2,1,0:T(8,128)} %bitcast.10), calls=%async_computation.1 | async-start | bytes 2097152 | tf_op jit(solution)/shard_map/all_to_all | solution.py:730
  94.3 19.1 %all-to-all-done.1 = f32[128,16,128]{2,1,0:T(8,128)S(1)} async-done(((f32[128,16,128]{2,1,0:T(8,128)}), f32[128,16,128]{2,1,0:T(8,128)S(1)}, u32[]{:S(2)}, u32[]{:S(2)}) %all-to-all-start.1) | async-done | bytes 1048608 | tf_op jit(solution)/shard_map/all_to_all | solution.py:730
  113.4 4.4 %shard_map.186 = f32[1,7,96,512]{3,2,1,0:T(8,128)} custom-call(f32[2048,128]{1,0:T(8,128)S(1)} %bitcast.20, f32[35]{0:T(128)S(1)} %reshape.59.yield_ref, f32[14]{0:T(128)S(1)} %pad_maximum_fusion.rates_ref, f32[1,512]{1,0:T(1,128)S(1)} %copy-done.11, bf16[512,512]{1,0:T(8,128)(2,1)S(1)} %copy-done.7, bf16[512,512]{1,0:T(8,128)(2,1)S(1)} %copy-done.8, ...), custom_call_target="tpu_custom_call" | custom-call | flops 2000000000 | bytes 1048576 | tf_op jit(solution)/shard_map/pallas_call | solution.py:71
  (60 shorter events, 4.8 us)
Async XLA Ops:
  0.6 57.3 %copy-start = (s32[32,270,1]{1,2,0:T(1,128)S(1)}, s32[32,270,1]{1,2,0:T(1,128)}, u32[]{:S(2)}) copy-start(s32[32,270,1]{1,2,0:T(1,128)} %param.28) | copy-start | bytes 103684
  2.9 8.8 %collective-permute-start = (f32[6,8,2880]{2,1,0:T(8,128)S(1)}, f32[6,8,2880]{2,1,0:T(8,128)S(1)}, u32[]{:S(2)}, u32[]{:S(2)}) collective-permute-start(f32[6,8,2880]{2,1,0:T(8,128)S(1)} %get-tuple-element.30), channel_id=1, source_target_pairs={{0,1},{2,3},{4,5},{6,7},{8,9},{10,11},{12,13},{14,15},{16,17},{18,... | collective-permute-start | bytes 1658888 | tf_op jit(solution)/shard_map/ppermute | solution.py:657
  4.3 10.9 %collective-permute-start.1 = (f32[6,8,2880]{2,1,0:T(8,128)S(1)}, f32[6,8,2880]{2,1,0:T(8,128)S(1)}, u32[]{:S(2)}, u32[]{:S(2)}) collective-permute-start(f32[6,8,2880]{2,1,0:T(8,128)S(1)} %get-tuple-element.31), channel_id=1, source_target_pairs={{1,2},{3,4},{5,6},{7,8},{9,10},{11,12},{13,14},{15,16},{17,18},{19... | collective-permute-start | bytes 1658888 | tf_op jit(solution)/shard_map/ppermute | solution.py:657
  7.5 4.2 %collective-permute-start.2 = (f32[6,2,1,2880]{3,2,1,0:T(1,128)S(1)}, f32[6,2,1,2880]{3,2,1,0:T(1,128)S(1)}, u32[]{:S(2)}, u32[]{:S(2)}) collective-permute-start(f32[6,2,1,2880]{3,2,1,0:T(1,128)S(1)} %get-tuple-element.32), channel_id=1, source_target_pairs={{0,32},{64,96},{32,0},{96,64},{1,33},{65,97},{33,1},{97,65},{2,34}... | collective-permute-start | bytes 414728 | tf_op jit(solution)/shard_map/ppermute | solution.py:657
  9.2 2.5 %collective-permute-start.3 = (f32[6,2,1,2880]{3,2,1,0:T(1,128)S(1)}, f32[6,2,1,2880]{3,2,1,0:T(1,128)S(1)}, u32[]{:S(2)}, u32[]{:S(2)}) collective-permute-start(f32[6,2,1,2880]{3,2,1,0:T(1,128)S(1)} %get-tuple-element.33), channel_id=1, source_target_pairs={{32,64},{64,32},{33,65},{65,33},{34,66},{66,34},{35,67},{67,35},{3... | collective-permute-start | bytes 414728 | tf_op jit(solution)/shard_map/ppermute | solution.py:657
  10.9 13.0 %copy-start.3 = (s32[1,23040]{1,0:T(1,128)S(1)}, s32[1,23040]{1,0:T(1,128)}, u32[]{:S(2)}) copy-start(s32[1,23040]{1,0:T(1,128)} %order_ref.1) | copy-start | bytes 276484
  10.9 13.0 %copy-start.4 = (s32[32]{0:T(128)S(1)}, s32[32]{0:T(128)}, u32[]{:S(2)}) copy-start(s32[32]{0:T(128)} %units_ref.3) | copy-start | bytes 388
  16.6 11.0 %collective-permute-start.4 = (f32[5,8,2880]{2,1,0:T(8,128)S(1)}, f32[5,8,2880]{2,1,0:T(8,128)S(1)}, u32[]{:S(2)}, u32[]{:S(2)}) collective-permute-start(f32[5,8,2880]{2,1,0:T(8,128)S(1)} %get-tuple-element.35), channel_id=1, source_target_pairs={{0,1},{2,3},{4,5},{6,7},{8,9},{10,11},{12,13},{14,15},{16,17},{18,... | collective-permute-start | bytes 1382408 | tf_op jit(solution)/shard_map/ppermute | solution.py:657
  16.7 10.9 %collective-permute-start.5 = (f32[5,8,2880]{2,1,0:T(8,128)S(1)}, f32[5,8,2880]{2,1,0:T(8,128)S(1)}, u32[]{:S(2)}, u32[]{:S(2)}) collective-permute-start(f32[5,8,2880]{2,1,0:T(8,128)S(1)} %get-tuple-element.36), channel_id=1, source_target_pairs={{1,2},{3,4},{5,6},{7,8},{9,10},{11,12},{13,14},{15,16},{17,18},{19... | collective-permute-start | bytes 1382408 | tf_op jit(solution)/shard_map/ppermute | solution.py:657
  20.3 7.3 %collective-permute-start.6 = (f32[5,2,1,2880]{3,2,1,0:T(1,128)S(1)}, f32[5,2,1,2880]{3,2,1,0:T(1,128)S(1)}, u32[]{:S(2)}, u32[]{:S(2)}) collective-permute-start(f32[5,2,1,2880]{3,2,1,0:T(1,128)S(1)} %get-tuple-element.37), channel_id=1, source_target_pairs={{0,32},{64,96},{32,0},{96,64},{1,33},{65,97},{33,1},{97,65},{2,34}... | collective-permute-start | bytes 345608 | tf_op jit(solution)/shard_map/ppermute | solution.py:657
  23.3 4.2 %collective-permute-start.7 = (f32[5,2,1,2880]{3,2,1,0:T(1,128)S(1)}, f32[5,2,1,2880]{3,2,1,0:T(1,128)S(1)}, u32[]{:S(2)}, u32[]{:S(2)}) collective-permute-start(f32[5,2,1,2880]{3,2,1,0:T(1,128)S(1)} %get-tuple-element.38), channel_id=1, source_target_pairs={{32,64},{64,32},{33,65},{65,33},{34,66},{66,34},{35,67},{67,35},{3... | collective-permute-start | bytes 345608 | tf_op jit(solution)/shard_map/ppermute | solution.py:657
  28.7 3.4 %copy-start.6 = (s32[32]{0:T(128)S(1)}, s32[32]{0:T(128)}, u32[]{:S(2)}) copy-start(s32[32]{0:T(128)} %copy-done.5) | copy-start | bytes 388
  28.7 3.4 %collective-permute-start.8 = (f32[23,80,128]{2,1,0:T(8,128)S(1)}, f32[23,80,128]{2,1,0:T(8,128)S(1)}, u32[]{:S(2)}, u32[]{:S(2)}) collective-permute-start(f32[23,80,128]{2,1,0:T(8,128)S(1)} %shard_map.182.mine_ref), channel_id=1, source_target_pairs={{0,1},{2,3},{4,5},{6,7},{8,9},{10,11},{12,13},{14,15},{16,17},{18,... | collective-permute-start | bytes 2826248 | tf_op jit(solution)/shard_map/ppermute | solution.py:657
  45.1 12.0 %copy-start.13 = (f32[5,64]{1,0:T(8,128)S(1)}, f32[5,64]{1,0:T(8,128)}, u32[]{:S(2)}) copy-start(f32[5,64]{1,0:T(8,128)} %param.21) | copy-start | bytes 3844
  45.1 34.9 %all-to-all-start = ((f32[16,192,128]{2,1,0:T(8,128)}), f32[16,192,128]{2,1,0:T(8,128)S(1)}, u32[]{:S(2)}, u32[]{:S(2)}) async-start(f32[16,192,128]{2,1,0:T(8,128)} %bitcast.7), calls=%async_computation | async-start | bytes 3145728 | tf_op jit(solution)/shard_map/all_to_all | solution.py:725
  80.1 14.1 %copy-start.12 = (f32[7,5]{1,0:T(8,128)S(1)}, f32[7,5]{1,0:T(8,128)}, u32[]{:S(2)}) copy-start(f32[7,5]{1,0:T(8,128)} %param.23) | copy-start | bytes 424
  86.7 7.6 %copy-start.14 = (f32[7]{0:T(128)S(1)}, f32[7]{0:T(128)}, u32[]{:S(2)}) copy-start(f32[7]{0:T(128)} %param.25) | copy-start | bytes 88
  86.7 7.6 %copy-start.15 = (f32[7]{0:T(128)S(1)}, f32[7]{0:T(128)}, u32[]{:S(2)}) copy-start(f32[7]{0:T(128)} %param.24) | copy-start | bytes 88
  86.7 26.7 %copy-start.7 = (bf16[512,512]{1,0:T(8,128)(2,1)S(1)}, bf16[512,512]{1,0:T(8,128)(2,1)}, u32[]{:S(2)}) copy-start(bf16[512,512]{1,0:T(8,128)(2,1)} %constant.116.clone.fwd_high) | copy-start | bytes 1572868
  86.7 26.7 %copy-start.8 = (bf16[512,512]{1,0:T(8,128)(2,1)S(1)}, bf16[512,512]{1,0:T(8,128)(2,1)}, u32[]{:S(2)}) copy-start(bf16[512,512]{1,0:T(8,128)(2,1)} %constant.117.clone.fwd_low) | copy-start | bytes 1572868
  86.7 26.7 %copy-start.9 = (bf16[512,512]{1,0:T(8,128)(2,1)S(1)}, bf16[512,512]{1,0:T(8,128)(2,1)}, u32[]{:S(2)}) copy-start(bf16[512,512]{1,0:T(8,128)(2,1)} %constant.118.clone.inv_high) | copy-start | bytes 1572868
  86.7 26.7 %copy-start.10 = (bf16[512,512]{1,0:T(8,128)(2,1)S(1)}, bf16[512,512]{1,0:T(8,128)(2,1)}, u32[]{:S(2)}) copy-start(bf16[512,512]{1,0:T(8,128)(2,1)} %constant.119.clone.inv_low) | copy-start | bytes 1572868
  86.7 26.7 %copy-start.11 = (f32[1,512]{1,0:T(1,128)S(1)}, f32[1,512]{1,0:T(1,128)}, u32[]{:S(2)}) copy-start(f32[1,512]{1,0:T(1,128)} %constant.131.waves_ref) | copy-start | bytes 6148
  86.7 26.6 %all-to-all-start.1 = ((f32[128,16,128]{2,1,0:T(8,128)}), f32[128,16,128]{2,1,0:T(8,128)S(1)}, u32[]{:S(2)}, u32[]{:S(2)}) async-start(f32[128,16,128]{2,1,0:T(8,128)} %bitcast.10), calls=%async_computation.1 | async-start | bytes 2097152 | tf_op jit(solution)/shard_map/all_to_all | solution.py:730
  (3 other events, 3.0 us)

commit v12 on v11

--- a/solution.py
+++ b/solution.py
@@ -156,7 +156,7 @@
     return call(
         interior_kernel,
         on_chip((SPECIES, 2, BAND_LATS, NLON)),
-        [HELD] * 4 + [HBM] * len(ready),
+        [HELD] * (4 + len(ready)),
         VMEM,
         flops=8_000_000,
     )(density, *winds, *ready)
@@ -242,7 +242,7 @@
 def list_places(units, order):
     places, starts = call(
         places_kernel,
-        (sds((1, ORDER_PAD), jnp.int32), sds(units.shape, jnp.int32)),
+        (on_chip((1, ORDER_PAD), jnp.int32), sds(units.shape, jnp.int32)),
         [SMEM, VMEM],
         (VMEM, SMEM),
         flops=1_000_000,
@@ -371,10 +371,10 @@
 
 
 def pack_kernel(
-    core_ref, starts_ref, units_ref, order_hbm, other_ref, _,
+    core_ref, starts_ref, units_ref, list_ref, other_ref, _,
     out_hbm, table_ref, order_ref, planes, msg_ref, sems, order_sem,
 ):
-    fetch = pltpu.make_async_copy(order_hbm, order_ref, order_sem)
+    fetch = pltpu.make_async_copy(list_ref, order_ref, order_sem)
     fetch.start()
     core = core_ref[0]
     fill_planes(planes, other_ref)
@@ -426,7 +426,7 @@
     outgoing, _ = call(
         pack_kernel,
         (sds((16 * PEER_ROWS, LANES)), on_chip((BAND_LATS * LON_PAD, LANES))),
-        [SMEM, SMEM, SMEM, HBM, HELD, HELD],
+        [SMEM, SMEM, SMEM, HELD, HELD, HELD],
         (HBM, VMEM),
         [
             pltpu.SMEM((ORDER_PAD,), jnp.int32),
@@ -711,9 +711,9 @@
         jnp.swapaxes(coefs, 2, 3).reshape(-1, 1),
     )
 
-    inside = interior(neutrals, winds)
+    inside = interior(neutrals, winds, (places,))
     density, *halo = faces(side, neutrals, inside, winds, first_halo, first_halo, False)
-    inside = interior(density, winds, (places, starts))
+    inside = interior(density, winds)
     (mine,) = faces(side, density, inside, winds, exchange(*halo), first_halo, True)
     owners = lax.axis_size("lev")
     other = swap(mine, "lev", 0)

time: 118 us -> 118 us (level)
    unnamed x32 -> x26, local copies, waits for them, and re-layouts: 3.08 us -> 1.92 us
  transfers between devices with their start and end apart: 11 -> 11, of which waited for: 4 -> 5; matrix products, arithmetic and copies ran while one was open for 2% -> 2% of each run, Pallas kernels for 12% -> 12%
where the time goes in v12:
time: 118 us
  Pallas kernels  43.2 us (37%)
  waiting for transfers between devices  35.7 us (30%)
  starting transfers between devices  32.6 us (28%)
  local copies, waits for them, and re-layouts  3.96 us (3%)
  between operations  1.67 us (1%)
    pallas_call x11, Pallas kernels, placed(): return run(*(place(x, spec) for x, spec in zip(args, in_specs)))  43.2 us
    all_to_all x1, waiting for transfers between devices, on_device(): lax.all_to_all(items.reshape(PEERS, ITEM_ROWS, LANES), ('band', 'lev'), 0...  19.1 us
    ppermute x9, starting transfers between devices, swap(): lax.ppermute(x, axis, [(i, i + 1) for i in lows] + [(i + 1, i) for i in l...  14.4 us
    all_to_all x1, waiting for transfers between devices, on_device(): lax.all_to_all(outgoing.reshape(16, PEER_ROWS, LANES), 'lev', 0, 0, axis_...  12.1 us
    all_to_all x1, starting transfers between devices, on_device(): lax.all_to_all(outgoing.reshape(16, PEER_ROWS, LANES), 'lev', 0, 0, axis_...  10.8 us
    all_to_all x1, starting transfers between devices, on_device(): lax.all_to_all(items.reshape(PEERS, ITEM_ROWS, LANES), ('band', 'lev'), 0...  7.39 us
    ppermute x9, waiting for transfers between devices, swap(): lax.ppermute(x, axis, [(i, i + 1) for i in lows] + [(i + 1, i) for i in l...  4.51 us
  transfers between devices with their start and end apart: 11, of which 5 were waited for; matrix products, arithmetic and copies ran while one was open for 2% of the time, Pallas kernels for 12%

profile of v12, /device:TPU:1, one launch (start us, length us, event | category | flops | bytes accessed | tf_op | source)
XLA Modules:
  0.0 117.8 jit_solution(6508779056134660922)
XLA Ops:
  0.8 2.1 %shard_map.178 = (f32[5,2,8,2880]{3,2,1,0:T(8,128)S(1)}, f32[2,8,2880]{2,1,0:T(8,128)S(1)}, f32[2,8,2880]{2,1,0:T(8,128)S(1)}, f32[2,8,2880]{2,1,0:T(8,128)S(1)}...) custom-call(s32[2]{0:T(128)S(1)} %pad_add_fusion.side_ref, ...), custom_call_target="tpu_custom_call" | custom-call | flops 1000000 | bytes 1048576 | tf_op jit(solution)/shard_map/pallas_call | solution.py:71
  2.9 1.5 %collective-permute-start = (f32[6,8,2880]{2,1,0:T(8,128)S(1)}, f32[6,8,2880]{2,1,0:T(8,128)S(1)}, u32[]{:S(2)}, u32[]{:S(2)}) collective-permute-start(f32[6,8,2880]{2,1,0:T(8,128)S(1)} %get-tuple-element.30), channel_id=1, source_target_pairs={{0,1},{2,3},{4,5},{6,7},{8,9},{10,11},{12,13},{14,15},{16,17},{18,... | collective-permute-start | bytes 1658888 | tf_op jit(solution)/shard_map/ppermute | solution.py:657
  4.4 3.1 %collective-permute-start.1 = (f32[6,8,2880]{2,1,0:T(8,128)S(1)}, f32[6,8,2880]{2,1,0:T(8,128)S(1)}, u32[]{:S(2)}, u32[]{:S(2)}) collective-permute-start(f32[6,8,2880]{2,1,0:T(8,128)S(1)} %get-tuple-element.31), channel_id=1, source_target_pairs={{1,2},{3,4},{5,6},{7,8},{9,10},{11,12},{13,14},{15,16},{17,18},{19... | collective-permute-start | bytes 1658888 | tf_op jit(solution)/shard_map/ppermute | solution.py:657
  7.5 1.7 %collective-permute-start.2 = (f32[6,2,1,2880]{3,2,1,0:T(1,128)S(1)}, f32[6,2,1,2880]{3,2,1,0:T(1,128)S(1)}, u32[]{:S(2)}, u32[]{:S(2)}) collective-permute-start(f32[6,2,1,2880]{3,2,1,0:T(1,128)S(1)} %get-tuple-element.32), channel_id=1, source_target_pairs={{0,32},{64,96},{32,0},{96,64},{1,33},{65,97},{33,1},{97,65},{2,34}... | collective-permute-start | bytes 414728 | tf_op jit(solution)/shard_map/ppermute | solution.py:657
  9.9 1.3 %shard_map.176 = (s32[1,23552]{1,0:T(1,128)S(1)}, s32[32]{0:T(128)S(1)}) custom-call(s32[32]{0:T(128)S(1)} %copy-done.3, s32[1,23040]{1,0:T(1,128)S(1)} %copy-done.2), custom_call_target="tpu_custom_call" | custom-call | flops 1000000 | bytes 1048576 | tf_op jit(solution)/shard_map/pallas_call | solution.py:71
  11.2 1.1 shard_map.179.inside_ref
  12.3 2.9 %collective-permute-done.1.refs_1_.refs_5_ = f32[6,8,2880]{2,1,0:T(8,128)S(1)} collective-permute-done((f32[6,8,2880]{2,1,0:T(8,128)S(1)}, f32[6,8,2880]{2,1,0:T(8,128)S(1)}, u32[]{:S(2)}, u32[]{:S(2)}) %collective-permute-start.1) | collective-permute-done | bytes 552992 | tf_op jit(solution)/shard_map/ppermute | solution.py:657
  15.3 1.3 %shard_map.180 = (f32[5,2,8,2880]{3,2,1,0:T(8,128)S(1)}, f32[5,8,2880]{2,1,0:T(8,128)S(1)}, f32[5,8,2880]{2,1,0:T(8,128)S(1)}, f32[5,2,1,2880]{3,2,1,0:T(1,128)S(1)}, f32[5,2,1,2880]{3,2,1,0:T(1,128)S(1)}) custom-call(s32[2]{0:T(128)S(1)} %pad_add_fusion.side_ref, f32[5,2,8,2880]{3,2,1,0:T(8,128)S(1)} %get-tuple-element.26.n_ref, ...), custom_call_target="tpu_custom_call" | custom-call | flops 2000000 | bytes 1048576 | tf_op jit(solution)/shard_map/pallas_call | solution.py:71
  16.7 3.6 %collective-permute-start.5 = (f32[5,8,2880]{2,1,0:T(8,128)S(1)}, f32[5,8,2880]{2,1,0:T(8,128)S(1)}, u32[]{:S(2)}, u32[]{:S(2)}) collective-permute-start(f32[5,8,2880]{2,1,0:T(8,128)S(1)} %get-tuple-element.36), channel_id=1, source_target_pairs={{1,2},{3,4},{5,6},{7,8},{9,10},{11,12},{13,14},{15,16},{17,18},{19... | collective-permute-start | bytes 1382408 | tf_op jit(solution)/shard_map/ppermute | solution.py:657
  20.3 3.0 %collective-permute-start.6 = (f32[5,2,1,2880]{3,2,1,0:T(1,128)S(1)}, f32[5,2,1,2880]{3,2,1,0:T(1,128)S(1)}, u32[]{:S(2)}, u32[]{:S(2)}) collective-permute-start(f32[5,2,1,2880]{3,2,1,0:T(1,128)S(1)} %get-tuple-element.37), channel_id=1, source_target_pairs={{0,32},{64,96},{32,0},{96,64},{1,33},{65,97},{33,1},{97,65},{2,34}... | collective-permute-start | bytes 345608 | tf_op jit(solution)/shard_map/ppermute | solution.py:657
  24.0 1.1 shard_map.181.inside_ref
  25.5 1.1 collective-permute-done.5.refs_1_
  26.6 1.1 shard_map.182.mine_ref
  27.8 3.3 %shard_map.183._ = f32[23552,128]{1,0:T(8,128)S(1)} custom-call(f32[23,80,128]{2,1,0:T(8,128)S(1)} %shard_map.182.mine_ref), custom_call_target="tpu_custom_call" | custom-call | flops 8000000 | bytes 1048576 | tf_op jit(solution)/shard_map/pallas_call | solution.py:71
  31.1 13.0 %shard_map.184 = (f32[3072,128]{1,0:T(8,128)}, f32[23552,128]{1,0:T(8,128)S(1)}) custom-call(s32[1]{0:T(128)} %bitcast.core_ref, s32[32]{0:T(128)S(1)} %get-tuple-element.23.starts_ref, s32[32]{0:T(128)S(1)} %copy-done.3, s32[23552]{0:T(1024)S(1)} %bitcast.22, f32[23,80,128]{2,1,0:T(8,128)S(1)} %collective-permute-done.8.other_ref, ...), custom_call_target="tpu_custom_call", output_to_operand_aliasing={{1}: (5, {})} | custom-call | flops 30000000 | bytes 1048576 | tf_op jit(solution)/shard_map/pallas_call | solution.py:71
  44.2 10.8 %all-to-all-start = ((f32[16,192,128]{2,1,0:T(8,128)}), f32[16,192,128]{2,1,0:T(8,128)S(1)}, u32[]{:S(2)}, u32[]{:S(2)}) async-start(f32[16,192,128]{2,1,0:T(8,128)} %bitcast.7), calls=%async_computation | async-start | bytes 3145728 | tf_op jit(solution)/shard_map/all_to_all | solution.py:725
  55.8 0.7 dynamic_slice.12.units_ref
  58.2 1.8 %copy-done.1 = f32[32,8,2880]{2,1,0:T(8,128)S(1)} copy-done((f32[32,8,2880]{2,1,0:T(8,128)S(1)}, f32[32,8,2880]{2,1,0:T(8,128)}, u32[]{:S(2)}) %copy-start.1) | copy-done | bytes 2949144
  60.0 7.8 %shard_map.177 = (s32[384]{0:T(512)S(1)}, f32[9,32,128]{2,1,0:T(8,128)S(1)}, f32[960,128]{1,0:T(8,128)S(1)}) custom-call(s32[1]{0:T(128)} %dynamic_slice.12.units_ref, s32[270]{0:T(512)S(1)} %dynamic-slice_reduce_fusion.owner_ref, s32[1152]{0:T(1024)S(1)} %get-tuple-element.45.rows_ref, s32[9,128]{1,0:T(8,128)S(1)} %get-tuple-element.44.sel_ref, ...), custom_call_target="tpu_custom_call" | custom-call | flops 20000000 | bytes 1048576 | tf_op jit(solution)/shard_map/pallas_call | solution.py:71
  68.0 12.1 %all-to-all-done = f32[16,192,128]{2,1,0:T(8,128)S(1)} async-done(((f32[16,192,128]{2,1,0:T(8,128)}), f32[16,192,128]{2,1,0:T(8,128)S(1)}, u32[]{:S(2)}, u32[]{:S(2)}) %all-to-all-start) | async-done | bytes 1572896 | tf_op jit(solution)/shard_map/all_to_all | solution.py:725
  80.1 6.7 %shard_map.185 = (f32[1,1,5,64,1080]{4,3,2,1,0:T(8,128)}, f32[2048,128]{1,0:T(8,128)}) custom-call(s32[1]{0:T(128)} %bitcast.core_ref, s32[1]{0:T(128)} %dynamic_slice.12.units_ref, s32[384]{0:T(512)S(1)} %get-tuple-element.24.table_ref, f32[3072,128]{1,0:T(8,128)S(1)} %bitcast.18, f32[960,128]{1,0:T(8,128)S(1)} %get-tuple-element.40.coef_ref, ...), custom_call_target="tpu_custom_call" | custom-call | flops 40000000 | bytes 1048576 | tf_op jit(solution)/shard_map/pallas_call | solution.py:71
  86.8 7.4 %all-to-all-start.1 = ((f32[128,16,128]{2,1,0:T(8,128)}), f32[128,16,128]{2,1,0:T(8,128)S(1)}, u32[]{:S(2)}, u32[]{:S(2)}) async-start(f32[128,16,128]{2,1,0:T(8,128)} %bitcast.10), calls=%async_computation.1 | async-start | bytes 2097152 | tf_op jit(solution)/shard_map/all_to_all | solution.py:730
  94.4 19.1 %all-to-all-done.1 = f32[128,16,128]{2,1,0:T(8,128)S(1)} async-done(((f32[128,16,128]{2,1,0:T(8,128)}), f32[128,16,128]{2,1,0:T(8,128)S(1)}, u32[]{:S(2)}, u32[]{:S(2)}) %all-to-all-start.1) | async-done | bytes 1048608 | tf_op jit(solution)/shard_map/all_to_all | solution.py:730
  113.5 4.3 %shard_map.186 = f32[1,7,96,512]{3,2,1,0:T(8,128)} custom-call(f32[2048,128]{1,0:T(8,128)S(1)} %bitcast.20, f32[35]{0:T(128)S(1)} %reshape.59.yield_ref, f32[14]{0:T(128)S(1)} %pad_maximum_fusion.rates_ref, f32[1,512]{1,0:T(1,128)S(1)} %copy-done.8, bf16[512,512]{1,0:T(8,128)(2,1)S(1)} %copy-done.4, bf16[512,512]{1,0:T(8,128)(2,1)S(1)} %copy-done.5, ...), custom_call_target="tpu_custom_call" | custom-call | flops 2000000000 | bytes 1048576 | tf_op jit(solution)/shard_map/pallas_call | solution.py:71
  (54 shorter events, 4.1 us)
Async XLA Ops:
  0.6 57.4 %copy-start = (s32[32,270,1]{1,2,0:T(1,128)S(1)}, s32[32,270,1]{1,2,0:T(1,128)}, u32[]{:S(2)}) copy-start(s32[32,270,1]{1,2,0:T(1,128)} %param.28) | copy-start | bytes 103684
  0.6 9.2 %copy-start.2 = (s32[1,23040]{1,0:T(1,128)S(1)}, s32[1,23040]{1,0:T(1,128)}, u32[]{:S(2)}) copy-start(s32[1,23040]{1,0:T(1,128)} %order_ref.1) | copy-start | bytes 276484
  0.7 9.2 %copy-start.3 = (s32[32]{0:T(128)S(1)}, s32[32]{0:T(128)}, u32[]{:S(2)}) copy-start(s32[32]{0:T(128)} %units_ref.3) | copy-start | bytes 388
  2.9 9.4 %collective-permute-start = (f32[6,8,2880]{2,1,0:T(8,128)S(1)}, f32[6,8,2880]{2,1,0:T(8,128)S(1)}, u32[]{:S(2)}, u32[]{:S(2)}) collective-permute-start(f32[6,8,2880]{2,1,0:T(8,128)S(1)} %get-tuple-element.30), channel_id=1, source_target_pairs={{0,1},{2,3},{4,5},{6,7},{8,9},{10,11},{12,13},{14,15},{16,17},{18,... | collective-permute-start | bytes 1658888 | tf_op jit(solution)/shard_map/ppermute | solution.py:657
  4.4 10.9 %collective-permute-start.1 = (f32[6,8,2880]{2,1,0:T(8,128)S(1)}, f32[6,8,2880]{2,1,0:T(8,128)S(1)}, u32[]{:S(2)}, u32[]{:S(2)}) collective-permute-start(f32[6,8,2880]{2,1,0:T(8,128)S(1)} %get-tuple-element.31), channel_id=1, source_target_pairs={{1,2},{3,4},{5,6},{7,8},{9,10},{11,12},{13,14},{15,16},{17,18},{19... | collective-permute-start | bytes 1658888 | tf_op jit(solution)/shard_map/ppermute | solution.py:657
  7.5 4.8 %collective-permute-start.2 = (f32[6,2,1,2880]{3,2,1,0:T(1,128)S(1)}, f32[6,2,1,2880]{3,2,1,0:T(1,128)S(1)}, u32[]{:S(2)}, u32[]{:S(2)}) collective-permute-start(f32[6,2,1,2880]{3,2,1,0:T(1,128)S(1)} %get-tuple-element.32), channel_id=1, source_target_pairs={{0,32},{64,96},{32,0},{96,64},{1,33},{65,97},{33,1},{97,65},{2,34}... | collective-permute-start | bytes 414728 | tf_op jit(solution)/shard_map/ppermute | solution.py:657
  9.2 3.1 %collective-permute-start.3 = (f32[6,2,1,2880]{3,2,1,0:T(1,128)S(1)}, f32[6,2,1,2880]{3,2,1,0:T(1,128)S(1)}, u32[]{:S(2)}, u32[]{:S(2)}) collective-permute-start(f32[6,2,1,2880]{3,2,1,0:T(1,128)S(1)} %get-tuple-element.33), channel_id=1, source_target_pairs={{32,64},{64,32},{33,65},{65,33},{34,66},{66,34},{35,67},{67,35},{3... | collective-permute-start | bytes 414728 | tf_op jit(solution)/shard_map/ppermute | solution.py:657
  16.6 8.9 %collective-permute-start.4 = (f32[5,8,2880]{2,1,0:T(8,128)S(1)}, f32[5,8,2880]{2,1,0:T(8,128)S(1)}, u32[]{:S(2)}, u32[]{:S(2)}) collective-permute-start(f32[5,8,2880]{2,1,0:T(8,128)S(1)} %get-tuple-element.35), channel_id=1, source_target_pairs={{0,1},{2,3},{4,5},{6,7},{8,9},{10,11},{12,13},{14,15},{16,17},{18,... | collective-permute-start | bytes 1382408 | tf_op jit(solution)/shard_map/ppermute | solution.py:657
  16.7 9.9 %collective-permute-start.5 = (f32[5,8,2880]{2,1,0:T(8,128)S(1)}, f32[5,8,2880]{2,1,0:T(8,128)S(1)}, u32[]{:S(2)}, u32[]{:S(2)}) collective-permute-start(f32[5,8,2880]{2,1,0:T(8,128)S(1)} %get-tuple-element.36), channel_id=1, source_target_pairs={{1,2},{3,4},{5,6},{7,8},{9,10},{11,12},{13,14},{15,16},{17,18},{19... | collective-permute-start | bytes 1382408 | tf_op jit(solution)/shard_map/ppermute | solution.py:657
  20.3 5.2 %collective-permute-start.6 = (f32[5,2,1,2880]{3,2,1,0:T(1,128)S(1)}, f32[5,2,1,2880]{3,2,1,0:T(1,128)S(1)}, u32[]{:S(2)}, u32[]{:S(2)}) collective-permute-start(f32[5,2,1,2880]{3,2,1,0:T(1,128)S(1)} %get-tuple-element.37), channel_id=1, source_target_pairs={{0,32},{64,96},{32,0},{96,64},{1,33},{65,97},{33,1},{97,65},{2,34}... | collective-permute-start | bytes 345608 | tf_op jit(solution)/shard_map/ppermute | solution.py:657
  23.3 2.2 %collective-permute-start.7 = (f32[5,2,1,2880]{3,2,1,0:T(1,128)S(1)}, f32[5,2,1,2880]{3,2,1,0:T(1,128)S(1)}, u32[]{:S(2)}, u32[]{:S(2)}) collective-permute-start(f32[5,2,1,2880]{3,2,1,0:T(1,128)S(1)} %get-tuple-element.38), channel_id=1, source_target_pairs={{32,64},{64,32},{33,65},{65,33},{34,66},{66,34},{35,67},{67,35},{3... | collective-permute-start | bytes 345608 | tf_op jit(solution)/shard_map/ppermute | solution.py:657
  27.7 3.4 %collective-permute-start.8 = (f32[23,80,128]{2,1,0:T(8,128)S(1)}, f32[23,80,128]{2,1,0:T(8,128)S(1)}, u32[]{:S(2)}, u32[]{:S(2)}) collective-permute-start(f32[23,80,128]{2,1,0:T(8,128)S(1)} %shard_map.182.mine_ref), channel_id=1, source_target_pairs={{0,1},{2,3},{4,5},{6,7},{8,9},{10,11},{12,13},{14,15},{16,17},{18,... | collective-permute-start | bytes 2826248 | tf_op jit(solution)/shard_map/ppermute | solution.py:657
  44.2 13.0 %copy-start.10 = (f32[5,64]{1,0:T(8,128)S(1)}, f32[5,64]{1,0:T(8,128)}, u32[]{:S(2)}) copy-start(f32[5,64]{1,0:T(8,128)} %param.21) | copy-start | bytes 3844
  44.2 35.9 %all-to-all-start = ((f32[16,192,128]{2,1,0:T(8,128)}), f32[16,192,128]{2,1,0:T(8,128)S(1)}, u32[]{:S(2)}, u32[]{:S(2)}) async-start(f32[16,192,128]{2,1,0:T(8,128)} %bitcast.7), calls=%async_computation | async-start | bytes 3145728 | tf_op jit(solution)/shard_map/all_to_all | solution.py:725
  58.2 1.9 %copy-start.1 = (f32[32,8,2880]{2,1,0:T(8,128)S(1)}, f32[32,8,2880]{2,1,0:T(8,128)}, u32[]{:S(2)}) copy-start(f32[32,8,2880]{2,1,0:T(8,128)} %param.22) | copy-start | bytes 8847364
  80.1 14.2 %copy-start.9 = (f32[7,5]{1,0:T(8,128)S(1)}, f32[7,5]{1,0:T(8,128)}, u32[]{:S(2)}) copy-start(f32[7,5]{1,0:T(8,128)} %param.23) | copy-start | bytes 424
  86.8 7.6 %copy-start.11 = (f32[7]{0:T(128)S(1)}, f32[7]{0:T(128)}, u32[]{:S(2)}) copy-start(f32[7]{0:T(128)} %param.25) | copy-start | bytes 88
  86.8 7.6 %copy-start.12 = (f32[7]{0:T(128)S(1)}, f32[7]{0:T(128)}, u32[]{:S(2)}) copy-start(f32[7]{0:T(128)} %param.24) | copy-start | bytes 88
  86.8 26.7 %copy-start.4 = (bf16[512,512]{1,0:T(8,128)(2,1)S(1)}, bf16[512,512]{1,0:T(8,128)(2,1)}, u32[]{:S(2)}) copy-start(bf16[512,512]{1,0:T(8,128)(2,1)} %constant.116.clone.fwd_high) | copy-start | bytes 1572868
  86.8 26.7 %copy-start.5 = (bf16[512,512]{1,0:T(8,128)(2,1)S(1)}, bf16[512,512]{1,0:T(8,128)(2,1)}, u32[]{:S(2)}) copy-start(bf16[512,512]{1,0:T(8,128)(2,1)} %constant.117.clone.fwd_low) | copy-start | bytes 1572868
  86.8 26.7 %copy-start.6 = (bf16[512,512]{1,0:T(8,128)(2,1)S(1)}, bf16[512,512]{1,0:T(8,128)(2,1)}, u32[]{:S(2)}) copy-start(bf16[512,512]{1,0:T(8,128)(2,1)} %constant.118.clone.inv_high) | copy-start | bytes 1572868
  86.8 26.7 %copy-start.7 = (bf16[512,512]{1,0:T(8,128)(2,1)S(1)}, bf16[512,512]{1,0:T(8,128)(2,1)}, u32[]{:S(2)}) copy-start(bf16[512,512]{1,0:T(8,128)(2,1)} %constant.119.clone.inv_low) | copy-start | bytes 1572868
  86.8 26.7 %copy-start.8 = (f32[1,512]{1,0:T(1,128)S(1)}, f32[1,512]{1,0:T(1,128)}, u32[]{:S(2)}) copy-start(f32[1,512]{1,0:T(1,128)} %constant.131.waves_ref) | copy-start | bytes 6148
  86.8 26.6 %all-to-all-start.1 = ((f32[128,16,128]{2,1,0:T(8,128)}), f32[128,16,128]{2,1,0:T(8,128)S(1)}, u32[]{:S(2)}, u32[]{:S(2)}) async-start(f32[128,16,128]{2,1,0:T(8,128)} %bitcast.10), calls=%async_computation.1 | async-start | bytes 2097152 | tf_op jit(solution)/shard_map/all_to_all | solution.py:730

commit v13 on v12

--- a/solution.py
+++ b/solution.py
@@ -81,8 +81,16 @@
     return courant * jnp.where(courant > 0.0, upstream, downstream)
 
 
+def own_core():
+    return lax.rem(lax.axis_index("lev"), 2)
+
+
+def in_odd_band():
+    return lax.rem(lax.axis_index("band"), 2) == 1
+
+
 def edges_kernel(
-    side_ref, n_hbm, wlon_hbm, wlat_hbm, wlev_hbm,
+    n_hbm, wlon_hbm, wlat_hbm, wlev_hbm,
     n_ref, wlon_ref, wlat_ref, wlev_ref, inner_ref, outer_ref, row_ref, far_row_ref, sems,
 ):
     fetches = [
@@ -95,7 +103,7 @@
         fetch.start()
     for fetch in fetches[:-1]:
         fetch.wait()
-    core, odd = side_ref[0], side_ref[1] == 1
+    core, odd = own_core(), in_odd_band()
     inner_ref[SPECIES] = wlev_ref[0]
     outer_ref[SPECIES] = wlev_ref[0]
     for j in range(2):
@@ -114,7 +122,7 @@
     fetches[-1].wait()
 
 
-def edges(side, density, wind_lon, wind_lat, wind_lev):
+def edges(density, wind_lon, wind_lat, wind_lev):
     return call(
         edges_kernel,
         (
@@ -127,11 +135,11 @@
             on_chip((SPECIES + 1, 2, 1, NLON)),
             on_chip((SPECIES + 1, 2, 1, NLON)),
         ),
-        [SMEM] + [HBM] * 4,
+        [HBM] * 4,
         (VMEM,) * 8,
         [pltpu.SemaphoreType.DMA((SPECIES + 3,))],
         flops=1_000_000,
-    )(side, density, wind_lon, wind_lat, wind_lev)
+    )(density, wind_lon, wind_lat, wind_lev)
 
 
 def interior_kernel(n_ref, wlon_ref, wlat_ref, wlev_ref, *refs):
@@ -162,11 +170,11 @@
     )(density, *winds, *ready)
 
 
-def faces_kernel(side_ref, n_ref, inside_ref, wlat_ref, wlev_ref, *refs, last):
+def faces_kernel(n_ref, inside_ref, wlat_ref, wlev_ref, *refs, last):
     inner_ref, outer_ref, row_ref, far_row_ref = refs[:4]
     inner_wind, outer_wind, row_wind, far_row_wind = refs[4:8]
     outs = refs[8:]
-    odd = side_ref[1] == 1
+    odd = in_odd_band()
     row = lax.broadcasted_iota(jnp.int32, (BAND_LATS, NLON), 0)
 
     def advance(core):
@@ -202,10 +210,10 @@
                 outs[4][s, j] = jnp.where(odd, final, first)
 
     for core in range(2):
-        pl.when(side_ref[0] == core)(functools.partial(advance, core))
-
-
-def faces(side, density, inside, winds, halo, wind_halo, last):
+        pl.when(own_core() == core)(functools.partial(advance, core))
+
+
+def faces(density, inside, winds, halo, wind_halo, last):
     if last:
         out_shape = (on_chip((LON_BLOCKS, 2 * SPECIES * BAND_LATS, LANES)),)
     else:
@@ -219,10 +227,10 @@
     return call(
         functools.partial(faces_kernel, last=last),
         out_shape,
-        [SMEM] + [HELD] * 12,
+        [HELD] * 12,
         (VMEM,) * len(out_shape),
         flops=2_000_000,
-    )(side, density, inside, *winds[1:], *halo, *wind_halo)
+    )(density, inside, *winds[1:], *halo, *wind_halo)
 
 
 def places_kernel(units_ref, order_ref, place_ref, starts_ref):
@@ -371,12 +379,12 @@
 
 
 def pack_kernel(
-    core_ref, starts_ref, units_ref, list_ref, other_ref, _,
+    starts_ref, units_ref, list_ref, other_ref, _,
     out_hbm, table_ref, order_ref, planes, msg_ref, sems, order_sem,
 ):
     fetch = pltpu.make_async_copy(list_ref, order_ref, order_sem)
     fetch.start()
-    core = core_ref[0]
+    core = own_core()
     fill_planes(planes, other_ref)
     fill_table(planes, table_ref, lambda a: (a + BAND_LATS // 2, a))
 
@@ -422,11 +430,11 @@
         send(peer).wait()
 
 
-def pack(core, starts, units, order, other, table):
+def pack(starts, units, order, other, table):
     outgoing, _ = call(
         pack_kernel,
         (sds((16 * PEER_ROWS, LANES)), on_chip((BAND_LATS * LON_PAD, LANES))),
-        [SMEM, SMEM, SMEM, HELD, HELD, HELD],
+        [SMEM, SMEM, HELD, HELD, HELD],
         (HBM, VMEM),
         [
             pltpu.SMEM((ORDER_PAD,), jnp.int32),
@@ -436,16 +444,16 @@
             pltpu.SemaphoreType.DMA,
         ],
         flops=30_000_000,
-        aliases={5: 1},
-    )(core, starts, units, order, other, table)
+        aliases={4: 1},
+    )(starts, units, order, other, table)
     return outgoing
 
 
 def solve_kernel(
-    core_ref, units_ref, table_ref, got_ref, coef_ref, weight_ref, north_ref, state_hbm, items_hbm,
+    units_ref, table_ref, got_ref, coef_ref, weight_ref, north_ref, state_hbm, items_hbm,
     turned, natural, pairs, wide, tubes, state, items_ref, sems, item_sems,
 ):
-    core = core_ref[0]
+    core = own_core()
     live = TUBE_COLS * units_ref[0]
     lane = lax.broadcasted_iota(jnp.int32, (1, LANES), 1)
     low = lane < 64
@@ -540,11 +548,11 @@
         leave(s).wait()
 
 
-def solve(core, units, table, got, coefs, weights, north):
+def solve(units, table, got, coefs, weights, north):
     return call(
         solve_kernel,
         (sds((1, 1, SPECIES, NLEV, COL_CAP)), sds((PEERS * ITEM_ROWS, LANES))),
-        [SMEM, SMEM, SMEM] + [HELD] * 4,
+        [SMEM, SMEM] + [HELD] * 4,
         (HBM, HBM),
         [
             pltpu.VMEM((2, 8 * LEVEL_PITCH, LANES), f32),
@@ -558,7 +566,7 @@
             pltpu.SemaphoreType.DMA((4,)),
         ],
         flops=40_000_000,
-    )(core, units, table, got, coefs, weights, north)
+    )(units, table, got, coefs, weights, north)
 
 
 def halves(x):
@@ -681,8 +689,7 @@
 ):
     lev = lax.axis_index("lev")
 
-    side = jnp.stack([lev % 2, lax.axis_index("band") % 2]).astype(jnp.int32)
-    neutrals, *rest = edges(side, neutrals, wind_lon, wind_lat, wind_lev)
+    neutrals, *rest = edges(neutrals, wind_lon, wind_lat, wind_lev)
     winds, first_halo = rest[:3], exchange(*rest[3:])
 
     places, starts = list_places(column_units, column_order)
@@ -712,20 +719,19 @@
     )
 
     inside = interior(neutrals, winds, (places,))
-    density, *halo = faces(side, neutrals, inside, winds, first_halo, first_halo, False)
+    density, *halo = faces(neutrals, inside, winds, first_halo, first_halo, False)
     inside = interior(density, winds)
-    (mine,) = faces(side, density, inside, winds, exchange(*halo), first_halo, True)
+    (mine,) = faces(density, inside, winds, exchange(*halo), first_halo, True)
     owners = lax.axis_size("lev")
     other = swap(mine, "lev", 0)
     columns = own_table(mine)
 
-    core = (lev % 2).reshape(1)
     parity = [[2 * i + c for i in range(owners // 2)] for c in range(2)]
-    outgoing = pack(core, starts, column_units, places, other, columns)
+    outgoing = pack(starts, column_units, places, other, columns)
     got = lax.all_to_all(
         outgoing.reshape(16, PEER_ROWS, LANES), "lev", 0, 0, axis_index_groups=parity, tiled=True
     ).reshape(16 * PEER_ROWS, LANES)
-    column_state, items = solve(core, own_units, table, got, coefs, own_weights, own_north)
+    column_state, items = solve(own_units, table, got, coefs, own_weights, own_north)
 
     items = lax.all_to_all(
         items.reshape(PEERS, ITEM_ROWS, LANES), ("band", "lev"), 0, 0, tiled=True

time: 118 us -> 117 us (level)
  Pallas kernels: 43.2 us -> 41.5 us
    pallas_call x11, Pallas kernels: 43.2 us -> 41.5 us  [placed(): return run(*(place(x, spec) for x, spec in zip(args, in_specs)))]
    unnamed x26 -> x28, local copies, waits for them, and re-layouts: 1.92 us -> 2.57 us
  transfers between devices with their start and end apart: 11 -> 11, of which waited for: 5 -> 5; matrix products, arithmetic and copies ran while one was open for 2% -> 2% of each run, Pallas kernels for 12% -> 13%
where the time goes in v13:
time: 117 us; the launch traced here: 116 us
  Pallas kernels  41.5 us (35%)
  waiting for transfers between devices  35.1 us (30%)
  starting transfers between devices  32.6 us (28%)
  local copies, waits for them, and re-layouts  4.61 us (4%)
  between operations  1.66 us (1%)
    pallas_call x11, Pallas kernels, placed(): return run(*(place(x, spec) for x, spec in zip(args, in_specs)))  41.5 us
    all_to_all x1, waiting for transfers between devices, on_device(): lax.all_to_all(items.reshape(PEERS, ITEM_ROWS, LANES), ('band', 'lev'), 0...  19.1 us
    ppermute x9, starting transfers between devices, swap(): lax.ppermute(x, axis, [(i, i + 1) for i in lows] + [(i + 1, i) for i in l...  14.4 us
    all_to_all x1, waiting for transfers between devices, on_device(): lax.all_to_all(outgoing.reshape(16, PEER_ROWS, LANES), 'lev', 0, 0, axis_...  12.1 us
    all_to_all x1, starting transfers between devices, on_device(): lax.all_to_all(outgoing.reshape(16, PEER_ROWS, LANES), 'lev', 0, 0, axis_...  10.8 us
    all_to_all x1, starting transfers between devices, on_device(): lax.all_to_all(items.reshape(PEERS, ITEM_ROWS, LANES), ('band', 'lev'), 0...  7.39 us
    ppermute x9, waiting for transfers between devices, swap(): lax.ppermute(x, axis, [(i, i + 1) for i in lows] + [(i + 1, i) for i in l...  3.93 us
    unnamed x28, local copies, waits for them, and re-layouts  2.57 us
  transfers between devices with their start and end apart: 11, of which 5 were waited for; matrix products, arithmetic and copies ran while one was open for 2% of the time, Pallas kernels for 13%

profile of v13, /device:TPU:1, one launch (start us, length us, event | category | flops | bytes accessed | tf_op | source)
XLA Modules:
  0.0 116.2 jit_solution(15563974642954046816)
XLA Ops:
  0.7 1.6 %shard_map.178 = (f32[5,2,8,2880]{3,2,1,0:T(8,128)S(1)}, f32[2,8,2880]{2,1,0:T(8,128)S(1)}, f32[2,8,2880]{2,1,0:T(8,128)S(1)}, f32[2,8,2880]{2,1,0:T(8,128)S(1)}...) custom-call(f32[5,2,8,2880]{3,2,1,0:T(8,128)} %n_hbm.1, ...), custom_call_target="tpu_custom_call" | custom-call | flops 1000000 | bytes 1048576 | tf_op jit(solution)/shard_map/pallas_call | solution.py:71
  2.3 1.5 %collective-permute-start = (f32[6,8,2880]{2,1,0:T(8,128)S(1)}, f32[6,8,2880]{2,1,0:T(8,128)S(1)}, u32[]{:S(2)}, u32[]{:S(2)}) collective-permute-start(f32[6,8,2880]{2,1,0:T(8,128)S(1)} %get-tuple-element.30), channel_id=1, source_target_pairs={{0,1},{2,3},{4,5},{6,7},{8,9},{10,11},{12,13},{14,15},{16,17},{18,... | collective-permute-start | bytes 1658888 | tf_op jit(solution)/shard_map/ppermute | solution.py:665
  3.7 3.1 %collective-permute-start.1 = (f32[6,8,2880]{2,1,0:T(8,128)S(1)}, f32[6,8,2880]{2,1,0:T(8,128)S(1)}, u32[]{:S(2)}, u32[]{:S(2)}) collective-permute-start(f32[6,8,2880]{2,1,0:T(8,128)S(1)} %get-tuple-element.31), channel_id=1, source_target_pairs={{1,2},{3,4},{5,6},{7,8},{9,10},{11,12},{13,14},{15,16},{17,18},{19... | collective-permute-start | bytes 1658888 | tf_op jit(solution)/shard_map/ppermute | solution.py:665
  6.9 1.7 %collective-permute-start.2 = (f32[6,2,1,2880]{3,2,1,0:T(1,128)S(1)}, f32[6,2,1,2880]{3,2,1,0:T(1,128)S(1)}, u32[]{:S(2)}, u32[]{:S(2)}) collective-permute-start(f32[6,2,1,2880]{3,2,1,0:T(1,128)S(1)} %get-tuple-element.32), channel_id=1, source_target_pairs={{0,32},{64,96},{32,0},{96,64},{1,33},{65,97},{33,1},{97,65},{2,34}... | collective-permute-start | bytes 414728 | tf_op jit(solution)/shard_map/ppermute | solution.py:665
  8.6 0.7 collective-permute-start.3
  9.9 1.3 %shard_map.176 = (s32[1,23552]{1,0:T(1,128)S(1)}, s32[32]{0:T(128)S(1)}) custom-call(s32[32]{0:T(128)S(1)} %copy-done.3, s32[1,23040]{1,0:T(1,128)S(1)} %copy-done.2), custom_call_target="tpu_custom_call" | custom-call | flops 1000000 | bytes 1048576 | tf_op jit(solution)/shard_map/pallas_call | solution.py:71
  11.3 1.0 shard_map.179.inside_ref
  12.3 2.3 %collective-permute-done.1.refs_1_.refs_5_ = f32[6,8,2880]{2,1,0:T(8,128)S(1)} collective-permute-done((f32[6,8,2880]{2,1,0:T(8,128)S(1)}, f32[6,8,2880]{2,1,0:T(8,128)S(1)}, u32[]{:S(2)}, u32[]{:S(2)}) %collective-permute-start.1) | collective-permute-done | bytes 552992 | tf_op jit(solution)/shard_map/ppermute | solution.py:665
  14.7 0.8 shard_map.180
  15.5 3.6 %collective-permute-start.5 = (f32[5,8,2880]{2,1,0:T(8,128)S(1)}, f32[5,8,2880]{2,1,0:T(8,128)S(1)}, u32[]{:S(2)}, u32[]{:S(2)}) collective-permute-start(f32[5,8,2880]{2,1,0:T(8,128)S(1)} %get-tuple-element.36), channel_id=1, source_target_pairs={{1,2},{3,4},{5,6},{7,8},{9,10},{11,12},{13,14},{15,16},{17,18},{19... | collective-permute-start | bytes 1382408 | tf_op jit(solution)/shard_map/ppermute | solution.py:665
  19.1 3.0 %collective-permute-start.6 = (f32[5,2,1,2880]{3,2,1,0:T(1,128)S(1)}, f32[5,2,1,2880]{3,2,1,0:T(1,128)S(1)}, u32[]{:S(2)}, u32[]{:S(2)}) collective-permute-start(f32[5,2,1,2880]{3,2,1,0:T(1,128)S(1)} %get-tuple-element.37), channel_id=1, source_target_pairs={{0,32},{64,96},{32,0},{96,64},{1,33},{65,97},{33,1},{97,65},{2,34}... | collective-permute-start | bytes 345608 | tf_op jit(solution)/shard_map/ppermute | solution.py:665
  22.8 1.0 shard_map.181.inside_ref
  24.4 1.1 collective-permute-done.5.refs_1_
  26.1 3.3 %shard_map.183._ = f32[23552,128]{1,0:T(8,128)S(1)} custom-call(f32[23,80,128]{2,1,0:T(8,128)S(1)} %shard_map.182.mine_ref), custom_call_target="tpu_custom_call" | custom-call | flops 8000000 | bytes 1048576 | tf_op jit(solution)/shard_map/pallas_call | solution.py:71
  29.4 13.0 %shard_map.184 = (f32[3072,128]{1,0:T(8,128)}, f32[23552,128]{1,0:T(8,128)S(1)}) custom-call(s32[32]{0:T(128)S(1)} %get-tuple-element.23.starts_ref, s32[32]{0:T(128)S(1)} %copy-done.4, s32[23552]{0:T(1024)S(1)} %bitcast.20, f32[23,80,128]{2,1,0:T(8,128)S(1)} %collective-permute-done.8.other_ref, ...), custom_call_target="tpu_custom_call", output_to_operand_aliasing={{1}: (4, {})} | custom-call | flops 30000000 | bytes 1048576 | tf_op jit(solution)/shard_map/pallas_call | solution.py:71
  42.5 10.8 %all-to-all-start = ((f32[16,192,128]{2,1,0:T(8,128)}), f32[16,192,128]{2,1,0:T(8,128)S(1)}, u32[]{:S(2)}, u32[]{:S(2)}) async-start(f32[16,192,128]{2,1,0:T(8,128)} %bitcast.5), calls=%async_computation | async-start | bytes 3145728 | tf_op jit(solution)/shard_map/all_to_all | solution.py:731
  54.2 0.7 dynamic_slice.12.units_ref
  56.5 1.8 %copy-done.1 = f32[32,8,2880]{2,1,0:T(8,128)S(1)} copy-done((f32[32,8,2880]{2,1,0:T(8,128)S(1)}, f32[32,8,2880]{2,1,0:T(8,128)}, u32[]{:S(2)}) %copy-start.1) | copy-done | bytes 2949144
  58.3 7.8 %shard_map.177 = (s32[384]{0:T(512)S(1)}, f32[9,32,128]{2,1,0:T(8,128)S(1)}, f32[960,128]{1,0:T(8,128)S(1)}) custom-call(s32[1]{0:T(128)} %dynamic_slice.12.units_ref, s32[270]{0:T(512)S(1)} %dynamic-slice_reduce_fusion.owner_ref, s32[1152]{0:T(1024)S(1)} %get-tuple-element.45.rows_ref, s32[9,128]{1,0:T(8,128)S(1)} %get-tuple-element.44.sel_ref, ...), custom_call_target="tpu_custom_call" | custom-call | flops 20000000 | bytes 1048576 | tf_op jit(solution)/shard_map/pallas_call | solution.py:71
  66.3 12.1 %all-to-all-done = f32[16,192,128]{2,1,0:T(8,128)S(1)} async-done(((f32[16,192,128]{2,1,0:T(8,128)}), f32[16,192,128]{2,1,0:T(8,128)S(1)}, u32[]{:S(2)}, u32[]{:S(2)}) %all-to-all-start) | async-done | bytes 1572896 | tf_op jit(solution)/shard_map/all_to_all | solution.py:731
  78.4 6.7 %shard_map.185 = (f32[1,1,5,64,1080]{4,3,2,1,0:T(8,128)}, f32[2048,128]{1,0:T(8,128)}) custom-call(s32[1]{0:T(128)} %dynamic_slice.12.units_ref, s32[384]{0:T(512)S(1)} %get-tuple-element.24.table_ref, f32[3072,128]{1,0:T(8,128)S(1)} %bitcast.16, f32[960,128]{1,0:T(8,128)S(1)} %get-tuple-element.40.coef_ref, f32[9,32,128]{2,1,0:T(8,128)S(1)} %get-tuple-element.41.weight_ref, ...), custom_call_target="tpu_custom_call" | custom-call | flops 40000000 | bytes 1048576 | tf_op jit(solution)/shard_map/pallas_call | solution.py:71
  85.1 7.4 %all-to-all-start.1 = ((f32[128,16,128]{2,1,0:T(8,128)}), f32[128,16,128]{2,1,0:T(8,128)S(1)}, u32[]{:S(2)}, u32[]{:S(2)}) async-start(f32[128,16,128]{2,1,0:T(8,128)} %bitcast.8), calls=%async_computation.1 | async-start | bytes 2097152 | tf_op jit(solution)/shard_map/all_to_all | solution.py:736
  92.7 19.1 %all-to-all-done.1 = f32[128,16,128]{2,1,0:T(8,128)S(1)} async-done(((f32[128,16,128]{2,1,0:T(8,128)}), f32[128,16,128]{2,1,0:T(8,128)S(1)}, u32[]{:S(2)}, u32[]{:S(2)}) %all-to-all-start.1) | async-done | bytes 1048608 | tf_op jit(solution)/shard_map/all_to_all | solution.py:736
  111.8 4.4 %shard_map.186 = f32[1,7,96,512]{3,2,1,0:T(8,128)} custom-call(f32[2048,128]{1,0:T(8,128)S(1)} %bitcast.18, f32[35]{0:T(128)S(1)} %reshape.55.yield_ref, f32[14]{0:T(128)S(1)} %pad_maximum_fusion.rates_ref, f32[1,512]{1,0:T(1,128)S(1)} %copy-done.9, bf16[512,512]{1,0:T(8,128)(2,1)S(1)} %copy-done.5, bf16[512,512]{1,0:T(8,128)(2,1)S(1)} %copy-done.6, ...), custom_call_target="tpu_custom_call" | custom-call | flops 2000000000 | bytes 1048576 | tf_op jit(solution)/shard_map/pallas_call | solution.py:71
  (55 shorter events, 4.6 us)
Async XLA Ops:
  0.6 55.7 %copy-start = (s32[32,270,1]{1,2,0:T(1,128)S(1)}, s32[32,270,1]{1,2,0:T(1,128)}, u32[]{:S(2)}) copy-start(s32[32,270,1]{1,2,0:T(1,128)} %param.28) | copy-start | bytes 103684
  0.6 8.6 %copy-start.2 = (s32[1,23040]{1,0:T(1,128)S(1)}, s32[1,23040]{1,0:T(1,128)}, u32[]{:S(2)}) copy-start(s32[1,23040]{1,0:T(1,128)} %order_ref.1) | copy-start | bytes 276484
  2.3 10.0 %collective-permute-start = (f32[6,8,2880]{2,1,0:T(8,128)S(1)}, f32[6,8,2880]{2,1,0:T(8,128)S(1)}, u32[]{:S(2)}, u32[]{:S(2)}) collective-permute-start(f32[6,8,2880]{2,1,0:T(8,128)S(1)} %get-tuple-element.30), channel_id=1, source_target_pairs={{0,1},{2,3},{4,5},{6,7},{8,9},{10,11},{12,13},{14,15},{16,17},{18,... | collective-permute-start | bytes 1658888 | tf_op jit(solution)/shard_map/ppermute | solution.py:665
  3.7 10.9 %collective-permute-start.1 = (f32[6,8,2880]{2,1,0:T(8,128)S(1)}, f32[6,8,2880]{2,1,0:T(8,128)S(1)}, u32[]{:S(2)}, u32[]{:S(2)}) collective-permute-start(f32[6,8,2880]{2,1,0:T(8,128)S(1)} %get-tuple-element.31), channel_id=1, source_target_pairs={{1,2},{3,4},{5,6},{7,8},{9,10},{11,12},{13,14},{15,16},{17,18},{19... | collective-permute-start | bytes 1658888 | tf_op jit(solution)/shard_map/ppermute | solution.py:665
  6.9 5.4 %collective-permute-start.2 = (f32[6,2,1,2880]{3,2,1,0:T(1,128)S(1)}, f32[6,2,1,2880]{3,2,1,0:T(1,128)S(1)}, u32[]{:S(2)}, u32[]{:S(2)}) collective-permute-start(f32[6,2,1,2880]{3,2,1,0:T(1,128)S(1)} %get-tuple-element.32), channel_id=1, source_target_pairs={{0,32},{64,96},{32,0},{96,64},{1,33},{65,97},{33,1},{97,65},{2,34}... | collective-permute-start | bytes 414728 | tf_op jit(solution)/shard_map/ppermute | solution.py:665
  8.6 3.7 %collective-permute-start.3 = (f32[6,2,1,2880]{3,2,1,0:T(1,128)S(1)}, f32[6,2,1,2880]{3,2,1,0:T(1,128)S(1)}, u32[]{:S(2)}, u32[]{:S(2)}) collective-permute-start(f32[6,2,1,2880]{3,2,1,0:T(1,128)S(1)} %get-tuple-element.33), channel_id=1, source_target_pairs={{32,64},{64,32},{33,65},{65,33},{34,66},{66,34},{35,67},{67,35},{3... | collective-permute-start | bytes 414728 | tf_op jit(solution)/shard_map/ppermute | solution.py:665
  15.4 9.0 %collective-permute-start.4 = (f32[5,8,2880]{2,1,0:T(8,128)S(1)}, f32[5,8,2880]{2,1,0:T(8,128)S(1)}, u32[]{:S(2)}, u32[]{:S(2)}) collective-permute-start(f32[5,8,2880]{2,1,0:T(8,128)S(1)} %get-tuple-element.35), channel_id=1, source_target_pairs={{0,1},{2,3},{4,5},{6,7},{8,9},{10,11},{12,13},{14,15},{16,17},{18,... | collective-permute-start | bytes 1382408 | tf_op jit(solution)/shard_map/ppermute | solution.py:665
  15.5 9.9 %collective-permute-start.5 = (f32[5,8,2880]{2,1,0:T(8,128)S(1)}, f32[5,8,2880]{2,1,0:T(8,128)S(1)}, u32[]{:S(2)}, u32[]{:S(2)}) collective-permute-start(f32[5,8,2880]{2,1,0:T(8,128)S(1)} %get-tuple-element.36), channel_id=1, source_target_pairs={{1,2},{3,4},{5,6},{7,8},{9,10},{11,12},{13,14},{15,16},{17,18},{19... | collective-permute-start | bytes 1382408 | tf_op jit(solution)/shard_map/ppermute | solution.py:665
  19.1 5.2 %collective-permute-start.6 = (f32[5,2,1,2880]{3,2,1,0:T(1,128)S(1)}, f32[5,2,1,2880]{3,2,1,0:T(1,128)S(1)}, u32[]{:S(2)}, u32[]{:S(2)}) collective-permute-start(f32[5,2,1,2880]{3,2,1,0:T(1,128)S(1)} %get-tuple-element.37), channel_id=1, source_target_pairs={{0,32},{64,96},{32,0},{96,64},{1,33},{65,97},{33,1},{97,65},{2,34}... | collective-permute-start | bytes 345608 | tf_op jit(solution)/shard_map/ppermute | solution.py:665
  22.2 2.2 %collective-permute-start.7 = (f32[5,2,1,2880]{3,2,1,0:T(1,128)S(1)}, f32[5,2,1,2880]{3,2,1,0:T(1,128)S(1)}, u32[]{:S(2)}, u32[]{:S(2)}) collective-permute-start(f32[5,2,1,2880]{3,2,1,0:T(1,128)S(1)} %get-tuple-element.38), channel_id=1, source_target_pairs={{32,64},{64,32},{33,65},{65,33},{34,66},{66,34},{35,67},{67,35},{3... | collective-permute-start | bytes 345608 | tf_op jit(solution)/shard_map/ppermute | solution.py:665
  26.0 3.4 %copy-start.4 = (s32[32]{0:T(128)S(1)}, s32[32]{0:T(128)}, u32[]{:S(2)}) copy-start(s32[32]{0:T(128)} %units_ref.3) | copy-start | bytes 388
  26.0 3.4 %collective-permute-start.8 = (f32[23,80,128]{2,1,0:T(8,128)S(1)}, f32[23,80,128]{2,1,0:T(8,128)S(1)}, u32[]{:S(2)}, u32[]{:S(2)}) collective-permute-start(f32[23,80,128]{2,1,0:T(8,128)S(1)} %shard_map.182.mine_ref), channel_id=1, source_target_pairs={{0,1},{2,3},{4,5},{6,7},{8,9},{10,11},{12,13},{14,15},{16,17},{18,... | collective-permute-start | bytes 2826248 | tf_op jit(solution)/shard_map/ppermute | solution.py:665
  42.5 13.0 %copy-start.11 = (f32[5,64]{1,0:T(8,128)S(1)}, f32[5,64]{1,0:T(8,128)}, u32[]{:S(2)}) copy-start(f32[5,64]{1,0:T(8,128)} %param.21) | copy-start | bytes 3844
  42.5 35.9 %all-to-all-start = ((f32[16,192,128]{2,1,0:T(8,128)}), f32[16,192,128]{2,1,0:T(8,128)S(1)}, u32[]{:S(2)}, u32[]{:S(2)}) async-start(f32[16,192,128]{2,1,0:T(8,128)} %bitcast.5), calls=%async_computation | async-start | bytes 3145728 | tf_op jit(solution)/shard_map/all_to_all | solution.py:731
  56.5 1.9 %copy-start.1 = (f32[32,8,2880]{2,1,0:T(8,128)S(1)}, f32[32,8,2880]{2,1,0:T(8,128)}, u32[]{:S(2)}) copy-start(f32[32,8,2880]{2,1,0:T(8,128)} %param.22) | copy-start | bytes 8847364
  78.4 14.2 %copy-start.10 = (f32[7,5]{1,0:T(8,128)S(1)}, f32[7,5]{1,0:T(8,128)}, u32[]{:S(2)}) copy-start(f32[7,5]{1,0:T(8,128)} %param.23) | copy-start | bytes 424
  85.1 7.6 %copy-start.12 = (f32[7]{0:T(128)S(1)}, f32[7]{0:T(128)}, u32[]{:S(2)}) copy-start(f32[7]{0:T(128)} %param.25) | copy-start | bytes 88
  85.1 7.6 %copy-start.13 = (f32[7]{0:T(128)S(1)}, f32[7]{0:T(128)}, u32[]{:S(2)}) copy-start(f32[7]{0:T(128)} %param.24) | copy-start | bytes 88
  85.1 26.7 %copy-start.5 = (bf16[512,512]{1,0:T(8,128)(2,1)S(1)}, bf16[512,512]{1,0:T(8,128)(2,1)}, u32[]{:S(2)}) copy-start(bf16[512,512]{1,0:T(8,128)(2,1)} %constant.94.clone.fwd_high) | copy-start | bytes 1572868
  85.1 26.7 %copy-start.6 = (bf16[512,512]{1,0:T(8,128)(2,1)S(1)}, bf16[512,512]{1,0:T(8,128)(2,1)}, u32[]{:S(2)}) copy-start(bf16[512,512]{1,0:T(8,128)(2,1)} %constant.95.clone.fwd_low) | copy-start | bytes 1572868
  85.1 26.7 %copy-start.7 = (bf16[512,512]{1,0:T(8,128)(2,1)S(1)}, bf16[512,512]{1,0:T(8,128)(2,1)}, u32[]{:S(2)}) copy-start(bf16[512,512]{1,0:T(8,128)(2,1)} %constant.96.clone.inv_high) | copy-start | bytes 1572868
  85.1 26.7 %copy-start.8 = (bf16[512,512]{1,0:T(8,128)(2,1)S(1)}, bf16[512,512]{1,0:T(8,128)(2,1)}, u32[]{:S(2)}) copy-start(bf16[512,512]{1,0:T(8,128)(2,1)} %constant.97.clone.inv_low) | copy-start | bytes 1572868
  85.1 26.7 %copy-start.9 = (f32[1,512]{1,0:T(1,128)S(1)}, f32[1,512]{1,0:T(1,128)}, u32[]{:S(2)}) copy-start(f32[1,512]{1,0:T(1,128)} %constant.109.waves_ref) | copy-start | bytes 6148
  85.1 26.6 %all-to-all-start.1 = ((f32[128,16,128]{2,1,0:T(8,128)}), f32[128,16,128]{2,1,0:T(8,128)S(1)}, u32[]{:S(2)}, u32[]{:S(2)}) async-start(f32[128,16,128]{2,1,0:T(8,128)} %bitcast.8), calls=%async_computation.1 | async-start | bytes 2097152 | tf_op jit(solution)/shard_map/all_to_all | solution.py:736
  (1 other events, 0.7 us)

commit v14 on v13

--- a/solution.py
+++ b/solution.py
@@ -45,6 +45,7 @@
 HELD = pl.BlockSpec(memory_space=pltpu.VMEM)
 SMEM = pl.BlockSpec(memory_space=pltpu.SMEM)
 HBM = pl.BlockSpec(memory_space=pltpu.HBM)
+ANY = pl.BlockSpec(memory_space=pl.ANY)
 
 
 def on_chip(shape, dtype=f32):
@@ -379,11 +380,17 @@
 
 
 def pack_kernel(
-    starts_ref, units_ref, list_ref, other_ref, _,
-    out_hbm, table_ref, order_ref, planes, msg_ref, sems, order_sem,
+    starts_any, units_any, list_ref, other_ref, _,
+    out_hbm, table_ref, starts_ref, units_ref, order_ref, planes, msg_ref, sems, fetch_sems,
 ):
-    fetch = pltpu.make_async_copy(list_ref, order_ref, order_sem)
-    fetch.start()
+    fetches = [
+        pltpu.make_async_copy(source, target, fetch_sems.at[i])
+        for i, (source, target) in enumerate(
+            ((starts_any, starts_ref), (units_any, units_ref), (list_ref, order_ref))
+        )
+    ]
+    for fetch in fetches:
+        fetch.start()
     core = own_core()
     fill_planes(planes, other_ref)
     fill_table(planes, table_ref, lambda a: (a + BAND_LATS // 2, a))
@@ -395,7 +402,8 @@
         rows = pl.ds(pl.multiple_of(peer * PEER_ROWS, PEER_ROWS), PEER_ROWS)
         return pltpu.make_async_copy(msg_ref.at[rows, :], out_hbm.at[rows, :], sems.at[peer])
 
-    fetch.wait()
+    for fetch in fetches:
+        fetch.wait()
 
     @pl.loop(0, 16)
     def _(peer):
@@ -434,14 +442,16 @@
     outgoing, _ = call(
         pack_kernel,
         (sds((16 * PEER_ROWS, LANES)), on_chip((BAND_LATS * LON_PAD, LANES))),
-        [SMEM, SMEM, HELD, HELD, HELD],
+        [ANY, ANY, HELD, HELD, HELD],
         (HBM, VMEM),
         [
+            pltpu.SMEM(starts.shape, jnp.int32),
+            pltpu.SMEM(units.shape, jnp.int32),
             pltpu.SMEM((ORDER_PAD,), jnp.int32),
             pltpu.VMEM((LON_BLOCKS, 2 * PLANES * PITCH, LANES), f32),
             pltpu.VMEM((16 * PEER_ROWS, LANES), f32),
             pltpu.SemaphoreType.DMA((16,)),
-            pltpu.SemaphoreType.DMA,
+            pltpu.SemaphoreType.DMA((3,)),
         ],
         flops=30_000_000,
         aliases={4: 1},
@@ -450,11 +460,16 @@
 
 
 def solve_kernel(
-    units_ref, table_ref, got_ref, coef_ref, weight_ref, north_ref, state_hbm, items_hbm,
-    turned, natural, pairs, wide, tubes, state, items_ref, sems, item_sems,
+    units_any, table_any, got_ref, coef_ref, weight_ref, north_ref, state_hbm, items_hbm,
+    units_ref, table_ref, turned, natural, pairs, wide, tubes, state, items_ref, sems, item_sems, fetch_sems,
 ):
+    fetches = [
+        pltpu.make_async_copy(units_any, units_ref, fetch_sems.at[0]),
+        pltpu.make_async_copy(table_any, table_ref, fetch_sems.at[1]),
+    ]
+    for fetch in fetches:
+        fetch.start()
     core = own_core()
-    live = TUBE_COLS * units_ref[0]
     lane = lax.broadcasted_iota(jnp.int32, (1, LANES), 1)
     low = lane < 64
     quarter = lax.div(lane, 32)
@@ -469,6 +484,10 @@
                 flipped = rows.T
                 turned[part, pl.ds(out + 64 * core, 64), :] = flipped[:64]
                 turned[part, pl.ds(out + 64 - 64 * core, 64), :] = flipped[64:]
+
+    for fetch in fetches:
+        fetch.wait()
+    live = TUBE_COLS * units_ref[0]
 
     def leave(s):
         return pltpu.make_async_copy(state.at[s], state_hbm.at[0, 0, s], sems.at[s])
@@ -552,9 +571,11 @@
     return call(
         solve_kernel,
         (sds((1, 1, SPECIES, NLEV, COL_CAP)), sds((PEERS * ITEM_ROWS, LANES))),
-        [SMEM, SMEM] + [HELD] * 4,
+        [ANY, ANY] + [HELD] * 4,
         (HBM, HBM),
         [
+            pltpu.SMEM(units.shape, jnp.int32),
+            pltpu.SMEM(table.shape, jnp.int32),
             pltpu.VMEM((2, 8 * LEVEL_PITCH, LANES), f32),
             pltpu.VMEM((3, 8 * PITCH, LANES), f32),
             pltpu.VMEM((3, PAIRS, LANES), f32),
@@ -564,6 +585,7 @@
             pltpu.VMEM((PEERS * ITEM_ROWS, LANES), f32),
             pltpu.SemaphoreType.DMA((SPECIES,)),
             pltpu.SemaphoreType.DMA((4,)),
+            pltpu.SemaphoreType.DMA((2,)),
         ],
         flops=40_000_000,
     )(units, table, got, coefs, weights, north)
@@ -581,9 +603,15 @@
 
 
 def lines_kernel(
-    items_ref, yield_ref, rates_ref, waves_ref, fwd_high, fwd_low, inv_high, inv_low, out_hbm,
-    spec_in, spec, mixed, done, sems,
+    items_ref, yield_any, rates_any, waves_ref, fwd_high, fwd_low, inv_high, inv_low, out_hbm,
+    yield_ref, rates_ref, spec_in, spec, mixed, done, sems, fetch_sems,
 ):
+    fetches = [
+        pltpu.make_async_copy(yield_any, yield_ref, fetch_sems.at[0]),
+        pltpu.make_async_copy(rates_any, rates_ref, fetch_sems.at[1]),
+    ]
+    for fetch in fetches:
+        fetch.start()
     tubes = 32 * PEER_SLOTS
     for b in range(4):
         for s in range(SPECIES):
@@ -597,6 +625,8 @@
         x = jnp.concatenate([spec_in[b, pl.ds(row, half), :] for b in range(4)], axis=1)
         spec[pl.ds(row, half), :] = product(x, fwd_high[...], fwd_low[...])
 
+    for fetch in fetches:
+        fetch.wait()
     waves = waves_ref[...]
     for i in range(IONS):
         keep = (1.0 - rates_ref[IONS + i]) + rates_ref[i] * waves
@@ -645,14 +675,17 @@
     by_ion = call(
         lines_kernel,
         sds((1, IONS, tubes, LINE_PTS)),
-        [HELD, SMEM, SMEM] + [HELD] * 5,
+        [HELD, ANY, ANY] + [HELD] * 5,
         HBM,
         [
+            pltpu.SMEM((IONS * SPECIES,), f32),
+            pltpu.SMEM((2 * IONS,), f32),
             pltpu.VMEM((4, SPECIES * tubes, LANES), f32),
             pltpu.VMEM((SPECIES * tubes, LINE_PTS), f32),
             pltpu.VMEM((IONS, tubes, LINE_PTS), f32),
             pltpu.VMEM((IONS, tubes, LINE_PTS), f32),
             pltpu.SemaphoreType.DMA((IONS,)),
+            pltpu.SemaphoreType.DMA((2,)),
         ],
         flops=2_000_000_000,
     )(items, ion_yield.reshape(-1), jnp.concatenate([ion_spread, ion_loss]), waves, *parts(basis.T), *parts(basis))

time: 117 us -> 115 us (0.983)
  Pallas kernels: 41.5 us -> 39.6 us
    pallas_call x11, Pallas kernels: 41.5 us -> 39.6 us  [placed(): return run(*(place(x, spec) for x, spec in zip(args, in_specs)))]
where the time goes in v14:
time: 115 us; the launch traced here: 114 us
  Pallas kernels  39.6 us (34%)
  waiting for transfers between devices  35.1 us (31%)
  starting transfers between devices  32.6 us (28%)
  local copies, waits for them, and re-layouts  4.61 us (4%)
  between operations  1.66 us (1%)
    pallas_call x11, Pallas kernels, placed(): return run(*(place(x, spec) for x, spec in zip(args, in_specs)))  39.6 us
    all_to_all x1, waiting for transfers between devices, on_device(): lax.all_to_all(items.reshape(PEERS, ITEM_ROWS, LANES), ('band', 'lev'), 0...  19.1 us
    ppermute x9, starting transfers between devices, swap(): lax.ppermute(x, axis, [(i, i + 1) for i in lows] + [(i + 1, i) for i in l...  14.4 us
    all_to_all x1, waiting for transfers between devices, on_device(): lax.all_to_all(outgoing.reshape(16, PEER_ROWS, LANES), 'lev', 0, 0, axis_...  12.1 us
    all_to_all x1, starting transfers between devices, on_device(): lax.all_to_all(outgoing.reshape(16, PEER_ROWS, LANES), 'lev', 0, 0, axis_...  10.8 us
    all_to_all x1, starting transfers between devices, on_device(): lax.all_to_all(items.reshape(PEERS, ITEM_ROWS, LANES), ('band', 'lev'), 0...  7.39 us
    ppermute x9, waiting for transfers between devices, swap(): lax.ppermute(x, axis, [(i, i + 1) for i in lows] + [(i + 1, i) for i in l...  3.93 us
    unnamed x28, local copies, waits for them, and re-layouts  2.57 us
  transfers between devices with their start and end apart: 11, of which 5 were waited for; matrix products, arithmetic and copies ran while one was open for 2% of the time, Pallas kernels for 13%

profile of v14, /device:TPU:1, one launch (start us, length us, event | category | flops | bytes accessed | tf_op | source)
XLA Modules:
  0.0 114.3 jit_solution(17104237035047147554)
XLA Ops:
  0.7 1.6 %shard_map.178 = (f32[5,2,8,2880]{3,2,1,0:T(8,128)S(1)}, f32[2,8,2880]{2,1,0:T(8,128)S(1)}, f32[2,8,2880]{2,1,0:T(8,128)S(1)}, f32[2,8,2880]{2,1,0:T(8,128)S(1)}...) custom-call(f32[5,2,8,2880]{3,2,1,0:T(8,128)} %n_hbm.1, ...), custom_call_target="tpu_custom_call" | custom-call | flops 1000000 | bytes 1048576 | tf_op jit(solution)/shard_map/pallas_call | solution.py:72
  2.3 1.5 %collective-permute-start = (f32[6,8,2880]{2,1,0:T(8,128)S(1)}, f32[6,8,2880]{2,1,0:T(8,128)S(1)}, u32[]{:S(2)}, u32[]{:S(2)}) collective-permute-start(f32[6,8,2880]{2,1,0:T(8,128)S(1)} %get-tuple-element.30), channel_id=1, source_target_pairs={{0,1},{2,3},{4,5},{6,7},{8,9},{10,11},{12,13},{14,15},{16,17},{18,... | collective-permute-start | bytes 1658888 | tf_op jit(solution)/shard_map/ppermute | solution.py:698
  3.7 3.1 %collective-permute-start.1 = (f32[6,8,2880]{2,1,0:T(8,128)S(1)}, f32[6,8,2880]{2,1,0:T(8,128)S(1)}, u32[]{:S(2)}, u32[]{:S(2)}) collective-permute-start(f32[6,8,2880]{2,1,0:T(8,128)S(1)} %get-tuple-element.31), channel_id=1, source_target_pairs={{1,2},{3,4},{5,6},{7,8},{9,10},{11,12},{13,14},{15,16},{17,18},{19... | collective-permute-start | bytes 1658888 | tf_op jit(solution)/shard_map/ppermute | solution.py:698
  6.9 1.7 %collective-permute-start.2 = (f32[6,2,1,2880]{3,2,1,0:T(1,128)S(1)}, f32[6,2,1,2880]{3,2,1,0:T(1,128)S(1)}, u32[]{:S(2)}, u32[]{:S(2)}) collective-permute-start(f32[6,2,1,2880]{3,2,1,0:T(1,128)S(1)} %get-tuple-element.32), channel_id=1, source_target_pairs={{0,32},{64,96},{32,0},{96,64},{1,33},{65,97},{33,1},{97,65},{2,34}... | collective-permute-start | bytes 414728 | tf_op jit(solution)/shard_map/ppermute | solution.py:698
  8.6 0.7 collective-permute-start.3
  9.9 1.3 %shard_map.176 = (s32[1,23552]{1,0:T(1,128)S(1)}, s32[32]{0:T(128)S(1)}) custom-call(s32[32]{0:T(128)S(1)} %copy-done.3, s32[1,23040]{1,0:T(1,128)S(1)} %copy-done.2), custom_call_target="tpu_custom_call" | custom-call | flops 1000000 | bytes 1048576 | tf_op jit(solution)/shard_map/pallas_call | solution.py:72
  11.3 1.0 shard_map.179.inside_ref
  12.3 2.3 %collective-permute-done.1.refs_1_.refs_5_ = f32[6,8,2880]{2,1,0:T(8,128)S(1)} collective-permute-done((f32[6,8,2880]{2,1,0:T(8,128)S(1)}, f32[6,8,2880]{2,1,0:T(8,128)S(1)}, u32[]{:S(2)}, u32[]{:S(2)}) %collective-permute-start.1) | collective-permute-done | bytes 552992 | tf_op jit(solution)/shard_map/ppermute | solution.py:698
  14.7 0.8 shard_map.180
  15.5 3.6 %collective-permute-start.5 = (f32[5,8,2880]{2,1,0:T(8,128)S(1)}, f32[5,8,2880]{2,1,0:T(8,128)S(1)}, u32[]{:S(2)}, u32[]{:S(2)}) collective-permute-start(f32[5,8,2880]{2,1,0:T(8,128)S(1)} %get-tuple-element.36), channel_id=1, source_target_pairs={{1,2},{3,4},{5,6},{7,8},{9,10},{11,12},{13,14},{15,16},{17,18},{19... | collective-permute-start | bytes 1382408 | tf_op jit(solution)/shard_map/ppermute | solution.py:698
  19.1 3.0 %collective-permute-start.6 = (f32[5,2,1,2880]{3,2,1,0:T(1,128)S(1)}, f32[5,2,1,2880]{3,2,1,0:T(1,128)S(1)}, u32[]{:S(2)}, u32[]{:S(2)}) collective-permute-start(f32[5,2,1,2880]{3,2,1,0:T(1,128)S(1)} %get-tuple-element.37), channel_id=1, source_target_pairs={{0,32},{64,96},{32,0},{96,64},{1,33},{65,97},{33,1},{97,65},{2,34}... | collective-permute-start | bytes 345608 | tf_op jit(solution)/shard_map/ppermute | solution.py:698
  22.8 1.0 shard_map.181.inside_ref
  24.4 1.1 collective-permute-done.5.refs_1_
  26.1 3.3 %shard_map.183._ = f32[23552,128]{1,0:T(8,128)S(1)} custom-call(f32[23,80,128]{2,1,0:T(8,128)S(1)} %shard_map.182.mine_ref), custom_call_target="tpu_custom_call" | custom-call | flops 8000000 | bytes 1048576 | tf_op jit(solution)/shard_map/pallas_call | solution.py:72
  29.4 12.5 %shard_map.184 = (f32[3072,128]{1,0:T(8,128)}, f32[23552,128]{1,0:T(8,128)S(1)}) custom-call(s32[32]{0:T(128)S(1)} %get-tuple-element.23.starts_any, s32[32]{0:T(128)S(1)} %copy-done.4, s32[23552]{0:T(1024)S(1)} %bitcast.20, f32[23,80,128]{2,1,0:T(8,128)S(1)} %collective-permute-done.8.other_ref, ...), custom_call_target="tpu_custom_call", output_to_operand_aliasing={{1}: (4, {})} | custom-call | flops 30000000 | bytes 1048576 | tf_op jit(solution)/shard_map/pallas_call | solution.py:72
  41.9 10.8 %all-to-all-start = ((f32[16,192,128]{2,1,0:T(8,128)}), f32[16,192,128]{2,1,0:T(8,128)S(1)}, u32[]{:S(2)}, u32[]{:S(2)}) async-start(f32[16,192,128]{2,1,0:T(8,128)} %bitcast.5), calls=%async_computation | async-start | bytes 3145728 | tf_op jit(solution)/shard_map/all_to_all | solution.py:764
  53.6 0.7 dynamic_slice.12.units_ref.units_any
  55.9 1.8 %copy-done.1 = f32[32,8,2880]{2,1,0:T(8,128)S(1)} copy-done((f32[32,8,2880]{2,1,0:T(8,128)S(1)}, f32[32,8,2880]{2,1,0:T(8,128)}, u32[]{:S(2)}) %copy-start.1) | copy-done | bytes 2949144
  57.8 7.8 %shard_map.177 = (s32[384]{0:T(512)S(1)}, f32[9,32,128]{2,1,0:T(8,128)S(1)}, f32[960,128]{1,0:T(8,128)S(1)}) custom-call(s32[1]{0:T(128)} %dynamic_slice.12.units_ref.units_any, s32[270]{0:T(512)S(1)} %dynamic-slice_reduce_fusion.owner_ref, s32[1152]{0:T(1024)S(1)} %get-tuple-element.45.rows_ref, s32[9,128]{1,0:T(8,128)S(1)} %get-tuple-element.44.sel_ref, ...), custom_call_target="tpu_custom_call" | custom-call | flops 20000000 | bytes 1048576 | tf_op jit(solution)/shard_map/pallas_call | solution.py:72
  65.7 12.1 %all-to-all-done = f32[16,192,128]{2,1,0:T(8,128)S(1)} async-done(((f32[16,192,128]{2,1,0:T(8,128)}), f32[16,192,128]{2,1,0:T(8,128)S(1)}, u32[]{:S(2)}, u32[]{:S(2)}) %all-to-all-start) | async-done | bytes 1572896 | tf_op jit(solution)/shard_map/all_to_all | solution.py:764
  77.8 6.1 %shard_map.185 = (f32[1,1,5,64,1080]{4,3,2,1,0:T(8,128)}, f32[2048,128]{1,0:T(8,128)}) custom-call(s32[1]{0:T(128)} %dynamic_slice.12.units_ref.units_any, s32[384]{0:T(512)S(1)} %get-tuple-element.24.table_any, f32[3072,128]{1,0:T(8,128)S(1)} %bitcast.16, f32[960,128]{1,0:T(8,128)S(1)} %get-tuple-element.40.coef_ref, ...), custom_call_target="tpu_custom_call" | custom-call | flops 40000000 | bytes 1048576 | tf_op jit(solution)/shard_map/pallas_call | solution.py:72
  84.1 7.4 %all-to-all-start.1 = ((f32[128,16,128]{2,1,0:T(8,128)}), f32[128,16,128]{2,1,0:T(8,128)S(1)}, u32[]{:S(2)}, u32[]{:S(2)}) async-start(f32[128,16,128]{2,1,0:T(8,128)} %bitcast.8), calls=%async_computation.1 | async-start | bytes 2097152 | tf_op jit(solution)/shard_map/all_to_all | solution.py:769
  91.6 19.1 %all-to-all-done.1 = f32[128,16,128]{2,1,0:T(8,128)S(1)} async-done(((f32[128,16,128]{2,1,0:T(8,128)}), f32[128,16,128]{2,1,0:T(8,128)S(1)}, u32[]{:S(2)}, u32[]{:S(2)}) %all-to-all-start.1) | async-done | bytes 1048608 | tf_op jit(solution)/shard_map/all_to_all | solution.py:769
  110.7 3.5 %shard_map.186 = f32[1,7,96,512]{3,2,1,0:T(8,128)} custom-call(f32[2048,128]{1,0:T(8,128)S(1)} %bitcast.18, f32[35]{0:T(128)S(1)} %reshape.55.yield_any, f32[14]{0:T(128)S(1)} %pad_maximum_fusion.rates_any, f32[1,512]{1,0:T(1,128)S(1)} %copy-done.9, bf16[512,512]{1,0:T(8,128)(2,1)S(1)} %copy-done.5, bf16[512,512]{1,0:T(8,128)(2,1)S(1)} %copy-done.6, ...), custom_call_target="tpu_custom_call" | custom-call | flops 2000000000 | bytes 1048576 | tf_op jit(solution)/shard_map/pallas_call | solution.py:72
  (55 shorter events, 4.6 us)
Async XLA Ops:
  0.6 55.1 %copy-start = (s32[32,270,1]{1,2,0:T(1,128)S(1)}, s32[32,270,1]{1,2,0:T(1,128)}, u32[]{:S(2)}) copy-start(s32[32,270,1]{1,2,0:T(1,128)} %param.28) | copy-start | bytes 103684
  0.6 8.6 %copy-start.2 = (s32[1,23040]{1,0:T(1,128)S(1)}, s32[1,23040]{1,0:T(1,128)}, u32[]{:S(2)}) copy-start(s32[1,23040]{1,0:T(1,128)} %order_ref.1) | copy-start | bytes 276484
  2.3 10.0 %collective-permute-start = (f32[6,8,2880]{2,1,0:T(8,128)S(1)}, f32[6,8,2880]{2,1,0:T(8,128)S(1)}, u32[]{:S(2)}, u32[]{:S(2)}) collective-permute-start(f32[6,8,2880]{2,1,0:T(8,128)S(1)} %get-tuple-element.30), channel_id=1, source_target_pairs={{0,1},{2,3},{4,5},{6,7},{8,9},{10,11},{12,13},{14,15},{16,17},{18,... | collective-permute-start | bytes 1658888 | tf_op jit(solution)/shard_map/ppermute | solution.py:698
  3.7 10.9 %collective-permute-start.1 = (f32[6,8,2880]{2,1,0:T(8,128)S(1)}, f32[6,8,2880]{2,1,0:T(8,128)S(1)}, u32[]{:S(2)}, u32[]{:S(2)}) collective-permute-start(f32[6,8,2880]{2,1,0:T(8,128)S(1)} %get-tuple-element.31), channel_id=1, source_target_pairs={{1,2},{3,4},{5,6},{7,8},{9,10},{11,12},{13,14},{15,16},{17,18},{19... | collective-permute-start | bytes 1658888 | tf_op jit(solution)/shard_map/ppermute | solution.py:698
  6.9 5.4 %collective-permute-start.2 = (f32[6,2,1,2880]{3,2,1,0:T(1,128)S(1)}, f32[6,2,1,2880]{3,2,1,0:T(1,128)S(1)}, u32[]{:S(2)}, u32[]{:S(2)}) collective-permute-start(f32[6,2,1,2880]{3,2,1,0:T(1,128)S(1)} %get-tuple-element.32), channel_id=1, source_target_pairs={{0,32},{64,96},{32,0},{96,64},{1,33},{65,97},{33,1},{97,65},{2,34}... | collective-permute-start | bytes 414728 | tf_op jit(solution)/shard_map/ppermute | solution.py:698
  8.6 3.7 %collective-permute-start.3 = (f32[6,2,1,2880]{3,2,1,0:T(1,128)S(1)}, f32[6,2,1,2880]{3,2,1,0:T(1,128)S(1)}, u32[]{:S(2)}, u32[]{:S(2)}) collective-permute-start(f32[6,2,1,2880]{3,2,1,0:T(1,128)S(1)} %get-tuple-element.33), channel_id=1, source_target_pairs={{32,64},{64,32},{33,65},{65,33},{34,66},{66,34},{35,67},{67,35},{3... | collective-permute-start | bytes 414728 | tf_op jit(solution)/shard_map/ppermute | solution.py:698
  15.4 9.0 %collective-permute-start.4 = (f32[5,8,2880]{2,1,0:T(8,128)S(1)}, f32[5,8,2880]{2,1,0:T(8,128)S(1)}, u32[]{:S(2)}, u32[]{:S(2)}) collective-permute-start(f32[5,8,2880]{2,1,0:T(8,128)S(1)} %get-tuple-element.35), channel_id=1, source_target_pairs={{0,1},{2,3},{4,5},{6,7},{8,9},{10,11},{12,13},{14,15},{16,17},{18,... | collective-permute-start | bytes 1382408 | tf_op jit(solution)/shard_map/ppermute | solution.py:698
  15.5 9.9 %collective-permute-start.5 = (f32[5,8,2880]{2,1,0:T(8,128)S(1)}, f32[5,8,2880]{2,1,0:T(8,128)S(1)}, u32[]{:S(2)}, u32[]{:S(2)}) collective-permute-start(f32[5,8,2880]{2,1,0:T(8,128)S(1)} %get-tuple-element.36), channel_id=1, source_target_pairs={{1,2},{3,4},{5,6},{7,8},{9,10},{11,12},{13,14},{15,16},{17,18},{19... | collective-permute-start | bytes 1382408 | tf_op jit(solution)/shard_map/ppermute | solution.py:698
  19.1 5.2 %collective-permute-start.6 = (f32[5,2,1,2880]{3,2,1,0:T(1,128)S(1)}, f32[5,2,1,2880]{3,2,1,0:T(1,128)S(1)}, u32[]{:S(2)}, u32[]{:S(2)}) collective-permute-start(f32[5,2,1,2880]{3,2,1,0:T(1,128)S(1)} %get-tuple-element.37), channel_id=1, source_target_pairs={{0,32},{64,96},{32,0},{96,64},{1,33},{65,97},{33,1},{97,65},{2,34}... | collective-permute-start | bytes 345608 | tf_op jit(solution)/shard_map/ppermute | solution.py:698
  22.2 2.2 %collective-permute-start.7 = (f32[5,2,1,2880]{3,2,1,0:T(1,128)S(1)}, f32[5,2,1,2880]{3,2,1,0:T(1,128)S(1)}, u32[]{:S(2)}, u32[]{:S(2)}) collective-permute-start(f32[5,2,1,2880]{3,2,1,0:T(1,128)S(1)} %get-tuple-element.38), channel_id=1, source_target_pairs={{32,64},{64,32},{33,65},{65,33},{34,66},{66,34},{35,67},{67,35},{3... | collective-permute-start | bytes 345608 | tf_op jit(solution)/shard_map/ppermute | solution.py:698
  26.0 3.4 %copy-start.4 = (s32[32]{0:T(128)S(1)}, s32[32]{0:T(128)}, u32[]{:S(2)}) copy-start(s32[32]{0:T(128)} %units_any.1) | copy-start | bytes 388
  26.0 3.4 %collective-permute-start.8 = (f32[23,80,128]{2,1,0:T(8,128)S(1)}, f32[23,80,128]{2,1,0:T(8,128)S(1)}, u32[]{:S(2)}, u32[]{:S(2)}) collective-permute-start(f32[23,80,128]{2,1,0:T(8,128)S(1)} %shard_map.182.mine_ref), channel_id=1, source_target_pairs={{0,1},{2,3},{4,5},{6,7},{8,9},{10,11},{12,13},{14,15},{16,17},{18,... | collective-permute-start | bytes 2826248 | tf_op jit(solution)/shard_map/ppermute | solution.py:698
  41.9 13.0 %copy-start.11 = (f32[5,64]{1,0:T(8,128)S(1)}, f32[5,64]{1,0:T(8,128)}, u32[]{:S(2)}) copy-start(f32[5,64]{1,0:T(8,128)} %param.21) | copy-start | bytes 3844
  41.9 35.9 %all-to-all-start = ((f32[16,192,128]{2,1,0:T(8,128)}), f32[16,192,128]{2,1,0:T(8,128)S(1)}, u32[]{:S(2)}, u32[]{:S(2)}) async-start(f32[16,192,128]{2,1,0:T(8,128)} %bitcast.5), calls=%async_computation | async-start | bytes 3145728 | tf_op jit(solution)/shard_map/all_to_all | solution.py:764
  55.9 1.9 %copy-start.1 = (f32[32,8,2880]{2,1,0:T(8,128)S(1)}, f32[32,8,2880]{2,1,0:T(8,128)}, u32[]{:S(2)}) copy-start(f32[32,8,2880]{2,1,0:T(8,128)} %param.22) | copy-start | bytes 8847364
  77.8 13.6 %copy-start.10 = (f32[7,5]{1,0:T(8,128)S(1)}, f32[7,5]{1,0:T(8,128)}, u32[]{:S(2)}) copy-start(f32[7,5]{1,0:T(8,128)} %param.23) | copy-start | bytes 424
  84.0 7.6 %copy-start.12 = (f32[7]{0:T(128)S(1)}, f32[7]{0:T(128)}, u32[]{:S(2)}) copy-start(f32[7]{0:T(128)} %param.25) | copy-start | bytes 88
  84.0 7.6 %copy-start.13 = (f32[7]{0:T(128)S(1)}, f32[7]{0:T(128)}, u32[]{:S(2)}) copy-start(f32[7]{0:T(128)} %param.24) | copy-start | bytes 88
  84.0 26.7 %copy-start.5 = (bf16[512,512]{1,0:T(8,128)(2,1)S(1)}, bf16[512,512]{1,0:T(8,128)(2,1)}, u32[]{:S(2)}) copy-start(bf16[512,512]{1,0:T(8,128)(2,1)} %constant.94.clone.fwd_high) | copy-start | bytes 1572868
  84.0 26.7 %copy-start.6 = (bf16[512,512]{1,0:T(8,128)(2,1)S(1)}, bf16[512,512]{1,0:T(8,128)(2,1)}, u32[]{:S(2)}) copy-start(bf16[512,512]{1,0:T(8,128)(2,1)} %constant.95.clone.fwd_low) | copy-start | bytes 1572868
  84.0 26.7 %copy-start.7 = (bf16[512,512]{1,0:T(8,128)(2,1)S(1)}, bf16[512,512]{1,0:T(8,128)(2,1)}, u32[]{:S(2)}) copy-start(bf16[512,512]{1,0:T(8,128)(2,1)} %constant.96.clone.inv_high) | copy-start | bytes 1572868
  84.0 26.7 %copy-start.8 = (bf16[512,512]{1,0:T(8,128)(2,1)S(1)}, bf16[512,512]{1,0:T(8,128)(2,1)}, u32[]{:S(2)}) copy-start(bf16[512,512]{1,0:T(8,128)(2,1)} %constant.97.clone.inv_low) | copy-start | bytes 1572868
  84.1 26.7 %copy-start.9 = (f32[1,512]{1,0:T(1,128)S(1)}, f32[1,512]{1,0:T(1,128)}, u32[]{:S(2)}) copy-start(f32[1,512]{1,0:T(1,128)} %constant.109.waves_ref) | copy-start | bytes 6148
  84.1 26.6 %all-to-all-start.1 = ((f32[128,16,128]{2,1,0:T(8,128)}), f32[128,16,128]{2,1,0:T(8,128)S(1)}, u32[]{:S(2)}, u32[]{:S(2)}) async-start(f32[128,16,128]{2,1,0:T(8,128)} %bitcast.8), calls=%async_computation.1 | async-start | bytes 2097152 | tf_op jit(solution)/shard_map/all_to_all | solution.py:769
  (1 other events, 0.7 us)

commit v15 on v14

--- a/solution.py
+++ b/solution.py
@@ -234,26 +234,28 @@
     )(density, inside, *winds[1:], *halo, *wind_halo)
 
 
-def places_kernel(units_ref, order_ref, place_ref, starts_ref):
-    def advance(owner, start):
-        starts_ref[owner] = start
-        return start + units_ref[owner]
-
-    lax.fori_loop(0, units_ref.shape[0], advance, jnp.int32(0))
+def places_kernel(units_any, order_ref, place_ref, starts_ref, units_ref, sem):
+    fetch = pltpu.make_async_copy(units_any, units_ref, sem)
+    fetch.start()
     order = order_ref[...]
-    lat = jnp.zeros_like(order)
-    for i in range(1, BAND_LATS):
-        lat = lat + (order >= i * NLON).astype(jnp.int32)
+    lat = ((order >> 6) * 1457) >> 16
     place_ref[:, :BAND_COLS] = order + lat * (LON_PAD - NLON)
     place_ref[:, BAND_COLS:] = jnp.zeros((1, ORDER_PAD - BAND_COLS), jnp.int32)
+    fetch.wait()
+
+    start = jnp.int32(0)
+    for owner in range(units_ref.shape[0]):
+        starts_ref[owner] = start
+        start = start + units_ref[owner]
 
 
 def list_places(units, order):
     places, starts = call(
         places_kernel,
         (on_chip((1, ORDER_PAD), jnp.int32), sds(units.shape, jnp.int32)),
-        [SMEM, VMEM],
+        [HBM, VMEM],
         (VMEM, SMEM),
+        [pltpu.SMEM(units.shape, jnp.int32), pltpu.SemaphoreType.DMA],
         flops=1_000_000,
     )(units, order)
     return places.reshape(-1), starts

time: 115 us -> 115 us (level)
    unnamed x28 -> x26, local copies, waits for them, and re-layouts: 2.57 us -> 1.92 us
where the time goes in v15:
time: 115 us; the launch traced here: 114 us
  Pallas kernels  39.3 us (34%)
  waiting for transfers between devices  36 us (31%)
  starting transfers between devices  32.6 us (28%)
  local copies, waits for them, and re-layouts  3.85 us (3%)
  between operations  1.66 us (1%)
    pallas_call x11, Pallas kernels, placed(): return run(*(place(x, spec) for x, spec in zip(args, in_specs)))  39.3 us
    all_to_all x1, waiting for transfers between devices, on_device(): lax.all_to_all(items.reshape(PEERS, ITEM_ROWS, LANES), ('band', 'lev'), 0...  19.1 us
    ppermute x9, starting transfers between devices, swap(): lax.ppermute(x, axis, [(i, i + 1) for i in lows] + [(i + 1, i) for i in l...  14.4 us
    all_to_all x1, waiting for transfers between devices, on_device(): lax.all_to_all(outgoing.reshape(16, PEER_ROWS, LANES), 'lev', 0, 0, axis_...  12.4 us
    all_to_all x1, starting transfers between devices, on_device(): lax.all_to_all(outgoing.reshape(16, PEER_ROWS, LANES), 'lev', 0, 0, axis_...  10.8 us
    all_to_all x1, starting transfers between devices, on_device(): lax.all_to_all(items.reshape(PEERS, ITEM_ROWS, LANES), ('band', 'lev'), 0...  7.39 us
    ppermute x9, waiting for transfers between devices, swap(): lax.ppermute(x, axis, [(i, i + 1) for i in lows] + [(i + 1, i) for i in l...  4.63 us
  transfers between devices with their start and end apart: 11, of which 5 were waited for; matrix products, arithmetic and copies ran while one was open for 2% of the time, Pallas kernels for 13%

profile of v15, /device:TPU:1, one launch (start us, length us, event | category | flops | bytes accessed | tf_op | source)
XLA Modules:
  0.0 114.1 jit_solution(7249811087943951132)
XLA Ops:
  0.7 1.6 %shard_map.178 = (f32[5,2,8,2880]{3,2,1,0:T(8,128)S(1)}, f32[2,8,2880]{2,1,0:T(8,128)S(1)}, f32[2,8,2880]{2,1,0:T(8,128)S(1)}, f32[2,8,2880]{2,1,0:T(8,128)S(1)}...) custom-call(f32[5,2,8,2880]{3,2,1,0:T(8,128)} %n_hbm.1, ...), custom_call_target="tpu_custom_call" | custom-call | flops 1000000 | bytes 1048576 | tf_op jit(solution)/shard_map/pallas_call | solution.py:72
  2.3 1.5 %collective-permute-start = (f32[6,8,2880]{2,1,0:T(8,128)S(1)}, f32[6,8,2880]{2,1,0:T(8,128)S(1)}, u32[]{:S(2)}, u32[]{:S(2)}) collective-permute-start(f32[6,8,2880]{2,1,0:T(8,128)S(1)} %get-tuple-element.30), channel_id=1, source_target_pairs={{0,1},{2,3},{4,5},{6,7},{8,9},{10,11},{12,13},{14,15},{16,17},{18,... | collective-permute-start | bytes 1658888 | tf_op jit(solution)/shard_map/ppermute | solution.py:700
  3.7 3.1 %collective-permute-start.1 = (f32[6,8,2880]{2,1,0:T(8,128)S(1)}, f32[6,8,2880]{2,1,0:T(8,128)S(1)}, u32[]{:S(2)}, u32[]{:S(2)}) collective-permute-start(f32[6,8,2880]{2,1,0:T(8,128)S(1)} %get-tuple-element.31), channel_id=1, source_target_pairs={{1,2},{3,4},{5,6},{7,8},{9,10},{11,12},{13,14},{15,16},{17,18},{19... | collective-permute-start | bytes 1658888 | tf_op jit(solution)/shard_map/ppermute | solution.py:700
  6.9 1.7 %collective-permute-start.2 = (f32[6,2,1,2880]{3,2,1,0:T(1,128)S(1)}, f32[6,2,1,2880]{3,2,1,0:T(1,128)S(1)}, u32[]{:S(2)}, u32[]{:S(2)}) collective-permute-start(f32[6,2,1,2880]{3,2,1,0:T(1,128)S(1)} %get-tuple-element.32), channel_id=1, source_target_pairs={{0,32},{64,96},{32,0},{96,64},{1,33},{65,97},{33,1},{97,65},{2,34}... | collective-permute-start | bytes 414728 | tf_op jit(solution)/shard_map/ppermute | solution.py:700
  8.6 0.7 collective-permute-start.3
  9.3 1.3 %shard_map.176 = (s32[1,23552]{1,0:T(1,128)S(1)}, s32[32]{0:T(128)S(1)}) custom-call(s32[32]{0:T(128)} %units_any.3, s32[1,23040]{1,0:T(1,128)S(1)} %copy-done.2), custom_call_target="tpu_custom_call" | custom-call | flops 1000000 | bytes 1048576 | tf_op jit(solution)/shard_map/pallas_call | solution.py:72
  10.6 1.0 shard_map.179.inside_ref
  11.6 3.0 %collective-permute-done.1.refs_1_.refs_5_ = f32[6,8,2880]{2,1,0:T(8,128)S(1)} collective-permute-done((f32[6,8,2880]{2,1,0:T(8,128)S(1)}, f32[6,8,2880]{2,1,0:T(8,128)S(1)}, u32[]{:S(2)}, u32[]{:S(2)}) %collective-permute-start.1) | collective-permute-done | bytes 552992 | tf_op jit(solution)/shard_map/ppermute | solution.py:700
  14.7 0.8 shard_map.180
  15.5 3.6 %collective-permute-start.5 = (f32[5,8,2880]{2,1,0:T(8,128)S(1)}, f32[5,8,2880]{2,1,0:T(8,128)S(1)}, u32[]{:S(2)}, u32[]{:S(2)}) collective-permute-start(f32[5,8,2880]{2,1,0:T(8,128)S(1)} %get-tuple-element.36), channel_id=1, source_target_pairs={{1,2},{3,4},{5,6},{7,8},{9,10},{11,12},{13,14},{15,16},{17,18},{19... | collective-permute-start | bytes 1382408 | tf_op jit(solution)/shard_map/ppermute | solution.py:700
  19.1 3.0 %collective-permute-start.6 = (f32[5,2,1,2880]{3,2,1,0:T(1,128)S(1)}, f32[5,2,1,2880]{3,2,1,0:T(1,128)S(1)}, u32[]{:S(2)}, u32[]{:S(2)}) collective-permute-start(f32[5,2,1,2880]{3,2,1,0:T(1,128)S(1)} %get-tuple-element.37), channel_id=1, source_target_pairs={{0,32},{64,96},{32,0},{96,64},{1,33},{65,97},{33,1},{97,65},{2,34}... | collective-permute-start | bytes 345608 | tf_op jit(solution)/shard_map/ppermute | solution.py:700
  22.2 0.7 collective-permute-start.7
  22.8 1.0 shard_map.181.inside_ref
  24.4 1.1 collective-permute-done.5.refs_1_
  26.1 3.3 %shard_map.183._ = f32[23552,128]{1,0:T(8,128)S(1)} custom-call(f32[23,80,128]{2,1,0:T(8,128)S(1)} %shard_map.182.mine_ref), custom_call_target="tpu_custom_call" | custom-call | flops 8000000 | bytes 1048576 | tf_op jit(solution)/shard_map/pallas_call | solution.py:72
  29.4 12.5 %shard_map.184 = (f32[3072,128]{1,0:T(8,128)}, f32[23552,128]{1,0:T(8,128)S(1)}) custom-call(s32[32]{0:T(128)S(1)} %get-tuple-element.23.starts_any, s32[32]{0:T(128)S(1)} %copy-done.3, s32[23552]{0:T(1024)S(1)} %bitcast.20, f32[23,80,128]{2,1,0:T(8,128)S(1)} %collective-permute-done.8.other_ref, ...), custom_call_target="tpu_custom_call", output_to_operand_aliasing={{1}: (4, {})} | custom-call | flops 30000000 | bytes 1048576 | tf_op jit(solution)/shard_map/pallas_call | solution.py:72
  41.9 10.8 %all-to-all-start = ((f32[16,192,128]{2,1,0:T(8,128)}), f32[16,192,128]{2,1,0:T(8,128)S(1)}, u32[]{:S(2)}, u32[]{:S(2)}) async-start(f32[16,192,128]{2,1,0:T(8,128)} %bitcast.5), calls=%async_computation | async-start | bytes 3145728 | tf_op jit(solution)/shard_map/all_to_all | solution.py:766
  55.8 1.8 %copy-done.1 = f32[32,8,2880]{2,1,0:T(8,128)S(1)} copy-done((f32[32,8,2880]{2,1,0:T(8,128)S(1)}, f32[32,8,2880]{2,1,0:T(8,128)}, u32[]{:S(2)}) %copy-start.1) | copy-done | bytes 2949144
  57.7 7.7 %shard_map.177 = (s32[384]{0:T(512)S(1)}, f32[9,32,128]{2,1,0:T(8,128)S(1)}, f32[960,128]{1,0:T(8,128)S(1)}) custom-call(s32[1]{0:T(128)} %dynamic_slice.12.units_ref.units_any, s32[270]{0:T(512)S(1)} %dynamic-slice_reduce_fusion.owner_ref, s32[1152]{0:T(1024)S(1)} %get-tuple-element.45.rows_ref, s32[9,128]{1,0:T(8,128)S(1)} %get-tuple-element.44.sel_ref, ...), custom_call_target="tpu_custom_call" | custom-call | flops 20000000 | bytes 1048576 | tf_op jit(solution)/shard_map/pallas_call | solution.py:72
  65.5 12.4 %all-to-all-done = f32[16,192,128]{2,1,0:T(8,128)S(1)} async-done(((f32[16,192,128]{2,1,0:T(8,128)}), f32[16,192,128]{2,1,0:T(8,128)S(1)}, u32[]{:S(2)}, u32[]{:S(2)}) %all-to-all-start) | async-done | bytes 1572896 | tf_op jit(solution)/shard_map/all_to_all | solution.py:766
  77.8 6.0 %shard_map.185 = (f32[1,1,5,64,1080]{4,3,2,1,0:T(8,128)}, f32[2048,128]{1,0:T(8,128)}) custom-call(s32[1]{0:T(128)} %dynamic_slice.12.units_ref.units_any, s32[384]{0:T(512)S(1)} %get-tuple-element.24.table_any, f32[3072,128]{1,0:T(8,128)S(1)} %bitcast.16, f32[960,128]{1,0:T(8,128)S(1)} %get-tuple-element.40.coef_ref, ...), custom_call_target="tpu_custom_call" | custom-call | flops 40000000 | bytes 1048576 | tf_op jit(solution)/shard_map/pallas_call | solution.py:72
  83.9 7.4 %all-to-all-start.1 = ((f32[128,16,128]{2,1,0:T(8,128)}), f32[128,16,128]{2,1,0:T(8,128)S(1)}, u32[]{:S(2)}, u32[]{:S(2)}) async-start(f32[128,16,128]{2,1,0:T(8,128)} %bitcast.8), calls=%async_computation.1 | async-start | bytes 2097152 | tf_op jit(solution)/shard_map/all_to_all | solution.py:771
  91.5 19.1 %all-to-all-done.1 = f32[128,16,128]{2,1,0:T(8,128)S(1)} async-done(((f32[128,16,128]{2,1,0:T(8,128)}), f32[128,16,128]{2,1,0:T(8,128)S(1)}, u32[]{:S(2)}, u32[]{:S(2)}) %all-to-all-start.1) | async-done | bytes 1048608 | tf_op jit(solution)/shard_map/all_to_all | solution.py:771
  110.6 3.5 %shard_map.186 = f32[1,7,96,512]{3,2,1,0:T(8,128)} custom-call(f32[2048,128]{1,0:T(8,128)S(1)} %bitcast.18, f32[35]{0:T(128)S(1)} %reshape.55.yield_any, f32[14]{0:T(128)S(1)} %pad_maximum_fusion.rates_any, f32[1,512]{1,0:T(1,128)S(1)} %copy-done.8, bf16[512,512]{1,0:T(8,128)(2,1)S(1)} %copy-done.4, bf16[512,512]{1,0:T(8,128)(2,1)S(1)} %copy-done.5, ...), custom_call_target="tpu_custom_call" | custom-call | flops 2000000000 | bytes 1048576 | tf_op jit(solution)/shard_map/pallas_call | solution.py:72
  (53 shorter events, 3.9 us)
Async XLA Ops:
  0.6 55.0 %copy-start = (s32[32,270,1]{1,2,0:T(1,128)S(1)}, s32[32,270,1]{1,2,0:T(1,128)}, u32[]{:S(2)}) copy-start(s32[32,270,1]{1,2,0:T(1,128)} %param.28) | copy-start | bytes 103684
  0.6 8.6 %copy-start.2 = (s32[1,23040]{1,0:T(1,128)S(1)}, s32[1,23040]{1,0:T(1,128)}, u32[]{:S(2)}) copy-start(s32[1,23040]{1,0:T(1,128)} %order_ref.1) | copy-start | bytes 276484
  2.3 9.3 %collective-permute-start = (f32[6,8,2880]{2,1,0:T(8,128)S(1)}, f32[6,8,2880]{2,1,0:T(8,128)S(1)}, u32[]{:S(2)}, u32[]{:S(2)}) collective-permute-start(f32[6,8,2880]{2,1,0:T(8,128)S(1)} %get-tuple-element.30), channel_id=1, source_target_pairs={{0,1},{2,3},{4,5},{6,7},{8,9},{10,11},{12,13},{14,15},{16,17},{18,... | collective-permute-start | bytes 1658888 | tf_op jit(solution)/shard_map/ppermute | solution.py:700
  3.7 10.9 %collective-permute-start.1 = (f32[6,8,2880]{2,1,0:T(8,128)S(1)}, f32[6,8,2880]{2,1,0:T(8,128)S(1)}, u32[]{:S(2)}, u32[]{:S(2)}) collective-permute-start(f32[6,8,2880]{2,1,0:T(8,128)S(1)} %get-tuple-element.31), channel_id=1, source_target_pairs={{1,2},{3,4},{5,6},{7,8},{9,10},{11,12},{13,14},{15,16},{17,18},{19... | collective-permute-start | bytes 1658888 | tf_op jit(solution)/shard_map/ppermute | solution.py:700
  6.9 4.7 %collective-permute-start.2 = (f32[6,2,1,2880]{3,2,1,0:T(1,128)S(1)}, f32[6,2,1,2880]{3,2,1,0:T(1,128)S(1)}, u32[]{:S(2)}, u32[]{:S(2)}) collective-permute-start(f32[6,2,1,2880]{3,2,1,0:T(1,128)S(1)} %get-tuple-element.32), channel_id=1, source_target_pairs={{0,32},{64,96},{32,0},{96,64},{1,33},{65,97},{33,1},{97,65},{2,34}... | collective-permute-start | bytes 414728 | tf_op jit(solution)/shard_map/ppermute | solution.py:700
  8.6 3.0 %collective-permute-start.3 = (f32[6,2,1,2880]{3,2,1,0:T(1,128)S(1)}, f32[6,2,1,2880]{3,2,1,0:T(1,128)S(1)}, u32[]{:S(2)}, u32[]{:S(2)}) collective-permute-start(f32[6,2,1,2880]{3,2,1,0:T(1,128)S(1)} %get-tuple-element.33), channel_id=1, source_target_pairs={{32,64},{64,32},{33,65},{65,33},{34,66},{66,34},{35,67},{67,35},{3... | collective-permute-start | bytes 414728 | tf_op jit(solution)/shard_map/ppermute | solution.py:700
  15.4 9.0 %collective-permute-start.4 = (f32[5,8,2880]{2,1,0:T(8,128)S(1)}, f32[5,8,2880]{2,1,0:T(8,128)S(1)}, u32[]{:S(2)}, u32[]{:S(2)}) collective-permute-start(f32[5,8,2880]{2,1,0:T(8,128)S(1)} %get-tuple-element.35), channel_id=1, source_target_pairs={{0,1},{2,3},{4,5},{6,7},{8,9},{10,11},{12,13},{14,15},{16,17},{18,... | collective-permute-start | bytes 1382408 | tf_op jit(solution)/shard_map/ppermute | solution.py:700
  15.5 9.9 %collective-permute-start.5 = (f32[5,8,2880]{2,1,0:T(8,128)S(1)}, f32[5,8,2880]{2,1,0:T(8,128)S(1)}, u32[]{:S(2)}, u32[]{:S(2)}) collective-permute-start(f32[5,8,2880]{2,1,0:T(8,128)S(1)} %get-tuple-element.36), channel_id=1, source_target_pairs={{1,2},{3,4},{5,6},{7,8},{9,10},{11,12},{13,14},{15,16},{17,18},{19... | collective-permute-start | bytes 1382408 | tf_op jit(solution)/shard_map/ppermute | solution.py:700
  19.1 5.2 %collective-permute-start.6 = (f32[5,2,1,2880]{3,2,1,0:T(1,128)S(1)}, f32[5,2,1,2880]{3,2,1,0:T(1,128)S(1)}, u32[]{:S(2)}, u32[]{:S(2)}) collective-permute-start(f32[5,2,1,2880]{3,2,1,0:T(1,128)S(1)} %get-tuple-element.37), channel_id=1, source_target_pairs={{0,32},{64,96},{32,0},{96,64},{1,33},{65,97},{33,1},{97,65},{2,34}... | collective-permute-start | bytes 345608 | tf_op jit(solution)/shard_map/ppermute | solution.py:700
  22.2 2.2 %collective-permute-start.7 = (f32[5,2,1,2880]{3,2,1,0:T(1,128)S(1)}, f32[5,2,1,2880]{3,2,1,0:T(1,128)S(1)}, u32[]{:S(2)}, u32[]{:S(2)}) collective-permute-start(f32[5,2,1,2880]{3,2,1,0:T(1,128)S(1)} %get-tuple-element.38), channel_id=1, source_target_pairs={{32,64},{64,32},{33,65},{65,33},{34,66},{66,34},{35,67},{67,35},{3... | collective-permute-start | bytes 345608 | tf_op jit(solution)/shard_map/ppermute | solution.py:700
  26.0 3.4 %copy-start.3 = (s32[32]{0:T(128)S(1)}, s32[32]{0:T(128)}, u32[]{:S(2)}) copy-start(s32[32]{0:T(128)} %units_any.3) | copy-start | bytes 388
  26.0 3.4 %collective-permute-start.8 = (f32[23,80,128]{2,1,0:T(8,128)S(1)}, f32[23,80,128]{2,1,0:T(8,128)S(1)}, u32[]{:S(2)}, u32[]{:S(2)}) collective-permute-start(f32[23,80,128]{2,1,0:T(8,128)S(1)} %shard_map.182.mine_ref), channel_id=1, source_target_pairs={{0,1},{2,3},{4,5},{6,7},{8,9},{10,11},{12,13},{14,15},{16,17},{18,... | collective-permute-start | bytes 2826248 | tf_op jit(solution)/shard_map/ppermute | solution.py:700
  41.9 12.9 %copy-start.10 = (f32[5,64]{1,0:T(8,128)S(1)}, f32[5,64]{1,0:T(8,128)}, u32[]{:S(2)}) copy-start(f32[5,64]{1,0:T(8,128)} %param.21) | copy-start | bytes 3844
  41.9 35.9 %all-to-all-start = ((f32[16,192,128]{2,1,0:T(8,128)}), f32[16,192,128]{2,1,0:T(8,128)S(1)}, u32[]{:S(2)}, u32[]{:S(2)}) async-start(f32[16,192,128]{2,1,0:T(8,128)} %bitcast.5), calls=%async_computation | async-start | bytes 3145728 | tf_op jit(solution)/shard_map/all_to_all | solution.py:766
  55.8 1.9 %copy-start.1 = (f32[32,8,2880]{2,1,0:T(8,128)S(1)}, f32[32,8,2880]{2,1,0:T(8,128)}, u32[]{:S(2)}) copy-start(f32[32,8,2880]{2,1,0:T(8,128)} %param.22) | copy-start | bytes 8847364
  77.8 13.5 %copy-start.9 = (f32[7,5]{1,0:T(8,128)S(1)}, f32[7,5]{1,0:T(8,128)}, u32[]{:S(2)}) copy-start(f32[7,5]{1,0:T(8,128)} %param.23) | copy-start | bytes 424
  83.8 7.6 %copy-start.11 = (f32[7]{0:T(128)S(1)}, f32[7]{0:T(128)}, u32[]{:S(2)}) copy-start(f32[7]{0:T(128)} %param.25) | copy-start | bytes 88
  83.9 7.6 %copy-start.12 = (f32[7]{0:T(128)S(1)}, f32[7]{0:T(128)}, u32[]{:S(2)}) copy-start(f32[7]{0:T(128)} %param.24) | copy-start | bytes 88
  83.9 26.7 %copy-start.4 = (bf16[512,512]{1,0:T(8,128)(2,1)S(1)}, bf16[512,512]{1,0:T(8,128)(2,1)}, u32[]{:S(2)}) copy-start(bf16[512,512]{1,0:T(8,128)(2,1)} %constant.94.clone.fwd_high) | copy-start | bytes 1572868
  83.9 26.7 %copy-start.5 = (bf16[512,512]{1,0:T(8,128)(2,1)S(1)}, bf16[512,512]{1,0:T(8,128)(2,1)}, u32[]{:S(2)}) copy-start(bf16[512,512]{1,0:T(8,128)(2,1)} %constant.95.clone.fwd_low) | copy-start | bytes 1572868
  83.9 26.7 %copy-start.6 = (bf16[512,512]{1,0:T(8,128)(2,1)S(1)}, bf16[512,512]{1,0:T(8,128)(2,1)}, u32[]{:S(2)}) copy-start(bf16[512,512]{1,0:T(8,128)(2,1)} %constant.96.clone.inv_high) | copy-start | bytes 1572868
  83.9 26.7 %copy-start.7 = (bf16[512,512]{1,0:T(8,128)(2,1)S(1)}, bf16[512,512]{1,0:T(8,128)(2,1)}, u32[]{:S(2)}) copy-start(bf16[512,512]{1,0:T(8,128)(2,1)} %constant.97.clone.inv_low) | copy-start | bytes 1572868
  83.9 26.7 %copy-start.8 = (f32[1,512]{1,0:T(1,128)S(1)}, f32[1,512]{1,0:T(1,128)}, u32[]{:S(2)}) copy-start(f32[1,512]{1,0:T(1,128)} %constant.109.waves_ref) | copy-start | bytes 6148
  83.9 26.6 %all-to-all-start.1 = ((f32[128,16,128]{2,1,0:T(8,128)}), f32[128,16,128]{2,1,0:T(8,128)S(1)}, u32[]{:S(2)}, u32[]{:S(2)}) async-start(f32[128,16,128]{2,1,0:T(8,128)} %bitcast.8), calls=%async_computation.1 | async-start | bytes 2097152 | tf_op jit(solution)/shard_map/all_to_all | solution.py:771
